TPU v7x, 32 devices: a whole 2x2x4 slice. The times are simulated.
32 devices in a mesh: gz: 8 (over z, y), gy: 4 (over x, core).
Axes of the slice: x: 2, y: 2, z: 4, core: 2. Of those that a mesh axis runs over, the one named last changes fastest.
Arguments:
- right_side: float32 [8, 16, 256, 512], P(None, 'gz', 'gy'), may hold values from -8 to 8
- diagonal: float32 [16, 256, 512], P('gz', 'gy'), may hold values from 0.1 to 4
Outputs:
- solution: float32 [8, 16, 256, 512], P(None, 'gz', 'gy')
- hessenberg: float32 [24, 32], replicated
All inputs are finite; a program needn't handle non-finite values.
Results may differ from a plain program's by a relative error of at most 0.0003.
Values sent between devices are 32-bit elements; how exact they have to be, the bound alone decides.
No kernel may reach another device: no remote copies, remote signals or barrier semaphores. Data moves between devices by JAX's collectives and lax.ppermute only.
A program may use at most 64 MiB of HBM per device.

v0:
```python
import jax
import jax.numpy as jnp
from jax import lax
from jax.sharding import PartitionSpec as P

ITERS = 3


def extended(array, sides, width):
    for axis, dim in sides:
        peers, length = (lax.axis_size(axis), array.shape[dim])
        up = [(i, (i + 1) % peers) for i in range(peers - 1)]
        down = [(j, i) for i, j in up]
        last = lax.slice_in_dim(array, length - width, length, axis=dim)
        leading = lax.slice_in_dim(array, 0, width, axis=dim)
        before = lax.ppermute(last, axis, up)
        after = lax.ppermute(leading, axis, down)
        array = jnp.concatenate([before, array, after], axis=dim)
    return array


def stencil(padded, field, diagonal):
    padded = jnp.pad(padded, ((0, 0), (0, 0), (0, 0), (1, 1)))
    beside = padded[:, 2:, 1:-1, 1:-1] + padded[:, :-2, 1:-1, 1:-1]
    beside = beside + padded[:, 1:-1, 2:, 1:-1] + padded[:, 1:-1, :-2, 1:-1]
    beside = beside + padded[:, 1:-1, 1:-1, 2:] + padded[:, 1:-1, 1:-1, :-2]
    return (6.0 + diagonal)[None] * field - beside


def apply_op(field, diagonal):
    padded = extended(field, (("gz", 1), ("gy", 2)), 1)
    return stencil(padded, field, diagonal)


def inner(left, right):
    return jnp.dot(left, right.T, precision=lax.Precision.HIGHEST)


def body(right_side, diagonal):
    shape = right_side.shape
    blocks_n = shape[0]
    flat_rhs = right_side.reshape(blocks_n, -1)
    lower0 = jnp.linalg.cholesky(lax.psum(inner(flat_rhs, flat_rhs), ("gz", "gy")))
    basis = [jax.scipy.linalg.solve_triangular(lower0, flat_rhs, lower=True)]
    rows_out = []
    work = apply_op(basis[0].reshape(shape), diagonal).reshape(blocks_n, -1)
    for step in range(ITERS):
        local = jnp.stack([inner(work, vec) for vec in basis], axis=0)
        coeff, gram_work = lax.psum((local, inner(work, work)), ("gz", "gy"))
        gram = gram_work
        for index in range(step + 1):
            gram = gram - jnp.dot(coeff[index], coeff[index].T, precision=lax.Precision.HIGHEST)
        reduced = work
        for index in range(step + 1):
            reduced = reduced - jnp.dot(coeff[index], basis[index], precision=lax.Precision.HIGHEST)
        more = step + 1 < ITERS
        lower = jnp.linalg.cholesky(gram)
        basis.append(jax.scipy.linalg.solve_triangular(lower, reduced, lower=True))
        if more:
            work = apply_op(basis[-1].reshape(shape), diagonal).reshape(blocks_n, -1)
        pieces = [coeff[index] for index in range(step + 1)]
        pieces = (
            pieces + [lower] + [jnp.zeros((blocks_n, blocks_n), jnp.float32)] * (ITERS - 1 - step)
        )
        rows_out.append(jnp.concatenate(pieces, axis=1))
    hessenberg = jnp.concatenate(rows_out, axis=0)
    normal = jnp.dot(hessenberg, hessenberg.T, precision=lax.Precision.HIGHEST)
    factor = jnp.linalg.cholesky(normal)
    target = jnp.dot(hessenberg[:, :blocks_n], lower0.T, precision=lax.Precision.HIGHEST)
    coeffs = jax.scipy.linalg.cho_solve((factor, True), target)
    stacked = jnp.concatenate(basis[:ITERS], axis=0)
    solution = jnp.dot(coeffs.T, stacked, precision=lax.Precision.HIGHEST)
    return (solution.reshape(shape), hessenberg)


def solution(mesh):
    in_specs = (P(None, "gz", "gy", None), P("gz", "gy", None))
    out_specs = (P(None, "gz", "gy", None), P())
    return jax.shard_map(body, mesh=mesh, in_specs=in_specs, out_specs=out_specs, check_vma=False)
```

profile of v0, /device:TPU:0, one launch (start us, length us, event | category | flops | bytes accessed | tf_op | source)
XLA Modules:
  0.0 452.4 jit_solution(8485363738929407699)
XLA Ops:
  0.6 8.2 %fusion.21 = f32[8,8]{0,1:T(8,128)S(1)} fusion(f32[8,2,64,512]{3,2,1,0:T(8,128)} %param.5), kind=kOutput, calls=%fused_computation.68 | convolution fusion | flops 50331648 | bytes 2097408 | tf_op jit(solution)/shard_map/dot_general | solution.py:36
  8.9 42.0 %psum.49 = f32[8,8]{0,1:T(8,128)S(1)} all-reduce(f32[8,8]{0,1:T(8,128)S(1)} %fusion.21), channel_id=1, replica_groups=mesh['gz'=8,'gy'=4] {'gz','gy'}, use_global_device_ids=true, to_apply=%region_0.0 | all-reduce | flops 64 | bytes 512 | tf_op jit(solution)/shard_map/psum | solution.py:43
  58.2 5.0 %collective-permute-start.1 = (f32[8,1,64,512]{3,0,2,1:T(8,128)S(1)}, f32[8,1,64,512]{3,0,2,1:T(8,128)S(1)}, u32[]{:S(2)}, u32[]{:S(2)}) collective-permute-start(f32[8,1,64,512]{3,0,2,1:T(8,128)S(1)} %get-tuple-element.26), channel_id=1, source_target_pairs={{0,4},{4,8},{8,12},{12,16},{16,20},{20,24},{24,28},{1,5},{5,9},{9,... | collective-permute-start | bytes 3145736 | tf_op jit(solution)/shard_map/ppermute | solution.py:16
  63.2 19.7 %collective-permute-done = f32[8,1,64,512]{3,0,2,1:T(8,128)S(1)} collective-permute-done((f32[8,1,64,512]{3,0,2,1:T(8,128)S(1)}, f32[8,1,64,512]{3,0,2,1:T(8,128)S(1)}, u32[]{:S(2)}, u32[]{:S(2)}) %collective-permute-start) | collective-permute-done | bytes 1048608 | tf_op jit(solution)/shard_map/ppermute | solution.py:17
  82.9 22.2 %collective-permute-done.1 = f32[8,1,64,512]{3,0,2,1:T(8,128)S(1)} collective-permute-done((f32[8,1,64,512]{3,0,2,1:T(8,128)S(1)}, f32[8,1,64,512]{3,0,2,1:T(8,128)S(1)}, u32[]{:S(2)}, u32[]{:S(2)}) %collective-permute-start.1) | collective-permute-done | bytes 1048608 | tf_op jit(solution)/shard_map/ppermute | solution.py:16
  110.3 3.9 select_maximum_fusion.8
  116.3 4.6 %convolution_bitcast_fusion.7 = f32[8,8]{0,1:T(8,128)S(1)} fusion(f32[8,2,64,512]{3,0,2,1:T(8,128)S(1)} %fusion.15), kind=kOutput, calls=%fused_computation.79 | convolution fusion | flops 50331648 | bytes 2097408 | tf_op jit(solution)/shard_map/dot_general | solution.py:36
  120.9 4.9 %fusion.55 = f32[8,8]{1,0:T(8,128)S(1)} fusion(f32[8,65536]{1,0:T(8,128)S(1)} %bitcast.140, f32[8,65536]{1,0:T(8,128)S(1)} %fusion.36), kind=kOutput, calls=%fused_computation.154 | convolution fusion | flops 50331648 | bytes 4194560 | tf_op jit(solution)/shard_map/dot_general | solution.py:36
  125.8 43.6 %all-reduce.5 = (f32[8,8]{1,0:T(8,128)S(1)}, f32[8,8]{0,1:T(8,128)S(1)}) all-reduce(f32[8,8]{1,0:T(8,128)S(1)} %fusion.55, f32[8,8]{0,1:T(8,128)S(1)} %convolution_bitcast_fusion.7), channel_id=1, replica_groups=mesh['gz'=8,'gy'=4] {'gz','gy'}, use_global_device_ids=true, to_apply=%region_3.6 | all-reduce | flops 128 | bytes 1024 | tf_op jit(solution)/shard_map/psum | solution.py:49
  169.5 4.7 %convolution_subtract_fusion.2 = f32[8,65536]{1,0:T(8,128)} fusion(f32[8,65536]{1,0:T(8,128)} %bitcast.141, f32[8,8]{1,0:T(8,128)S(1)} %get-tuple-element.10, f32[8,65536]{1,0:T(8,128)S(1)} %fusion.36), kind=kOutput, calls=%fused_computation.2 | convolution fusion | flops 50855936 | bytes 6291712 | tf_op jit(solution)/shard_map/dot_general | solution.py:55
  177.0 3.5 fusion.34
  182.0 4.9 %collective-permute-start.5 = (f32[8,1,64,512]{3,0,2,1:T(8,128)S(1)}, f32[8,1,64,512]{3,0,2,1:T(8,128)S(1)}, u32[]{:S(2)}, u32[]{:S(2)}) collective-permute-start(f32[8,1,64,512]{3,0,2,1:T(8,128)S(1)} %get-tuple-element.24), channel_id=1, source_target_pairs={{0,4},{4,8},{8,12},{12,16},{16,20},{20,24},{24,28},{1,5},{5,9},{9,... | collective-permute-start | bytes 3145736 | tf_op jit(solution)/shard_map/ppermute | solution.py:16
  186.9 19.8 %collective-permute-done.4 = f32[8,1,64,512]{3,0,2,1:T(8,128)S(1)} collective-permute-done((f32[8,1,64,512]{3,0,2,1:T(8,128)S(1)}, f32[8,1,64,512]{3,0,2,1:T(8,128)S(1)}, u32[]{:S(2)}, u32[]{:S(2)}) %collective-permute-start.4) | collective-permute-done | bytes 1048608 | tf_op jit(solution)/shard_map/ppermute | solution.py:17
  206.7 21.8 %collective-permute-done.5 = f32[8,1,64,512]{3,0,2,1:T(8,128)S(1)} collective-permute-done((f32[8,1,64,512]{3,0,2,1:T(8,128)S(1)}, f32[8,1,64,512]{3,0,2,1:T(8,128)S(1)}, u32[]{:S(2)}, u32[]{:S(2)}) %collective-permute-start.5) | collective-permute-done | bytes 1048608 | tf_op jit(solution)/shard_map/ppermute | solution.py:16
  229.8 3.4 collective-permute-start.7
  233.7 3.9 select_maximum_fusion.4
  239.8 4.9 %convolution_bitcast_fusion.6 = f32[1,8,8]{2,1,0:T(8,128)S(1)} fusion(f32[8,65536]{1,0:T(8,128)S(1)} %bitcast.137, f32[8,65536]{1,0:T(8,128)S(1)} %fusion.36), kind=kOutput, calls=%fused_computation.78 | convolution fusion | flops 50331648 | bytes 4194560 | tf_op jit(solution)/shard_map/dot_general | solution.py:36
  244.6 4.9 %convolution_bitcast_fusion.5 = f32[1,8,8]{2,1,0:T(8,128)S(1)} fusion(f32[8,65536]{1,0:T(8,128)S(1)} %bitcast.138, f32[8,65536]{1,0:T(8,128)S(1)} %fusion.34), kind=kOutput, calls=%fused_computation.77 | convolution fusion | flops 50331648 | bytes 4194560 | tf_op jit(solution)/shard_map/dot_general | solution.py:36
  249.6 4.6 %convolution_bitcast_fusion.4 = f32[8,8]{0,1:T(8,128)S(1)} fusion(f32[8,2,64,512]{3,0,2,1:T(8,128)S(1)} %fusion.11), kind=kOutput, calls=%fused_computation.76 | convolution fusion | flops 50331648 | bytes 2097408 | tf_op jit(solution)/shard_map/dot_general | solution.py:36
  254.1 43.2 %all-reduce.4 = (f32[2,8,8]{2,1,0:T(8,128)S(1)}, f32[8,8]{0,1:T(8,128)S(1)}) all-reduce(f32[2,8,8]{2,1,0:T(8,128)S(1)} %pad_maximum_fusion.34, f32[8,8]{0,1:T(8,128)S(1)} %convolution_bitcast_fusion.4), channel_id=1, replica_groups=mesh['gz'=8,'gy'=4] {'gz','gy'}, use_global_device_ids=true, to_apply=%region_5.8 | all-reduce | flops 192 | bytes 1536 | tf_op jit(solution)/shard_map/psum | solution.py:49
  297.4 4.7 %convolution_subtract_fusion.1 = f32[8,65536]{1,0:T(8,128)} fusion(f32[8,65536]{1,0:T(8,128)} %bitcast.139, f32[8,65536]{1,0:T(8,128)S(1)} %fusion.36, f32[2,8,8]{2,1,0:T(8,128)S(1)} %get-tuple-element.8), kind=kOutput, calls=%fused_computation.1 | convolution fusion | flops 50855936 | bytes 6295552 | tf_op jit(solution)/shard_map/dot_general | solution.py:55
  305.1 4.1 convolution_subtract_fusion
  312.7 4.9 %collective-permute-start.9 = (f32[8,1,64,512]{3,0,2,1:T(8,128)S(1)}, f32[8,1,64,512]{3,0,2,1:T(8,128)S(1)}, u32[]{:S(2)}, u32[]{:S(2)}) collective-permute-start(f32[8,1,64,512]{3,0,2,1:T(8,128)S(1)} %get-tuple-element.22), channel_id=1, source_target_pairs={{0,4},{4,8},{8,12},{12,16},{16,20},{20,24},{24,28},{1,5},{5,9},{9,... | collective-permute-start | bytes 3145736 | tf_op jit(solution)/shard_map/ppermute | solution.py:16
  317.6 19.8 %collective-permute-done.8 = f32[8,1,64,512]{3,0,2,1:T(8,128)S(1)} collective-permute-done((f32[8,1,64,512]{3,0,2,1:T(8,128)S(1)}, f32[8,1,64,512]{3,0,2,1:T(8,128)S(1)}, u32[]{:S(2)}, u32[]{:S(2)}) %collective-permute-start.8) | collective-permute-done | bytes 1048608 | tf_op jit(solution)/shard_map/ppermute | solution.py:17
  337.3 21.8 %collective-permute-done.9 = f32[8,1,64,512]{3,0,2,1:T(8,128)S(1)} collective-permute-done((f32[8,1,64,512]{3,0,2,1:T(8,128)S(1)}, f32[8,1,64,512]{3,0,2,1:T(8,128)S(1)}, u32[]{:S(2)}, u32[]{:S(2)}) %collective-permute-start.9) | collective-permute-done | bytes 1048608 | tf_op jit(solution)/shard_map/ppermute | solution.py:16
  364.4 3.9 select_maximum_fusion
  370.6 4.9 %convolution_bitcast_fusion.3 = f32[1,8,8]{2,1,0:T(8,128)S(1)} fusion(f32[8,65536]{1,0:T(8,128)S(1)} %bitcast.134, f32[8,65536]{1,0:T(8,128)S(1)} %fusion.36), kind=kOutput, calls=%fused_computation.74 | convolution fusion | flops 50331648 | bytes 4194560 | tf_op jit(solution)/shard_map/dot_general | solution.py:36
  375.5 4.9 %convolution_bitcast_fusion.2 = f32[1,8,8]{2,1,0:T(8,128)S(1)} fusion(f32[8,65536]{1,0:T(8,128)S(1)} %bitcast.135, f32[8,65536]{1,0:T(8,128)S(1)} %copy-done.1), kind=kOutput, calls=%fused_computation.73 | convolution fusion | flops 50331648 | bytes 4194560 | tf_op jit(solution)/shard_map/dot_general | solution.py:36
  380.4 4.9 %convolution_bitcast_fusion.1 = f32[1,8,8]{2,1,0:T(8,128)S(1)} fusion(f32[8,65536]{1,0:T(8,128)S(1)} %bitcast.136, f32[8,65536]{1,0:T(8,128)S(1)} %fusion.32), kind=kOutput, calls=%fused_computation.72 | convolution fusion | flops 50331648 | bytes 4194560 | tf_op jit(solution)/shard_map/dot_general | solution.py:36
  385.3 4.6 %convolution_bitcast_fusion = f32[8,8]{0,1:T(8,128)S(1)} fusion(f32[8,2,64,512]{3,0,2,1:T(8,128)S(1)} %fusion.7), kind=kOutput, calls=%fused_computation.71 | convolution fusion | flops 50331648 | bytes 2097408 | tf_op jit(solution)/shard_map/dot_general | solution.py:36
  389.9 44.3 %all-reduce.3 = (f32[8,8]{0,1:T(8,128)S(1)}, f32[3,8,8]{2,1,0:T(8,128)S(1)}) all-reduce(f32[8,8]{0,1:T(8,128)S(1)} %convolution_bitcast_fusion, f32[3,8,8]{2,1,0:T(8,128)S(1)} %pad_maximum_fusion.33), channel_id=1, replica_groups=mesh['gz'=8,'gy'=4] {'gz','gy'}, use_global_device_ids=true, to_apply=%region_8.11 | all-reduce | flops 256 | bytes 2048 | tf_op jit(solution)/shard_map/psum | solution.py:49
  443.6 5.9 %fusion = f32[8,65536]{1,0:T(8,128)S(1)} fusion(f32[24,8]{1,0:T(8,128)S(1)} %fusion.27, f32[8,65536]{1,0:T(8,128)} %copy-done.2, f32[8,65536]{1,0:T(8,128)} %copy-done, f32[8,65536]{1,0:T(8,128)S(1)} %fusion.36), kind=kOutput, calls=%fused_computation.5 | convolution fusion | flops 154140672 | bytes 8389376 | tf_op jit(solution)/shard_map/dot_general | solution.py:72
  (96 shorter events, 48.7 us)
Async XLA Ops:
  0.6 52.9 %copy-start.5 = (f32[8,2,64,512]{3,2,1,0:T(8,128)S(1)}, f32[8,2,64,512]{3,2,1,0:T(8,128)}, u32[]{:S(2)}) copy-start(f32[8,2,64,512]{3,2,1,0:T(8,128)} %param.5) | copy-start | bytes 6291460
  56.9 26.0 %collective-permute-start = (f32[8,1,64,512]{3,0,2,1:T(8,128)S(1)}, f32[8,1,64,512]{3,0,2,1:T(8,128)S(1)}, u32[]{:S(2)}, u32[]{:S(2)}) collective-permute-start(f32[8,1,64,512]{3,0,2,1:T(8,128)S(1)} %get-tuple-element.27), channel_id=1, source_target_pairs={{4,0},{8,4},{12,8},{16,12},{20,16},{24,20},{28,24},{5,1},{9,5},{13... | collective-permute-start | bytes 3145736 | tf_op jit(solution)/shard_map/ppermute | solution.py:17
  58.2 51.5 %copy-start.6 = (f32[2,64,512]{2,1,0:T(8,128)S(1)}, f32[2,64,512]{2,1,0:T(8,128)}, u32[]{:S(2)}) copy-start(f32[2,64,512]{2,1,0:T(8,128)} %param.6) | copy-start | bytes 786436
  58.2 46.9 %collective-permute-start.1 = (f32[8,1,64,512]{3,0,2,1:T(8,128)S(1)}, f32[8,1,64,512]{3,0,2,1:T(8,128)S(1)}, u32[]{:S(2)}, u32[]{:S(2)}) collective-permute-start(f32[8,1,64,512]{3,0,2,1:T(8,128)S(1)} %get-tuple-element.26), channel_id=1, source_target_pairs={{0,4},{4,8},{8,12},{12,16},{16,20},{20,24},{24,28},{1,5},{5,9},{9,... | collective-permute-start | bytes 3145736 | tf_op jit(solution)/shard_map/ppermute | solution.py:16
  105.1 4.6 %collective-permute-start.2 = (f32[8,4,1,512]{3,0,2,1:T(8,128)S(1)}, f32[8,4,1,512]{3,0,2,1:T(8,128)S(1)}, u32[]{:S(2)}, u32[]{:S(2)}) collective-permute-start(f32[8,4,1,512]{3,0,2,1:T(8,128)S(1)} %get-tuple-element.21), channel_id=1, source_target_pairs={{1,0},{2,1},{3,2},{5,4},{6,5},{7,6},{9,8},{10,9},{11,10},{13,12},{... | collective-permute-start | bytes 196616 | tf_op jit(solution)/shard_map/ppermute | solution.py:17
  106.4 3.9 collective-permute-start.3
  116.3 4.6 %copy-start.4 = (f32[8,2,64,512]{3,0,2,1:T(8,128)}, f32[8,2,64,512]{3,0,2,1:T(8,128)S(1)}, u32[]{:S(2)}) copy-start(f32[8,2,64,512]{3,0,2,1:T(8,128)S(1)} %fusion.15) | copy-start | bytes 6291460
  180.5 64.1 %copy-start = (f32[8,65536]{1,0:T(8,128)}, f32[8,65536]{1,0:T(8,128)S(1)}, u32[]{:S(2)}) copy-start(f32[8,65536]{1,0:T(8,128)S(1)} %fusion.34) | copy-start | bytes 6291460
  180.7 26.0 %collective-permute-start.4 = (f32[8,1,64,512]{3,0,2,1:T(8,128)S(1)}, f32[8,1,64,512]{3,0,2,1:T(8,128)S(1)}, u32[]{:S(2)}, u32[]{:S(2)}) collective-permute-start(f32[8,1,64,512]{3,0,2,1:T(8,128)S(1)} %get-tuple-element.25), channel_id=1, source_target_pairs={{4,0},{8,4},{12,8},{16,12},{20,16},{24,20},{28,24},{5,1},{9,5},{13... | collective-permute-start | bytes 3145736 | tf_op jit(solution)/shard_map/ppermute | solution.py:17
  182.0 46.5 %collective-permute-start.5 = (f32[8,1,64,512]{3,0,2,1:T(8,128)S(1)}, f32[8,1,64,512]{3,0,2,1:T(8,128)S(1)}, u32[]{:S(2)}, u32[]{:S(2)}) collective-permute-start(f32[8,1,64,512]{3,0,2,1:T(8,128)S(1)} %get-tuple-element.24), channel_id=1, source_target_pairs={{0,4},{4,8},{8,12},{12,16},{16,20},{20,24},{24,28},{1,5},{5,9},{9,... | collective-permute-start | bytes 3145736 | tf_op jit(solution)/shard_map/ppermute | solution.py:16
  228.5 4.7 %collective-permute-start.6 = (f32[8,4,1,512]{3,0,2,1:T(8,128)S(1)}, f32[8,4,1,512]{3,0,2,1:T(8,128)S(1)}, u32[]{:S(2)}, u32[]{:S(2)}) collective-permute-start(f32[8,4,1,512]{3,0,2,1:T(8,128)S(1)} %get-tuple-element.19), channel_id=1, source_target_pairs={{1,0},{2,1},{3,2},{5,4},{6,5},{7,6},{9,8},{10,9},{11,10},{13,12},{... | collective-permute-start | bytes 196616 | tf_op jit(solution)/shard_map/ppermute | solution.py:17
  229.8 3.9 collective-permute-start.7
  239.8 9.8 %copy-start.3 = (f32[8,2,64,512]{3,0,2,1:T(8,128)}, f32[8,2,64,512]{3,0,2,1:T(8,128)S(1)}, u32[]{:S(2)}) copy-start(f32[8,2,64,512]{3,0,2,1:T(8,128)S(1)} %fusion.11) | copy-start | bytes 6291460
  311.2 69.2 %copy-start.2 = (f32[8,65536]{1,0:T(8,128)}, f32[8,65536]{1,0:T(8,128)S(1)}, u32[]{:S(2)}) copy-start(f32[8,65536]{1,0:T(8,128)S(1)} %fusion.32) | copy-start | bytes 6291460
  311.4 26.0 %collective-permute-start.8 = (f32[8,1,64,512]{3,0,2,1:T(8,128)S(1)}, f32[8,1,64,512]{3,0,2,1:T(8,128)S(1)}, u32[]{:S(2)}, u32[]{:S(2)}) collective-permute-start(f32[8,1,64,512]{3,0,2,1:T(8,128)S(1)} %get-tuple-element.23), channel_id=1, source_target_pairs={{4,0},{8,4},{12,8},{16,12},{20,16},{24,20},{28,24},{5,1},{9,5},{13... | collective-permute-start | bytes 3145736 | tf_op jit(solution)/shard_map/ppermute | solution.py:17
  312.7 46.5 %collective-permute-start.9 = (f32[8,1,64,512]{3,0,2,1:T(8,128)S(1)}, f32[8,1,64,512]{3,0,2,1:T(8,128)S(1)}, u32[]{:S(2)}, u32[]{:S(2)}) collective-permute-start(f32[8,1,64,512]{3,0,2,1:T(8,128)S(1)} %get-tuple-element.22), channel_id=1, source_target_pairs={{0,4},{4,8},{8,12},{12,16},{16,20},{20,24},{24,28},{1,5},{5,9},{9,... | collective-permute-start | bytes 3145736 | tf_op jit(solution)/shard_map/ppermute | solution.py:16
  359.1 4.4 collective-permute-start.10
  360.4 3.9 collective-permute-start.11
  370.6 4.9 %copy-start.1 = (f32[8,65536]{1,0:T(8,128)S(1)}, f32[8,65536]{1,0:T(8,128)}, u32[]{:S(2)}) copy-start(f32[8,65536]{1,0:T(8,128)} %copy-done) | copy-start | bytes 6291460
  436.9 12.6 %copy-start.7 = (f32[24,32]{1,0:T(8,128)}, f32[24,32]{1,0:T(8,128)S(1)}, u32[]{:S(2)}) copy-start(f32[24,32]{1,0:T(8,128)S(1)} %maximum_maximum_fusion) | copy-start | bytes 9220
where the time goes:
time: 461 us; the launch traced here: 452 us
  blocking collectives  173 us (38%)
  waiting for transfers between devices  127 us (28%)
  matrix products  80.2 us (17%)
  other arithmetic  33.7 us (7%)
  starting transfers between devices  32.2 us (7%)
  local copies, waits for them, and re-layouts  4.69 us (1%)
    psum x3, blocking collectives, body(): coeff, gram_work = lax.psum((local, inner(work, work)), ('gz', 'gy'))  131 us
    ppermute x6, waiting for transfers between devices, extended(): before = lax.ppermute(last, axis, up)  67.8 us
    ppermute x6, waiting for transfers between devices, extended(): after = lax.ppermute(leading, axis, down)  59.2 us
    dot_general x10, matrix products, inner(): return jnp.dot(left, right.T, precision=lax.Precision.HIGHEST)  51.3 us
    psum x1, blocking collectives, body(): lax.psum(inner(flat_rhs, flat_rhs), ('gz', 'gy'))  42 us
    ppermute x6, starting transfers between devices, extended(): before = lax.ppermute(last, axis, up)  24.5 us
    dot_general x3, matrix products, body(): jnp.dot(coeff[index], basis[index], precision=lax.Precision.HIGHEST)  13.6 us
    concatenate x6, other arithmetic, extended(): array = jnp.concatenate([before, array, after], axis=dim)  11.6 us
  transfers between devices with their start and end apart: 12, of which 9 were waited for; matrix products, arithmetic and copies ran while one was open for 0% of the time, Pallas kernels for 0%

commit v1 on v0

v1 whole, which is shorter than its diff:
```python
import functools
import math

import jax
import jax.numpy as jnp
from jax import lax
from jax.experimental import pallas as pl
from jax.experimental.pallas import tpu as pltpu
from jax.sharding import PartitionSpec as P

ITERS = 3
EDGE = 4
CENTER, SPREAD = 7.6, 2.6
BETA = (0.0, 1.0, 1.5)
HIGHEST = lax.Precision.HIGHEST


def pairs(peers, step):
    return [(i, i + step) for i in range(peers) if 0 <= i + step < peers]


def swap_pairs(peers, bit):
    return [(i, i ^ bit) for i in range(peers)]


def all_sum(array, axes):
    for axis in axes:
        peers = lax.axis_size(axis)
        if peers & (peers - 1):
            array = lax.psum(array, axis)
            continue
        bit = 1
        while bit < peers:
            array = array + lax.ppermute(array, axis, swap_pairs(peers, bit))
            bit *= 2
    return array


def krylov_kernel(keep, got, low_keep, low_got, high_keep, high_got, basis_out, nu_out,
                  x0, x1, x2, x3, acc, sems, out_sems, *, blocks, half, width):
    place = lax.axis_index("gz")
    last = lax.axis_size("gz") - 2
    parity = lax.rem(place, 2)
    rows = half + 2 * EDGE
    mine, other = 2 * parity, 2 - 2 * parity
    copies = []
    for n, (ref, at) in enumerate((
        (keep, 4 + mine), (got, 4 + other), (low_keep, mine), (low_got, other),
        (high_keep, 8 + mine), (high_got, 8 + other),
    )):
        copies.append(pltpu.make_async_copy(ref, x0.at[:, pl.ds(at, 2)], sems.at[n]))
        copies[-1].start()
    for copy in copies:
        copy.wait()

    row = lax.broadcasted_iota(jnp.int32, (rows, width), 0)
    lane = lax.broadcasted_iota(jnp.int32, (rows, width), 1)
    at_y = lax.axis_index("gy")
    no_below = jnp.logical_and(at_y == lax.axis_size("gy") - 1, parity == 1)
    no_above = jnp.logical_and(at_y == 0, parity == 0)
    below = jnp.where(no_below, 0.0, 1.0)
    above = jnp.where(no_above, 0.0, 1.0)
    row_mask = jnp.where(row < half, 1.0, jnp.where(row < half + EDGE, below, above))
    has_low = jnp.where(place >= 2, 1.0, 0.0)
    has_high = jnp.where(place < last, 1.0, 0.0)

    def apply(src, src_at, dst, dst_at, before, before_at, count, first, beta):
        def layer(step, carry):
            index = first + step
            flag = jnp.where(index < 4, has_low, jnp.where(index < 8, 1.0, has_high))
            scale = row_mask * (flag * (1.0 / SPREAD))
            diag = scale * (x0[blocks, index] + (6.0 - CENTER))

            def vector(v, inner):
                mid = src[v, index - src_at]
                beside = src[v, index - src_at - 1] + src[v, index - src_at + 1]
                beside = beside + pltpu.roll(mid, 1, 0) + pltpu.roll(mid, rows - 1, 0)
                beside = beside + jnp.where(lane == 0, 0.0, pltpu.roll(mid, 1, 1))
                beside = beside + jnp.where(lane == width - 1, 0.0, pltpu.roll(mid, width - 1, 1))
                value = diag * mid - scale * beside
                if beta:
                    value = value - beta * before[v, index - before_at]
                dst[v, index - dst_at] = value
                return inner

            return lax.fori_loop(0, blocks, vector, carry)

        lax.fori_loop(0, count, layer, 0)

    apply(x0, 0, x1, 2, None, 0, 8, 2, 0.0)
    apply(x1, 2, x2, 3, x0, 0, 6, 3, BETA[1])
    outs = []
    for n, (ref, at) in enumerate(((x0, 4), (x1, 2), (x2, 1))):
        outs.append(pltpu.make_async_copy(
            ref.at[pl.ds(0, blocks), pl.ds(at, 4), pl.ds(0, half)], basis_out.at[n], out_sems.at[n]))
        outs[-1].start()
    apply(x2, 3, x3, 4, x1, 2, 4, 4, BETA[2])

    held = ((x0, 4), (x1, 2), (x2, 1), (x3, 0))
    tiles = half // 8
    chunks = width // 128
    upper = [(v, w) for v in range(blocks) for w in range(v, blocks)]
    for m in range(2 * ITERS + 1):
        (left, left_at), (right, right_at) = held[m // 2], held[(m + 1) // 2]

        def spot(step, sums, left=left, left_at=left_at, right=right, right_at=right_at):
            layer = step // tiles
            at = pl.multiple_of((step % tiles) * 8, 8)
            sums = list(sums)
            for c in range(chunks):
                lanes = pl.ds(128 * c, 128)
                rights = [right[w, layer + right_at, pl.ds(at, 8), lanes] for w in range(blocks)]
                for v in range(blocks):
                    if left is right:
                        one = rights[v]
                    else:
                        one = left[v, layer + left_at, pl.ds(at, 8), lanes]
                    for n, (a, b) in enumerate(upper):
                        if a == v:
                            sums[n] = sums[n] + one * rights[b]
            return tuple(sums)

        zeros = tuple(jnp.zeros((8, 128), jnp.float32) for _ in upper)
        sums = lax.fori_loop(0, 4 * tiles, spot, zeros)
        for n, (v, w) in enumerate(upper):
            total = jnp.sum(sums[n], axis=0, keepdims=True)
            acc[pl.ds(m * blocks * blocks + v * blocks + w, 1), :] = total
            if v != w:
                acc[pl.ds(m * blocks * blocks + w * blocks + v, 1), :] = total
    nu_out[...] = lax.dot_general(
        jnp.ones((8, 128), jnp.float32), acc[...], (((1,), (1,)), ((), ())),
        precision=HIGHEST, preferred_element_type=jnp.float32)
    for copy in outs:
        copy.wait()


def krylov(pieces, blocks, half, width):
    rows = half + 2 * EDGE
    moments = (2 * ITERS + 1) * blocks * blocks
    padded = -(-moments // 128) * 128
    hbm = pl.BlockSpec(memory_space=pl.ANY)
    return pl.pallas_call(
        functools.partial(krylov_kernel, blocks=blocks, half=half, width=width),
        out_shape=(
            jax.ShapeDtypeStruct((ITERS, blocks, 4, half, width), jnp.float32),
            jax.ShapeDtypeStruct((8, moments), jnp.float32),
        ),
        in_specs=[hbm] * 6,
        out_specs=(hbm, pl.BlockSpec(memory_space=pltpu.VMEM)),
        scratch_shapes=[
            pltpu.VMEM((blocks + 1, 12, rows, width), jnp.float32),
            pltpu.VMEM((blocks, 8, rows, width), jnp.float32),
            pltpu.VMEM((blocks, 6, rows, width), jnp.float32),
            pltpu.VMEM((blocks, 4, rows, width), jnp.float32),
            pltpu.VMEM((moments, 128), jnp.float32),
            pltpu.SemaphoreType.DMA((6,)),
            pltpu.SemaphoreType.DMA((ITERS,)),
        ],
        compiler_params=pltpu.CompilerParams(vmem_limit_bytes=60 << 20),
        name="krylov",
    )(*pieces)


def combine_kernel(at, weights, basis, out, *, blocks, width):
    chunks = width // 128
    sums = [[None] * chunks for _ in range(blocks)]
    for k in range(ITERS):
        for v in range(blocks):
            parts = [basis[k, v, 0, :, 128 * c:128 * c + 128] for c in range(chunks)]
            for w in range(blocks):
                scale = weights[k * blocks + v, w]
                for c in range(chunks):
                    term = scale * parts[c]
                    sums[w][c] = term if sums[w][c] is None else sums[w][c] + term
    for w in range(blocks):
        for c in range(chunks):
            out[w, 0, :, 128 * c:128 * c + 128] = sums[w][c]


def combine(at, weights, basis, half, width):
    blocks = basis.shape[1]
    return pl.pallas_call(
        functools.partial(combine_kernel, blocks=blocks, width=width),
        out_shape=jax.ShapeDtypeStruct((blocks, 2, half, width), jnp.float32),
        grid_spec=pltpu.PrefetchScalarGridSpec(
            num_scalar_prefetch=2,
            grid=(2, half // 8),
            in_specs=[pl.BlockSpec((ITERS, blocks, 1, 8, width), lambda l, t, at, e: (0, 0, at[0] + l, t, 0))],
            out_specs=pl.BlockSpec((blocks, 1, 8, width), lambda l, t, at, e: (0, l, t, 0)),
        ),
        name="combine",
    )(at, weights, basis)


def dense(nu, blocks):
    b1, b2 = BETA[1], BETA[2]
    g02 = nu[2] - b1 * nu[0]
    g03 = nu[3] - b2 * nu[1]
    g13 = nu[4] + b1 * g02 - b2 * nu[2]
    gram = jnp.concatenate([
        jnp.concatenate([nu[0], nu[1], g02, g03], axis=1),
        jnp.concatenate([nu[1], nu[2], nu[3], g13], axis=1),
        jnp.concatenate([g02, nu[3], nu[4], nu[5]], axis=1),
        jnp.concatenate([g03, g13, nu[5], nu[6]], axis=1),
    ], axis=0)
    size = ITERS * blocks
    factor = jnp.linalg.cholesky(gram)
    inverse = jax.scipy.linalg.solve_triangular(
        factor[:size, :size], jnp.eye(size, dtype=jnp.float32), lower=True)
    flat = factor.reshape(ITERS + 1, blocks, size + blocks)
    shifted = [SPREAD * flat[k + 1] + CENTER * flat[k]
               + (SPREAD * BETA[k] * flat[k - 1] if BETA[k] else 0.0) for k in range(ITERS)]
    hessenberg = jnp.dot(inverse, jnp.concatenate(shifted, axis=0), precision=HIGHEST)
    row = lax.broadcasted_iota(jnp.int32, hessenberg.shape, 0) // blocks
    col = lax.broadcasted_iota(jnp.int32, hessenberg.shape, 1) // blocks
    hessenberg = jnp.where(col <= row + 1, hessenberg, 0.0)
    normal = jnp.dot(hessenberg, hessenberg.T, precision=HIGHEST)
    target = jnp.dot(hessenberg[:, :blocks], factor[:blocks, :blocks].T, precision=HIGHEST)
    coeffs = jax.scipy.linalg.cho_solve((jnp.linalg.cholesky(normal), True), target)
    weights = jnp.dot(inverse.T, coeffs, precision=HIGHEST)
    return hessenberg, weights


def body(right_side, diagonal):
    blocks, layers, ny, width = right_side.shape
    half = ny // 2
    peers_z, peers_y = lax.axis_size("gz"), lax.axis_size("gy")
    parity = lax.axis_index("gz") % 2
    field = jnp.concatenate([right_side, diagonal[None]], axis=0)
    above = lax.ppermute(field[:, :, ny - EDGE:], "gy", pairs(peers_y, 1))
    under = lax.ppermute(field[:, :, :EDGE], "gy", pairs(peers_y, -1))
    first = jnp.concatenate([field[:, :, :half + EDGE], above], axis=2)
    second = jnp.concatenate([field[:, :, half:], under, field[:, :, half - EDGE:half]], axis=2)
    keep = jnp.where(parity == 0, first, second)
    send = jnp.where(parity == 0, second, first)
    got = lax.ppermute(send, "gz", swap_pairs(peers_z, 1))
    low_keep = lax.ppermute(keep, "gz", pairs(peers_z, 2))
    high_keep = lax.ppermute(keep, "gz", pairs(peers_z, -2))
    low_got = lax.ppermute(got, "gz", pairs(peers_z, 2))
    high_got = lax.ppermute(got, "gz", pairs(peers_z, -2))
    basis, nu = krylov((keep, got, low_keep, low_got, high_keep, high_got), blocks, half, width)
    nu = all_sum(nu[:1], ("gy", "gz")).reshape(2 * ITERS + 1, blocks, blocks)
    hessenberg, weights = dense(nu, blocks)
    mine = (2 * parity).astype(jnp.int32)
    theirs = combine((2 - mine)[None], weights, basis, half, width)
    back = lax.ppermute(theirs, "gz", swap_pairs(peers_z, 1))
    own = combine(mine[None], weights, basis, half, width)
    upper = jnp.where(parity == 0, own, back)
    lower = jnp.where(parity == 0, back, own)
    return jnp.concatenate([upper, lower], axis=2), hessenberg


def solution(mesh):
    in_specs = (P(None, "gz", "gy", None), P("gz", "gy", None))
    out_specs = (P(None, "gz", "gy", None), P())
    return jax.shard_map(body, mesh=mesh, in_specs=in_specs, out_specs=out_specs, check_vma=False)
```

time: 461 us -> 179 us (0.39); the launches traced: 452 us -> 178 us
  blocking collectives: 173 us -> 0 us
  matrix products: 80.2 us -> 1.84 us
  Pallas kernels: 0 us -> 43.1 us
  waiting for transfers between devices: 127 us -> 88 us
  other arithmetic: 33.7 us -> 19.2 us
  starting transfers between devices: 32.2 us -> 22 us
    psum x4 -> x0, blocking collectives: 173 us -> none  [the longest x3 131 us: body(): coeff, gram_work = lax.psum((local, inner(work, work)), ('gz', 'gy'))]
    dot_general x22 -> x4, matrix products: 72.4 us -> 1.27 us  [the longest x1 0.84 us: dense(): weights = jnp.dot(inverse.T, coeffs, precision=HIGHEST)]
    pallas_call x0 -> x3, Pallas kernels: none -> 43.1 us  [the longest x1 28.4 us: krylov(): pl.pallas_call(functools.partial(krylov_kernel, blocks=blocks, half=half,...]
    ppermute x12 -> x13, waiting for transfers between devices: 127 us -> 88 us  [the longest x1 28 us: body(): low_got = lax.ppermute(got, 'gz', pairs(peers_z, 2))]
    ppermute x12 -> x13, starting transfers between devices: 32.2 us -> 22 us  [the longest x5 5.57 us: all_sum(): array = array + lax.ppermute(array, axis, swap_pairs(peers, bit))]
    concatenate x7 -> x6, other arithmetic: 11.7 us -> 3.91 us  [the longest x3 2.22 us: body(): field = jnp.concatenate([right_side, diagonal[None]], axis=0)]
    another operation x5 -> x3, matrix products: 7.78 us -> 0.57 us  [the longest x2 0.36 us: dense(): jax.scipy.linalg.cho_solve((jnp.linalg.cholesky(normal), True), target)]
    sub x4 -> x1, other arithmetic: 6.53 us -> 0.01 us  [dense(): g13 = nu[4] + b1 * g02 - b2 * nu[2]]
  transfers between devices with their start and end apart: 12 -> 13, of which waited for: 9 -> 11; matrix products, arithmetic and copies ran while one was open for 0% -> 0% of each run, Pallas kernels for 0% -> 4%
where the time goes in v1:
time: 179 us; the launch traced here: 178 us
  waiting for transfers between devices  88 us (49%)
  Pallas kernels  43.1 us (24%)
  starting transfers between devices  22 us (12%)
  other arithmetic  19.2 us (11%)
  local copies, waits for them, and re-layouts  2.96 us (2%)
  matrix products  1.84 us (1%)
    pallas_call x1, Pallas kernels, krylov(): pl.pallas_call(functools.partial(krylov_kernel, blocks=blocks, half=half,...  28.4 us
    ppermute x1, waiting for transfers between devices, body(): low_got = lax.ppermute(got, 'gz', pairs(peers_z, 2))  28 us
    ppermute x1, waiting for transfers between devices, body(): got = lax.ppermute(send, 'gz', swap_pairs(peers_z, 1))  26.1 us
    pallas_call x2, Pallas kernels, combine(): pl.pallas_call(functools.partial(combine_kernel, blocks=blocks, width=wid...  14.8 us
    ppermute x1, waiting for transfers between devices, body(): back = lax.ppermute(theirs, 'gz', swap_pairs(peers_z, 1))  12.8 us
    ppermute x5, waiting for transfers between devices, all_sum(): array = array + lax.ppermute(array, axis, swap_pairs(peers, bit))  11.2 us
    ppermute x5, starting transfers between devices, all_sum(): array = array + lax.ppermute(array, axis, swap_pairs(peers, bit))  5.57 us
    ppermute x1, waiting for transfers between devices, body(): high_got = lax.ppermute(got, 'gz', pairs(peers_z, -2))  3.77 us
  transfers between devices with their start and end apart: 13, of which 11 were waited for; matrix products, arithmetic and copies ran while one was open for 0% of the time, Pallas kernels for 4%

profile of v1, /device:TPU:0, one launch (start us, length us, event | category | flops | bytes accessed | tf_op | source)
XLA Modules:
  0.0 178.0 jit_solution(17979352632195188728)
XLA Ops:
  0.6 2.0 %fusion.5 = (f32[9,2,4,512]{3,2,1,0:T(4,128)}, f32[9,2,4,512]{3,2,1,0:T(4,128)}) fusion(f32[8,2,64,512]{3,2,1,0:T(8,128)} %param.2, f32[1,2,64,512]{3,2,1,0:T(8,128)} %bitcast.30), kind=kLoop, calls=%fused_computation.20 | loop fusion | flops 73728 | bytes 2654208 | tf_op jit(solution)/shard_map/concatenate | solution.py:229
  2.6 3.0 %collective-permute-start = (f32[9,2,4,512]{3,2,1,0:T(4,128)}, f32[9,2,4,512]{3,2,1,0:T(4,128)}, u32[]{:S(2)}, u32[]{:S(2)}) collective-permute-start(f32[9,2,4,512]{3,2,1,0:T(4,128)} %get-tuple-element.18), channel_id=1, source_target_pairs={{0,1},{1,2},{2,3},{4,5},{5,6},{6,7},{8,9},{9,10},{10,11},{12,13},{... | collective-permute-start | bytes 442376 | tf_op jit(solution)/shard_map/ppermute | solution.py:230
  5.6 1.3 collective-permute-start.1
  7.3 3.4 %collective-permute-done.1 = f32[9,2,4,512]{3,2,1,0:T(4,128)} collective-permute-done((f32[9,2,4,512]{3,2,1,0:T(4,128)}, f32[9,2,4,512]{3,2,1,0:T(4,128)}, u32[]{:S(2)}, u32[]{:S(2)}) %collective-permute-start.1) | collective-permute-done | bytes 147488 | tf_op jit(solution)/shard_map/ppermute | solution.py:231
  10.7 1.5 fusion.3
  12.2 1.6 collective-permute-start.2
  13.8 3.6 %collective-permute-start.3 = (f32[9,2,40,512]{3,2,1,0:T(8,128)S(1)}, f32[9,2,40,512]{3,2,1,0:T(8,128)S(1)}, u32[]{:S(2)}, u32[]{:S(2)}) collective-permute-start(f32[9,2,40,512]{3,2,1,0:T(8,128)S(1)} %get-tuple-element.16.keep), channel_id=1, source_target_pairs={{0,8},{4,12},{8,16},{12,20},{16,24},{20,28},{1,9},{5,13},{9,17},{1... | collective-permute-start | bytes 4423688 | tf_op jit(solution)/shard_map/ppermute | solution.py:237
  17.4 1.3 collective-permute-start.5
  18.7 26.1 %collective-permute-done.2.got = f32[9,2,40,512]{3,2,1,0:T(8,128)S(1)} collective-permute-done((f32[9,2,40,512]{3,2,1,0:T(8,128)S(1)}, f32[9,2,40,512]{3,2,1,0:T(8,128)S(1)}, u32[]{:S(2)}, u32[]{:S(2)}) %collective-permute-start.2) | collective-permute-done | bytes 1474592 | tf_op jit(solution)/shard_map/ppermute | solution.py:236
  44.7 3.6 %collective-permute-start.4 = (f32[9,2,40,512]{3,2,1,0:T(8,128)S(1)}, f32[9,2,40,512]{3,2,1,0:T(8,128)S(1)}, u32[]{:S(2)}, u32[]{:S(2)}) collective-permute-start(f32[9,2,40,512]{3,2,1,0:T(8,128)S(1)} %collective-permute-done.2.got), channel_id=1, source_target_pairs={{0,8},{4,12},{8,16},{12,20},{16,24},{20,28},{1,9},{5,13},{9,17},{1... | collective-permute-start | bytes 4423688 | tf_op jit(solution)/shard_map/ppermute | solution.py:239
  48.3 1.3 collective-permute-start.6
  49.6 2.7 %collective-permute-done.5.high_keep = f32[9,2,40,512]{3,2,1,0:T(8,128)S(1)} collective-permute-done((f32[9,2,40,512]{3,2,1,0:T(8,128)S(1)}, f32[9,2,40,512]{3,2,1,0:T(8,128)S(1)}, u32[]{:S(2)}, u32[]{:S(2)}) %collective-permute-start.5) | collective-permute-done | bytes 1474592 | tf_op jit(solution)/shard_map/ppermute | solution.py:238
  52.3 28.0 %collective-permute-done.4.low_got = f32[9,2,40,512]{3,2,1,0:T(8,128)S(1)} collective-permute-done((f32[9,2,40,512]{3,2,1,0:T(8,128)S(1)}, f32[9,2,40,512]{3,2,1,0:T(8,128)S(1)}, u32[]{:S(2)}, u32[]{:S(2)}) %collective-permute-start.4) | collective-permute-done | bytes 1474592 | tf_op jit(solution)/shard_map/ppermute | solution.py:239
  80.3 1.1 copy-done.6
  81.4 3.8 %collective-permute-done.6.high_got = f32[9,2,40,512]{3,2,1,0:T(8,128)} collective-permute-done((f32[9,2,40,512]{3,2,1,0:T(8,128)S(1)}, f32[9,2,40,512]{3,2,1,0:T(8,128)}, u32[]{:S(2)}, u32[]{:S(2)}) %collective-permute-start.6) | collective-permute-done | bytes 1474592 | tf_op jit(solution)/shard_map/ppermute | solution.py:240
  85.2 28.4 %krylov.1 = (f32[3,8,4,32,512]{4,3,2,1,0:T(8,128)}, f32[8,448]{1,0:T(8,128)}) custom-call(f32[9,2,40,512]{3,2,1,0:T(8,128)} %copy-done.1, f32[9,2,40,512]{3,2,1,0:T(8,128)} %copy-done.3, f32[9,2,40,512]{3,2,1,0:T(8,128)} %copy-done.4, f32[9,2,40,512]{3,2,1,0:T(8,128)} %copy-done.6, f32[9,2,40,512]{3,2,1,0:T(8,128)} %copy-done.5, ...), custom_call_target="tpu_custom_call" | custom-call | tf_op jit(solution)/shard_map/krylov/pallas_call | solution.py:142
  116.6 3.6 %collective-permute-done.8 = f32[1,448]{1,0:T(1,128)S(1)} collective-permute-done((f32[1,448]{1,0:T(1,128)S(1)}, f32[1,448]{1,0:T(1,128)S(1)}, u32[]{:S(2)}, u32[]{:S(2)}) %collective-permute-start.8) | collective-permute-done | bytes 1824 | tf_op jit(solution)/shard_map/ppermute | solution.py:34
  121.0 2.7 %collective-permute-done.9 = f32[1,448]{1,0:T(1,128)S(1)} collective-permute-done((f32[1,448]{1,0:T(1,128)S(1)}, f32[1,448]{1,0:T(1,128)S(1)}, u32[]{:S(2)}, u32[]{:S(2)}) %collective-permute-start.9) | collective-permute-done | bytes 1824 | tf_op jit(solution)/shard_map/ppermute | solution.py:34
  123.8 1.5 collective-permute-start.10
  125.3 2.1 %collective-permute-done.10 = f32[1,448]{1,0:T(1,128)S(1)} collective-permute-done((f32[1,448]{1,0:T(1,128)S(1)}, f32[1,448]{1,0:T(1,128)S(1)}, u32[]{:S(2)}, u32[]{:S(2)}) %collective-permute-start.10) | collective-permute-done | bytes 1824 | tf_op jit(solution)/shard_map/ppermute | solution.py:34
  127.3 2.5 %collective-permute-start.11 = (f32[1,448]{1,0:T(1,128)S(1)}, f32[1,448]{1,0:T(1,128)S(1)}, u32[]{:S(2)}, u32[]{:S(2)}) collective-permute-start(f32[1,448]{1,0:T(1,128)S(1)} %add.76), channel_id=1, source_target_pairs={{0,16},{4,20},{8,24},{12,28},{16,0},{20,4},{24,8},{28,12},{1,17},{... | collective-permute-start | bytes 5384 | tf_op jit(solution)/shard_map/ppermute | solution.py:34
  129.9 2.0 %collective-permute-done.11 = f32[1,448]{1,0:T(1,128)S(1)} collective-permute-done((f32[1,448]{1,0:T(1,128)S(1)}, f32[1,448]{1,0:T(1,128)S(1)}, u32[]{:S(2)}, u32[]{:S(2)}) %collective-permute-start.11) | collective-permute-done | bytes 1824 | tf_op jit(solution)/shard_map/ppermute | solution.py:34
  133.1 2.9 %cholesky.31 = f32[32,32]{1,0:T(8,128)S(1)} custom-call(f32[32,32]{1,0:T(8,128)S(1)} %fusion.7), custom_call_target="Cholesky" | custom-call | tf_op jit(solution)/shard_map/jit(cholesky)/cholesky | solution.py:207
  137.4 1.8 %custom-call.17 = f32[1,24,24]{1,2,0:T(8,128)S(1)} custom-call(f32[1,24,24]{2,1,0:T(8,128)S(1)} %fusion.11), custom_call_target="InvertDiagBlocksLowerTriangular" | custom-call | tf_op jit(solution)/shard_map/jit(_solve_triangular)/triangular_solve | solution.py:208
  140.0 2.2 %cholesky.59 = f32[24,24]{1,0:T(8,128)S(1)} custom-call(f32[24,24]{1,0:T(8,128)S(1)} %fusion.21), custom_call_target="Cholesky" | custom-call | tf_op jit(solution)/shard_map/jit(cholesky)/cholesky | solution.py:219
  143.6 1.8 %custom-call.18 = f32[1,24,24]{1,2,0:T(8,128)S(1)} custom-call(f32[1,24,24]{2,1,0:T(8,128)S(1)} %fusion.8), custom_call_target="InvertDiagBlocksLowerTriangular" | custom-call | tf_op jit(solution)/shard_map/jit(_cho_solve)/triangular_solve | solution.py:219
  146.6 7.4 %combine.3 = f32[8,2,32,512]{3,2,1,0:T(8,128)} custom-call(s32[1]{0:T(128)} %bitcast.8.at, f32[24,8]{1,0:T(8,128)} %fusion.29.weights, f32[3,8,4,32,512]{4,3,2,1,0:T(8,128)} %get-tuple-element.5.basis), custom_call_target="tpu_custom_call" | custom-call | tf_op jit(solution)/shard_map/combine/pallas_call | solution.py:182
  154.0 0.9 collective-permute-start.12
  154.9 7.4 %combine.2 = f32[8,2,32,512]{3,2,1,0:T(8,128)} custom-call(s32[1]{0:T(128)} %bitcast.at, f32[24,8]{1,0:T(8,128)} %fusion.29.weights, f32[3,8,4,32,512]{4,3,2,1,0:T(8,128)} %get-tuple-element.5.basis), custom_call_target="tpu_custom_call" | custom-call | tf_op jit(solution)/shard_map/combine/pallas_call | solution.py:182
  162.2 12.8 %collective-permute-done.12 = f32[8,2,32,512]{3,2,1,0:T(8,128)S(1)} collective-permute-done((f32[8,2,32,512]{3,2,1,0:T(8,128)}, f32[8,2,32,512]{3,2,1,0:T(8,128)S(1)}, u32[]{:S(2)}, u32[]{:S(2)}) %collective-permute-start.12) | collective-permute-done | bytes 1048608 | tf_op jit(solution)/shard_map/ppermute | solution.py:246
  175.0 1.4 broadcast_select_fusion.1
  176.5 1.5 pad_maximum_fusion
  (67 shorter events, 10.1 us)
Async XLA Ops:
  0.6 6.3 %copy-start.2 = (f32[2,64,512]{2,1,0:T(8,128)S(1)}, f32[2,64,512]{2,1,0:T(8,128)}, u32[]{:S(2)}) copy-start(f32[2,64,512]{2,1,0:T(8,128)} %param.3) | copy-start | bytes 786436
  0.6 6.3 %copy-start = (f32[8,2,64,512]{3,2,1,0:T(8,128)S(1)}, f32[8,2,64,512]{3,2,1,0:T(8,128)}, u32[]{:S(2)}) copy-start(f32[8,2,64,512]{3,2,1,0:T(8,128)} %param.2) | copy-start | bytes 6291460
  2.6 4.7 %collective-permute-start = (f32[9,2,4,512]{3,2,1,0:T(4,128)}, f32[9,2,4,512]{3,2,1,0:T(4,128)}, u32[]{:S(2)}, u32[]{:S(2)}) collective-permute-start(f32[9,2,4,512]{3,2,1,0:T(4,128)} %get-tuple-element.18), channel_id=1, source_target_pairs={{0,1},{1,2},{2,3},{4,5},{5,6},{6,7},{8,9},{9,10},{10,11},{12,13},{... | collective-permute-start | bytes 442376 | tf_op jit(solution)/shard_map/ppermute | solution.py:230
  5.6 5.1 %collective-permute-start.1 = (f32[9,2,4,512]{3,2,1,0:T(4,128)}, f32[9,2,4,512]{3,2,1,0:T(4,128)}, u32[]{:S(2)}, u32[]{:S(2)}) collective-permute-start(f32[9,2,4,512]{3,2,1,0:T(4,128)} %get-tuple-element.17), channel_id=1, source_target_pairs={{1,0},{2,1},{3,2},{5,4},{6,5},{7,6},{9,8},{10,9},{11,10},{13,12},{... | collective-permute-start | bytes 442376 | tf_op jit(solution)/shard_map/ppermute | solution.py:231
  12.2 5.2 %copy-start.1 = (f32[9,2,40,512]{3,2,1,0:T(8,128)}, f32[9,2,40,512]{3,2,1,0:T(8,128)S(1)}, u32[]{:S(2)}) copy-start(f32[9,2,40,512]{3,2,1,0:T(8,128)S(1)} %get-tuple-element.16.keep) | copy-start | bytes 4423684
  12.2 32.5 %collective-permute-start.2 = (f32[9,2,40,512]{3,2,1,0:T(8,128)S(1)}, f32[9,2,40,512]{3,2,1,0:T(8,128)S(1)}, u32[]{:S(2)}, u32[]{:S(2)}) collective-permute-start(f32[9,2,40,512]{3,2,1,0:T(8,128)S(1)} %get-tuple-element.15), channel_id=1, source_target_pairs={{0,4},{4,0},{8,12},{12,8},{16,20},{20,16},{24,28},{28,24},{1,5},{5... | collective-permute-start | bytes 4423688 | tf_op jit(solution)/shard_map/ppermute | solution.py:236
  13.8 35.8 %collective-permute-start.3 = (f32[9,2,40,512]{3,2,1,0:T(8,128)S(1)}, f32[9,2,40,512]{3,2,1,0:T(8,128)S(1)}, u32[]{:S(2)}, u32[]{:S(2)}) collective-permute-start(f32[9,2,40,512]{3,2,1,0:T(8,128)S(1)} %get-tuple-element.16.keep), channel_id=1, source_target_pairs={{0,8},{4,12},{8,16},{12,20},{16,24},{20,28},{1,9},{5,13},{9,17},{1... | collective-permute-start | bytes 4423688 | tf_op jit(solution)/shard_map/ppermute | solution.py:237
  17.4 34.9 %collective-permute-start.5 = (f32[9,2,40,512]{3,2,1,0:T(8,128)S(1)}, f32[9,2,40,512]{3,2,1,0:T(8,128)S(1)}, u32[]{:S(2)}, u32[]{:S(2)}) collective-permute-start(f32[9,2,40,512]{3,2,1,0:T(8,128)S(1)} %get-tuple-element.16.keep), channel_id=1, source_target_pairs={{8,0},{12,4},{16,8},{20,12},{24,16},{28,20},{9,1},{13,5},{17,9},{2... | collective-permute-start | bytes 4423688 | tf_op jit(solution)/shard_map/ppermute | solution.py:238
  44.7 40.5 %copy-start.3 = (f32[9,2,40,512]{3,2,1,0:T(8,128)}, f32[9,2,40,512]{3,2,1,0:T(8,128)S(1)}, u32[]{:S(2)}) copy-start(f32[9,2,40,512]{3,2,1,0:T(8,128)S(1)} %collective-permute-done.2.got) | copy-start | bytes 4423684
  44.7 35.6 %collective-permute-start.4 = (f32[9,2,40,512]{3,2,1,0:T(8,128)S(1)}, f32[9,2,40,512]{3,2,1,0:T(8,128)S(1)}, u32[]{:S(2)}, u32[]{:S(2)}) collective-permute-start(f32[9,2,40,512]{3,2,1,0:T(8,128)S(1)} %collective-permute-done.2.got), channel_id=1, source_target_pairs={{0,8},{4,12},{8,16},{12,20},{16,24},{20,28},{1,9},{5,13},{9,17},{1... | collective-permute-start | bytes 4423688 | tf_op jit(solution)/shard_map/ppermute | solution.py:239
  48.3 36.9 %collective-permute-start.6 = (f32[9,2,40,512]{3,2,1,0:T(8,128)S(1)}, f32[9,2,40,512]{3,2,1,0:T(8,128)}, u32[]{:S(2)}, u32[]{:S(2)}) collective-permute-start(f32[9,2,40,512]{3,2,1,0:T(8,128)S(1)} %collective-permute-done.2.got), channel_id=1, source_target_pairs={{8,0},{12,4},{16,8},{20,12},{24,16},{28,20},{9,1},{13,5},{17,9},{2... | collective-permute-start | bytes 4423688 | tf_op jit(solution)/shard_map/ppermute | solution.py:240
  49.6 35.6 %copy-start.4 = (f32[9,2,40,512]{3,2,1,0:T(8,128)}, f32[9,2,40,512]{3,2,1,0:T(8,128)S(1)}, u32[]{:S(2)}) copy-start(f32[9,2,40,512]{3,2,1,0:T(8,128)S(1)} %collective-permute-done.3.low_keep) | copy-start | bytes 4423684
  52.3 28.0 %copy-start.5 = (f32[9,2,40,512]{3,2,1,0:T(8,128)}, f32[9,2,40,512]{3,2,1,0:T(8,128)S(1)}, u32[]{:S(2)}) copy-start(f32[9,2,40,512]{3,2,1,0:T(8,128)S(1)} %collective-permute-done.5.high_keep) | copy-start | bytes 4423684
  80.3 1.1 copy-start.6
  114.3 1.5 collective-permute-start.7
  116.6 3.6 %collective-permute-start.8 = (f32[1,448]{1,0:T(1,128)S(1)}, f32[1,448]{1,0:T(1,128)S(1)}, u32[]{:S(2)}, u32[]{:S(2)}) collective-permute-start(f32[1,448]{1,0:T(1,128)S(1)} %slice_add_fusion), channel_id=1, source_target_pairs={{0,2},{1,3},{2,0},{3,1},{4,6},{5,7},{6,4},{7,5},{8,10},{9,11},{10,... | collective-permute-start | bytes 5384 | tf_op jit(solution)/shard_map/ppermute | solution.py:34
  120.2 3.6 %collective-permute-start.9 = (f32[1,448]{1,0:T(1,128)S(1)}, f32[1,448]{1,0:T(1,128)S(1)}, u32[]{:S(2)}, u32[]{:S(2)}) collective-permute-start(f32[1,448]{1,0:T(1,128)S(1)} %add.74), channel_id=1, source_target_pairs={{0,4},{4,0},{8,12},{12,8},{16,20},{20,16},{24,28},{28,24},{1,5},{5... | collective-permute-start | bytes 5384 | tf_op jit(solution)/shard_map/ppermute | solution.py:34
  123.8 3.6 %collective-permute-start.10 = (f32[1,448]{1,0:T(1,128)S(1)}, f32[1,448]{1,0:T(1,128)S(1)}, u32[]{:S(2)}, u32[]{:S(2)}) collective-permute-start(f32[1,448]{1,0:T(1,128)S(1)} %add.75), channel_id=1, source_target_pairs={{0,8},{4,12},{8,0},{12,4},{16,24},{20,28},{24,16},{28,20},{1,9},{5... | collective-permute-start | bytes 5384 | tf_op jit(solution)/shard_map/ppermute | solution.py:34
  127.3 4.5 %collective-permute-start.11 = (f32[1,448]{1,0:T(1,128)S(1)}, f32[1,448]{1,0:T(1,128)S(1)}, u32[]{:S(2)}, u32[]{:S(2)}) collective-permute-start(f32[1,448]{1,0:T(1,128)S(1)} %add.76), channel_id=1, source_target_pairs={{0,16},{4,20},{8,24},{12,28},{16,0},{20,4},{24,8},{28,12},{1,17},{... | collective-permute-start | bytes 5384 | tf_op jit(solution)/shard_map/ppermute | solution.py:34
  139.6 14.4 %copy-start.7 = (f32[24,32]{1,0:T(8,128)}, f32[24,32]{1,0:T(8,128)S(1)}, u32[]{:S(2)}) copy-start(f32[24,32]{1,0:T(8,128)S(1)} %convolution_select_fusion) | copy-start | bytes 9220
  154.0 21.0 %collective-permute-start.12 = (f32[8,2,32,512]{3,2,1,0:T(8,128)}, f32[8,2,32,512]{3,2,1,0:T(8,128)S(1)}, u32[]{:S(2)}, u32[]{:S(2)}) collective-permute-start(f32[8,2,32,512]{3,2,1,0:T(8,128)} %combine.3), channel_id=1, source_target_pairs={{0,4},{4,0},{8,12},{12,8},{16,20},{20,16},{24,28},{28,24},{1,5},{5... | collective-permute-start | bytes 3145736 | tf_op jit(solution)/shard_map/ppermute | solution.py:246

commit v2 on v1

--- a/solution.py
+++ b/solution.py
@@ -36,19 +36,15 @@
     return array
 
 
-def krylov_kernel(keep, got, low_keep, low_got, high_keep, high_got, basis_out, nu_out,
-                  x0, x1, x2, x3, acc, sems, out_sems, *, blocks, half, width):
+def krylov_kernel(*refs, blocks, half, width):
+    (layers, (basis_out, nu_out, x0, x1, x2, x3, acc, sems, out_sems)) = (refs[:10], refs[10:])
     place = lax.axis_index("gz")
     last = lax.axis_size("gz") - 2
     parity = lax.rem(place, 2)
     rows = half + 2 * EDGE
-    mine, other = 2 * parity, 2 - 2 * parity
     copies = []
-    for n, (ref, at) in enumerate((
-        (keep, 4 + mine), (got, 4 + other), (low_keep, mine), (low_got, other),
-        (high_keep, 8 + mine), (high_got, 8 + other),
-    )):
-        copies.append(pltpu.make_async_copy(ref, x0.at[:, pl.ds(at, 2)], sems.at[n]))
+    for n, ref in enumerate(layers):
+        copies.append(pltpu.make_async_copy(ref, x0.at[:, n], sems.at[n]))
         copies[-1].start()
     for copy in copies:
         copy.wait()
@@ -61,13 +57,15 @@
     below = jnp.where(no_below, 0.0, 1.0)
     above = jnp.where(no_above, 0.0, 1.0)
     row_mask = jnp.where(row < half, 1.0, jnp.where(row < half + EDGE, below, above))
-    has_low = jnp.where(place >= 2, 1.0, 0.0)
-    has_high = jnp.where(place < last, 1.0, 0.0)
+    downward = jnp.where(place >= 2, 1.0, 0.0)
+    upward = jnp.where(place < last, 1.0, 0.0)
+    has_low = jnp.where(parity == 0, downward, upward)
+    has_high = jnp.where(parity == 0, upward, downward)
 
     def apply(src, src_at, dst, dst_at, before, before_at, count, first, beta):
         def layer(step, carry):
             index = first + step
-            flag = jnp.where(index < 4, has_low, jnp.where(index < 8, 1.0, has_high))
+            flag = jnp.where(index < 3, has_low, jnp.where(index < 7, 1.0, has_high))
             scale = row_mask * (flag * (1.0 / SPREAD))
             diag = scale * (x0[blocks, index] + (6.0 - CENTER))
 
@@ -87,16 +85,16 @@
 
         lax.fori_loop(0, count, layer, 0)
 
-    apply(x0, 0, x1, 2, None, 0, 8, 2, 0.0)
-    apply(x1, 2, x2, 3, x0, 0, 6, 3, BETA[1])
+    apply(x0, 0, x1, 1, None, 0, 8, 1, 0.0)
+    apply(x1, 1, x2, 2, x0, 0, 6, 2, BETA[1])
     outs = []
-    for n, (ref, at) in enumerate(((x0, 4), (x1, 2), (x2, 1))):
+    for n, (ref, at) in enumerate(((x0, 3), (x1, 2), (x2, 1))):
         outs.append(pltpu.make_async_copy(
             ref.at[pl.ds(0, blocks), pl.ds(at, 4), pl.ds(0, half)], basis_out.at[n], out_sems.at[n]))
         outs[-1].start()
-    apply(x2, 3, x3, 4, x1, 2, 4, 4, BETA[2])
-
-    held = ((x0, 4), (x1, 2), (x2, 1), (x3, 0))
+    apply(x2, 2, x3, 3, x1, 1, 4, 3, BETA[2])
+
+    held = ((x0, 3), (x1, 2), (x2, 1), (x3, 0))
     tiles = half // 8
     chunks = width // 128
     upper = [(v, w) for v in range(blocks) for w in range(v, blocks)]
@@ -145,15 +143,15 @@
             jax.ShapeDtypeStruct((ITERS, blocks, 4, half, width), jnp.float32),
             jax.ShapeDtypeStruct((8, moments), jnp.float32),
         ),
-        in_specs=[hbm] * 6,
+        in_specs=[hbm] * 10,
         out_specs=(hbm, pl.BlockSpec(memory_space=pltpu.VMEM)),
         scratch_shapes=[
-            pltpu.VMEM((blocks + 1, 12, rows, width), jnp.float32),
+            pltpu.VMEM((blocks + 1, 10, rows, width), jnp.float32),
             pltpu.VMEM((blocks, 8, rows, width), jnp.float32),
             pltpu.VMEM((blocks, 6, rows, width), jnp.float32),
             pltpu.VMEM((blocks, 4, rows, width), jnp.float32),
             pltpu.VMEM((moments, 128), jnp.float32),
-            pltpu.SemaphoreType.DMA((6,)),
+            pltpu.SemaphoreType.DMA((10,)),
             pltpu.SemaphoreType.DMA((ITERS,)),
         ],
         compiler_params=pltpu.CompilerParams(vmem_limit_bytes=60 << 20),
@@ -161,7 +159,7 @@
     )(*pieces)
 
 
-def combine_kernel(at, weights, basis, out, *, blocks, width):
+def combine_kernel(weights, basis, out, *, blocks, width):
     chunks = width // 128
     sums = [[None] * chunks for _ in range(blocks)]
     for k in range(ITERS):
@@ -177,19 +175,19 @@
             out[w, 0, :, 128 * c:128 * c + 128] = sums[w][c]
 
 
-def combine(at, weights, basis, half, width):
+def combine(first, weights, basis, half, width):
     blocks = basis.shape[1]
     return pl.pallas_call(
         functools.partial(combine_kernel, blocks=blocks, width=width),
         out_shape=jax.ShapeDtypeStruct((blocks, 2, half, width), jnp.float32),
-        grid_spec=pltpu.PrefetchScalarGridSpec(
-            num_scalar_prefetch=2,
-            grid=(2, half // 8),
-            in_specs=[pl.BlockSpec((ITERS, blocks, 1, 8, width), lambda l, t, at, e: (0, 0, at[0] + l, t, 0))],
-            out_specs=pl.BlockSpec((blocks, 1, 8, width), lambda l, t, at, e: (0, l, t, 0)),
-        ),
+        grid=(2, half // 8),
+        in_specs=[
+            pl.BlockSpec(memory_space=pltpu.SMEM),
+            pl.BlockSpec((ITERS, blocks, 1, 8, width), lambda l, t: (0, 0, first + l, t, 0)),
+        ],
+        out_specs=pl.BlockSpec((blocks, 1, 8, width), lambda l, t: (0, l, t, 0)),
         name="combine",
-    )(at, weights, basis)
+    )(weights, basis)
 
 
 def dense(nu, blocks):
@@ -225,29 +223,39 @@
     blocks, layers, ny, width = right_side.shape
     half = ny // 2
     peers_z, peers_y = lax.axis_size("gz"), lax.axis_size("gy")
-    parity = lax.axis_index("gz") % 2
+    even = lax.axis_index("gz") % 2 == 0
     field = jnp.concatenate([right_side, diagonal[None]], axis=0)
     above = lax.ppermute(field[:, :, ny - EDGE:], "gy", pairs(peers_y, 1))
     under = lax.ppermute(field[:, :, :EDGE], "gy", pairs(peers_y, -1))
     first = jnp.concatenate([field[:, :, :half + EDGE], above], axis=2)
     second = jnp.concatenate([field[:, :, half:], under, field[:, :, half - EDGE:half]], axis=2)
-    keep = jnp.where(parity == 0, first, second)
-    send = jnp.where(parity == 0, second, first)
-    got = lax.ppermute(send, "gz", swap_pairs(peers_z, 1))
-    low_keep = lax.ppermute(keep, "gz", pairs(peers_z, 2))
-    high_keep = lax.ppermute(keep, "gz", pairs(peers_z, -2))
-    low_got = lax.ppermute(got, "gz", pairs(peers_z, 2))
-    high_got = lax.ppermute(got, "gz", pairs(peers_z, -2))
-    basis, nu = krylov((keep, got, low_keep, low_got, high_keep, high_got), blocks, half, width)
+
+    swap = swap_pairs(peers_z, 1)
+    inward = [(i, j) for i, j in pairs(peers_z, 2) if i % 2 == 0] + [(i, j) for i, j in pairs(peers_z, -2) if i % 2]
+    outward = [(j, i) for i, j in inward]
+    send_near = jnp.where(even, second[:, 1], first[:, 0])
+    send_far = jnp.where(even, second[:, 0], first[:, 1])
+    keep_near = jnp.where(even, first[:, 1], second[:, 0])
+    keep_far = jnp.where(even, first[:, 0], second[:, 1])
+    got_near = lax.ppermute(send_near, "gz", swap)
+    in_one = lax.ppermute(keep_near, "gz", inward)
+    out_one = lax.ppermute(keep_far, "gz", outward)
+    got_far = lax.ppermute(send_far, "gz", swap)
+    out_two = lax.ppermute(keep_near, "gz", outward)
+    in_two = lax.ppermute(got_near, "gz", inward)
+    out_three = lax.ppermute(got_near, "gz", outward)
+    in_three = lax.ppermute(got_far, "gz", inward)
+    pieces = (in_one, in_two, in_three, keep_far, keep_near, got_near, got_far, out_one, out_two, out_three)
+    basis, nu = krylov(pieces, blocks, half, width)
     nu = all_sum(nu[:1], ("gy", "gz")).reshape(2 * ITERS + 1, blocks, blocks)
     hessenberg, weights = dense(nu, blocks)
-    mine = (2 * parity).astype(jnp.int32)
-    theirs = combine((2 - mine)[None], weights, basis, half, width)
-    back = lax.ppermute(theirs, "gz", swap_pairs(peers_z, 1))
-    own = combine(mine[None], weights, basis, half, width)
-    upper = jnp.where(parity == 0, own, back)
-    lower = jnp.where(parity == 0, back, own)
-    return jnp.concatenate([upper, lower], axis=2), hessenberg
+    theirs = combine(2, weights, basis, half, width)
+    back = lax.ppermute(theirs, "gz", swap)
+    own = combine(0, weights, basis, half, width)
+    parts = [[jnp.where(even, own[:, 0], back[:, 0]), jnp.where(even, back[:, 1], own[:, 1])],
+             [jnp.where(even, own[:, 1], back[:, 1]), jnp.where(even, back[:, 0], own[:, 0])]]
+    whole = jnp.stack([jnp.concatenate(part, axis=1) for part in parts], axis=1)
+    return whole, hessenberg
 
 
 def solution(mesh):

time: 179 us -> 162 us (0.905)
  waiting for transfers between devices: 88 us -> 63.2 us
  starting transfers between devices: 22 us -> 30.8 us
  local copies, waits for them, and re-layouts: 2.96 us -> 5.42 us
  Pallas kernels: 43.1 us -> 41 us
    ppermute x6 -> x9, waiting for transfers between devices: 73.3 us -> 51.7 us  [the longest x1 15.4 us: body(): out_three = lax.ppermute(got_near, 'gz', outward)]
    ppermute x6 -> x9, starting transfers between devices: 12.2 us -> 21.6 us  [the longest x1 5.3 us: body(): in_three = lax.ppermute(got_far, 'gz', inward)]
    ppermute x1, waiting for transfers between devices: 3.43 us -> 0.01 us  [body(): under = lax.ppermute(field[:, :, :EDGE], 'gy', pairs(peers_y, -1))]
    unnamed x16 -> x29, local copies, waits for them, and re-layouts: 1.15 us -> 3.61 us
  transfers between devices with their start and end apart: 13 -> 16, of which waited for: 11 -> 10; matrix products, arithmetic and copies ran while one was open for 0% -> 1% of each run, Pallas kernels for 4% -> 4%
where the time goes in v2:
time: 162 us; the launch traced here: 161 us
  waiting for transfers between devices  63.2 us (39%)
  Pallas kernels  41 us (25%)
  starting transfers between devices  30.8 us (19%)
  other arithmetic  17.6 us (11%)
  local copies, waits for them, and re-layouts  5.42 us (3%)
  matrix products  1.84 us (1%)
    pallas_call x1, Pallas kernels, krylov(): pl.pallas_call(functools.partial(krylov_kernel, blocks=blocks, half=half,...  27.9 us
    ppermute x1, waiting for transfers between devices, body(): out_three = lax.ppermute(got_near, 'gz', outward)  15.4 us
    pallas_call x2, Pallas kernels, combine(): pl.pallas_call(functools.partial(combine_kernel, blocks=blocks, width=wid...  13.1 us
    ppermute x1, waiting for transfers between devices, body(): back = lax.ppermute(theirs, 'gz', swap)  13 us
    ppermute x5, waiting for transfers between devices, all_sum(): array = array + lax.ppermute(array, axis, swap_pairs(peers, bit))  11.5 us
    ppermute x1, waiting for transfers between devices, body(): got_near = lax.ppermute(send_near, 'gz', swap)  10.5 us
    ppermute x1, waiting for transfers between devices, body(): got_far = lax.ppermute(send_far, 'gz', swap)  9.99 us
    ppermute x1, starting transfers between devices, body(): in_three = lax.ppermute(got_far, 'gz', inward)  5.3 us
  transfers between devices with their start and end apart: 16, of which 10 were waited for; matrix products, arithmetic and copies ran while one was open for 1% of the time, Pallas kernels for 4%

profile of v2, /device:TPU:0, one launch (start us, length us, event | category | flops | bytes accessed | tf_op | source)
XLA Modules:
  0.0 160.9 jit_solution(12155156200238482908)
XLA Ops:
  0.6 1.3 fusion.6
  1.9 1.3 collective-permute-start.1
  3.2 3.0 %collective-permute-start = (f32[9,2,4,512]{3,2,0,1:T(4,128)S(1)}, f32[9,2,4,512]{3,2,0,1:T(4,128)S(1)}, u32[]{:S(2)}, u32[]{:S(2)}) collective-permute-start(f32[9,2,4,512]{3,2,0,1:T(4,128)S(1)} %get-tuple-element.23), channel_id=1, source_target_pairs={{0,1},{1,2},{2,3},{4,5},{5,6},{6,7},{8,9},{9,10},{10,11},{12,13},{... | collective-permute-start | bytes 442376 | tf_op jit(solution)/shard_map/ppermute | solution.py:228
  6.3 1.3 fusion
  9.4 3.1 %collective-permute-start.3 = (f32[9,40,512]{2,1,0:T(8,128)S(1)}, f32[9,40,512]{2,1,0:T(8,128)S(1)}, u32[]{:S(2)}, u32[]{:S(2)}) collective-permute-start(f32[9,40,512]{2,1,0:T(8,128)S(1)} %get-tuple-element.21), channel_id=1, source_target_pairs={{0,4},{4,0},{8,12},{12,8},{16,20},{20,16},{24,28},{28,24},{1,5},{5... | collective-permute-start | bytes 2211848 | tf_op jit(solution)/shard_map/ppermute | solution.py:240
  12.5 3.5 %collective-permute-start.2 = (f32[9,40,512]{2,1,0:T(8,128)S(1)}, f32[9,40,512]{2,1,0:T(8,128)S(1)}, u32[]{:S(2)}, u32[]{:S(2)}) collective-permute-start(f32[9,40,512]{2,1,0:T(8,128)S(1)} %get-tuple-element.22.refs_4_), channel_id=1, source_target_pairs={{0,8},{8,16},{16,24},{12,4},{20,12},{28,20},{1,9},{9,17},{17,25},{... | collective-permute-start | bytes 2211848 | tf_op jit(solution)/shard_map/ppermute | solution.py:241
  16.1 1.3 collective-permute-start.8
  17.4 1.3 collective-permute-start.7
  18.7 10.5 %collective-permute-done.3.refs_5_ = f32[9,40,512]{2,1,0:T(8,128)S(1)} collective-permute-done((f32[9,40,512]{2,1,0:T(8,128)S(1)}, f32[9,40,512]{2,1,0:T(8,128)S(1)}, u32[]{:S(2)}, u32[]{:S(2)}) %collective-permute-start.3) | collective-permute-done | bytes 737312 | tf_op jit(solution)/shard_map/ppermute | solution.py:240
  29.2 4.5 %collective-permute-start.4 = (f32[9,40,512]{2,1,0:T(8,128)S(1)}, f32[9,40,512]{2,1,0:T(8,128)S(1)}, u32[]{:S(2)}, u32[]{:S(2)}) collective-permute-start(f32[9,40,512]{2,1,0:T(8,128)S(1)} %collective-permute-done.3.refs_5_), channel_id=1, source_target_pairs={{0,8},{8,16},{16,24},{12,4},{20,12},{28,20},{1,9},{9,17},{17,25},{... | collective-permute-start | bytes 2211848 | tf_op jit(solution)/shard_map/ppermute | solution.py:245
  33.7 1.3 collective-permute-start.9
  35.0 10.0 %collective-permute-done.5.refs_6_ = f32[9,40,512]{2,1,0:T(8,128)S(1)} collective-permute-done((f32[9,40,512]{2,1,0:T(8,128)S(1)}, f32[9,40,512]{2,1,0:T(8,128)S(1)}, u32[]{:S(2)}, u32[]{:S(2)}) %collective-permute-start.5) | collective-permute-done | bytes 737312 | tf_op jit(solution)/shard_map/ppermute | solution.py:243
  45.0 5.3 %collective-permute-start.6 = (f32[9,40,512]{2,1,0:T(8,128)S(1)}, f32[9,40,512]{2,1,0:T(8,128)}, u32[]{:S(2)}, u32[]{:S(2)}) collective-permute-start(f32[9,40,512]{2,1,0:T(8,128)S(1)} %collective-permute-done.5.refs_6_), channel_id=1, source_target_pairs={{0,8},{8,16},{16,24},{12,4},{20,12},{28,20},{1,9},{9,17},{17,25},{... | collective-permute-start | bytes 2211848 | tf_op jit(solution)/shard_map/ppermute | solution.py:247
  50.3 2.8 %collective-permute-done.7.refs_7_ = f32[9,40,512]{2,1,0:T(8,128)S(1)} collective-permute-done((f32[9,40,512]{2,1,0:T(8,128)S(1)}, f32[9,40,512]{2,1,0:T(8,128)S(1)}, u32[]{:S(2)}, u32[]{:S(2)}) %collective-permute-start.7) | collective-permute-done | bytes 737312 | tf_op jit(solution)/shard_map/ppermute | solution.py:242
  53.1 15.4 %collective-permute-done.9.refs_9_ = f32[9,40,512]{2,1,0:T(8,128)S(1)} collective-permute-done((f32[9,40,512]{2,1,0:T(8,128)S(1)}, f32[9,40,512]{2,1,0:T(8,128)S(1)}, u32[]{:S(2)}, u32[]{:S(2)}) %collective-permute-start.9) | collective-permute-done | bytes 737312 | tf_op jit(solution)/shard_map/ppermute | solution.py:246
  69.5 27.9 %krylov.1 = (f32[3,8,4,32,512]{4,3,2,1,0:T(8,128)}, f32[8,448]{1,0:T(8,128)}) custom-call(f32[9,40,512]{2,1,0:T(8,128)} %copy-done.7, f32[9,40,512]{2,1,0:T(8,128)} %copy-done.11, f32[9,40,512]{2,1,0:T(8,128)} %collective-permute-done.6.refs_2_, f32[9,40,512]{2,1,0:T(8,128)} %copy-done.4, f32[9,40,512]{2,1,0:T(8,128)} %copy-done.5, f32[9,40,512]{2,1,0:T(8,128)} %copy-done.6, ...), custom_call_target="tpu_custom_call" | custom-call | tf_op jit(solution)/shard_map/krylov/pallas_call | solution.py:140
  100.0 3.6 %collective-permute-done.11 = f32[1,448]{1,0:T(1,128)S(1)} collective-permute-done((f32[1,448]{1,0:T(1,128)S(1)}, f32[1,448]{1,0:T(1,128)S(1)}, u32[]{:S(2)}, u32[]{:S(2)}) %collective-permute-start.11) | collective-permute-done | bytes 1824 | tf_op jit(solution)/shard_map/ppermute | solution.py:34
  104.4 2.8 %collective-permute-done.12 = f32[1,448]{1,0:T(1,128)S(1)} collective-permute-done((f32[1,448]{1,0:T(1,128)S(1)}, f32[1,448]{1,0:T(1,128)S(1)}, u32[]{:S(2)}, u32[]{:S(2)}) %collective-permute-start.12) | collective-permute-done | bytes 1824 | tf_op jit(solution)/shard_map/ppermute | solution.py:34
  107.2 1.5 collective-permute-start.13
  108.7 2.0 %collective-permute-done.13 = f32[1,448]{1,0:T(1,128)S(1)} collective-permute-done((f32[1,448]{1,0:T(1,128)S(1)}, f32[1,448]{1,0:T(1,128)S(1)}, u32[]{:S(2)}, u32[]{:S(2)}) %collective-permute-start.13) | collective-permute-done | bytes 1824 | tf_op jit(solution)/shard_map/ppermute | solution.py:34
  110.8 2.5 %collective-permute-start.14 = (f32[1,448]{1,0:T(1,128)S(1)}, f32[1,448]{1,0:T(1,128)S(1)}, u32[]{:S(2)}, u32[]{:S(2)}) collective-permute-start(f32[1,448]{1,0:T(1,128)S(1)} %add.76), channel_id=1, source_target_pairs={{0,16},{4,20},{8,24},{12,28},{16,0},{20,4},{24,8},{28,12},{1,17},{... | collective-permute-start | bytes 5384 | tf_op jit(solution)/shard_map/ppermute | solution.py:34
  113.3 1.9 %collective-permute-done.14 = f32[1,448]{1,0:T(1,128)S(1)} collective-permute-done((f32[1,448]{1,0:T(1,128)S(1)}, f32[1,448]{1,0:T(1,128)S(1)}, u32[]{:S(2)}, u32[]{:S(2)}) %collective-permute-start.14) | collective-permute-done | bytes 1824 | tf_op jit(solution)/shard_map/ppermute | solution.py:34
  116.6 2.9 %cholesky.31 = f32[32,32]{1,0:T(8,128)S(1)} custom-call(f32[32,32]{1,0:T(8,128)S(1)} %fusion.7), custom_call_target="Cholesky" | custom-call | tf_op jit(solution)/shard_map/jit(cholesky)/cholesky | solution.py:205
  120.9 1.8 %custom-call.17 = f32[1,24,24]{1,2,0:T(8,128)S(1)} custom-call(f32[1,24,24]{2,1,0:T(8,128)S(1)} %fusion.11), custom_call_target="InvertDiagBlocksLowerTriangular" | custom-call | tf_op jit(solution)/shard_map/jit(_solve_triangular)/triangular_solve | solution.py:206
  123.4 2.2 %cholesky.59 = f32[24,24]{1,0:T(8,128)S(1)} custom-call(f32[24,24]{1,0:T(8,128)S(1)} %fusion.21), custom_call_target="Cholesky" | custom-call | tf_op jit(solution)/shard_map/jit(cholesky)/cholesky | solution.py:217
  127.0 1.8 %custom-call.18 = f32[1,24,24]{1,2,0:T(8,128)S(1)} custom-call(f32[1,24,24]{2,1,0:T(8,128)S(1)} %fusion.8), custom_call_target="InvertDiagBlocksLowerTriangular" | custom-call | tf_op jit(solution)/shard_map/jit(_cho_solve)/triangular_solve | solution.py:217
  130.0 6.5 %combine.3 = f32[8,2,32,512]{3,2,1,0:T(8,128)} custom-call(f32[24,8]{1,0:T(8,128)} %fusion.29.weights, f32[3,8,4,32,512]{4,3,2,1,0:T(8,128)} %get-tuple-element.5.basis), custom_call_target="tpu_custom_call" | custom-call | tf_op jit(solution)/shard_map/combine/pallas_call | solution.py:180
  136.6 1.3 collective-permute-start.15
  137.9 6.5 %combine.2 = f32[8,2,32,512]{3,2,1,0:T(8,128)} custom-call(f32[24,8]{1,0:T(8,128)} %fusion.29.weights, f32[3,8,4,32,512]{4,3,2,1,0:T(8,128)} %get-tuple-element.5.basis), custom_call_target="tpu_custom_call" | custom-call | tf_op jit(solution)/shard_map/combine/pallas_call | solution.py:180
  144.4 13.0 %collective-permute-done.15 = f32[8,2,32,512]{3,2,1,0:T(8,128)S(1)} collective-permute-done((f32[8,2,32,512]{3,2,1,0:T(8,128)}, f32[8,2,32,512]{3,2,1,0:T(8,128)S(1)}, u32[]{:S(2)}, u32[]{:S(2)}) %collective-permute-start.15) | collective-permute-done | bytes 1048608 | tf_op jit(solution)/shard_map/ppermute | solution.py:253
  157.4 1.4 select_bitcast_fusion.6
  159.4 1.5 copy.47
  (90 shorter events, 12.6 us)
Async XLA Ops:
  0.6 5.7 %copy-start.3 = (f32[2,64,512]{2,1,0:T(8,128)S(1)}, f32[2,64,512]{2,1,0:T(8,128)}, u32[]{:S(2)}) copy-start(f32[2,64,512]{2,1,0:T(8,128)} %param.3) | copy-start | bytes 786436
  0.6 5.7 %copy-start = (f32[8,2,64,512]{3,2,1,0:T(8,128)S(1)}, f32[8,2,64,512]{3,2,1,0:T(8,128)}, u32[]{:S(2)}) copy-start(f32[8,2,64,512]{3,2,1,0:T(8,128)} %param.2) | copy-start | bytes 6291460
  1.9 5.7 %collective-permute-start.1 = (f32[9,2,4,512]{3,2,0,1:T(4,128)S(1)}, f32[9,2,4,512]{3,2,0,1:T(4,128)S(1)}, u32[]{:S(2)}, u32[]{:S(2)}) collective-permute-start(f32[9,2,4,512]{3,2,0,1:T(4,128)S(1)} %get-tuple-element.24), channel_id=1, source_target_pairs={{1,0},{2,1},{3,2},{5,4},{6,5},{7,6},{9,8},{10,9},{11,10},{13,12},{... | collective-permute-start | bytes 442376 | tf_op jit(solution)/shard_map/ppermute | solution.py:229
  3.2 4.7 %collective-permute-start = (f32[9,2,4,512]{3,2,0,1:T(4,128)S(1)}, f32[9,2,4,512]{3,2,0,1:T(4,128)S(1)}, u32[]{:S(2)}, u32[]{:S(2)}) collective-permute-start(f32[9,2,4,512]{3,2,0,1:T(4,128)S(1)} %get-tuple-element.23), channel_id=1, source_target_pairs={{0,1},{1,2},{2,3},{4,5},{5,6},{6,7},{8,9},{9,10},{10,11},{12,13},{... | collective-permute-start | bytes 442376 | tf_op jit(solution)/shard_map/ppermute | solution.py:228
  7.7 1.4 copy-start.2
  9.4 60.0 %copy-start.4 = (f32[9,40,512]{2,1,0:T(8,128)}, f32[9,40,512]{2,1,0:T(8,128)S(1)}, u32[]{:S(2)}) copy-start(f32[9,40,512]{2,1,0:T(8,128)S(1)} %get-tuple-element.19.refs_3_) | copy-start | bytes 2211844
  9.4 60.0 %copy-start.5 = (f32[9,40,512]{2,1,0:T(8,128)}, f32[9,40,512]{2,1,0:T(8,128)S(1)}, u32[]{:S(2)}) copy-start(f32[9,40,512]{2,1,0:T(8,128)S(1)} %get-tuple-element.22.refs_4_) | copy-start | bytes 2211844
  9.4 19.8 %collective-permute-start.3 = (f32[9,40,512]{2,1,0:T(8,128)S(1)}, f32[9,40,512]{2,1,0:T(8,128)S(1)}, u32[]{:S(2)}, u32[]{:S(2)}) collective-permute-start(f32[9,40,512]{2,1,0:T(8,128)S(1)} %get-tuple-element.21), channel_id=1, source_target_pairs={{0,4},{4,0},{8,12},{12,8},{16,20},{20,16},{24,28},{28,24},{1,5},{5... | collective-permute-start | bytes 2211848 | tf_op jit(solution)/shard_map/ppermute | solution.py:240
  12.5 21.2 %collective-permute-start.2 = (f32[9,40,512]{2,1,0:T(8,128)S(1)}, f32[9,40,512]{2,1,0:T(8,128)S(1)}, u32[]{:S(2)}, u32[]{:S(2)}) collective-permute-start(f32[9,40,512]{2,1,0:T(8,128)S(1)} %get-tuple-element.22.refs_4_), channel_id=1, source_target_pairs={{0,8},{8,16},{16,24},{12,4},{20,12},{28,20},{1,9},{9,17},{17,25},{... | collective-permute-start | bytes 2211848 | tf_op jit(solution)/shard_map/ppermute | solution.py:241
  16.0 29.0 %collective-permute-start.5 = (f32[9,40,512]{2,1,0:T(8,128)S(1)}, f32[9,40,512]{2,1,0:T(8,128)S(1)}, u32[]{:S(2)}, u32[]{:S(2)}) collective-permute-start(f32[9,40,512]{2,1,0:T(8,128)S(1)} %get-tuple-element.20), channel_id=1, source_target_pairs={{0,4},{4,0},{8,12},{12,8},{16,20},{20,16},{24,28},{28,24},{1,5},{5... | collective-permute-start | bytes 2211848 | tf_op jit(solution)/shard_map/ppermute | solution.py:243
  16.1 34.2 %collective-permute-start.8 = (f32[9,40,512]{2,1,0:T(8,128)S(1)}, f32[9,40,512]{2,1,0:T(8,128)S(1)}, u32[]{:S(2)}, u32[]{:S(2)}) collective-permute-start(f32[9,40,512]{2,1,0:T(8,128)S(1)} %get-tuple-element.22.refs_4_), channel_id=1, source_target_pairs={{8,0},{16,8},{24,16},{4,12},{12,20},{20,28},{9,1},{17,9},{25,17},{... | collective-permute-start | bytes 2211848 | tf_op jit(solution)/shard_map/ppermute | solution.py:244
  17.4 35.8 %collective-permute-start.7 = (f32[9,40,512]{2,1,0:T(8,128)S(1)}, f32[9,40,512]{2,1,0:T(8,128)S(1)}, u32[]{:S(2)}, u32[]{:S(2)}) collective-permute-start(f32[9,40,512]{2,1,0:T(8,128)S(1)} %get-tuple-element.19.refs_3_), channel_id=1, source_target_pairs={{8,0},{16,8},{24,16},{4,12},{12,20},{20,28},{9,1},{17,9},{25,17},{... | collective-permute-start | bytes 2211848 | tf_op jit(solution)/shard_map/ppermute | solution.py:242
  29.2 40.2 %copy-start.6 = (f32[9,40,512]{2,1,0:T(8,128)}, f32[9,40,512]{2,1,0:T(8,128)S(1)}, u32[]{:S(2)}) copy-start(f32[9,40,512]{2,1,0:T(8,128)S(1)} %collective-permute-done.3.refs_5_) | copy-start | bytes 2211844
  29.2 23.9 %collective-permute-start.4 = (f32[9,40,512]{2,1,0:T(8,128)S(1)}, f32[9,40,512]{2,1,0:T(8,128)S(1)}, u32[]{:S(2)}, u32[]{:S(2)}) collective-permute-start(f32[9,40,512]{2,1,0:T(8,128)S(1)} %collective-permute-done.3.refs_5_), channel_id=1, source_target_pairs={{0,8},{8,16},{16,24},{12,4},{20,12},{28,20},{1,9},{9,17},{17,25},{... | collective-permute-start | bytes 2211848 | tf_op jit(solution)/shard_map/ppermute | solution.py:245
  33.7 35.7 %copy-start.7 = (f32[9,40,512]{2,1,0:T(8,128)}, f32[9,40,512]{2,1,0:T(8,128)S(1)}, u32[]{:S(2)}) copy-start(f32[9,40,512]{2,1,0:T(8,128)S(1)} %collective-permute-done.2.refs_0_) | copy-start | bytes 2211844
  33.7 34.8 %collective-permute-start.9 = (f32[9,40,512]{2,1,0:T(8,128)S(1)}, f32[9,40,512]{2,1,0:T(8,128)S(1)}, u32[]{:S(2)}, u32[]{:S(2)}) collective-permute-start(f32[9,40,512]{2,1,0:T(8,128)S(1)} %collective-permute-done.3.refs_5_), channel_id=1, source_target_pairs={{8,0},{16,8},{24,16},{4,12},{12,20},{20,28},{9,1},{17,9},{25,17},{... | collective-permute-start | bytes 2211848 | tf_op jit(solution)/shard_map/ppermute | solution.py:246
  45.0 24.4 %copy-start.8 = (f32[9,40,512]{2,1,0:T(8,128)}, f32[9,40,512]{2,1,0:T(8,128)S(1)}, u32[]{:S(2)}) copy-start(f32[9,40,512]{2,1,0:T(8,128)S(1)} %collective-permute-done.5.refs_6_) | copy-start | bytes 2211844
  45.0 24.4 %collective-permute-start.6 = (f32[9,40,512]{2,1,0:T(8,128)S(1)}, f32[9,40,512]{2,1,0:T(8,128)}, u32[]{:S(2)}, u32[]{:S(2)}) collective-permute-start(f32[9,40,512]{2,1,0:T(8,128)S(1)} %collective-permute-done.5.refs_6_), channel_id=1, source_target_pairs={{0,8},{8,16},{16,24},{12,4},{20,12},{28,20},{1,9},{9,17},{17,25},{... | collective-permute-start | bytes 2211848 | tf_op jit(solution)/shard_map/ppermute | solution.py:247
  50.3 18.2 %copy-start.9 = (f32[9,40,512]{2,1,0:T(8,128)}, f32[9,40,512]{2,1,0:T(8,128)S(1)}, u32[]{:S(2)}) copy-start(f32[9,40,512]{2,1,0:T(8,128)S(1)} %collective-permute-done.8.refs_8_) | copy-start | bytes 2211844
  53.1 15.4 %copy-start.10 = (f32[9,40,512]{2,1,0:T(8,128)}, f32[9,40,512]{2,1,0:T(8,128)S(1)}, u32[]{:S(2)}) copy-start(f32[9,40,512]{2,1,0:T(8,128)S(1)} %collective-permute-done.7.refs_7_) | copy-start | bytes 2211844
  53.1 15.4 %copy-start.11 = (f32[9,40,512]{2,1,0:T(8,128)}, f32[9,40,512]{2,1,0:T(8,128)S(1)}, u32[]{:S(2)}) copy-start(f32[9,40,512]{2,1,0:T(8,128)S(1)} %collective-permute-done.4.refs_1_) | copy-start | bytes 2211844
  68.5 0.9 copy-start.12
  98.1 1.2 collective-permute-start.10
  100.0 3.6 %collective-permute-start.11 = (f32[1,448]{1,0:T(1,128)S(1)}, f32[1,448]{1,0:T(1,128)S(1)}, u32[]{:S(2)}, u32[]{:S(2)}) collective-permute-start(f32[1,448]{1,0:T(1,128)S(1)} %slice_add_fusion), channel_id=1, source_target_pairs={{0,2},{1,3},{2,0},{3,1},{4,6},{5,7},{6,4},{7,5},{8,10},{9,11},{10,... | collective-permute-start | bytes 5384 | tf_op jit(solution)/shard_map/ppermute | solution.py:34
  103.6 3.6 %collective-permute-start.12 = (f32[1,448]{1,0:T(1,128)S(1)}, f32[1,448]{1,0:T(1,128)S(1)}, u32[]{:S(2)}, u32[]{:S(2)}) collective-permute-start(f32[1,448]{1,0:T(1,128)S(1)} %add.74), channel_id=1, source_target_pairs={{0,4},{4,0},{8,12},{12,8},{16,20},{20,16},{24,28},{28,24},{1,5},{5... | collective-permute-start | bytes 5384 | tf_op jit(solution)/shard_map/ppermute | solution.py:34
  107.2 3.6 %collective-permute-start.13 = (f32[1,448]{1,0:T(1,128)S(1)}, f32[1,448]{1,0:T(1,128)S(1)}, u32[]{:S(2)}, u32[]{:S(2)}) collective-permute-start(f32[1,448]{1,0:T(1,128)S(1)} %add.75), channel_id=1, source_target_pairs={{0,8},{4,12},{8,0},{12,4},{16,24},{20,28},{24,16},{28,20},{1,9},{5... | collective-permute-start | bytes 5384 | tf_op jit(solution)/shard_map/ppermute | solution.py:34
  110.8 4.5 %collective-permute-start.14 = (f32[1,448]{1,0:T(1,128)S(1)}, f32[1,448]{1,0:T(1,128)S(1)}, u32[]{:S(2)}, u32[]{:S(2)}) collective-permute-start(f32[1,448]{1,0:T(1,128)S(1)} %add.76), channel_id=1, source_target_pairs={{0,16},{4,20},{8,24},{12,28},{16,0},{20,4},{24,8},{28,12},{1,17},{... | collective-permute-start | bytes 5384 | tf_op jit(solution)/shard_map/ppermute | solution.py:34
  123.1 13.5 %copy-start.13 = (f32[24,32]{1,0:T(8,128)}, f32[24,32]{1,0:T(8,128)S(1)}, u32[]{:S(2)}) copy-start(f32[24,32]{1,0:T(8,128)S(1)} %convolution_select_fusion) | copy-start | bytes 9220
  136.6 20.8 %collective-permute-start.15 = (f32[8,2,32,512]{3,2,1,0:T(8,128)}, f32[8,2,32,512]{3,2,1,0:T(8,128)S(1)}, u32[]{:S(2)}, u32[]{:S(2)}) collective-permute-start(f32[8,2,32,512]{3,2,1,0:T(8,128)} %combine.3), channel_id=1, source_target_pairs={{0,4},{4,0},{8,12},{12,8},{16,20},{20,16},{24,28},{28,24},{1,5},{5... | collective-permute-start | bytes 3145736 | tf_op jit(solution)/shard_map/ppermute | solution.py:253
  144.4 14.5 %copy-start.1 = (f32[8,2,32,512]{3,2,1,0:T(8,128)S(1)}, f32[8,2,32,512]{3,2,1,0:T(8,128)}, u32[]{:S(2)}) copy-start(f32[8,2,32,512]{3,2,1,0:T(8,128)} %combine.2) | copy-start | bytes 3145732

commit v3 on v2

v3 whole, which is shorter than its diff:
```python
import functools

import jax
import jax.numpy as jnp
import numpy as np
from jax import lax
from jax.experimental import pallas as pl
from jax.experimental.pallas import tpu as pltpu
from jax.sharding import PartitionSpec as P

ITERS = 3
EDGE = 4
CENTER, SPREAD = 7.6, 2.6
BETA = (0.0, 1.0, 1.5)
HIGHEST = lax.Precision.HIGHEST


def pairs(peers, step):
    return [(i, i + step) for i in range(peers) if 0 <= i + step < peers]


def swap_pairs(peers, bit):
    return [(i, i ^ bit) for i in range(peers)]


def all_sum(array, axes):
    for axis in axes:
        peers = lax.axis_size(axis)
        if peers & (peers - 1):
            array = lax.psum(array, axis)
            continue
        bit = 1
        while bit < peers:
            array = array + lax.ppermute(array, axis, swap_pairs(peers, bit))
            bit *= 2
    return array


def row_masks(half, width):
    rows = half + 2 * EDGE
    parity = lax.rem(lax.axis_index("gz"), 2)
    at_y = lax.axis_index("gy")
    no_below = jnp.logical_and(at_y == lax.axis_size("gy") - 1, parity == 1)
    no_above = jnp.logical_and(at_y == 0, parity == 0)
    row = lax.broadcasted_iota(jnp.int32, (rows, width), 0)
    below = jnp.where(no_below, 0.0, 1.0)
    above = jnp.where(no_above, 0.0, 1.0)
    return jnp.where(row < half, 1.0, jnp.where(row < half + EDGE, below, above))


def side_flags():
    place = lax.axis_index("gz")
    parity = lax.rem(place, 2)
    downward = jnp.where(place >= 2, 1.0, 0.0)
    upward = jnp.where(place < lax.axis_size("gz") - 2, 1.0, 0.0)
    return (jnp.where(parity == 0, downward, upward), jnp.where(parity == 0, upward, downward))


def set_scales(scale_ref, diag_ref, fields, blocks, slots, half, width):
    scale_ref[...] = row_masks(half, width) * (1.0 / SPREAD)
    low, high = side_flags()
    for slot, (layer, ref) in enumerate(zip(slots, fields)):
        value = scale_ref[...] * (ref[blocks] + (6.0 - CENTER))
        if layer < 4:
            value = value * low
        if layer > 7:
            value = value * high
        diag_ref[slot] = value


def step_of(scale, diag, low, mid, high, before, beta, flag=None):
    rows, width = mid.shape
    lane = lax.broadcasted_iota(jnp.int32, (rows, width), 1)
    beside = low + high
    beside = beside + pltpu.roll(mid, 1, 0) + pltpu.roll(mid, rows - 1, 0)
    beside = beside + jnp.where(lane == 0, 0.0, pltpu.roll(mid, 1, 1))
    beside = beside + jnp.where(lane == width - 1, 0.0, pltpu.roll(mid, width - 1, 1))
    if flag is not None:
        scale = scale * flag
    value = diag * mid - scale * beside
    if beta:
        value = value - beta * before
    return value


def gram_part(acc, views, moment, layers, blocks, half, width, start):
    left, right = views[moment // 2], views[(moment + 1) // 2]
    upper = [(v, w) for v in range(blocks) for w in range(v, blocks)]

    def spot(step, sums):
        at = pl.multiple_of(step * 8, 8)
        sums = list(sums)
        for layer in layers:
            for c in range(width // 128):
                lanes = pl.ds(128 * c, 128)
                rights = [right[layer][w, pl.ds(at, 8), lanes] for w in range(blocks)]
                for v in range(blocks):
                    one = rights[v] if left is right else left[layer][v, pl.ds(at, 8), lanes]
                    for n, (a, b) in enumerate(upper):
                        if a == v:
                            sums[n] = sums[n] + one * rights[b]
        return tuple(sums)

    zeros = tuple(jnp.zeros((8, 128), jnp.float32) for _ in upper)
    sums = lax.fori_loop(0, half // 8, spot, zeros)
    base = moment * len(upper)
    for n in range(len(upper)):
        acc[base + n] = sums[n] if start is None else sums[n] + start[base + n]


EARLY = {0: (4, 5, 6, 7), 1: (5, 6, 7), 2: (5, 6, 7), 3: (6, 7), 4: (6, 7)}
LATE = {1: (4,), 2: (4,), 3: (4, 5), 4: (4, 5), 5: (4, 5, 6, 7), 6: (4, 5, 6, 7)}


def early_kernel(*refs, blocks, half, width):
    fields = dict(zip((4, 5, 6, 7, 8, 9), refs[:6]))
    x1, x2, acc, scale_ref, diag_ref = refs[6:]
    slots = (5, 6, 7, 8)
    set_scales(scale_ref, diag_ref, [fields[n] for n in slots], blocks, slots, half, width)
    flag = side_flags()[1]

    def vector(v, carry):
        for slot, n in enumerate(slots):
            x1[slot, v] = step_of(
                scale_ref[...], diag_ref[slot], fields[n - 1][v], fields[n][v], fields[n + 1][v],
                None, 0.0, flag if n == 8 else None)
        for slot, n in enumerate((6, 7)):
            x2[slot, v] = step_of(
                scale_ref[...], diag_ref[n - 5], x1[n - 6, v], x1[n - 5, v], x1[n - 4, v],
                fields[n][v], BETA[1])
        return carry

    lax.fori_loop(0, blocks, vector, 0)
    views = (fields, {n: x1.at[n - 5] for n in slots}, {n: x2.at[n - 6] for n in (6, 7)})
    for moment, layers in EARLY.items():
        gram_part(acc, views, moment, layers, blocks, half, width, None)


def late_kernel(*refs, blocks, half, width):
    fields = dict(zip(range(1, 11), refs[:10]))
    near1, near2, start, x1, x2, nu_out, far1, far2, x3, acc, scale_ref, diag_ref = refs[10:]
    slots = tuple(range(2, 10))
    set_scales(scale_ref, diag_ref, [fields[n] for n in slots], blocks, slots, half, width)
    low, high = side_flags()
    one = {2: far1.at[0], 3: far1.at[1], 4: x1, 9: far1.at[2], **{n: near1.at[n - 5] for n in (5, 6, 7, 8)}}
    two = {3: far2.at[0], 4: x2.at[0], 5: x2.at[1], 6: near2.at[0], 7: near2.at[1], 8: far2.at[1]}
    three = {n: x3.at[n - 4] for n in (4, 5, 6, 7)}

    def flag_of(n):
        return low if n < 4 else high if n > 7 else None

    def vector(v, carry):
        for n in (2, 3, 4, 9):
            one[n][v] = step_of(
                scale_ref[...], diag_ref[n - 2], fields[n - 1][v], fields[n][v], fields[n + 1][v],
                None, 0.0, flag_of(n))
        for n in (3, 4, 5, 8):
            two[n][v] = step_of(
                scale_ref[...], diag_ref[n - 2], one[n - 1][v], one[n][v], one[n + 1][v],
                fields[n][v], BETA[1], flag_of(n))
        for n in (4, 5, 6, 7):
            three[n][v] = step_of(
                scale_ref[...], diag_ref[n - 2], two[n - 1][v], two[n][v], two[n + 1][v],
                one[n][v], BETA[2])
        return carry

    lax.fori_loop(0, blocks, vector, 0)
    views = (fields, one, two, three)
    upper = [(v, w) for v in range(blocks) for w in range(v, blocks)]
    acc[pl.ds(0, len(upper))] = start[pl.ds(0, len(upper))]
    for moment, layers in LATE.items():
        gram_part(acc, views, moment, layers, blocks, half, width, start if moment in EARLY else None)
    total = jnp.sum(acc[...], axis=1)
    nu_out[...] = lax.dot_general(
        jnp.ones((8, 128), jnp.float32), total, (((1,), (1,)), ((), ())),
        precision=HIGHEST, preferred_element_type=jnp.float32)


def krylov(pieces, blocks, half, width):
    rows = half + 2 * EDGE
    moments = 2 * ITERS + 1
    count = blocks * (blocks + 1) // 2
    vmem = pl.BlockSpec(memory_space=pltpu.VMEM)
    sizes = dict(blocks=blocks, half=half, width=width)
    layer = (blocks, rows, width)
    cells = blocks * rows * width

    def out(*shape):
        return jax.ShapeDtypeStruct(shape, jnp.float32)

    near1, near2, start = pl.pallas_call(
        functools.partial(early_kernel, **sizes),
        out_shape=(out(4, *layer), out(2, *layer), out(len(EARLY) * count, 8, 128)),
        in_specs=[vmem] * 6,
        out_specs=(vmem,) * 3,
        scratch_shapes=[pltpu.VMEM((rows, width), jnp.float32), pltpu.VMEM((4, rows, width), jnp.float32)],
        compiler_params=pltpu.CompilerParams(vmem_limit_bytes=20 << 20),
        cost_estimate=pl.CostEstimate(flops=400 * cells, bytes_accessed=16 * cells, transcendentals=0),
        name="early",
    )(*pieces[3:9])
    x1, x2, nu = pl.pallas_call(
        functools.partial(late_kernel, **sizes),
        out_shape=(out(*layer), out(2, *layer), out(8, moments * count)),
        in_specs=[vmem] * 13,
        out_specs=(vmem,) * 3,
        scratch_shapes=[
            pltpu.VMEM((3, *layer), jnp.float32),
            pltpu.VMEM((2, *layer), jnp.float32),
            pltpu.VMEM((4, *layer), jnp.float32),
            pltpu.VMEM((moments * count, 8, 128), jnp.float32),
            pltpu.VMEM((rows, width), jnp.float32),
            pltpu.VMEM((8, rows, width), jnp.float32),
        ],
        compiler_params=pltpu.CompilerParams(vmem_limit_bytes=34 << 20),
        cost_estimate=pl.CostEstimate(flops=400 * cells, bytes_accessed=16 * cells, transcendentals=0),
        name="late",
    )(*pieces, near1, near2, start)
    return near1, near2, x1, x2, nu


def combine_kernel(weights, *refs, blocks, half, width, places):
    out = refs[-1]
    for layer in range(2):
        terms = [(refs[ref].at[at] if at is not None else refs[ref]) for ref, at in places[layer]]

        def tile(step, carry, terms=terms, layer=layer):
            at = pl.multiple_of(step * 8, 8)
            for c in range(width // 128):
                lanes = pl.ds(128 * c, 128)
                sums = [None] * blocks
                for k, term in enumerate(terms):
                    for v in range(blocks):
                        part = term[v, pl.ds(at, 8), lanes]
                        for w in range(blocks):
                            value = weights[k * blocks + v, w] * part
                            sums[w] = value if sums[w] is None else sums[w] + value
                for w in range(blocks):
                    out[w, layer, pl.ds(at, 8), lanes] = sums[w]
            return carry

        lax.fori_loop(0, half // 8, tile, 0)


def combine(weights, arrays, places, blocks, half, width):
    vmem = pl.BlockSpec(memory_space=pltpu.VMEM)
    return pl.pallas_call(
        functools.partial(combine_kernel, blocks=blocks, half=half, width=width, places=places),
        out_shape=jax.ShapeDtypeStruct((blocks, 2, half, width), jnp.float32),
        in_specs=[pl.BlockSpec(memory_space=pltpu.SMEM)] + [vmem] * len(arrays),
        out_specs=vmem,
        compiler_params=pltpu.CompilerParams(vmem_limit_bytes=16 << 20),
        name="combine",
    )(weights, *arrays)


def full_moments(nu, blocks):
    count = blocks * (blocks + 1) // 2
    pick = np.zeros((count, blocks * blocks), np.float32)
    n = 0
    for v in range(blocks):
        for w in range(v, blocks):
            pick[n, v * blocks + w] = pick[n, w * blocks + v] = 1.0
            n += 1
    full = jnp.dot(nu.reshape(-1, count), pick, precision=HIGHEST)
    return full.reshape(-1, blocks, blocks)


def dense(nu, blocks):
    b1, b2 = BETA[1], BETA[2]
    g02 = nu[2] - b1 * nu[0]
    g03 = nu[3] - b2 * nu[1]
    g13 = nu[4] + b1 * g02 - b2 * nu[2]
    gram = jnp.concatenate([
        jnp.concatenate([nu[0], nu[1], g02, g03], axis=1),
        jnp.concatenate([nu[1], nu[2], nu[3], g13], axis=1),
        jnp.concatenate([g02, nu[3], nu[4], nu[5]], axis=1),
        jnp.concatenate([g03, g13, nu[5], nu[6]], axis=1),
    ], axis=0)
    size = ITERS * blocks
    factor = jnp.linalg.cholesky(gram)
    inverse = jax.scipy.linalg.solve_triangular(
        factor[:size, :size], jnp.eye(size, dtype=jnp.float32), lower=True)
    flat = factor.reshape(ITERS + 1, blocks, size + blocks)
    shifted = [SPREAD * flat[k + 1] + CENTER * flat[k]
               + (SPREAD * BETA[k] * flat[k - 1] if BETA[k] else 0.0) for k in range(ITERS)]
    hessenberg = jnp.dot(inverse, jnp.concatenate(shifted, axis=0), precision=HIGHEST)
    row = lax.broadcasted_iota(jnp.int32, hessenberg.shape, 0) // blocks
    col = lax.broadcasted_iota(jnp.int32, hessenberg.shape, 1) // blocks
    hessenberg = jnp.where(col <= row + 1, hessenberg, 0.0)
    normal = jnp.dot(hessenberg, hessenberg.T, precision=HIGHEST)
    target = jnp.dot(hessenberg[:, :blocks], factor[:blocks, :blocks].T, precision=HIGHEST)
    coeffs = jax.scipy.linalg.cho_solve((jnp.linalg.cholesky(normal), True), target)
    weights = jnp.dot(inverse.T, coeffs, precision=HIGHEST)
    return hessenberg, weights


def body(right_side, diagonal):
    blocks, layers, ny, width = right_side.shape
    half = ny // 2
    peers_z, peers_y = lax.axis_size("gz"), lax.axis_size("gy")
    even = lax.axis_index("gz") % 2 == 0
    field = jnp.concatenate([right_side, diagonal[None]], axis=0)
    above = lax.ppermute(field[:, :, ny - EDGE:], "gy", pairs(peers_y, 1))
    under = lax.ppermute(field[:, :, :EDGE], "gy", pairs(peers_y, -1))
    first = jnp.concatenate([field[:, :, :half + EDGE], above], axis=2)
    second = jnp.concatenate([field[:, :, half:], under, field[:, :, half - EDGE:half]], axis=2)

    swap = swap_pairs(peers_z, 1)
    inward = [(i, j) for i, j in pairs(peers_z, 2) if i % 2 == 0] + [(i, j) for i, j in pairs(peers_z, -2) if i % 2]
    outward = [(j, i) for i, j in inward]
    send_near = jnp.where(even, second[:, 1], first[:, 0])
    send_far = jnp.where(even, second[:, 0], first[:, 1])
    keep_near = jnp.where(even, first[:, 1], second[:, 0])
    keep_far = jnp.where(even, first[:, 0], second[:, 1])
    got_near = lax.ppermute(send_near, "gz", swap)
    in_one = lax.ppermute(keep_near, "gz", inward)
    out_one = lax.ppermute(keep_far, "gz", outward)
    got_far = lax.ppermute(send_far, "gz", swap)
    out_two = lax.ppermute(keep_near, "gz", outward)
    in_two = lax.ppermute(got_near, "gz", inward)
    out_three = lax.ppermute(got_near, "gz", outward)
    in_three = lax.ppermute(got_far, "gz", inward)
    pieces = (in_one, in_two, in_three, keep_far, keep_near, got_near, got_far, out_one, out_two, out_three)
    near1, near2, x1, x2, nu = krylov(pieces, blocks, half, width)
    nu = full_moments(all_sum(nu[:1], ("gy", "gz")), blocks)
    hessenberg, weights = dense(nu, blocks)
    theirs = combine(
        weights, (got_near, got_far, near1, near2),
        (((0, None), (2, 1), (3, 0)), ((1, None), (2, 2), (3, 1))), blocks, half, width)
    back = lax.ppermute(theirs, "gz", swap)
    own = combine(
        weights, (keep_far, keep_near, x1, near1, x2),
        (((0, None), (2, None), (4, 0)), ((1, None), (3, 0), (4, 1))), blocks, half, width)
    parts = [[jnp.where(even, own[:, 0], back[:, 0]), jnp.where(even, back[:, 1], own[:, 1])],
             [jnp.where(even, own[:, 1], back[:, 1]), jnp.where(even, back[:, 0], own[:, 0])]]
    whole = jnp.stack([jnp.concatenate(part, axis=1) for part in parts], axis=1)
    return whole, hessenberg


def solution(mesh):
    in_specs = (P(None, "gz", "gy", None), P("gz", "gy", None))
    out_specs = (P(None, "gz", "gy", None), P())
    return jax.shard_map(body, mesh=mesh, in_specs=in_specs, out_specs=out_specs, check_vma=False)
```

time: 162 us -> 142 us (0.88)
  Pallas kernels: 41 us -> 20.2 us
  starting transfers between devices: 30.8 us -> 37.1 us
  waiting for transfers between devices: 63.2 us -> 57 us
  local copies, waits for them, and re-layouts: 5.42 us -> 9.33 us
  other arithmetic: 17.6 us -> 15.8 us
    pallas_call x3 -> x4, Pallas kernels: 41 us -> 20.2 us  [the longest x1 8.49 us: krylov(): pl.pallas_call(functools.partial(late_kernel, **sizes), out_shape=(out(*l...]
    ppermute x1, waiting for transfers between devices: 15.4 us -> 10.1 us  [body(): out_three = lax.ppermute(got_near, 'gz', outward)]
    ppermute x1, waiting for transfers between devices: 0.01 us -> 4.72 us  [body(): in_three = lax.ppermute(got_far, 'gz', inward)]
    unnamed x29 -> x35, local copies, waits for them, and re-layouts: 3.61 us -> 8.21 us
    ppermute x1, waiting for transfers between devices: 10.5 us -> 6.76 us  [body(): got_near = lax.ppermute(send_near, 'gz', swap)]
    ppermute x1, waiting for transfers between devices: 13 us -> 15.8 us  [body(): back = lax.ppermute(theirs, 'gz', swap)]
    ppermute x1, waiting for transfers between devices: 2.8 us -> 0.01 us  [body(): out_one = lax.ppermute(keep_far, 'gz', outward)]
    ppermute x1, starting transfers between devices: 0.07 us -> 2.81 us  [body(): got_far = lax.ppermute(send_far, 'gz', swap)]
  transfers between devices with their start and end apart: 16 -> 16, of which waited for: 10 -> 11; matrix products, arithmetic and copies ran while one was open for 1% -> 1% of each run, Pallas kernels for 4% -> 6%
where the time goes in v3:
time: 142 us
  waiting for transfers between devices  57 us (40%)
  starting transfers between devices  37.1 us (26%)
  Pallas kernels  20.2 us (14%)
  other arithmetic  15.8 us (11%)
  local copies, waits for them, and re-layouts  9.33 us (7%)
    ppermute x1, waiting for transfers between devices, body(): back = lax.ppermute(theirs, 'gz', swap)  15.8 us
    ppermute x1, waiting for transfers between devices, body(): out_three = lax.ppermute(got_near, 'gz', outward)  10.1 us
    ppermute x1, waiting for transfers between devices, body(): got_far = lax.ppermute(send_far, 'gz', swap)  10 us
    ppermute x5, waiting for transfers between devices, all_sum(): array = array + lax.ppermute(array, axis, swap_pairs(peers, bit))  9.36 us
    pallas_call x1, Pallas kernels, krylov(): pl.pallas_call(functools.partial(late_kernel, **sizes), out_shape=(out(*l...  8.49 us
    unnamed x35, local copies, waits for them, and re-layouts  8.21 us
    ppermute x5, starting transfers between devices, all_sum(): array = array + lax.ppermute(array, axis, swap_pairs(peers, bit))  7.51 us
    ppermute x1, waiting for transfers between devices, body(): got_near = lax.ppermute(send_near, 'gz', swap)  6.76 us
  transfers between devices with their start and end apart: 16, of which 11 were waited for; matrix products, arithmetic and copies ran while one was open for 1% of the time, Pallas kernels for 6%

profile of v3, /device:TPU:0, one launch (start us, length us, event | category | flops | bytes accessed | tf_op | source)
XLA Modules:
  0.0 141.7 jit_solution(12984778455341591585)
XLA Ops:
  1.9 1.3 collective-permute-start.1
  3.2 3.0 %collective-permute-start = (f32[9,2,4,512]{3,2,0,1:T(4,128)S(1)}, f32[9,2,4,512]{3,2,0,1:T(4,128)S(1)}, u32[]{:S(2)}, u32[]{:S(2)}) collective-permute-start(f32[9,2,4,512]{3,2,0,1:T(4,128)S(1)} %get-tuple-element.31), channel_id=1, source_target_pairs={{0,1},{1,2},{2,3},{4,5},{5,6},{6,7},{8,9},{9,10},{10,11},{12,13},{... | collective-permute-start | bytes 442376 | tf_op jit(solution)/shard_map/ppermute | solution.py:303
  9.4 3.1 %collective-permute-start.3 = (f32[9,40,512]{2,1,0:T(8,128)S(1)}, f32[9,40,512]{2,1,0:T(8,128)S(1)}, u32[]{:S(2)}, u32[]{:S(2)}) collective-permute-start(f32[9,40,512]{2,1,0:T(8,128)S(1)} %get-tuple-element.29), channel_id=1, source_target_pairs={{0,4},{4,0},{8,12},{12,8},{16,20},{20,16},{24,28},{28,24},{1,5},{5... | collective-permute-start | bytes 2211848 | tf_op jit(solution)/shard_map/ppermute | solution.py:315
  12.5 1.3 collective-permute-start.8
  13.8 2.8 %collective-permute-start.5 = (f32[9,40,512]{2,1,0:T(8,128)S(1)}, f32[9,40,512]{2,1,0:T(8,128)S(1)}, u32[]{:S(2)}, u32[]{:S(2)}) collective-permute-start(f32[9,40,512]{2,1,0:T(8,128)S(1)} %get-tuple-element.28), channel_id=1, source_target_pairs={{0,4},{4,0},{8,12},{12,8},{16,20},{20,16},{24,28},{28,24},{1,5},{5... | collective-permute-start | bytes 2211848 | tf_op jit(solution)/shard_map/ppermute | solution.py:318
  17.9 4.6 %collective-permute-start.2 = (f32[9,40,512]{2,1,0:T(8,128)S(1)}, f32[9,40,512]{2,1,0:T(8,128)S(1)}, u32[]{:S(2)}, u32[]{:S(2)}) collective-permute-start(f32[9,40,512]{2,1,0:T(8,128)S(1)} %get-tuple-element.30.refs_1_.refs_4_), channel_id=1, source_target_pairs={{0,8},{8,16},{16,24},{12,4},{20,12},{28,20},{1,9},{9,17},{17,25},{... | collective-permute-start | bytes 2211848 | tf_op jit(solution)/shard_map/ppermute | solution.py:316
  22.5 6.8 %collective-permute-done.3.refs_2_.refs_5_.refs_0_ = f32[9,40,512]{2,1,0:T(8,128)S(1)} collective-permute-done((f32[9,40,512]{2,1,0:T(8,128)S(1)}, f32[9,40,512]{2,1,0:T(8,128)S(1)}, u32[]{:S(2)}, u32[]{:S(2)}) %collective-permute-start.3) | collective-permute-done | bytes 737312 | tf_op jit(solution)/shard_map/ppermute | solution.py:315
  29.2 4.5 %collective-permute-start.4 = (f32[9,40,512]{2,1,0:T(8,128)S(1)}, f32[9,40,512]{2,1,0:T(8,128)S(1)}, u32[]{:S(2)}, u32[]{:S(2)}) collective-permute-start(f32[9,40,512]{2,1,0:T(8,128)S(1)} %collective-permute-done.3.refs_2_.refs_5_.refs_0_), channel_id=1, source_target_pairs={{0,8},{8,16},{16,24},{12,4},{20,12},{28,20},{1,9},{9,17},{17,25},{... | collective-permute-start | bytes 2211848 | tf_op jit(solution)/shard_map/ppermute | solution.py:320
  33.7 1.3 collective-permute-start.9
  35.0 10.0 %collective-permute-done.5.refs_3_.refs_6_.refs_1_ = f32[9,40,512]{2,1,0:T(8,128)S(1)} collective-permute-done((f32[9,40,512]{2,1,0:T(8,128)S(1)}, f32[9,40,512]{2,1,0:T(8,128)S(1)}, u32[]{:S(2)}, u32[]{:S(2)}) %collective-permute-start.5) | collective-permute-done | bytes 737312 | tf_op jit(solution)/shard_map/ppermute | solution.py:318
  45.0 4.5 %collective-permute-start.6 = (f32[9,40,512]{2,1,0:T(8,128)S(1)}, f32[9,40,512]{2,1,0:T(8,128)S(1)}, u32[]{:S(2)}, u32[]{:S(2)}) collective-permute-start(f32[9,40,512]{2,1,0:T(8,128)S(1)} %collective-permute-done.5.refs_3_.refs_6_.refs_1_), channel_id=1, source_target_pairs={{0,8},{8,16},{16,24},{12,4},{20,12},{28,20},{1,9},{9,17},{17,25},{... | collective-permute-start | bytes 2211848 | tf_op jit(solution)/shard_map/ppermute | solution.py:322
  49.5 5.3 %early.1 = (f32[4,8,40,512]{3,2,1,0:T(8,128)S(1)}, f32[2,8,40,512]{3,2,1,0:T(8,128)S(1)}, f32[180,8,128]{2,1,0:T(8,128)S(1)}) custom-call(f32[9,40,512]{2,1,0:T(8,128)S(1)} %get-tuple-element.27.refs_0_.refs_3_, f32[9,40,512]{2,1,0:T(8,128)S(1)} %get-tuple-element.30.refs_1_.refs_4_, f32[9,40,512]{2,1,0:T(8,128)S(1)} %collective-permute-done.3.refs_2_.refs_5_.refs_0_, ...), custom_call_target="tpu_custom_call" | custom-call | flops 65536000 | bytes 2621440 | tf_op jit(solution)/shard_map/early/pallas_call | solution.py:191
  55.1 10.1 %collective-permute-done.9.refs_9_ = f32[9,40,512]{2,1,0:T(8,128)S(1)} collective-permute-done((f32[9,40,512]{2,1,0:T(8,128)S(1)}, f32[9,40,512]{2,1,0:T(8,128)S(1)}, u32[]{:S(2)}, u32[]{:S(2)}) %collective-permute-start.9) | collective-permute-done | bytes 737312 | tf_op jit(solution)/shard_map/ppermute | solution.py:321
  65.2 4.7 %collective-permute-done.6.refs_2_ = f32[9,40,512]{2,1,0:T(8,128)S(1)} collective-permute-done((f32[9,40,512]{2,1,0:T(8,128)S(1)}, f32[9,40,512]{2,1,0:T(8,128)S(1)}, u32[]{:S(2)}, u32[]{:S(2)}) %collective-permute-start.6) | collective-permute-done | bytes 737312 | tf_op jit(solution)/shard_map/ppermute | solution.py:322
  69.9 8.5 %late.1 = (f32[8,40,512]{2,1,0:T(8,128)S(1)}, f32[2,8,40,512]{3,2,1,0:T(8,128)S(1)}, f32[8,252]{1,0:T(8,128)S(1)}) custom-call(f32[9,40,512]{2,1,0:T(8,128)S(1)} %collective-permute-done.2.refs_0_, f32[9,40,512]{2,1,0:T(8,128)S(1)} %collective-permute-done.4.refs_1_, f32[9,40,512]{2,1,0:T(8,128)S(1)} %collective-permute-done.6.refs_2_, ...), custom_call_target="tpu_custom_call" | custom-call | flops 65536000 | bytes 2621440 | tf_op jit(solution)/shard_map/late/pallas_call | solution.py:201
  81.5 3.6 %collective-permute-done.11 = f32[1,252]{1,0:T(1,128)S(1)} collective-permute-done((f32[1,252]{1,0:T(1,128)S(1)}, f32[1,252]{1,0:T(1,128)S(1)}, u32[]{:S(2)}, u32[]{:S(2)}) %collective-permute-start.11) | collective-permute-done | bytes 1040 | tf_op jit(solution)/shard_map/ppermute | solution.py:34
  85.1 2.4 %collective-permute-start.12 = (f32[1,252]{1,0:T(1,128)S(1)}, f32[1,252]{1,0:T(1,128)S(1)}, u32[]{:S(2)}, u32[]{:S(2)}) collective-permute-start(f32[1,252]{1,0:T(1,128)S(1)} %add.74), channel_id=1, source_target_pairs={{0,4},{4,0},{8,12},{12,8},{16,20},{20,16},{24,28},{28,24},{1,5},{5... | collective-permute-start | bytes 3032 | tf_op jit(solution)/shard_map/ppermute | solution.py:34
  87.5 1.5 %collective-permute-done.12 = f32[1,252]{1,0:T(1,128)S(1)} collective-permute-done((f32[1,252]{1,0:T(1,128)S(1)}, f32[1,252]{1,0:T(1,128)S(1)}, u32[]{:S(2)}, u32[]{:S(2)}) %collective-permute-start.12) | collective-permute-done | bytes 1040 | tf_op jit(solution)/shard_map/ppermute | solution.py:34
  89.1 2.1 %collective-permute-start.13 = (f32[1,252]{1,0:T(1,128)S(1)}, f32[1,252]{1,0:T(1,128)S(1)}, u32[]{:S(2)}, u32[]{:S(2)}) collective-permute-start(f32[1,252]{1,0:T(1,128)S(1)} %add.75), channel_id=1, source_target_pairs={{0,8},{4,12},{8,0},{12,4},{16,24},{20,28},{24,16},{28,20},{1,9},{5... | collective-permute-start | bytes 3032 | tf_op jit(solution)/shard_map/ppermute | solution.py:34
  91.2 1.5 %collective-permute-done.13 = f32[1,252]{1,0:T(1,128)S(1)} collective-permute-done((f32[1,252]{1,0:T(1,128)S(1)}, f32[1,252]{1,0:T(1,128)S(1)}, u32[]{:S(2)}, u32[]{:S(2)}) %collective-permute-start.13) | collective-permute-done | bytes 1040 | tf_op jit(solution)/shard_map/ppermute | solution.py:34
  92.7 3.0 %collective-permute-start.14 = (f32[1,252]{1,0:T(1,128)S(1)}, f32[1,252]{1,0:T(1,128)S(1)}, u32[]{:S(2)}, u32[]{:S(2)}) collective-permute-start(f32[1,252]{1,0:T(1,128)S(1)} %add.76), channel_id=1, source_target_pairs={{0,16},{4,20},{8,24},{12,28},{16,0},{20,4},{24,8},{28,12},{1,17},{... | collective-permute-start | bytes 3032 | tf_op jit(solution)/shard_map/ppermute | solution.py:34
  95.7 1.5 %collective-permute-done.14 = f32[1,252]{1,0:T(1,128)S(1)} collective-permute-done((f32[1,252]{1,0:T(1,128)S(1)}, f32[1,252]{1,0:T(1,128)S(1)}, u32[]{:S(2)}, u32[]{:S(2)}) %collective-permute-start.14) | collective-permute-done | bytes 1040 | tf_op jit(solution)/shard_map/ppermute | solution.py:34
  98.7 2.9 %cholesky.31 = f32[32,32]{1,0:T(8,128)S(1)} custom-call(f32[32,32]{1,0:T(8,128)S(1)} %fusion.7), custom_call_target="Cholesky" | custom-call | tf_op jit(solution)/shard_map/jit(cholesky)/cholesky | solution.py:280
  103.0 1.8 %custom-call.17 = f32[1,24,24]{1,2,0:T(8,128)S(1)} custom-call(f32[1,24,24]{2,1,0:T(8,128)S(1)} %fusion.11), custom_call_target="InvertDiagBlocksLowerTriangular" | custom-call | tf_op jit(solution)/shard_map/jit(_solve_triangular)/triangular_solve | solution.py:281
  105.6 2.2 %cholesky.59 = f32[24,24]{1,0:T(8,128)S(1)} custom-call(f32[24,24]{1,0:T(8,128)S(1)} %fusion.21), custom_call_target="Cholesky" | custom-call | tf_op jit(solution)/shard_map/jit(cholesky)/cholesky | solution.py:292
  109.2 1.8 %custom-call.18 = f32[1,24,24]{1,2,0:T(8,128)S(1)} custom-call(f32[1,24,24]{2,1,0:T(8,128)S(1)} %fusion.8), custom_call_target="InvertDiagBlocksLowerTriangular" | custom-call | tf_op jit(solution)/shard_map/jit(_cho_solve)/triangular_solve | solution.py:292
  113.8 1.3 copy-done.7
  115.2 3.2 %combine.3 = f32[8,2,32,512]{3,2,1,0:T(8,128)S(1)} custom-call(f32[24,8]{1,0:T(8,128)S(1)} %fusion.30.weights, f32[9,40,512]{2,1,0:T(8,128)S(1)} %copy-done.3, f32[9,40,512]{2,1,0:T(8,128)S(1)} %copy-done.5, f32[4,8,40,512]{3,2,1,0:T(8,128)S(1)} %get-tuple-element.8.refs_10_.refs_3_.refs_2_, f32[2,8,40,512]{3,2,1,0:T(8,128)S(1)} %copy-done.7), custom_call_target="tpu_custom_call" | custom-call | tf_op jit(solution)/shard_map/combine/pallas_call | solution.py:246
  118.4 2.0 %collective-permute-start.15 = (f32[8,2,32,512]{3,2,1,0:T(8,128)S(1)}, f32[8,2,32,512]{3,2,1,0:T(8,128)S(1)}, u32[]{:S(2)}, u32[]{:S(2)}) collective-permute-start(f32[8,2,32,512]{3,2,1,0:T(8,128)S(1)} %combine.3), channel_id=1, source_target_pairs={{0,4},{4,0},{8,12},{12,8},{16,20},{20,16},{24,28},{28,24},{1,5},{5... | collective-permute-start | bytes 3145736 | tf_op jit(solution)/shard_map/ppermute | solution.py:330
  120.4 3.2 %combine.2 = f32[8,2,32,512]{3,2,1,0:T(8,128)S(1)} custom-call(f32[24,8]{1,0:T(8,128)S(1)} %fusion.30.weights, f32[9,40,512]{2,1,0:T(8,128)S(1)} %get-tuple-element.27.refs_0_.refs_3_, f32[9,40,512]{2,1,0:T(8,128)S(1)} %copy-done.1, f32[8,40,512]{2,1,0:T(8,128)S(1)} %copy-done.11, f32[4,8,40,512]{3,2,1,0:T(8,128)S(1)} %get-tuple-element.8.refs_10_.refs_3_.refs_2_, ...), custom_call_target="tpu_custom_call" | custom-call | tf_op jit(solution)/shard_map/combine/pallas_call | solution.py:246
  123.6 15.8 %collective-permute-done.15 = f32[8,2,32,512]{3,2,1,0:T(8,128)S(1)} collective-permute-done((f32[8,2,32,512]{3,2,1,0:T(8,128)S(1)}, f32[8,2,32,512]{3,2,1,0:T(8,128)S(1)}, u32[]{:S(2)}, u32[]{:S(2)}) %collective-permute-start.15) | collective-permute-done | bytes 1048608 | tf_op jit(solution)/shard_map/ppermute | solution.py:330
  140.2 1.5 %copy.48 = f32[8,2,64,512]{3,2,1,0:T(8,128)} copy(f32[8,2,64,512]{3,2,0,1:T(8,128)S(1)} %pad_maximum_fusion) | data formatting | bytes 4194304
  (99 shorter events, 17.5 us)
Async XLA Ops:
  0.6 5.7 %copy-start.14 = (f32[2,64,512]{2,1,0:T(8,128)S(1)}, f32[2,64,512]{2,1,0:T(8,128)}, u32[]{:S(2)}) copy-start(f32[2,64,512]{2,1,0:T(8,128)} %param.4) | copy-start | bytes 786436
  0.6 5.7 %copy-start.12 = (f32[8,2,64,512]{3,2,1,0:T(8,128)S(1)}, f32[8,2,64,512]{3,2,1,0:T(8,128)}, u32[]{:S(2)}) copy-start(f32[8,2,64,512]{3,2,1,0:T(8,128)} %param.3) | copy-start | bytes 6291460
  1.9 5.7 %collective-permute-start.1 = (f32[9,2,4,512]{3,2,0,1:T(4,128)S(1)}, f32[9,2,4,512]{3,2,0,1:T(4,128)S(1)}, u32[]{:S(2)}, u32[]{:S(2)}) collective-permute-start(f32[9,2,4,512]{3,2,0,1:T(4,128)S(1)} %get-tuple-element.32), channel_id=1, source_target_pairs={{1,0},{2,1},{3,2},{5,4},{6,5},{7,6},{9,8},{10,9},{11,10},{13,12},{... | collective-permute-start | bytes 442376 | tf_op jit(solution)/shard_map/ppermute | solution.py:304
  3.2 4.7 %collective-permute-start = (f32[9,2,4,512]{3,2,0,1:T(4,128)S(1)}, f32[9,2,4,512]{3,2,0,1:T(4,128)S(1)}, u32[]{:S(2)}, u32[]{:S(2)}) collective-permute-start(f32[9,2,4,512]{3,2,0,1:T(4,128)S(1)} %get-tuple-element.31), channel_id=1, source_target_pairs={{0,1},{1,2},{2,3},{4,5},{5,6},{6,7},{8,9},{9,10},{10,11},{12,13},{... | collective-permute-start | bytes 442376 | tf_op jit(solution)/shard_map/ppermute | solution.py:303
  7.7 1.4 copy-start.13
  9.4 60.5 %copy-start = (f32[9,40,512]{2,1,0:T(8,128)}, f32[9,40,512]{2,1,0:T(8,128)S(1)}, u32[]{:S(2)}) copy-start(f32[9,40,512]{2,1,0:T(8,128)S(1)} %get-tuple-element.30.refs_1_.refs_4_) | copy-start | bytes 2211844
  9.4 19.8 %collective-permute-start.3 = (f32[9,40,512]{2,1,0:T(8,128)S(1)}, f32[9,40,512]{2,1,0:T(8,128)S(1)}, u32[]{:S(2)}, u32[]{:S(2)}) collective-permute-start(f32[9,40,512]{2,1,0:T(8,128)S(1)} %get-tuple-element.29), channel_id=1, source_target_pairs={{0,4},{4,0},{8,12},{12,8},{16,20},{20,16},{24,28},{28,24},{1,5},{5... | collective-permute-start | bytes 2211848 | tf_op jit(solution)/shard_map/ppermute | solution.py:315
  12.5 21.2 %collective-permute-start.8 = (f32[9,40,512]{2,1,0:T(8,128)S(1)}, f32[9,40,512]{2,1,0:T(8,128)S(1)}, u32[]{:S(2)}, u32[]{:S(2)}) collective-permute-start(f32[9,40,512]{2,1,0:T(8,128)S(1)} %get-tuple-element.30.refs_1_.refs_4_), channel_id=1, source_target_pairs={{8,0},{16,8},{24,16},{4,12},{12,20},{20,28},{9,1},{17,9},{25,17},{... | collective-permute-start | bytes 2211848 | tf_op jit(solution)/shard_map/ppermute | solution.py:319
  13.8 31.3 %collective-permute-start.5 = (f32[9,40,512]{2,1,0:T(8,128)S(1)}, f32[9,40,512]{2,1,0:T(8,128)S(1)}, u32[]{:S(2)}, u32[]{:S(2)}) collective-permute-start(f32[9,40,512]{2,1,0:T(8,128)S(1)} %get-tuple-element.28), channel_id=1, source_target_pairs={{0,4},{4,0},{8,12},{12,8},{16,20},{20,16},{24,28},{28,24},{1,5},{5... | collective-permute-start | bytes 2211848 | tf_op jit(solution)/shard_map/ppermute | solution.py:318
  16.6 32.9 %collective-permute-start.7 = (f32[9,40,512]{2,1,0:T(8,128)S(1)}, f32[9,40,512]{2,1,0:T(8,128)S(1)}, u32[]{:S(2)}, u32[]{:S(2)}) collective-permute-start(f32[9,40,512]{2,1,0:T(8,128)S(1)} %get-tuple-element.27.refs_0_.refs_3_), channel_id=1, source_target_pairs={{8,0},{16,8},{24,16},{4,12},{12,20},{20,28},{9,1},{17,9},{25,17},{... | collective-permute-start | bytes 2211848 | tf_op jit(solution)/shard_map/ppermute | solution.py:317
  17.9 36.9 %collective-permute-start.2 = (f32[9,40,512]{2,1,0:T(8,128)S(1)}, f32[9,40,512]{2,1,0:T(8,128)S(1)}, u32[]{:S(2)}, u32[]{:S(2)}) collective-permute-start(f32[9,40,512]{2,1,0:T(8,128)S(1)} %get-tuple-element.30.refs_1_.refs_4_), channel_id=1, source_target_pairs={{0,8},{8,16},{16,24},{12,4},{20,12},{28,20},{1,9},{9,17},{17,25},{... | collective-permute-start | bytes 2211848 | tf_op jit(solution)/shard_map/ppermute | solution.py:316
  29.2 40.7 %copy-start.2 = (f32[9,40,512]{2,1,0:T(8,128)}, f32[9,40,512]{2,1,0:T(8,128)S(1)}, u32[]{:S(2)}) copy-start(f32[9,40,512]{2,1,0:T(8,128)S(1)} %collective-permute-done.3.refs_2_.refs_5_.refs_0_) | copy-start | bytes 2211844
  29.2 25.8 %collective-permute-start.4 = (f32[9,40,512]{2,1,0:T(8,128)S(1)}, f32[9,40,512]{2,1,0:T(8,128)S(1)}, u32[]{:S(2)}, u32[]{:S(2)}) collective-permute-start(f32[9,40,512]{2,1,0:T(8,128)S(1)} %collective-permute-done.3.refs_2_.refs_5_.refs_0_), channel_id=1, source_target_pairs={{0,8},{8,16},{16,24},{12,4},{20,12},{28,20},{1,9},{9,17},{17,25},{... | collective-permute-start | bytes 2211848 | tf_op jit(solution)/shard_map/ppermute | solution.py:320
  33.7 31.5 %collective-permute-start.9 = (f32[9,40,512]{2,1,0:T(8,128)S(1)}, f32[9,40,512]{2,1,0:T(8,128)S(1)}, u32[]{:S(2)}, u32[]{:S(2)}) collective-permute-start(f32[9,40,512]{2,1,0:T(8,128)S(1)} %collective-permute-done.3.refs_2_.refs_5_.refs_0_), channel_id=1, source_target_pairs={{8,0},{16,8},{24,16},{4,12},{12,20},{20,28},{9,1},{17,9},{25,17},{... | collective-permute-start | bytes 2211848 | tf_op jit(solution)/shard_map/ppermute | solution.py:321
  45.0 24.9 %copy-start.4 = (f32[9,40,512]{2,1,0:T(8,128)}, f32[9,40,512]{2,1,0:T(8,128)S(1)}, u32[]{:S(2)}) copy-start(f32[9,40,512]{2,1,0:T(8,128)S(1)} %collective-permute-done.5.refs_3_.refs_6_.refs_1_) | copy-start | bytes 2211844
  45.0 24.9 %collective-permute-start.6 = (f32[9,40,512]{2,1,0:T(8,128)S(1)}, f32[9,40,512]{2,1,0:T(8,128)S(1)}, u32[]{:S(2)}, u32[]{:S(2)}) collective-permute-start(f32[9,40,512]{2,1,0:T(8,128)S(1)} %collective-permute-done.5.refs_3_.refs_6_.refs_1_), channel_id=1, source_target_pairs={{0,8},{8,16},{16,24},{12,4},{20,12},{28,20},{1,9},{9,17},{17,25},{... | collective-permute-start | bytes 2211848 | tf_op jit(solution)/shard_map/ppermute | solution.py:322
  54.8 23.6 %copy-start.6 = (f32[2,8,40,512]{3,2,1,0:T(8,128)}, f32[2,8,40,512]{3,2,1,0:T(8,128)S(1)}, u32[]{:S(2)}) copy-start(f32[2,8,40,512]{3,2,1,0:T(8,128)S(1)} %get-tuple-element.9.refs_11_.refs_3_) | copy-start | bytes 3932164
  69.9 27.4 %copy-start.16 = (f32[36,64]{1,0:T(8,128)S(1)}, f32[36,64]{1,0:T(8,128)}, u32[]{:S(2)}) copy-start(f32[36,64]{1,0:T(8,128)} %constant.148.clone) | copy-start | bytes 27652
  78.4 1.1 copy-start.8
  80.3 1.2 collective-permute-start.10
  81.5 3.6 %collective-permute-start.11 = (f32[1,252]{1,0:T(1,128)S(1)}, f32[1,252]{1,0:T(1,128)S(1)}, u32[]{:S(2)}, u32[]{:S(2)}) collective-permute-start(f32[1,252]{1,0:T(1,128)S(1)} %slice_add_fusion), channel_id=1, source_target_pairs={{0,2},{1,3},{2,0},{3,1},{4,6},{5,7},{6,4},{7,5},{8,10},{9,11},{10,... | collective-permute-start | bytes 3032 | tf_op jit(solution)/shard_map/ppermute | solution.py:34
  85.1 4.0 %collective-permute-start.12 = (f32[1,252]{1,0:T(1,128)S(1)}, f32[1,252]{1,0:T(1,128)S(1)}, u32[]{:S(2)}, u32[]{:S(2)}) collective-permute-start(f32[1,252]{1,0:T(1,128)S(1)} %add.74), channel_id=1, source_target_pairs={{0,4},{4,0},{8,12},{12,8},{16,20},{20,16},{24,28},{28,24},{1,5},{5... | collective-permute-start | bytes 3032 | tf_op jit(solution)/shard_map/ppermute | solution.py:34
  89.1 3.6 %collective-permute-start.13 = (f32[1,252]{1,0:T(1,128)S(1)}, f32[1,252]{1,0:T(1,128)S(1)}, u32[]{:S(2)}, u32[]{:S(2)}) collective-permute-start(f32[1,252]{1,0:T(1,128)S(1)} %add.75), channel_id=1, source_target_pairs={{0,8},{4,12},{8,0},{12,4},{16,24},{20,28},{24,16},{28,20},{1,9},{5... | collective-permute-start | bytes 3032 | tf_op jit(solution)/shard_map/ppermute | solution.py:34
  92.7 4.5 %collective-permute-start.14 = (f32[1,252]{1,0:T(1,128)S(1)}, f32[1,252]{1,0:T(1,128)S(1)}, u32[]{:S(2)}, u32[]{:S(2)}) collective-permute-start(f32[1,252]{1,0:T(1,128)S(1)} %add.76), channel_id=1, source_target_pairs={{0,16},{4,20},{8,24},{12,28},{16,0},{20,4},{24,8},{28,12},{1,17},{... | collective-permute-start | bytes 3032 | tf_op jit(solution)/shard_map/ppermute | solution.py:34
  105.2 13.2 %copy-start.15 = (f32[24,32]{1,0:T(8,128)}, f32[24,32]{1,0:T(8,128)S(1)}, u32[]{:S(2)}) copy-start(f32[24,32]{1,0:T(8,128)S(1)} %convolution_select_fusion) | copy-start | bytes 9220
  111.6 1.1 copy-start.3
  112.7 1.1 copy-start.5
  113.8 1.3 copy-start.7
  115.1 5.2 %copy-start.1 = (f32[9,40,512]{2,1,0:T(8,128)S(1)}, f32[9,40,512]{2,1,0:T(8,128)}, u32[]{:S(2)}) copy-start(f32[9,40,512]{2,1,0:T(8,128)} %copy-done) | copy-start | bytes 2211844
  115.2 5.2 %copy-start.9 = (f32[2,8,40,512]{3,2,1,0:T(8,128)S(1)}, f32[2,8,40,512]{3,2,1,0:T(8,128)}, u32[]{:S(2)}) copy-start(f32[2,8,40,512]{3,2,1,0:T(8,128)} %copy-done.8) | copy-start | bytes 3932164
  115.2 5.2 %copy-start.11 = (f32[8,40,512]{2,1,0:T(8,128)S(1)}, f32[8,40,512]{2,1,0:T(8,128)}, u32[]{:S(2)}) copy-start(f32[8,40,512]{2,1,0:T(8,128)} %copy-done.10) | copy-start | bytes 1966084
  118.4 21.0 %collective-permute-start.15 = (f32[8,2,32,512]{3,2,1,0:T(8,128)S(1)}, f32[8,2,32,512]{3,2,1,0:T(8,128)S(1)}, u32[]{:S(2)}, u32[]{:S(2)}) collective-permute-start(f32[8,2,32,512]{3,2,1,0:T(8,128)S(1)} %combine.3), channel_id=1, source_target_pairs={{0,4},{4,0},{8,12},{12,8},{16,20},{20,16},{24,28},{28,24},{1,5},{5... | collective-permute-start | bytes 3145736 | tf_op jit(solution)/shard_map/ppermute | solution.py:330
  (1 other events, 0.8 us)

commit v4 on v3

--- a/solution.py
+++ b/solution.py
@@ -24,16 +24,11 @@
 
 
 def all_sum(array, axes):
+    peers = 1
     for axis in axes:
-        peers = lax.axis_size(axis)
-        if peers & (peers - 1):
-            array = lax.psum(array, axis)
-            continue
-        bit = 1
-        while bit < peers:
-            array = array + lax.ppermute(array, axis, swap_pairs(peers, bit))
-            bit *= 2
-    return array
+        peers *= lax.axis_size(axis)
+    spread = jnp.broadcast_to(array[None], (peers, *array.shape))
+    return jnp.sum(lax.all_to_all(spread, axes, 0, 0), axis=0)
 
 
 def row_masks(half, width):
@@ -112,37 +107,57 @@
 LATE = {1: (4,), 2: (4,), 3: (4, 5), 4: (4, 5), 5: (4, 5, 6, 7), 6: (4, 5, 6, 7)}
 
 
+def first_kernel(*refs, blocks, half, width):
+    fields = dict(zip((5, 6, 7, 8), refs[:4]))
+    x1, sent, scale_ref, diag_ref = refs[4:]
+    set_scales(scale_ref, diag_ref, [fields[n] for n in (6, 7)], blocks, (6, 7), half, width)
+
+    def vector(v, carry):
+        for slot, n in enumerate((6, 7)):
+            value = step_of(
+                scale_ref[...], diag_ref[slot], fields[n - 1][v], fields[n][v], fields[n + 1][v], None, 0.0)
+            x1[slot, v] = value
+            sent[slot, v] = value[:half]
+        return carry
+
+    lax.fori_loop(0, blocks, vector, 0)
+
+
 def early_kernel(*refs, blocks, half, width):
     fields = dict(zip((4, 5, 6, 7, 8, 9), refs[:6]))
-    x1, x2, acc, scale_ref, diag_ref = refs[6:]
+    before, x1, x2, near_sent, far_sent, acc, scale_ref, diag_ref = refs[6:]
     slots = (5, 6, 7, 8)
     set_scales(scale_ref, diag_ref, [fields[n] for n in slots], blocks, slots, half, width)
     flag = side_flags()[1]
+    one = {5: x1.at[0], 6: before.at[0], 7: before.at[1], 8: x1.at[1]}
 
     def vector(v, carry):
-        for slot, n in enumerate(slots):
-            x1[slot, v] = step_of(
-                scale_ref[...], diag_ref[slot], fields[n - 1][v], fields[n][v], fields[n + 1][v],
+        for n in (5, 8):
+            one[n][v] = step_of(
+                scale_ref[...], diag_ref[n - 5], fields[n - 1][v], fields[n][v], fields[n + 1][v],
                 None, 0.0, flag if n == 8 else None)
-        for slot, n in enumerate((6, 7)):
-            x2[slot, v] = step_of(
-                scale_ref[...], diag_ref[n - 5], x1[n - 6, v], x1[n - 5, v], x1[n - 4, v],
+        for slot, (n, sent) in enumerate(((6, near_sent), (7, far_sent))):
+            value = step_of(
+                scale_ref[...], diag_ref[n - 5], one[n - 1][v], one[n][v], one[n + 1][v],
                 fields[n][v], BETA[1])
+            x2[slot, v] = value
+            sent[v] = value[:half]
         return carry
 
     lax.fori_loop(0, blocks, vector, 0)
-    views = (fields, {n: x1.at[n - 5] for n in slots}, {n: x2.at[n - 6] for n in (6, 7)})
+    views = (fields, one, {n: x2.at[n - 6] for n in (6, 7)})
     for moment, layers in EARLY.items():
         gram_part(acc, views, moment, layers, blocks, half, width, None)
 
 
 def late_kernel(*refs, blocks, half, width):
     fields = dict(zip(range(1, 11), refs[:10]))
-    near1, near2, start, x1, x2, nu_out, far1, far2, x3, acc, scale_ref, diag_ref = refs[10:]
+    mid1, near1, near2, start, x1, x2, nu_out, far1, far2, x3, acc, scale_ref, diag_ref = refs[10:]
     slots = tuple(range(2, 10))
     set_scales(scale_ref, diag_ref, [fields[n] for n in slots], blocks, slots, half, width)
     low, high = side_flags()
-    one = {2: far1.at[0], 3: far1.at[1], 4: x1, 9: far1.at[2], **{n: near1.at[n - 5] for n in (5, 6, 7, 8)}}
+    one = {2: far1.at[0], 3: far1.at[1], 4: x1, 9: far1.at[2],
+           5: near1.at[0], 6: mid1.at[0], 7: mid1.at[1], 8: near1.at[1]}
     two = {3: far2.at[0], 4: x2.at[0], 5: x2.at[1], 6: near2.at[0], 7: near2.at[1], 8: far2.at[1]}
     three = {n: x3.at[n - 4] for n in (4, 5, 6, 7)}
 
@@ -176,7 +191,7 @@
         precision=HIGHEST, preferred_element_type=jnp.float32)
 
 
-def krylov(pieces, blocks, half, width):
+def kernels(blocks, half, width):
     rows = half + 2 * EDGE
     moments = 2 * ITERS + 1
     count = blocks * (blocks + 1) // 2
@@ -188,42 +203,77 @@
     def out(*shape):
         return jax.ShapeDtypeStruct(shape, jnp.float32)
 
-    near1, near2, start = pl.pallas_call(
-        functools.partial(early_kernel, **sizes),
-        out_shape=(out(4, *layer), out(2, *layer), out(len(EARLY) * count, 8, 128)),
-        in_specs=[vmem] * 6,
-        out_specs=(vmem,) * 3,
-        scratch_shapes=[pltpu.VMEM((rows, width), jnp.float32), pltpu.VMEM((4, rows, width), jnp.float32)],
-        compiler_params=pltpu.CompilerParams(vmem_limit_bytes=20 << 20),
-        cost_estimate=pl.CostEstimate(flops=400 * cells, bytes_accessed=16 * cells, transcendentals=0),
-        name="early",
-    )(*pieces[3:9])
-    x1, x2, nu = pl.pallas_call(
-        functools.partial(late_kernel, **sizes),
-        out_shape=(out(*layer), out(2, *layer), out(8, moments * count)),
-        in_specs=[vmem] * 13,
-        out_specs=(vmem,) * 3,
-        scratch_shapes=[
-            pltpu.VMEM((3, *layer), jnp.float32),
-            pltpu.VMEM((2, *layer), jnp.float32),
-            pltpu.VMEM((4, *layer), jnp.float32),
-            pltpu.VMEM((moments * count, 8, 128), jnp.float32),
-            pltpu.VMEM((rows, width), jnp.float32),
-            pltpu.VMEM((8, rows, width), jnp.float32),
-        ],
-        compiler_params=pltpu.CompilerParams(vmem_limit_bytes=34 << 20),
-        cost_estimate=pl.CostEstimate(flops=400 * cells, bytes_accessed=16 * cells, transcendentals=0),
-        name="late",
-    )(*pieces, near1, near2, start)
-    return near1, near2, x1, x2, nu
-
-
-def combine_kernel(weights, *refs, blocks, half, width, places):
-    out = refs[-1]
-    for layer in range(2):
-        terms = [(refs[ref].at[at] if at is not None else refs[ref]) for ref, at in places[layer]]
-
-        def tile(step, carry, terms=terms, layer=layer):
+    def params(mib):
+        return pltpu.CompilerParams(vmem_limit_bytes=mib << 20)
+
+    def cost(ops):
+        return pl.CostEstimate(flops=ops * cells, bytes_accessed=16 * cells, transcendentals=0)
+
+    def scales(count):
+        return [pltpu.VMEM((rows, width), jnp.float32), pltpu.VMEM((count, rows, width), jnp.float32)]
+
+    def first(*fields):
+        return pl.pallas_call(
+            functools.partial(first_kernel, **sizes),
+            out_shape=(out(2, *layer), out(2, blocks, half, width)),
+            in_specs=[vmem] * 4,
+            out_specs=(vmem,) * 2,
+            scratch_shapes=scales(2),
+            compiler_params=params(8),
+            cost_estimate=cost(40),
+            name="first",
+        )(*fields)
+
+    def early(*arrays):
+        return pl.pallas_call(
+            functools.partial(early_kernel, **sizes),
+            out_shape=(out(2, *layer), out(2, *layer), out(blocks, half, width), out(blocks, half, width),
+                       out(len(EARLY) * count, 8, 128)),
+            in_specs=[vmem] * 7,
+            out_specs=(vmem,) * 5,
+            scratch_shapes=scales(4),
+            compiler_params=params(12),
+            cost_estimate=cost(400),
+            name="early",
+        )(*arrays)
+
+    def late(*arrays):
+        return pl.pallas_call(
+            functools.partial(late_kernel, **sizes),
+            out_shape=(out(*layer), out(2, *layer), out(8, moments * count)),
+            in_specs=[vmem] * 14,
+            out_specs=(vmem,) * 3,
+            scratch_shapes=[
+                pltpu.VMEM((3, *layer), jnp.float32),
+                pltpu.VMEM((2, *layer), jnp.float32),
+                pltpu.VMEM((4, *layer), jnp.float32),
+                pltpu.VMEM((moments * count, 8, 128), jnp.float32),
+                *scales(8),
+            ],
+            compiler_params=params(18),
+            cost_estimate=cost(400),
+            name="late",
+        )(*arrays)
+
+    return first, early, late
+
+
+TERMS = (
+    ((0, None), (1, None), (2, 0)), ((3, None), (4, 0), (2, 1)),
+    ((5, None), (6, 0), (7, None)), ((8, None), (6, 1), (9, None)),
+)
+
+
+def combine_kernel(weights, *refs, blocks, half, width):
+    arrays, (out, buffer, sems) = refs[:-3], refs[-3:]
+    parity = lax.rem(lax.axis_index("gz"), 2)
+    copies = []
+    for n, (at_layer, at_half) in enumerate((
+        (parity, parity), (1 - parity, parity), (1 - parity, 1 - parity), (parity, 1 - parity),
+    )):
+        terms = [arrays[ref] if at is None else arrays[ref].at[at] for ref, at in TERMS[n]]
+
+        def tile(step, carry, terms=terms, n=n):
             at = pl.multiple_of(step * 8, 8)
             for c in range(width // 128):
                 lanes = pl.ds(128 * c, 128)
@@ -235,20 +285,28 @@
                             value = weights[k * blocks + v, w] * part
                             sums[w] = value if sums[w] is None else sums[w] + value
                 for w in range(blocks):
-                    out[w, layer, pl.ds(at, 8), lanes] = sums[w]
+                    buffer[n, w, pl.ds(at, 8), lanes] = sums[w]
             return carry
 
         lax.fori_loop(0, half // 8, tile, 0)
-
-
-def combine(weights, arrays, places, blocks, half, width):
+        copies.append(pltpu.make_async_copy(
+            buffer.at[n],
+            out.at[:, at_layer, pl.ds(pl.multiple_of(at_half * half, 8), half)],
+            sems.at[n]))
+        copies[-1].start()
+    for copy in copies:
+        copy.wait()
+
+
+def combine(weights, arrays, blocks, half, width):
     vmem = pl.BlockSpec(memory_space=pltpu.VMEM)
     return pl.pallas_call(
-        functools.partial(combine_kernel, blocks=blocks, half=half, width=width, places=places),
-        out_shape=jax.ShapeDtypeStruct((blocks, 2, half, width), jnp.float32),
+        functools.partial(combine_kernel, blocks=blocks, half=half, width=width),
+        out_shape=jax.ShapeDtypeStruct((blocks, 2, 2 * half, width), jnp.float32),
         in_specs=[pl.BlockSpec(memory_space=pltpu.SMEM)] + [vmem] * len(arrays),
-        out_specs=vmem,
-        compiler_params=pltpu.CompilerParams(vmem_limit_bytes=16 << 20),
+        out_specs=pl.BlockSpec(memory_space=pl.ANY),
+        scratch_shapes=[pltpu.VMEM((4, blocks, half, width), jnp.float32), pltpu.SemaphoreType.DMA((4,))],
+        compiler_params=pltpu.CompilerParams(vmem_limit_bytes=12 << 20),
         name="combine",
     )(weights, *arrays)
 
@@ -295,7 +353,7 @@
 
 
 def body(right_side, diagonal):
-    blocks, layers, ny, width = right_side.shape
+    blocks, _, ny, width = right_side.shape
     half = ny // 2
     peers_z, peers_y = lax.axis_size("gz"), lax.axis_size("gy")
     even = lax.axis_index("gz") % 2 == 0
@@ -312,32 +370,40 @@
     send_far = jnp.where(even, second[:, 0], first[:, 1])
     keep_near = jnp.where(even, first[:, 1], second[:, 0])
     keep_far = jnp.where(even, first[:, 0], second[:, 1])
-    got_near = lax.ppermute(send_near, "gz", swap)
-    in_one = lax.ppermute(keep_near, "gz", inward)
-    out_one = lax.ppermute(keep_far, "gz", outward)
-    got_far = lax.ppermute(send_far, "gz", swap)
-    out_two = lax.ppermute(keep_near, "gz", outward)
-    in_two = lax.ppermute(got_near, "gz", inward)
-    out_three = lax.ppermute(got_near, "gz", outward)
-    in_three = lax.ppermute(got_far, "gz", inward)
-    pieces = (in_one, in_two, in_three, keep_far, keep_near, got_near, got_far, out_one, out_two, out_three)
-    near1, near2, x1, x2, nu = krylov(pieces, blocks, half, width)
-    nu = full_moments(all_sum(nu[:1], ("gy", "gz")), blocks)
-    hessenberg, weights = dense(nu, blocks)
-    theirs = combine(
-        weights, (got_near, got_far, near1, near2),
-        (((0, None), (2, 1), (3, 0)), ((1, None), (2, 2), (3, 1))), blocks, half, width)
-    back = lax.ppermute(theirs, "gz", swap)
-    own = combine(
-        weights, (keep_far, keep_near, x1, near1, x2),
-        (((0, None), (2, None), (4, 0)), ((1, None), (3, 0), (4, 1))), blocks, half, width)
-    parts = [[jnp.where(even, own[:, 0], back[:, 0]), jnp.where(even, back[:, 1], own[:, 1])],
-             [jnp.where(even, own[:, 1], back[:, 1]), jnp.where(even, back[:, 0], own[:, 0])]]
-    whole = jnp.stack([jnp.concatenate(part, axis=1) for part in parts], axis=1)
-    return whole, hessenberg
+    first_step, early, late = kernels(blocks, half, width)
+
+    def move(array, links):
+        return lax.ppermute(array, "gz", links)
+
+    got_near = move(send_near, swap)
+    in_one = move(keep_near[:blocks], inward)
+    out_one = move(keep_far, outward)
+    got_far = move(send_far, swap)
+    out_two = move(keep_near, outward)
+    in_two = move(got_near, inward)
+    out_three = move(got_near[:blocks], outward)
+    in_three = move(got_far, inward)
+    mid1, sent1 = first_step(keep_near, got_near, got_far, out_one)
+    back1 = move(sent1, swap)
+    near1, near2, near_sent, far_sent, start = early(
+        keep_far, keep_near, got_near, got_far, out_one, out_two, mid1)
+    near_back2 = move(near_sent, swap)
+    x1, x2, nu = late(
+        in_one, in_two, in_three, keep_far, keep_near, got_near, got_far, out_one, out_two, out_three,
+        mid1, near1, near2, start)
+    nu = all_sum(nu[:1], ("gz", "gy"))
+    nu, far_sent = lax.optimization_barrier((nu, far_sent))
+    far_back2 = move(far_sent, swap)
+    hessenberg, weights = dense(full_moments(nu, blocks), blocks)
+    result = combine(
+        weights,
+        (keep_far, x1, x2, keep_near, near1, send_near, back1, near_back2, send_far, far_back2),
+        blocks, half, width)
+    return result, hessenberg
 
 
 def solution(mesh):
     in_specs = (P(None, "gz", "gy", None), P("gz", "gy", None))
     out_specs = (P(None, "gz", "gy", None), P())
+
     return jax.shard_map(body, mesh=mesh, in_specs=in_specs, out_specs=out_specs, check_vma=False)

time: 142 us -> 158 us (1.11)
  other arithmetic: 15.8 us -> 30.2 us
  waiting for transfers between devices: 57 us -> 47.3 us
  local copies, waits for them, and re-layouts: 9.33 us -> 18 us
  starting transfers between devices: 37.1 us -> 31.2 us
  matrix products: 1.35 us -> 6.08 us
  Pallas kernels: 20.2 us -> 22.4 us
    ppermute x14 -> x11, waiting for transfers between devices: 57 us -> 42.6 us  [move(): return lax.ppermute(array, 'gz', links)]
    ppermute x14 -> x11, starting transfers between devices: 32.7 us -> 22 us  [move(): return lax.ppermute(array, 'gz', links)]
    all_to_all x0 -> x1, starting transfers between devices: none -> 4.87 us  [all_sum(): return jnp.sum(lax.all_to_all(spread, axes, 0, 0), axis=0)]
    all_to_all x0 -> x1, waiting for transfers between devices: none -> 4.69 us  [all_sum(): return jnp.sum(lax.all_to_all(spread, axes, 0, 0), axis=0)]
    another operation x2, other arithmetic: 2.44 us -> 5.04 us  [dense(): jax.scipy.linalg.cho_solve((jnp.linalg.cholesky(normal), True), target)]
    another operation x3, other arithmetic: 2.91 us -> 4.86 us  [dense(): jnp.linalg.cholesky(normal)]
    unnamed x35 -> x28, local copies, waits for them, and re-layouts: 8.21 us -> 9.77 us
    pallas_call x2 -> x3, Pallas kernels: 13.8 us -> 15 us  [the longest x1 9.08 us: late(): pl.pallas_call(functools.partial(late_kernel, **sizes), out_shape=(out(*l...]
  transfers between devices with their start and end apart: 16 -> 14, of which waited for: 11 -> 5; matrix products, arithmetic and copies ran while one was open for 1% -> 27% of each run, Pallas kernels for 6% -> 4%
where the time goes in v4:
time: 158 us; the launch traced here: 156 us
  waiting for transfers between devices  47.3 us (30%)
  starting transfers between devices  31.2 us (20%)
  other arithmetic  30.2 us (19%)
  Pallas kernels  22.4 us (14%)
  local copies, waits for them, and re-layouts  18 us (11%)
  matrix products  6.08 us (4%)
    ppermute x11, waiting for transfers between devices, move(): return lax.ppermute(array, 'gz', links)  42.6 us
    ppermute x11, starting transfers between devices, move(): return lax.ppermute(array, 'gz', links)  22 us
    unnamed x28, local copies, waits for them, and re-layouts  9.77 us
    pallas_call x1, Pallas kernels, late(): pl.pallas_call(functools.partial(late_kernel, **sizes), out_shape=(out(*l...  9.08 us
    pallas_call x1, Pallas kernels, combine(): pl.pallas_call(functools.partial(combine_kernel, blocks=blocks, half=half...  7.38 us
    another operation x2, other arithmetic, dense(): jax.scipy.linalg.cho_solve((jnp.linalg.cholesky(normal), True), target)  5.04 us
    all_to_all x1, starting transfers between devices, all_sum(): return jnp.sum(lax.all_to_all(spread, axes, 0, 0), axis=0)  4.87 us
    another operation x3, other arithmetic, dense(): jnp.linalg.cholesky(normal)  4.86 us
  transfers between devices with their start and end apart: 14, of which 5 were waited for; matrix products, arithmetic and copies ran while one was open for 27% of the time, Pallas kernels for 4%

profile of v4, /device:TPU:0, one launch (start us, length us, event | category | flops | bytes accessed | tf_op | source)
XLA Modules:
  0.0 156.2 jit_solution(16338210278815857282)
XLA Ops:
  1.9 1.3 collective-permute-start.1
  3.2 3.0 %collective-permute-start = (f32[9,2,4,512]{3,2,0,1:T(4,128)S(1)}, f32[9,2,4,512]{3,2,0,1:T(4,128)S(1)}, u32[]{:S(2)}, u32[]{:S(2)}) collective-permute-start(f32[9,2,4,512]{3,2,0,1:T(4,128)S(1)} %get-tuple-element.39), channel_id=1, source_target_pairs={{0,1},{1,2},{2,3},{4,5},{5,6},{6,7},{8,9},{9,10},{10,11},{12,13},{... | collective-permute-start | bytes 442376 | tf_op jit(solution)/shard_map/ppermute | solution.py:361
  9.4 3.1 %collective-permute-start.3 = (f32[9,40,512]{2,1,0:T(8,128)S(1)}, f32[9,40,512]{2,1,0:T(8,128)S(1)}, u32[]{:S(2)}, u32[]{:S(2)}) collective-permute-start(f32[9,40,512]{2,1,0:T(8,128)S(1)} %get-tuple-element.37.refs_5_), channel_id=1, source_target_pairs={{0,4},{4,0},{8,12},{12,8},{16,20},{20,16},{24,28},{28,24},{1,5},{5... | collective-permute-start | bytes 2211848 | tf_op jit(solution)/shard_map/ppermute | solution.py:376
  13.9 1.3 collective-permute-start.8
  15.2 14.1 %collective-permute-done.3.refs_1_.refs_2_.refs_5_ = f32[9,40,512]{2,1,0:T(8,128)S(1)} collective-permute-done((f32[9,40,512]{2,1,0:T(8,128)S(1)}, f32[9,40,512]{2,1,0:T(8,128)S(1)}, u32[]{:S(2)}, u32[]{:S(2)}) %collective-permute-start.3) | collective-permute-done | bytes 737312 | tf_op jit(solution)/shard_map/ppermute | solution.py:376
  29.2 4.5 %collective-permute-start.4 = (f32[9,40,512]{2,1,0:T(8,128)S(1)}, f32[9,40,512]{2,1,0:T(8,128)S(1)}, u32[]{:S(2)}, u32[]{:S(2)}) collective-permute-start(f32[9,40,512]{2,1,0:T(8,128)S(1)} %collective-permute-done.3.refs_1_.refs_2_.refs_5_), channel_id=1, source_target_pairs={{0,8},{8,16},{16,24},{12,4},{20,12},{28,20},{1,9},{9,17},{17,25},{... | collective-permute-start | bytes 2211848 | tf_op jit(solution)/shard_map/ppermute | solution.py:376
  33.7 11.3 %collective-permute-done.5.refs_2_.refs_3_.refs_6_ = f32[9,40,512]{2,1,0:T(8,128)S(1)} collective-permute-done((f32[9,40,512]{2,1,0:T(8,128)S(1)}, f32[9,40,512]{2,1,0:T(8,128)S(1)}, u32[]{:S(2)}, u32[]{:S(2)}) %collective-permute-start.5) | collective-permute-done | bytes 737312 | tf_op jit(solution)/shard_map/ppermute | solution.py:376
  45.0 4.5 %collective-permute-start.6 = (f32[9,40,512]{2,1,0:T(8,128)S(1)}, f32[9,40,512]{2,1,0:T(8,128)S(1)}, u32[]{:S(2)}, u32[]{:S(2)}) collective-permute-start(f32[9,40,512]{2,1,0:T(8,128)S(1)} %collective-permute-done.5.refs_2_.refs_3_.refs_6_), channel_id=1, source_target_pairs={{0,8},{8,16},{16,24},{12,4},{20,12},{28,20},{1,9},{9,17},{17,25},{... | collective-permute-start | bytes 2211848 | tf_op jit(solution)/shard_map/ppermute | solution.py:376
  49.6 3.5 %collective-permute-start.2 = (f32[8,40,512]{2,1,0:T(8,128)S(1)}, f32[8,40,512]{2,1,0:T(8,128)S(1)}, u32[]{:S(2)}, u32[]{:S(2)}) collective-permute-start(f32[8,40,512]{2,1,0:T(8,128)S(1)} %slice_bitcast_fusion), channel_id=1, source_target_pairs={{0,8},{8,16},{16,24},{12,4},{20,12},{28,20},{1,9},{9,17},{17,25},{... | collective-permute-start | bytes 1966088 | tf_op jit(solution)/shard_map/ppermute | solution.py:376
  56.1 1.3 first.1
  58.4 4.7 %early.1 = (f32[2,8,40,512]{3,2,1,0:T(8,128)S(1)}, f32[2,8,40,512]{3,2,1,0:T(8,128)S(1)}, f32[8,32,512]{2,1,0:T(8,128)S(1)}, f32[8,32,512]{2,1,0:T(8,128)S(1)}, f32[180,8,128]{2,1,0:T(8,128)S(1)}) custom-call(f32[9,40,512]{2,1,0:T(8,128)S(1)} %get-tuple-element.35.refs_0_.refs_3_, f32[9,40,512]{2,1,0:T(8,128)S(1)} %bitcast.43, ...), custom_call_target="tpu_custom_call" | custom-call | flops 65536000 | bytes 2621440 | tf_op jit(solution)/shard_map/early/pallas_call | solution.py:228
  64.7 15.1 %collective-permute-done.2.refs_0_ = f32[8,40,512]{2,1,0:T(8,128)S(1)} collective-permute-done((f32[8,40,512]{2,1,0:T(8,128)S(1)}, f32[8,40,512]{2,1,0:T(8,128)S(1)}, u32[]{:S(2)}, u32[]{:S(2)}) %collective-permute-start.2) | collective-permute-done | bytes 655392 | tf_op jit(solution)/shard_map/ppermute | solution.py:376
  79.8 9.1 %late.1 = (f32[8,40,512]{2,1,0:T(8,128)S(1)}, f32[2,8,40,512]{3,2,1,0:T(8,128)S(1)}, f32[8,252]{1,0:T(8,128)S(1)}) custom-call(f32[8,40,512]{2,1,0:T(8,128)S(1)} %collective-permute-done.2.refs_0_, f32[9,40,512]{2,1,0:T(8,128)S(1)} %collective-permute-done.4.refs_1_, f32[9,40,512]{2,1,0:T(8,128)S(1)} %collective-permute-done.6.refs_2_, ...), custom_call_target="tpu_custom_call" | custom-call | flops 65536000 | bytes 2621440 | tf_op jit(solution)/shard_map/late/pallas_call | solution.py:241
  91.5 4.9 %all-to-all-start = ((f32[32,1,252]{2,1,0:T(1,128)}), f32[32,1,252]{2,1,0:T(1,128)S(1)}, u32[]{:S(2)}, u32[]{:S(2)}) async-start(f32[32,1,252]{2,1,0:T(1,128)} %broadcast_in_dim.21), calls=%async_computation | async-start | bytes 65536 | tf_op jit(solution)/shard_map/all_to_all | solution.py:31
  96.9 1.8 %collective-permute-start.11 = (f32[8,32,512]{2,1,0:T(8,128)}, f32[8,32,512]{2,1,0:T(8,128)}, u32[]{:S(2)}, u32[]{:S(2)}) collective-permute-start(f32[8,32,512]{2,1,0:T(8,128)} %copy-done.8), channel_id=1, source_target_pairs={{0,4},{4,0},{8,12},{12,8},{16,20},{20,16},{24,28},{28,24},{1,5},{5... | collective-permute-start | bytes 1572872 | tf_op jit(solution)/shard_map/ppermute | solution.py:376
  98.9 4.7 %all-to-all-done = f32[32,1,252]{2,1,0:T(1,128)S(1)} async-done(((f32[32,1,252]{2,1,0:T(1,128)}), f32[32,1,252]{2,1,0:T(1,128)S(1)}, u32[]{:S(2)}, u32[]{:S(2)}) %all-to-all-start) | async-done | bytes 32288 | tf_op jit(solution)/shard_map/all_to_all | solution.py:31
  104.7 1.3 reduce.44
  109.2 1.3 copy.45
  110.5 1.4 copy.46
  111.9 1.4 pad_maximum_fusion.1
  113.3 1.4 copy.47
  114.7 1.4 fusion.6
  116.1 3.6 %cholesky.31 = f32[32,32]{1,0:T(8,128)S(1)} custom-call(f32[32,32]{1,0:T(8,128)} %fusion.6), custom_call_target="Cholesky" | custom-call | tf_op jit(solution)/shard_map/jit(cholesky)/cholesky | solution.py:338
  122.2 2.4 %custom-call.17 = f32[1,24,24]{1,2,0:T(8,128)} custom-call(f32[1,24,24]{2,1,0:T(8,128)S(1)} %fusion.10), custom_call_target="InvertDiagBlocksLowerTriangular" | custom-call | tf_op jit(solution)/shard_map/jit(_solve_triangular)/triangular_solve | solution.py:339
  127.8 1.4 copy.48
  129.2 1.3 fusion.20
  130.5 3.5 %cholesky.59 = f32[24,24]{1,0:T(8,128)} custom-call(f32[24,24]{1,0:T(8,128)} %fusion.20), custom_call_target="Cholesky" | custom-call | tf_op jit(solution)/shard_map/jit(cholesky)/cholesky | solution.py:350
  135.4 1.9 %fusion.7 = f32[1,24,24]{2,1,0:T(8,128)} fusion(f32[24,24]{1,0:T(8,128)} %cholesky.59, pred[]{:T(512)} %compare_reduce_fusion), kind=kLoop, calls=%fused_computation.33 | loop fusion | flops 2304 | bytes 4609 | tf_op jit(solution)/shard_map/jit(_cho_solve)/triangular_solve | solution.py:350
  137.3 3.2 %custom-call.18 = f32[1,24,24]{1,2,0:T(8,128)} custom-call(f32[1,24,24]{2,1,0:T(8,128)} %fusion.7), custom_call_target="InvertDiagBlocksLowerTriangular" | custom-call | tf_op jit(solution)/shard_map/jit(_cho_solve)/triangular_solve | solution.py:350
  143.2 2.1 %collective-permute-done.12.refs_9_ = f32[8,32,512]{2,1,0:T(8,128)} collective-permute-done((f32[8,32,512]{2,1,0:T(8,128)}, f32[8,32,512]{2,1,0:T(8,128)}, u32[]{:S(2)}, u32[]{:S(2)}) %collective-permute-start.12) | collective-permute-done | bytes 524320 | tf_op jit(solution)/shard_map/ppermute | solution.py:376
  146.4 1.3 copy-done.3
  148.8 7.4 %combine.1 = f32[8,2,64,512]{3,2,1,0:T(8,128)} custom-call(f32[24,8]{1,0:T(8,128)S(1)} %fusion.29.weights, f32[9,40,512]{2,1,0:T(8,128)S(1)} %get-tuple-element.35.refs_0_.refs_3_, f32[8,40,512]{2,1,0:T(8,128)S(1)} %copy-done.5, f32[2,8,40,512]{3,2,1,0:T(8,128)S(1)} %copy-done.3, f32[9,40,512]{2,1,0:T(8,128)S(1)} %bitcast.45, ...), custom_call_target="tpu_custom_call" | custom-call | tf_op jit(solution)/shard_map/combine/pallas_call | solution.py:303
  (84 shorter events, 30.8 us)
Async XLA Ops:
  0.6 5.7 %copy-start.11 = (f32[2,64,512]{2,1,0:T(8,128)S(1)}, f32[2,64,512]{2,1,0:T(8,128)}, u32[]{:S(2)}) copy-start(f32[2,64,512]{2,1,0:T(8,128)} %param.4) | copy-start | bytes 786436
  0.6 5.7 %copy-start.9 = (f32[8,2,64,512]{3,2,1,0:T(8,128)S(1)}, f32[8,2,64,512]{3,2,1,0:T(8,128)}, u32[]{:S(2)}) copy-start(f32[8,2,64,512]{3,2,1,0:T(8,128)} %param.3) | copy-start | bytes 6291460
  1.9 5.7 %collective-permute-start.1 = (f32[9,2,4,512]{3,2,0,1:T(4,128)S(1)}, f32[9,2,4,512]{3,2,0,1:T(4,128)S(1)}, u32[]{:S(2)}, u32[]{:S(2)}) collective-permute-start(f32[9,2,4,512]{3,2,0,1:T(4,128)S(1)} %get-tuple-element.40), channel_id=1, source_target_pairs={{1,0},{2,1},{3,2},{5,4},{6,5},{7,6},{9,8},{10,9},{11,10},{13,12},{... | collective-permute-start | bytes 442376 | tf_op jit(solution)/shard_map/ppermute | solution.py:362
  3.2 4.7 %collective-permute-start = (f32[9,2,4,512]{3,2,0,1:T(4,128)S(1)}, f32[9,2,4,512]{3,2,0,1:T(4,128)S(1)}, u32[]{:S(2)}, u32[]{:S(2)}) collective-permute-start(f32[9,2,4,512]{3,2,0,1:T(4,128)S(1)} %get-tuple-element.39), channel_id=1, source_target_pairs={{0,1},{1,2},{2,3},{4,5},{5,6},{6,7},{8,9},{9,10},{10,11},{12,13},{... | collective-permute-start | bytes 442376 | tf_op jit(solution)/shard_map/ppermute | solution.py:361
  7.7 1.4 copy-start.10
  9.4 48.0 %copy-start = (f32[9,40,512]{2,1,0:T(8,128)}, f32[9,40,512]{2,1,0:T(8,128)S(1)}, u32[]{:S(2)}) copy-start(f32[9,40,512]{2,1,0:T(8,128)S(1)} %get-tuple-element.37.refs_5_) | copy-start | bytes 2211844
  9.4 19.8 %collective-permute-start.3 = (f32[9,40,512]{2,1,0:T(8,128)S(1)}, f32[9,40,512]{2,1,0:T(8,128)S(1)}, u32[]{:S(2)}, u32[]{:S(2)}) collective-permute-start(f32[9,40,512]{2,1,0:T(8,128)S(1)} %get-tuple-element.37.refs_5_), channel_id=1, source_target_pairs={{0,4},{4,0},{8,12},{12,8},{16,20},{20,16},{24,28},{28,24},{1,5},{5... | collective-permute-start | bytes 2211848 | tf_op jit(solution)/shard_map/ppermute | solution.py:376
  12.5 32.5 %collective-permute-start.5 = (f32[9,40,512]{2,1,0:T(8,128)S(1)}, f32[9,40,512]{2,1,0:T(8,128)S(1)}, u32[]{:S(2)}, u32[]{:S(2)}) collective-permute-start(f32[9,40,512]{2,1,0:T(8,128)S(1)} %get-tuple-element.36.refs_8_), channel_id=1, source_target_pairs={{0,4},{4,0},{8,12},{12,8},{16,20},{20,16},{24,28},{28,24},{1,5},{5... | collective-permute-start | bytes 2211848 | tf_op jit(solution)/shard_map/ppermute | solution.py:376
  12.6 40.5 %collective-permute-start.7 = (f32[9,40,512]{2,1,0:T(8,128)S(1)}, f32[9,40,512]{2,1,0:T(8,128)S(1)}, u32[]{:S(2)}, u32[]{:S(2)}) collective-permute-start(f32[9,40,512]{2,1,0:T(8,128)S(1)} %get-tuple-element.35.refs_0_.refs_3_), channel_id=1, source_target_pairs={{8,0},{16,8},{24,16},{4,12},{12,20},{20,28},{9,1},{17,9},{25,17},{... | collective-permute-start | bytes 2211848 | tf_op jit(solution)/shard_map/ppermute | solution.py:376
  13.9 44.6 %collective-permute-start.8 = (f32[9,40,512]{2,1,0:T(8,128)S(1)}, f32[9,40,512]{2,1,0:T(8,128)S(1)}, u32[]{:S(2)}, u32[]{:S(2)}) collective-permute-start(f32[9,40,512]{2,1,0:T(8,128)S(1)} %bitcast.41), channel_id=1, source_target_pairs={{8,0},{16,8},{24,16},{4,12},{12,20},{20,28},{9,1},{17,9},{25,17},{... | collective-permute-start | bytes 2211848 | tf_op jit(solution)/shard_map/ppermute | solution.py:376
  29.2 50.6 %collective-permute-start.4 = (f32[9,40,512]{2,1,0:T(8,128)S(1)}, f32[9,40,512]{2,1,0:T(8,128)S(1)}, u32[]{:S(2)}, u32[]{:S(2)}) collective-permute-start(f32[9,40,512]{2,1,0:T(8,128)S(1)} %collective-permute-done.3.refs_1_.refs_2_.refs_5_), channel_id=1, source_target_pairs={{0,8},{8,16},{16,24},{12,4},{20,12},{28,20},{1,9},{9,17},{17,25},{... | collective-permute-start | bytes 2211848 | tf_op jit(solution)/shard_map/ppermute | solution.py:376
  45.0 34.8 %collective-permute-start.6 = (f32[9,40,512]{2,1,0:T(8,128)S(1)}, f32[9,40,512]{2,1,0:T(8,128)S(1)}, u32[]{:S(2)}, u32[]{:S(2)}) collective-permute-start(f32[9,40,512]{2,1,0:T(8,128)S(1)} %collective-permute-done.5.refs_2_.refs_3_.refs_6_), channel_id=1, source_target_pairs={{0,8},{8,16},{16,24},{12,4},{20,12},{28,20},{1,9},{9,17},{17,25},{... | collective-permute-start | bytes 2211848 | tf_op jit(solution)/shard_map/ppermute | solution.py:376
  49.6 30.2 %collective-permute-start.2 = (f32[8,40,512]{2,1,0:T(8,128)S(1)}, f32[8,40,512]{2,1,0:T(8,128)S(1)}, u32[]{:S(2)}, u32[]{:S(2)}) collective-permute-start(f32[8,40,512]{2,1,0:T(8,128)S(1)} %slice_bitcast_fusion), channel_id=1, source_target_pairs={{0,8},{8,16},{16,24},{12,4},{20,12},{28,20},{1,9},{9,17},{17,25},{... | collective-permute-start | bytes 1966088 | tf_op jit(solution)/shard_map/ppermute | solution.py:376
  53.1 26.7 %collective-permute-start.9 = (f32[8,40,512]{2,1,0:T(8,128)S(1)}, f32[8,40,512]{2,1,0:T(8,128)S(1)}, u32[]{:S(2)}, u32[]{:S(2)}) collective-permute-start(f32[8,40,512]{2,1,0:T(8,128)S(1)} %slice.179), channel_id=1, source_target_pairs={{8,0},{16,8},{24,16},{4,12},{12,20},{20,28},{9,1},{17,9},{25,17},{... | collective-permute-start | bytes 1966088 | tf_op jit(solution)/shard_map/ppermute | solution.py:376
  57.4 1.0 copy-start.6
  63.1 0.8 copy-start.7
  63.9 0.8 copy-start.8
  88.9 1.1 copy-start.2
  90.0 0.8 copy-start.4
  91.5 12.1 %all-to-all-start = ((f32[32,1,252]{2,1,0:T(1,128)}), f32[32,1,252]{2,1,0:T(1,128)S(1)}, u32[]{:S(2)}, u32[]{:S(2)}) async-start(f32[32,1,252]{2,1,0:T(1,128)} %broadcast_in_dim.21), calls=%async_computation | async-start | bytes 65536 | tf_op jit(solution)/shard_map/all_to_all | solution.py:31
  96.9 46.3 %collective-permute-start.11 = (f32[8,32,512]{2,1,0:T(8,128)}, f32[8,32,512]{2,1,0:T(8,128)}, u32[]{:S(2)}, u32[]{:S(2)}) collective-permute-start(f32[8,32,512]{2,1,0:T(8,128)} %copy-done.8), channel_id=1, source_target_pairs={{0,4},{4,0},{8,12},{12,8},{16,20},{20,16},{24,28},{28,24},{1,5},{5... | collective-permute-start | bytes 1572872 | tf_op jit(solution)/shard_map/ppermute | solution.py:376
  98.6 44.5 %collective-permute-start.10 = (f32[2,8,32,512]{3,2,1,0:T(8,128)}, f32[2,8,32,512]{3,2,1,0:T(8,128)}, u32[]{:S(2)}, u32[]{:S(2)}) collective-permute-start(f32[2,8,32,512]{3,2,1,0:T(8,128)} %copy-done.6), channel_id=1, source_target_pairs={{0,4},{4,0},{8,12},{12,8},{16,20},{20,16},{24,28},{28,24},{1,5},{5... | collective-permute-start | bytes 3145736 | tf_op jit(solution)/shard_map/ppermute | solution.py:376
  121.7 23.6 %collective-permute-start.12 = (f32[8,32,512]{2,1,0:T(8,128)}, f32[8,32,512]{2,1,0:T(8,128)}, u32[]{:S(2)}, u32[]{:S(2)}) collective-permute-start(f32[8,32,512]{2,1,0:T(8,128)} %copy-done.7), channel_id=1, source_target_pairs={{0,4},{4,0},{8,12},{12,8},{16,20},{20,16},{24,28},{28,24},{1,5},{5... | collective-permute-start | bytes 1572872 | tf_op jit(solution)/shard_map/ppermute | solution.py:376
  125.6 0.6 copy-start.13
  127.0 29.2 %copy-start.12 = (f32[24,32]{1,0:T(8,128)}, f32[24,32]{1,0:T(8,128)S(1)}, u32[]{:S(2)}) copy-start(f32[24,32]{1,0:T(8,128)S(1)} %convolution_select_fusion) | copy-start | bytes 9220
  145.3 1.1 copy-start.1
  146.4 1.3 copy-start.3
  147.7 1.1 copy-start.5

commit v5 on v4

--- a/solution.py
+++ b/solution.py
@@ -23,12 +23,12 @@
     return [(i, i ^ bit) for i in range(peers)]
 
 
-def all_sum(array, axes):
+def all_parts(array, axes):
     peers = 1
     for axis in axes:
         peers *= lax.axis_size(axis)
     spread = jnp.broadcast_to(array[None], (peers, *array.shape))
-    return jnp.sum(lax.all_to_all(spread, axes, 0, 0), axis=0)
+    return lax.all_to_all(spread, axes, 0, 0)
 
 
 def row_masks(half, width):
@@ -103,7 +103,7 @@
         acc[base + n] = sums[n] if start is None else sums[n] + start[base + n]
 
 
-EARLY = {0: (4, 5, 6, 7), 1: (5, 6, 7), 2: (5, 6, 7), 3: (6, 7), 4: (6, 7)}
+EARLY = {0: (7,), 1: (5, 6, 7), 2: (5, 6, 7), 3: (6, 7), 4: (6, 7)}
 LATE = {1: (4,), 2: (4,), 3: (4, 5), 4: (4, 5), 5: (4, 5, 6, 7), 6: (4, 5, 6, 7)}
 
 
@@ -123,9 +123,14 @@
     lax.fori_loop(0, blocks, vector, 0)
 
 
+def zero_kernel(*refs, blocks, half, width):
+    fields = dict(zip((4, 5, 6), refs[:3]))
+    gram_part(refs[3], (fields,), 0, (4, 5, 6), blocks, half, width, None)
+
+
 def early_kernel(*refs, blocks, half, width):
     fields = dict(zip((4, 5, 6, 7, 8, 9), refs[:6]))
-    before, x1, x2, near_sent, far_sent, acc, scale_ref, diag_ref = refs[6:]
+    before, start, x1, x2, near_sent, far_sent, acc, x1_out, scale_ref, diag_ref, sem = refs[6:]
     slots = (5, 6, 7, 8)
     set_scales(scale_ref, diag_ref, [fields[n] for n in slots], blocks, slots, half, width)
     flag = side_flags()[1]
@@ -145,14 +150,17 @@
         return carry
 
     lax.fori_loop(0, blocks, vector, 0)
+    copy = pltpu.make_async_copy(x1.at[0, :, pl.ds(0, half)], x1_out, sem)
+    copy.start()
     views = (fields, one, {n: x2.at[n - 6] for n in (6, 7)})
     for moment, layers in EARLY.items():
-        gram_part(acc, views, moment, layers, blocks, half, width, None)
+        gram_part(acc, views, moment, layers, blocks, half, width, start if moment == 0 else None)
+    copy.wait()
 
 
 def late_kernel(*refs, blocks, half, width):
     fields = dict(zip(range(1, 11), refs[:10]))
-    mid1, near1, near2, start, x1, x2, nu_out, far1, far2, x3, acc, scale_ref, diag_ref = refs[10:]
+    mid1, near1, near2, start, x1_out, x2_out, nu_out, x1, x2, far1, far2, x3, acc, scale_ref, diag_ref, sems = refs[10:]
     slots = tuple(range(2, 10))
     set_scales(scale_ref, diag_ref, [fields[n] for n in slots], blocks, slots, half, width)
     low, high = side_flags()
@@ -180,6 +188,10 @@
         return carry
 
     lax.fori_loop(0, blocks, vector, 0)
+    copies = [pltpu.make_async_copy(x1.at[:, pl.ds(0, half)], x1_out, sems.at[0]),
+              pltpu.make_async_copy(x2.at[:, :, pl.ds(0, half)], x2_out, sems.at[1])]
+    for copy in copies:
+        copy.start()
     views = (fields, one, two, three)
     upper = [(v, w) for v in range(blocks) for w in range(v, blocks)]
     acc[pl.ds(0, len(upper))] = start[pl.ds(0, len(upper))]
@@ -189,6 +201,8 @@
     nu_out[...] = lax.dot_general(
         jnp.ones((8, 128), jnp.float32), total, (((1,), (1,)), ((), ())),
         precision=HIGHEST, preferred_element_type=jnp.float32)
+    for copy in copies:
+        copy.wait()
 
 
 def kernels(blocks, half, width):
@@ -196,6 +210,7 @@
     moments = 2 * ITERS + 1
     count = blocks * (blocks + 1) // 2
     vmem = pl.BlockSpec(memory_space=pltpu.VMEM)
+    hbm = pl.BlockSpec(memory_space=pl.ANY)
     sizes = dict(blocks=blocks, half=half, width=width)
     layer = (blocks, rows, width)
     cells = blocks * rows * width
@@ -224,14 +239,25 @@
             name="first",
         )(*fields)
 
+    def zero(*fields):
+        return pl.pallas_call(
+            functools.partial(zero_kernel, **sizes),
+            out_shape=out(count, 8, 128),
+            in_specs=[vmem] * 3,
+            out_specs=vmem,
+            compiler_params=params(4),
+            cost_estimate=cost(40),
+            name="zero",
+        )(*fields)
+
     def early(*arrays):
         return pl.pallas_call(
             functools.partial(early_kernel, **sizes),
             out_shape=(out(2, *layer), out(2, *layer), out(blocks, half, width), out(blocks, half, width),
-                       out(len(EARLY) * count, 8, 128)),
-            in_specs=[vmem] * 7,
-            out_specs=(vmem,) * 5,
-            scratch_shapes=scales(4),
+                       out(len(EARLY) * count, 8, 128), out(blocks, half, width)),
+            in_specs=[vmem] * 8,
+            out_specs=(vmem,) * 5 + (hbm,),
+            scratch_shapes=scales(4) + [pltpu.SemaphoreType.DMA],
             compiler_params=params(12),
             cost_estimate=cost(400),
             name="early",
@@ -240,116 +266,200 @@
     def late(*arrays):
         return pl.pallas_call(
             functools.partial(late_kernel, **sizes),
-            out_shape=(out(*layer), out(2, *layer), out(8, moments * count)),
+            out_shape=(out(blocks, half, width), out(2, blocks, half, width), out(8, moments * count)),
             in_specs=[vmem] * 14,
-            out_specs=(vmem,) * 3,
+            out_specs=(hbm, hbm, vmem),
             scratch_shapes=[
+                pltpu.VMEM(layer, jnp.float32),
+                pltpu.VMEM((2, *layer), jnp.float32),
                 pltpu.VMEM((3, *layer), jnp.float32),
                 pltpu.VMEM((2, *layer), jnp.float32),
                 pltpu.VMEM((4, *layer), jnp.float32),
                 pltpu.VMEM((moments * count, 8, 128), jnp.float32),
                 *scales(8),
+                pltpu.SemaphoreType.DMA((2,)),
             ],
-            compiler_params=params(18),
+            compiler_params=params(20),
             cost_estimate=cost(400),
             name="late",
         )(*arrays)
 
-    return first, early, late
-
-
-TERMS = (
-    ((0, None), (1, None), (2, 0)), ((3, None), (4, 0), (2, 1)),
-    ((5, None), (6, 0), (7, None)), ((8, None), (6, 1), (9, None)),
-)
-
-
-def combine_kernel(weights, *refs, blocks, half, width):
-    arrays, (out, buffer, sems) = refs[:-3], refs[-3:]
-    parity = lax.rem(lax.axis_index("gz"), 2)
-    copies = []
-    for n, (at_layer, at_half) in enumerate((
-        (parity, parity), (1 - parity, parity), (1 - parity, 1 - parity), (parity, 1 - parity),
-    )):
-        terms = [arrays[ref] if at is None else arrays[ref].at[at] for ref, at in TERMS[n]]
-
-        def tile(step, carry, terms=terms, n=n):
-            at = pl.multiple_of(step * 8, 8)
-            for c in range(width // 128):
-                lanes = pl.ds(128 * c, 128)
-                sums = [None] * blocks
-                for k, term in enumerate(terms):
-                    for v in range(blocks):
-                        part = term[v, pl.ds(at, 8), lanes]
-                        for w in range(blocks):
-                            value = weights[k * blocks + v, w] * part
-                            sums[w] = value if sums[w] is None else sums[w] + value
-                for w in range(blocks):
-                    buffer[n, w, pl.ds(at, 8), lanes] = sums[w]
-            return carry
-
-        lax.fori_loop(0, half // 8, tile, 0)
-        copies.append(pltpu.make_async_copy(
-            buffer.at[n],
-            out.at[:, at_layer, pl.ds(pl.multiple_of(at_half * half, 8), half)],
-            sems.at[n]))
-        copies[-1].start()
-    for copy in copies:
-        copy.wait()
-
-
-def combine(weights, arrays, blocks, half, width):
-    vmem = pl.BlockSpec(memory_space=pltpu.VMEM)
-    return pl.pallas_call(
-        functools.partial(combine_kernel, blocks=blocks, half=half, width=width),
-        out_shape=jax.ShapeDtypeStruct((blocks, 2, 2 * half, width), jnp.float32),
-        in_specs=[pl.BlockSpec(memory_space=pltpu.SMEM)] + [vmem] * len(arrays),
-        out_specs=pl.BlockSpec(memory_space=pl.ANY),
-        scratch_shapes=[pltpu.VMEM((4, blocks, half, width), jnp.float32), pltpu.SemaphoreType.DMA((4,))],
-        compiler_params=pltpu.CompilerParams(vmem_limit_bytes=12 << 20),
-        name="combine",
-    )(weights, *arrays)
-
-
-def full_moments(nu, blocks):
-    count = blocks * (blocks + 1) // 2
-    pick = np.zeros((count, blocks * blocks), np.float32)
-    n = 0
-    for v in range(blocks):
-        for w in range(v, blocks):
-            pick[n, v * blocks + w] = pick[n, w * blocks + v] = 1.0
-            n += 1
-    full = jnp.dot(nu.reshape(-1, count), pick, precision=HIGHEST)
-    return full.reshape(-1, blocks, blocks)
-
-
-def dense(nu, blocks):
+    return zero, first, early, late
+
+
+def moment_tables(blocks):
     b1, b2 = BETA[1], BETA[2]
-    g02 = nu[2] - b1 * nu[0]
-    g03 = nu[3] - b2 * nu[1]
-    g13 = nu[4] + b1 * g02 - b2 * nu[2]
-    gram = jnp.concatenate([
-        jnp.concatenate([nu[0], nu[1], g02, g03], axis=1),
-        jnp.concatenate([nu[1], nu[2], nu[3], g13], axis=1),
-        jnp.concatenate([g02, nu[3], nu[4], nu[5]], axis=1),
-        jnp.concatenate([g03, g13, nu[5], nu[6]], axis=1),
-    ], axis=0)
-    size = ITERS * blocks
-    factor = jnp.linalg.cholesky(gram)
-    inverse = jax.scipy.linalg.solve_triangular(
-        factor[:size, :size], jnp.eye(size, dtype=jnp.float32), lower=True)
-    flat = factor.reshape(ITERS + 1, blocks, size + blocks)
-    shifted = [SPREAD * flat[k + 1] + CENTER * flat[k]
-               + (SPREAD * BETA[k] * flat[k - 1] if BETA[k] else 0.0) for k in range(ITERS)]
-    hessenberg = jnp.dot(inverse, jnp.concatenate(shifted, axis=0), precision=HIGHEST)
+    size = 2 * ITERS + 1
+    unit = np.eye(size)
+    g02 = unit[2] - b1 * unit[0]
+    g03 = unit[3] - b2 * unit[1]
+    g13 = unit[4] + b1 * g02 - b2 * unit[2]
+    table = [[unit[0], unit[1], g02, g03], [unit[1], unit[2], unit[3], g13],
+             [g02, unit[3], unit[4], unit[5]], [g03, g13, unit[5], unit[6]]]
+    pairs_of = [(m, v, w) for m in range(size) for v in range(blocks) for w in range(v, blocks)]
+    rows = np.zeros((2, blocks, len(pairs_of)), np.float32)
+    cols = np.zeros((2, len(pairs_of), ITERS + 1, ITERS + 1, blocks), np.float32)
+    for n, (m, v, w) in enumerate(pairs_of):
+        rows[0, v, n] = 1.0
+        rows[1, w, n] = float(v != w)
+        for i in range(ITERS + 1):
+            for j in range(ITERS + 1):
+                cols[0, n, i, j, w] = table[i][j][m]
+                cols[1, n, i, j, v] = table[i][j][m]
+    return rows, cols.reshape(2, len(pairs_of), -1)
+
+
+def shift_table(blocks):
+    table = np.zeros((ITERS, ITERS + 1))
+    for k in range(ITERS):
+        table[k, k + 1] = SPREAD
+        table[k, k] = CENTER
+        if k:
+            table[k, k - 1] = SPREAD * BETA[k]
+    return np.kron(table, np.eye(blocks)).astype(np.float32)
+
+
+def contract(left, right, at_left, at_right):
+    return lax.dot_general(left, right, (((at_left,), (at_right,)), ((), ())),
+                           precision=HIGHEST, preferred_element_type=jnp.float32)
+
+
+def solve_small(parts, rows, cols, shift, blocks):
+    nu = jnp.sum(parts, axis=0)
+    wide = contract(rows[0] * nu, cols[0], 1, 0) + contract(rows[1] * nu, cols[1], 1, 0)
+    total, size = (ITERS + 1) * blocks, ITERS * blocks
+    gram = jnp.concatenate([wide[:, total * i:total * i + total] for i in range(ITERS + 1)], axis=0)
+    row = lax.broadcasted_iota(jnp.int32, (total, total), 0)
+    col = lax.broadcasted_iota(jnp.int32, (total, total), 1)
+    eye = jnp.where(row == col, 1.0, 0.0)
+    both = jnp.concatenate([gram, eye], axis=1)
+    below = lax.broadcasted_iota(jnp.int32, both.shape, 0)
+    for j in range(total - 1):
+        factor = both[:, j:j + 1] / both[j:j + 1, j:j + 1]
+        both = both - jnp.where(below > j, factor, 0.0) * both[j:j + 1]
+    pivots = jnp.sum(both[:, :total] * eye, axis=1, keepdims=True)
+    both = both / jnp.sqrt(pivots)
+    upper = jnp.where(row <= col, both[:, :total], 0.0)
+    inverse = both[:size, total:total + size]
+    hessenberg = contract(inverse, contract(shift, upper, 1, 1), 1, 0)
     row = lax.broadcasted_iota(jnp.int32, hessenberg.shape, 0) // blocks
     col = lax.broadcasted_iota(jnp.int32, hessenberg.shape, 1) // blocks
     hessenberg = jnp.where(col <= row + 1, hessenberg, 0.0)
-    normal = jnp.dot(hessenberg, hessenberg.T, precision=HIGHEST)
-    target = jnp.dot(hessenberg[:, :blocks], factor[:blocks, :blocks].T, precision=HIGHEST)
-    coeffs = jax.scipy.linalg.cho_solve((jnp.linalg.cholesky(normal), True), target)
-    weights = jnp.dot(inverse.T, coeffs, precision=HIGHEST)
-    return hessenberg, weights
+    normal = contract(hessenberg, hessenberg, 1, 1)
+    target = contract(hessenberg[:, :blocks], upper[:blocks, :blocks], 1, 0)
+    both = jnp.concatenate([normal, target], axis=1)
+    here = lax.broadcasted_iota(jnp.int32, both.shape, 0)
+    for j in range(size):
+        pivot = both[j:j + 1] / both[j:j + 1, j:j + 1]
+        both = jnp.where(here == j, pivot, both - both[:, j:j + 1] * pivot)
+    return hessenberg, contract(inverse.T, both[:, size:], 1, 0)
+
+
+def blend(buffer, terms, splat, blocks, half, width):
+    def tile(step, carry):
+        at = pl.multiple_of(step * 8, 8)
+        parts = [pl.ds(128 * c, 128) for c in range(width // 128)]
+        sums = [[None] * len(parts) for _ in range(blocks)]
+        for k, term in enumerate(terms):
+            for v in range(blocks):
+                values = [term[v, pl.ds(at, 8), lanes] for lanes in parts]
+                for w in range(blocks):
+                    scale = jnp.broadcast_to(splat[w, pl.ds(k * blocks + v, 1), :], (8, 128))
+                    for c, value in enumerate(values):
+                        value = scale * value
+                        sums[w][c] = value if sums[w][c] is None else sums[w][c] + value
+        for w in range(blocks):
+            for c, lanes in enumerate(parts):
+                buffer[w, pl.ds(at, 8), lanes] = sums[w][c]
+        return carry
+
+    lax.fori_loop(0, half // 8, tile, 0)
+
+
+def place_of(n, half):
+    parity = lax.rem(lax.axis_index("gz"), 2)
+    layer = (parity, 1 - parity, 1 - parity, parity)[n]
+    rows = (parity, parity, 1 - parity, 1 - parity)[n]
+    return layer, pl.ds(pl.multiple_of(rows * half, 8), half)
+
+
+TERMS = (((0, None), (1, None), (2, 0)), ((3, None), (4, None), (2, 1)), ((5, None), (6, 0), (7, None)))
+
+
+def finish_kernel(parts, rows, cols, shift, *refs, blocks, half, width):
+    arrays, (hess_out, splat, out, source, buffer, sems, out_sems) = refs[:8], refs[8:]
+    copies = []
+    for n, terms in enumerate(TERMS):
+        for k, (ref, at) in enumerate(terms):
+            ref = arrays[ref] if at is None else arrays[ref].at[at]
+            copy = pltpu.make_async_copy(
+                ref.at[pl.ds(0, blocks), pl.ds(0, half)], source.at[n, k], sems.at[n, k])
+            copy.start()
+            copies.append(copy)
+    hessenberg, weights = solve_small(parts[...], rows, cols, shift[...], blocks)
+    hess_out[...] = hessenberg
+    for w in range(blocks):
+        splat[w] = jnp.broadcast_to(weights[:, w:w + 1], (ITERS * blocks, 128))
+    for copy in copies:
+        copy.wait()
+    sends = []
+    for n in range(len(TERMS)):
+        blend(buffer.at[n], [source.at[n, k] for k in range(ITERS)], splat, blocks, half, width)
+        layer, at = place_of(n, half)
+        sends.append(pltpu.make_async_copy(buffer.at[n], out.at[:, layer, at], out_sems.at[n]))
+        sends[-1].start()
+    for send in sends:
+        send.wait()
+
+
+def last_kernel(splat, field, one, two, _, out, buffer, sem, *, blocks, half, width):
+    blend(buffer, [field, one.at[1], two], splat, blocks, half, width)
+    layer, at = place_of(len(TERMS), half)
+    send = pltpu.make_async_copy(buffer, out.at[:, layer, at], sem)
+    send.start()
+    send.wait()
+
+
+def finish(parts, arrays, blocks, half, width):
+    vmem = pl.BlockSpec(memory_space=pltpu.VMEM)
+    hbm = pl.BlockSpec(memory_space=pl.ANY)
+    rows, cols = moment_tables(blocks)
+    size = ITERS * blocks
+    piece = (blocks, half, width)
+    return pl.pallas_call(
+        functools.partial(finish_kernel, blocks=blocks, half=half, width=width),
+        out_shape=(
+            jax.ShapeDtypeStruct((size, size + blocks), jnp.float32),
+            jax.ShapeDtypeStruct((blocks, size, 128), jnp.float32),
+            jax.ShapeDtypeStruct((blocks, 2, 2 * half, width), jnp.float32),
+        ),
+        in_specs=[vmem] * 4 + [hbm] * len(arrays),
+        out_specs=(vmem, vmem, hbm),
+        scratch_shapes=[
+            pltpu.VMEM((len(TERMS), ITERS, *piece), jnp.float32),
+            pltpu.VMEM((len(TERMS), *piece), jnp.float32),
+            pltpu.SemaphoreType.DMA((len(TERMS), ITERS)),
+            pltpu.SemaphoreType.DMA((len(TERMS),)),
+        ],
+        compiler_params=pltpu.CompilerParams(vmem_limit_bytes=16 << 20),
+        cost_estimate=pl.CostEstimate(flops=300 * blocks * half * width, bytes_accessed=1 << 23, transcendentals=0),
+        name="finish",
+    )(parts, rows, cols, shift_table(blocks), *arrays)
+
+
+def last(splat, field, one, two, result, blocks, half, width):
+    vmem = pl.BlockSpec(memory_space=pltpu.VMEM)
+    hbm = pl.BlockSpec(memory_space=pl.ANY)
+    return pl.pallas_call(
+        functools.partial(last_kernel, blocks=blocks, half=half, width=width),
+        out_shape=jax.ShapeDtypeStruct(result.shape, result.dtype),
+        in_specs=[vmem] * 4 + [hbm],
+        out_specs=hbm,
+        scratch_shapes=[pltpu.VMEM((blocks, half, width), jnp.float32), pltpu.SemaphoreType.DMA],
+        input_output_aliases={4: 0},
+        compiler_params=pltpu.CompilerParams(vmem_limit_bytes=8 << 20),
+        name="last",
+    )(splat, field, one, two, result)
 
 
 def body(right_side, diagonal):
@@ -370,7 +480,7 @@
     send_far = jnp.where(even, second[:, 0], first[:, 1])
     keep_near = jnp.where(even, first[:, 1], second[:, 0])
     keep_far = jnp.where(even, first[:, 0], second[:, 1])
-    first_step, early, late = kernels(blocks, half, width)
+    zero, first_step, early, late = kernels(blocks, half, width)
 
     def move(array, links):
         return lax.ppermute(array, "gz", links)
@@ -383,23 +493,22 @@
     in_two = move(got_near, inward)
     out_three = move(got_near[:blocks], outward)
     in_three = move(got_far, inward)
+    nu_zero = zero(keep_far, keep_near, got_near)
     mid1, sent1 = first_step(keep_near, got_near, got_far, out_one)
     back1 = move(sent1, swap)
-    near1, near2, near_sent, far_sent, start = early(
-        keep_far, keep_near, got_near, got_far, out_one, out_two, mid1)
+    near1, near2, near_sent, far_sent, start, x1_near = early(
+        keep_far, keep_near, got_near, got_far, out_one, out_two, mid1, nu_zero)
     near_back2 = move(near_sent, swap)
-    x1, x2, nu = late(
+    x1_far, x2, nu = late(
         in_one, in_two, in_three, keep_far, keep_near, got_near, got_far, out_one, out_two, out_three,
         mid1, near1, near2, start)
-    nu = all_sum(nu[:1], ("gz", "gy"))
-    nu, far_sent = lax.optimization_barrier((nu, far_sent))
+    parts = all_parts(nu[:1], ("gz", "gy"))
+    parts, far_sent = lax.optimization_barrier((parts, far_sent))
     far_back2 = move(far_sent, swap)
-    hessenberg, weights = dense(full_moments(nu, blocks), blocks)
-    result = combine(
-        weights,
-        (keep_far, x1, x2, keep_near, near1, send_near, back1, near_back2, send_far, far_back2),
+    hessenberg, splat, result = finish(
+        parts, (keep_far, x1_far, x2, keep_near, x1_near, send_near, back1, near_back2),
         blocks, half, width)
-    return result, hessenberg
+    return last(splat, send_far, back1, far_back2, result, blocks, half, width), hessenberg
 
 
 def solution(mesh):

time: 158 us -> 127 us (0.80); the launches traced: 156 us -> 127 us
  other arithmetic: 30.2 us -> 3.31 us
  local copies, waits for them, and re-layouts: 18 us -> 9.96 us
  waiting for transfers between devices: 47.3 us -> 54.4 us
  matrix products: 6.08 us -> 0 us
  Pallas kernels: 22.4 us -> 27.7 us
    another operation x10 -> x0, other arithmetic: 16.7 us -> none  [the longest x2 5.04 us: dense(): jax.scipy.linalg.cho_solve((jnp.linalg.cholesky(normal), True), target)]
    concatenate x5 -> x0, local copies, waits for them, and re-layouts: 4.92 us -> none  [the longest x1 1.39 us: dense(): jnp.concatenate([jnp.concatenate([nu[0], nu[1], g02, g03], axis=1), jnp.c...]
    pallas_call x2 -> x4, Pallas kernels: 16.5 us -> 21.2 us  [the longest x1 10.3 us: finish(): pl.pallas_call(functools.partial(finish_kernel, blocks=blocks, half=half,...]
    div x4 -> x0, other arithmetic: 3.94 us -> none  [the longest x1 1.44 us: dense(): factor = jnp.linalg.cholesky(gram)]
    ppermute x11, waiting for transfers between devices: 42.6 us -> 46.4 us  [move(): return lax.ppermute(array, 'gz', links)]
    dot_general x5 -> x0, matrix products: 3.49 us -> none  [the longest x1 0.91 us: dense(): weights = jnp.dot(inverse.T, coeffs, precision=HIGHEST)]
    ppermute x1, waiting for transfers between devices: 0.01 us -> 2.65 us  [body(): under = lax.ppermute(field[:, :, :EDGE], 'gy', pairs(peers_y, -1))]
    another operation x3 -> x0, matrix products: 2.59 us -> none  [the longest x2 1.69 us: dense(): jax.scipy.linalg.cho_solve((jnp.linalg.cholesky(normal), True), target)]
  transfers between devices with their start and end apart: 14 -> 14, of which waited for: 5 -> 6; matrix products, arithmetic and copies ran while one was open for 27% -> 2% of each run, Pallas kernels for 4% -> 20%
where the time goes in v5:
time: 127 us
  waiting for transfers between devices  54.4 us (43%)
  starting transfers between devices  30.5 us (24%)
  Pallas kernels  27.7 us (22%)
  local copies, waits for them, and re-layouts  9.96 us (8%)
  other arithmetic  3.31 us (3%)
    ppermute x11, waiting for transfers between devices, move(): return lax.ppermute(array, 'gz', links)  46.4 us
    ppermute x11, starting transfers between devices, move(): return lax.ppermute(array, 'gz', links)  19.9 us
    pallas_call x1, Pallas kernels, finish(): pl.pallas_call(functools.partial(finish_kernel, blocks=blocks, half=half,...  10.3 us
    unnamed x32, local copies, waits for them, and re-layouts  9.25 us
    pallas_call x1, Pallas kernels, late(): pl.pallas_call(functools.partial(late_kernel, **sizes), out_shape=(out(bl...  8.68 us
    all_to_all x1, starting transfers between devices, all_parts(): return lax.all_to_all(spread, axes, 0, 0)  6.86 us
    all_to_all x1, waiting for transfers between devices, all_parts(): return lax.all_to_all(spread, axes, 0, 0)  5.4 us
    pallas_call x1, Pallas kernels, early(): pl.pallas_call(functools.partial(early_kernel, **sizes), out_shape=(out(2...  4.17 us
  transfers between devices with their start and end apart: 14, of which 6 were waited for; matrix products, arithmetic and copies ran while one was open for 2% of the time, Pallas kernels for 20%

profile of v5, /device:TPU:0, one launch (start us, length us, event | category | flops | bytes accessed | tf_op | source)
XLA Modules:
  0.0 126.8 jit_solution(400171069321312436)
XLA Ops:
  0.6 1.3 %fusion.5 = (f32[9,2,4,512]{3,2,0,1:T(4,128)S(1)}, f32[9,2,4,512]{3,2,0,1:T(4,128)S(1)}) fusion(f32[1,2,64,512]{3,2,0,1:T(8,128)} %bitcast.17, f32[8,2,64,512]{3,2,1,0:T(8,128)} %param.5), kind=kLoop, calls=%fused_computation.23 | loop fusion | flops 73728 | bytes 2654208 | tf_op jit(solution)/shard_map/concatenate | solution.py:470
  1.9 2.4 %collective-permute-start = (f32[9,2,4,512]{3,2,0,1:T(4,128)S(1)}, f32[9,2,4,512]{3,2,0,1:T(4,128)S(1)}, u32[]{:S(2)}, u32[]{:S(2)}) collective-permute-start(f32[9,2,4,512]{3,2,0,1:T(4,128)S(1)} %get-tuple-element.38), channel_id=1, source_target_pairs={{0,1},{1,2},{2,3},{4,5},{5,6},{6,7},{8,9},{9,10},{10,11},{12,13},{... | collective-permute-start | bytes 442376 | tf_op jit(solution)/shard_map/ppermute | solution.py:471
  4.3 1.3 %collective-permute-start.1 = (f32[9,2,4,512]{3,2,0,1:T(4,128)S(1)}, f32[9,2,4,512]{3,2,0,1:T(4,128)S(1)}, u32[]{:S(2)}, u32[]{:S(2)}) collective-permute-start(f32[9,2,4,512]{3,2,0,1:T(4,128)S(1)} %get-tuple-element.39), channel_id=1, source_target_pairs={{1,0},{2,1},{3,2},{5,4},{6,5},{7,6},{9,8},{10,9},{11,10},{13,12},{... | collective-permute-start | bytes 442376 | tf_op jit(solution)/shard_map/ppermute | solution.py:472
  5.7 1.3 %fusion = f32[9,2,36,512]{3,2,0,1:T(8,128)} fusion(f32[1,2,64,512]{3,2,0,1:T(8,128)S(1)} %bitcast.18, f32[8,2,64,512]{3,2,1,0:T(8,128)S(1)} %copy-done.13), kind=kLoop, calls=%fused_computation.8 | loop fusion | flops 331776 | bytes 3686400 | tf_op jit(solution)/shard_map/concatenate | solution.py:470
  7.0 2.7 %collective-permute-done.1 = f32[9,2,4,512]{3,2,0,1:T(4,128)S(1)} collective-permute-done((f32[9,2,4,512]{3,2,0,1:T(4,128)S(1)}, f32[9,2,4,512]{3,2,0,1:T(4,128)S(1)}, u32[]{:S(2)}, u32[]{:S(2)}) %collective-permute-start.1) | collective-permute-done | bytes 147488 | tf_op jit(solution)/shard_map/ppermute | solution.py:472
  10.4 1.6 %collective-permute-start.5 = (f32[9,40,512]{2,1,0:T(8,128)S(1)}, f32[9,40,512]{2,1,0:T(8,128)S(1)}, u32[]{:S(2)}, u32[]{:S(2)}) collective-permute-start(f32[9,40,512]{2,1,0:T(8,128)S(1)} %get-tuple-element.35.field), channel_id=1, source_target_pairs={{0,4},{4,0},{8,12},{12,8},{16,20},{20,16},{24,28},{28,24},{1,5},{5... | collective-permute-start | bytes 2211848 | tf_op jit(solution)/shard_map/ppermute | solution.py:486
  12.5 1.3 %collective-permute-start.7 = (f32[9,40,512]{2,1,0:T(8,128)S(1)}, f32[9,40,512]{2,1,0:T(8,128)S(1)}, u32[]{:S(2)}, u32[]{:S(2)}) collective-permute-start(f32[9,40,512]{2,1,0:T(8,128)S(1)} %get-tuple-element.34.refs_0_.refs_3_), channel_id=1, source_target_pairs={{8,0},{16,8},{24,16},{4,12},{12,20},{20,28},{9,1},{17,9},{25,17},{... | collective-permute-start | bytes 2211848 | tf_op jit(solution)/shard_map/ppermute | solution.py:486
  13.8 1.3 %collective-permute-start.8 = (f32[9,40,512]{2,1,0:T(8,128)S(1)}, f32[9,40,512]{2,1,0:T(8,128)S(1)}, u32[]{:S(2)}, u32[]{:S(2)}) collective-permute-start(f32[9,40,512]{2,1,0:T(8,128)S(1)} %bitcast.11), channel_id=1, source_target_pairs={{8,0},{16,8},{24,16},{4,12},{12,20},{20,28},{9,1},{17,9},{25,17},{... | collective-permute-start | bytes 2211848 | tf_op jit(solution)/shard_map/ppermute | solution.py:486
  15.1 12.0 %collective-permute-done.5.refs_2_.refs_3_.refs_6_ = f32[9,40,512]{2,1,0:T(8,128)S(1)} collective-permute-done((f32[9,40,512]{2,1,0:T(8,128)S(1)}, f32[9,40,512]{2,1,0:T(8,128)S(1)}, u32[]{:S(2)}, u32[]{:S(2)}) %collective-permute-start.5) | collective-permute-done | bytes 737312 | tf_op jit(solution)/shard_map/ppermute | solution.py:486
  27.1 3.5 %collective-permute-start.6 = (f32[9,40,512]{2,1,0:T(8,128)S(1)}, f32[9,40,512]{2,1,0:T(8,128)S(1)}, u32[]{:S(2)}, u32[]{:S(2)}) collective-permute-start(f32[9,40,512]{2,1,0:T(8,128)S(1)} %collective-permute-done.5.refs_2_.refs_3_.refs_6_), channel_id=1, source_target_pairs={{0,8},{8,16},{16,24},{12,4},{20,12},{28,20},{1,9},{9,17},{17,25},{... | collective-permute-start | bytes 2211848 | tf_op jit(solution)/shard_map/ppermute | solution.py:486
  30.6 12.3 %collective-permute-done.3.refs_1_.refs_2_.refs_5_ = f32[9,40,512]{2,1,0:T(8,128)S(1)} collective-permute-done((f32[9,40,512]{2,1,0:T(8,128)S(1)}, f32[9,40,512]{2,1,0:T(8,128)S(1)}, u32[]{:S(2)}, u32[]{:S(2)}) %collective-permute-start.3) | collective-permute-done | bytes 737312 | tf_op jit(solution)/shard_map/ppermute | solution.py:486
  42.9 3.5 %collective-permute-start.4 = (f32[9,40,512]{2,1,0:T(8,128)S(1)}, f32[9,40,512]{2,1,0:T(8,128)S(1)}, u32[]{:S(2)}, u32[]{:S(2)}) collective-permute-start(f32[9,40,512]{2,1,0:T(8,128)S(1)} %collective-permute-done.3.refs_1_.refs_2_.refs_5_), channel_id=1, source_target_pairs={{0,8},{8,16},{16,24},{12,4},{20,12},{28,20},{1,9},{9,17},{17,25},{... | collective-permute-start | bytes 2211848 | tf_op jit(solution)/shard_map/ppermute | solution.py:486
  46.5 3.5 %collective-permute-start.2 = (f32[8,40,512]{2,1,0:T(8,128)S(1)}, f32[8,40,512]{2,1,0:T(8,128)S(1)}, u32[]{:S(2)}, u32[]{:S(2)}) collective-permute-start(f32[8,40,512]{2,1,0:T(8,128)S(1)} %slice_bitcast_fusion), channel_id=1, source_target_pairs={{0,8},{8,16},{16,24},{12,4},{20,12},{28,20},{1,9},{9,17},{17,25},{... | collective-permute-start | bytes 1966088 | tf_op jit(solution)/shard_map/ppermute | solution.py:486
  50.0 1.3 %collective-permute-start.9 = (f32[8,40,512]{2,1,0:T(8,128)S(1)}, f32[8,40,512]{2,1,0:T(8,128)S(1)}, u32[]{:S(2)}, u32[]{:S(2)}) collective-permute-start(f32[8,40,512]{2,1,0:T(8,128)S(1)} %slice.69), channel_id=1, source_target_pairs={{8,0},{16,8},{24,16},{4,12},{12,20},{20,28},{9,1},{17,9},{25,17},{... | collective-permute-start | bytes 1966088 | tf_op jit(solution)/shard_map/ppermute | solution.py:486
  51.3 2.3 %first.1 = (f32[2,8,40,512]{3,2,1,0:T(8,128)S(1)}, f32[2,8,32,512]{3,2,1,0:T(8,128)}) custom-call(f32[9,40,512]{2,1,0:T(8,128)S(1)} %bitcast.12, f32[9,40,512]{2,1,0:T(8,128)S(1)} %collective-permute-done.3.refs_1_.refs_2_.refs_5_, f32[9,40,512]{2,1,0:T(8,128)S(1)} %collective-permute-done.5.refs_2_.refs_3_.refs_6_, ...), custom_call_target="tpu_custom_call" | custom-call | flops 6553600 | bytes 2621440 | tf_op jit(solution)/shard_map/first/pallas_call | solution.py:231
  53.6 1.0 collective-permute-start.10
  55.2 4.2 %early.1 = (f32[2,8,40,512]{3,2,1,0:T(8,128)S(1)}, f32[2,8,40,512]{3,2,1,0:T(8,128)S(1)}, f32[8,32,512]{2,1,0:T(8,128)S(1)}, f32[8,32,512]{2,1,0:T(8,128)S(1)}, ...) custom-call(f32[9,40,512]{2,1,0:T(8,128)S(1)} %get-tuple-element.34.refs_0_.refs_3_, f32[9,40,512]{2,1,0:T(8,128)S(1)} %bitcast.14, ...), custom_call_target="tpu_custom_call" | custom-call | flops 65536000 | bytes 2621440 | tf_op jit(solution)/shard_map/early/pallas_call | solution.py:254
  59.4 0.8 copy-done.11
  60.2 0.8 copy-done.12
  61.0 14.4 %collective-permute-done.2.refs_0_ = f32[8,40,512]{2,1,0:T(8,128)S(1)} collective-permute-done((f32[8,40,512]{2,1,0:T(8,128)S(1)}, f32[8,40,512]{2,1,0:T(8,128)S(1)}, u32[]{:S(2)}, u32[]{:S(2)}) %collective-permute-start.2) | collective-permute-done | bytes 655392 | tf_op jit(solution)/shard_map/ppermute | solution.py:486
  75.5 8.7 %late.1 = (f32[8,32,512]{2,1,0:T(8,128)S(1)}, f32[2,8,32,512]{3,2,1,0:T(8,128)S(1)}, f32[8,252]{1,0:T(8,128)S(1)}) custom-call(f32[8,40,512]{2,1,0:T(8,128)S(1)} %collective-permute-done.2.refs_0_, f32[9,40,512]{2,1,0:T(8,128)S(1)} %collective-permute-done.4.refs_1_, f32[9,40,512]{2,1,0:T(8,128)S(1)} %collective-permute-done.6.refs_2_, ...), custom_call_target="tpu_custom_call" | custom-call | flops 65536000 | bytes 2621440 | tf_op jit(solution)/shard_map/late/pallas_call | solution.py:267
  84.2 1.0 copy-done.2
  86.5 6.9 %all-to-all-start = ((f32[32,1,252]{2,1,0:T(1,128)}), f32[32,1,252]{2,1,0:T(1,128)S(1)}, u32[]{:S(2)}, u32[]{:S(2)}) async-start(f32[32,1,252]{2,1,0:T(1,128)} %broadcast_in_dim.13), calls=%async_computation | async-start | bytes 65536 | tf_op jit(solution)/shard_map/all_to_all | solution.py:31
  93.4 1.8 %collective-permute-start.11 = (f32[8,32,512]{2,1,0:T(8,128)}, f32[8,32,512]{2,1,0:T(8,128)}, u32[]{:S(2)}, u32[]{:S(2)}) collective-permute-start(f32[8,32,512]{2,1,0:T(8,128)} %copy-done.12), channel_id=1, source_target_pairs={{0,4},{4,0},{8,12},{12,8},{16,20},{20,16},{24,28},{28,24},{1,5},{5... | collective-permute-start | bytes 1572872 | tf_op jit(solution)/shard_map/ppermute | solution.py:486
  95.2 5.4 %all-to-all-done.parts = f32[32,1,252]{2,1,0:T(1,128)S(1)} async-done(((f32[32,1,252]{2,1,0:T(1,128)}), f32[32,1,252]{2,1,0:T(1,128)S(1)}, u32[]{:S(2)}, u32[]{:S(2)}) %all-to-all-start) | async-done | bytes 32288 | tf_op jit(solution)/shard_map/all_to_all | solution.py:31
  101.2 7.6 %collective-permute-done.11.refs_7_ = f32[8,32,512]{2,1,0:T(8,128)} collective-permute-done((f32[8,32,512]{2,1,0:T(8,128)}, f32[8,32,512]{2,1,0:T(8,128)}, u32[]{:S(2)}, u32[]{:S(2)}) %collective-permute-start.11) | collective-permute-done | bytes 524320 | tf_op jit(solution)/shard_map/ppermute | solution.py:486
  108.9 1.1 copy-done.1
  110.0 1.2 copy-done.3
  111.2 1.0 copy-done.5
  112.2 1.0 copy-done.7
  114.7 10.3 %finish.1 = (f32[24,32]{1,0:T(8,128)}, f32[8,24,128]{2,1,0:T(8,128)S(1)}, f32[8,2,64,512]{3,2,1,0:T(8,128)}) custom-call(f32[32,1,252]{2,1,0:T(1,128)S(1)} %all-to-all-done.parts, f32[2,8,252]{2,1,0:T(8,128)S(1)} %copy-done.9, f32[2,252,128]{2,1,0:T(8,128)S(1)} %copy-done.8, f32[24,32]{1,0:T(8,128)S(1)} %copy-done.10, ...), custom_call_target="tpu_custom_call" | custom-call | flops 39321600 | bytes 8388608 | tf_op jit(solution)/shard_map/finish/pallas_call | solution.py:429
  125.0 1.7 %last.1 = f32[8,2,64,512]{3,2,1,0:T(8,128)} custom-call(f32[8,24,128]{2,1,0:T(8,128)S(1)} %get-tuple-element.30.splat, f32[9,40,512]{2,1,0:T(8,128)S(1)} %get-tuple-element.35.field, f32[2,8,32,512]{3,2,1,0:T(8,128)S(1)} %collective-permute-done.10.refs_6_.one, f32[8,32,512]{2,1,0:T(8,128)S(1)} %collective-permute-done.12.two, ...), custom_call_target="tpu_custom_call", output_to_operand_aliasing={{}: (4, {})} | custom-call | tf_op jit(solution)/shard_map/last/pallas_call | solution.py:453
  (43 shorter events, 5.4 us)
Async XLA Ops:
  0.6 5.0 %copy-start.13 = (f32[8,2,64,512]{3,2,1,0:T(8,128)S(1)}, f32[8,2,64,512]{3,2,1,0:T(8,128)}, u32[]{:S(2)}) copy-start(f32[8,2,64,512]{3,2,1,0:T(8,128)} %param.5) | copy-start | bytes 6291460
  0.6 5.0 %copy-start.15 = (f32[2,64,512]{2,1,0:T(8,128)S(1)}, f32[2,64,512]{2,1,0:T(8,128)}, u32[]{:S(2)}) copy-start(f32[2,64,512]{2,1,0:T(8,128)} %param.6) | copy-start | bytes 786436
  1.9 8.0 %collective-permute-start = (f32[9,2,4,512]{3,2,0,1:T(4,128)S(1)}, f32[9,2,4,512]{3,2,0,1:T(4,128)S(1)}, u32[]{:S(2)}, u32[]{:S(2)}) collective-permute-start(f32[9,2,4,512]{3,2,0,1:T(4,128)S(1)} %get-tuple-element.38), channel_id=1, source_target_pairs={{0,1},{1,2},{2,3},{4,5},{5,6},{6,7},{8,9},{9,10},{10,11},{12,13},{... | collective-permute-start | bytes 442376 | tf_op jit(solution)/shard_map/ppermute | solution.py:471
  4.3 5.4 %collective-permute-start.1 = (f32[9,2,4,512]{3,2,0,1:T(4,128)S(1)}, f32[9,2,4,512]{3,2,0,1:T(4,128)S(1)}, u32[]{:S(2)}, u32[]{:S(2)}) collective-permute-start(f32[9,2,4,512]{3,2,0,1:T(4,128)S(1)} %get-tuple-element.39), channel_id=1, source_target_pairs={{1,0},{2,1},{3,2},{5,4},{6,5},{7,6},{9,8},{10,9},{11,10},{13,12},{... | collective-permute-start | bytes 442376 | tf_op jit(solution)/shard_map/ppermute | solution.py:472
  7.0 2.9 %copy-start.14 = (f32[9,2,36,512]{3,2,0,1:T(8,128)S(1)}, f32[9,2,36,512]{3,2,0,1:T(8,128)}, u32[]{:S(2)}) copy-start(f32[9,2,36,512]{3,2,0,1:T(8,128)} %fusion) | copy-start | bytes 3981316
  10.4 43.2 %copy-start = (f32[9,40,512]{2,1,0:T(8,128)}, f32[9,40,512]{2,1,0:T(8,128)S(1)}, u32[]{:S(2)}) copy-start(f32[9,40,512]{2,1,0:T(8,128)S(1)} %get-tuple-element.36.refs_5_) | copy-start | bytes 2211844
  10.4 16.7 %collective-permute-start.5 = (f32[9,40,512]{2,1,0:T(8,128)S(1)}, f32[9,40,512]{2,1,0:T(8,128)S(1)}, u32[]{:S(2)}, u32[]{:S(2)}) collective-permute-start(f32[9,40,512]{2,1,0:T(8,128)S(1)} %get-tuple-element.35.field), channel_id=1, source_target_pairs={{0,4},{4,0},{8,12},{12,8},{16,20},{20,16},{24,28},{28,24},{1,5},{5... | collective-permute-start | bytes 2211848 | tf_op jit(solution)/shard_map/ppermute | solution.py:486
  12.0 30.9 %collective-permute-start.3 = (f32[9,40,512]{2,1,0:T(8,128)S(1)}, f32[9,40,512]{2,1,0:T(8,128)S(1)}, u32[]{:S(2)}, u32[]{:S(2)}) collective-permute-start(f32[9,40,512]{2,1,0:T(8,128)S(1)} %get-tuple-element.36.refs_5_), channel_id=1, source_target_pairs={{0,4},{4,0},{8,12},{12,8},{16,20},{20,16},{24,28},{28,24},{1,5},{5... | collective-permute-start | bytes 2211848 | tf_op jit(solution)/shard_map/ppermute | solution.py:486
  12.5 37.5 %collective-permute-start.7 = (f32[9,40,512]{2,1,0:T(8,128)S(1)}, f32[9,40,512]{2,1,0:T(8,128)S(1)}, u32[]{:S(2)}, u32[]{:S(2)}) collective-permute-start(f32[9,40,512]{2,1,0:T(8,128)S(1)} %get-tuple-element.34.refs_0_.refs_3_), channel_id=1, source_target_pairs={{8,0},{16,8},{24,16},{4,12},{12,20},{20,28},{9,1},{17,9},{25,17},{... | collective-permute-start | bytes 2211848 | tf_op jit(solution)/shard_map/ppermute | solution.py:486
  13.8 39.8 %collective-permute-start.8 = (f32[9,40,512]{2,1,0:T(8,128)S(1)}, f32[9,40,512]{2,1,0:T(8,128)S(1)}, u32[]{:S(2)}, u32[]{:S(2)}) collective-permute-start(f32[9,40,512]{2,1,0:T(8,128)S(1)} %bitcast.11), channel_id=1, source_target_pairs={{8,0},{16,8},{24,16},{4,12},{12,20},{20,28},{9,1},{17,9},{25,17},{... | collective-permute-start | bytes 2211848 | tf_op jit(solution)/shard_map/ppermute | solution.py:486
  27.1 48.3 %collective-permute-start.6 = (f32[9,40,512]{2,1,0:T(8,128)S(1)}, f32[9,40,512]{2,1,0:T(8,128)S(1)}, u32[]{:S(2)}, u32[]{:S(2)}) collective-permute-start(f32[9,40,512]{2,1,0:T(8,128)S(1)} %collective-permute-done.5.refs_2_.refs_3_.refs_6_), channel_id=1, source_target_pairs={{0,8},{8,16},{16,24},{12,4},{20,12},{28,20},{1,9},{9,17},{17,25},{... | collective-permute-start | bytes 2211848 | tf_op jit(solution)/shard_map/ppermute | solution.py:486
  42.9 32.5 %collective-permute-start.4 = (f32[9,40,512]{2,1,0:T(8,128)S(1)}, f32[9,40,512]{2,1,0:T(8,128)S(1)}, u32[]{:S(2)}, u32[]{:S(2)}) collective-permute-start(f32[9,40,512]{2,1,0:T(8,128)S(1)} %collective-permute-done.3.refs_1_.refs_2_.refs_5_), channel_id=1, source_target_pairs={{0,8},{8,16},{16,24},{12,4},{20,12},{28,20},{1,9},{9,17},{17,25},{... | collective-permute-start | bytes 2211848 | tf_op jit(solution)/shard_map/ppermute | solution.py:486
  46.5 28.9 %collective-permute-start.2 = (f32[8,40,512]{2,1,0:T(8,128)S(1)}, f32[8,40,512]{2,1,0:T(8,128)S(1)}, u32[]{:S(2)}, u32[]{:S(2)}) collective-permute-start(f32[8,40,512]{2,1,0:T(8,128)S(1)} %slice_bitcast_fusion), channel_id=1, source_target_pairs={{0,8},{8,16},{16,24},{12,4},{20,12},{28,20},{1,9},{9,17},{17,25},{... | collective-permute-start | bytes 1966088 | tf_op jit(solution)/shard_map/ppermute | solution.py:486
  50.0 25.4 %collective-permute-start.9 = (f32[8,40,512]{2,1,0:T(8,128)S(1)}, f32[8,40,512]{2,1,0:T(8,128)S(1)}, u32[]{:S(2)}, u32[]{:S(2)}) collective-permute-start(f32[8,40,512]{2,1,0:T(8,128)S(1)} %slice.69), channel_id=1, source_target_pairs={{8,0},{16,8},{24,16},{4,12},{12,20},{20,28},{9,1},{17,9},{25,17},{... | collective-permute-start | bytes 1966088 | tf_op jit(solution)/shard_map/ppermute | solution.py:486
  53.6 55.2 %collective-permute-start.10 = (f32[2,8,32,512]{3,2,1,0:T(8,128)}, f32[2,8,32,512]{3,2,1,0:T(8,128)S(1)}, u32[]{:S(2)}, u32[]{:S(2)}) collective-permute-start(f32[2,8,32,512]{3,2,1,0:T(8,128)} %get-tuple-element.28), channel_id=1, source_target_pairs={{0,4},{4,0},{8,12},{12,8},{16,20},{20,16},{24,28},{28,24},{1,5},{5... | collective-permute-start | bytes 3145736 | tf_op jit(solution)/shard_map/ppermute | solution.py:486
  59.4 0.8 copy-start.11
  60.2 0.8 copy-start.12
  61.0 23.2 %copy-start.4 = (f32[8,32,512]{2,1,0:T(8,128)}, f32[8,32,512]{2,1,0:T(8,128)S(1)}, u32[]{:S(2)}) copy-start(f32[8,32,512]{2,1,0:T(8,128)S(1)} %get-tuple-element.27.refs_4_) | copy-start | bytes 1572868
  75.4 33.4 %copy-start.8 = (f32[2,252,128]{2,1,0:T(8,128)S(1)}, f32[2,252,128]{2,1,0:T(8,128)}, u32[]{:S(2)}) copy-start(f32[2,252,128]{2,1,0:T(8,128)} %constant.27.clone.cols) | copy-start | bytes 774148
  84.1 1.0 copy-start.2
  85.1 0.8 copy-start.6
  86.5 14.1 %all-to-all-start = ((f32[32,1,252]{2,1,0:T(1,128)}), f32[32,1,252]{2,1,0:T(1,128)S(1)}, u32[]{:S(2)}, u32[]{:S(2)}) async-start(f32[32,1,252]{2,1,0:T(1,128)} %broadcast_in_dim.13), calls=%async_computation | async-start | bytes 65536 | tf_op jit(solution)/shard_map/all_to_all | solution.py:31
  93.4 15.4 %collective-permute-start.11 = (f32[8,32,512]{2,1,0:T(8,128)}, f32[8,32,512]{2,1,0:T(8,128)}, u32[]{:S(2)}, u32[]{:S(2)}) collective-permute-start(f32[8,32,512]{2,1,0:T(8,128)} %copy-done.12), channel_id=1, source_target_pairs={{0,4},{4,0},{8,12},{12,8},{16,20},{20,16},{24,28},{28,24},{1,5},{5... | collective-permute-start | bytes 1572872 | tf_op jit(solution)/shard_map/ppermute | solution.py:486
  100.6 24.4 %collective-permute-start.12 = (f32[8,32,512]{2,1,0:T(8,128)}, f32[8,32,512]{2,1,0:T(8,128)S(1)}, u32[]{:S(2)}, u32[]{:S(2)}) collective-permute-start(f32[8,32,512]{2,1,0:T(8,128)} %copy-done.11), channel_id=1, source_target_pairs={{0,4},{4,0},{8,12},{12,8},{16,20},{20,16},{24,28},{28,24},{1,5},{5... | collective-permute-start | bytes 1572872 | tf_op jit(solution)/shard_map/ppermute | solution.py:486
  108.9 1.1 copy-start.1
  110.0 1.2 copy-start.3
  111.2 1.0 copy-start.5
  112.2 1.0 copy-start.7
  113.3 0.7 copy-start.9
  114.0 0.7 copy-start.10

commit v6 on v5

v6 whole, which is shorter than its diff:
```python
import functools

import jax
import jax.numpy as jnp
import numpy as np
from jax import lax
from jax.experimental import pallas as pl
from jax.experimental.pallas import tpu as pltpu
from jax.sharding import PartitionSpec as P

BLK = 8
ITERS = 3
EDGE = 4
CENTER, SPREAD = 7.6, 2.6
BETA = (0.0, 1.0, 1.5)
HIGHEST = lax.Precision.HIGHEST


def pairs(peers, step):
    return [(i, i + step) for i in range(peers) if 0 <= i + step < peers]


def swap_pairs(peers, bit):
    return [(i, i ^ bit) for i in range(peers)]


def row_masks(half, width):
    rows = half + 2 * EDGE
    parity = lax.rem(lax.axis_index("gz"), 2)
    at_y = lax.axis_index("gy")
    no_below = jnp.logical_and(at_y == lax.axis_size("gy") - 1, parity == 1)
    no_above = jnp.logical_and(at_y == 0, parity == 0)
    row = lax.broadcasted_iota(jnp.int32, (rows, width), 0)
    below = jnp.where(no_below, 0.0, 1.0)
    above = jnp.where(no_above, 0.0, 1.0)
    return jnp.where(row < half, 1.0, jnp.where(row < half + EDGE, below, above))


def side_flags():
    place = lax.axis_index("gz")
    parity = lax.rem(place, 2)
    downward = jnp.where(place >= 2, 1.0, 0.0)
    upward = jnp.where(place < lax.axis_size("gz") - 2, 1.0, 0.0)
    return (jnp.where(parity == 0, downward, upward), jnp.where(parity == 0, upward, downward))


def pick(view, part, i):
    return view[part][i] if isinstance(view, tuple) else view[i + part * (BLK // 2)]


def entry(view, v, rows, lanes):
    half = BLK // 2
    return view[v // half][v % half, rows, lanes] if isinstance(view, tuple) else view[v, rows, lanes]


def diag_of(view):
    return view[0][BLK // 2] if isinstance(view, tuple) else view[BLK]


def set_scales(scale_ref, diag_ref, fields, slots, half, width):
    scale_ref[...] = row_masks(half, width) * (1.0 / SPREAD)
    low, high = side_flags()
    for slot, layer in enumerate(slots):
        value = scale_ref[...] * (diag_of(fields[layer]) + (6.0 - CENTER))
        if layer < 4:
            value = value * low
        if layer > 7:
            value = value * high
        diag_ref[slot] = value


def step_of(scale, diag, low, mid, high, before, beta, flag=None, count=None):
    rows, width = mid.shape
    count = count or rows
    own = mid[:count]
    lane = lax.broadcasted_iota(jnp.int32, (count, width), 1)
    beside = low[:count] + high[:count]
    beside = beside + pltpu.roll(mid, 1, 0)[:count] + pltpu.roll(mid, rows - 1, 0)[:count]
    beside = beside + jnp.where(lane == 0, 0.0, pltpu.roll(own, 1, 1))
    beside = beside + jnp.where(lane == width - 1, 0.0, pltpu.roll(own, width - 1, 1))
    scale = scale[:count]
    if flag is not None:
        scale = scale * flag
    value = diag[:count] * own - scale * beside
    if beta:
        value = value - beta * before[:count]
    return value


def gram_part(acc, views, moment, layers, blocks, half, width, start):
    left, right = views[moment // 2], views[(moment + 1) // 2]
    upper = [(v, w) for v in range(blocks) for w in range(v, blocks)]

    def spot(step, sums):
        at = pl.ds(pl.multiple_of(step * 8, 8), 8)
        sums = list(sums)
        for layer in layers:
            for c in range(width // 128):
                lanes = pl.ds(128 * c, 128)
                rights = [entry(right[layer], w, at, lanes) for w in range(blocks)]
                for v in range(blocks):
                    one = rights[v] if left is right else entry(left[layer], v, at, lanes)
                    for n, (a, b) in enumerate(upper):
                        if a == v:
                            sums[n] = sums[n] + one * rights[b]
        return tuple(sums)

    zeros = tuple(jnp.zeros((8, 128), jnp.float32) for _ in upper)
    sums = lax.fori_loop(0, half // 8, spot, zeros)
    base = moment * len(upper)
    for n in range(len(upper)):
        acc[base + n] = sums[n] if start is None else sums[n] + start[base + n]


def half_loop(body):
    lax.fori_loop(0, BLK // 2, lambda i, carry: (body(i), carry)[1], 0)


EARLY = {0: (7,), 1: (5, 6, 7), 2: (5, 6, 7), 3: (6, 7), 4: (6, 7)}
LATE = {1: (4,), 2: (4,), 3: (4, 5), 4: (4, 5), 5: (4, 5, 6, 7), 6: (4, 5, 6, 7)}


def first_kernel(*refs, part, blocks, half, width):
    near, mid, far_one, far_two, out_one, x1, sent, scale_ref, diag_ref, sem = refs
    fields = {5: near, 6: mid, 7: (far_one, far_two), 8: out_one}
    set_scales(scale_ref, diag_ref, fields, (6, 7), half, width)

    def vector(i):
        for slot, n in enumerate((6, 7)):
            x1[slot, i] = step_of(
                scale_ref[...], diag_ref[slot], *[pick(fields[m], part, i) for m in (n - 1, n, n + 1)], None, 0.0)

    half_loop(vector)
    copy = pltpu.make_async_copy(x1.at[:, :, pl.ds(0, half)], sent, sem)
    copy.start()
    copy.wait()


def zero_kernel(*refs, layers, add, blocks, half, width):
    fields = dict(zip(layers, refs))
    gram_part(refs[-1], (fields,), 0, layers, blocks, half, width, refs[len(layers)] if add else None)


def early_kernel(*refs, blocks, half, width):
    (keep_far, keep_near, got_near, far_one, far_two, out_one, out_two, mid_one, mid_two, start,
     x1, x2, near_sent, far_sent, acc, x1_out, scale_ref, diag_ref, sems) = refs
    fields = {4: keep_far, 5: keep_near, 6: got_near, 7: (far_one, far_two), 8: out_one, 9: out_two}
    slots = (5, 6, 7, 8)
    set_scales(scale_ref, diag_ref, fields, slots, half, width)
    flag = side_flags()[1]
    one = {5: x1.at[0], 6: (mid_one.at[0], mid_two.at[0]), 7: (mid_one.at[1], mid_two.at[1]), 8: x1.at[1]}

    def vector(i):
        for part in range(2):
            v = i + part * (BLK // 2)
            for n in (5, 8):
                one[n][v] = step_of(
                    scale_ref[...], diag_ref[n - 5], *[pick(fields[m], part, i) for m in (n - 1, n, n + 1)],
                    None, 0.0, flag if n == 8 else None)
            for slot, n in enumerate((6, 7)):
                x2[slot, v] = step_of(
                    scale_ref[...], diag_ref[n - 5], *[pick(one[m], part, i) for m in (n - 1, n, n + 1)],
                    pick(fields[n], part, i), BETA[1])

    half_loop(vector)
    copies = [pltpu.make_async_copy(ref.at[:, pl.ds(0, half)], out, sems.at[n]) for n, (ref, out) in enumerate(
        ((x2.at[0], near_sent), (x2.at[1], far_sent), (x1.at[0], x1_out)))]
    for copy in copies:
        copy.start()
    views = (fields, one, {n: x2.at[n - 6] for n in (6, 7)})
    for moment, layers in EARLY.items():
        gram_part(acc, views, moment, layers, blocks, half, width, start if moment == 0 else None)
    for copy in copies:
        copy.wait()


def late_kernel(*refs, part, blocks, half, width):
    (in_one, in_two, in_three, keep_far, keep_near, got_near, far_one, far_two, out_one, out_two, out_three,
     mid_one, mid_two, near1, near2) = refs[:15]
    rest = refs[15:]
    if part == 0:
        x1, x2, x3, far1, far2, scale_ref, diag_ref = rest
        third = (in_three,)
    else:
        (before, x1_first, x2_first, x3_first, start, x1_out, x2_out, nu_out,
         x1, x2, x3, far1, far2, acc, scale_ref, diag_ref, sems) = rest
        third = (before, in_three)
    third = third + (None,) * (2 - len(third))
    fields = {1: in_one, 2: in_two, 3: third, 4: keep_far, 5: keep_near, 6: got_near, 7: (far_one, far_two),
              8: out_one, 9: out_two, 10: (out_three, out_three)}
    slots = tuple(range(2, 10))
    set_scales(scale_ref, diag_ref, fields, slots, half, width)
    low, high = side_flags()
    mine = {2: far1.at[0], 3: far1.at[1], 4: x1, 9: far1.at[2]}
    one = {5: near1.at[0], 8: near1.at[1], 6: (mid_one.at[0], mid_two.at[0]), 7: (mid_one.at[1], mid_two.at[1]),
           **{n: (ref, ref) for n, ref in mine.items()}}
    mine_two = {3: far2.at[0], 4: x2.at[0], 5: x2.at[1], 8: far2.at[1]}
    two = {6: near2.at[0], 7: near2.at[1], **{n: (ref, ref) for n, ref in mine_two.items()}}

    def flag_of(n):
        return low if n < 4 else high if n > 7 else None

    def vector(i):
        for n, count in ((2, half), (3, None), (4, None), (9, half)):
            value = step_of(
                scale_ref[...], diag_ref[n - 2], *[pick(fields[m], part, i) for m in (n - 1, n, n + 1)],
                None, 0.0, flag_of(n), count)
            mine[n][i, pl.ds(0, value.shape[0])] = value
        for n, count in ((3, half), (4, None), (5, None), (8, half)):
            value = step_of(
                scale_ref[...], diag_ref[n - 2], *[pick(one[m], part, i) for m in (n - 1, n, n + 1)],
                pick(fields[n], part, i), BETA[1], flag_of(n), count)
            mine_two[n][i, pl.ds(0, value.shape[0])] = value
        for n in (4, 5, 6, 7):
            x3[n - 4, i] = step_of(
                scale_ref[...], diag_ref[n - 2], *[pick(two[m], part, i) for m in (n - 1, n, n + 1)],
                pick(one[n], part, i), BETA[2], None, half)

    half_loop(vector)
    if part == 0:
        return
    copies = []
    for n, (x1_half, x2_half) in enumerate(((x1_first, x2_first), (x1, x2))):
        vectors = pl.ds(n * (BLK // 2), BLK // 2)
        copies.append(pltpu.make_async_copy(x1_half.at[:, pl.ds(0, half)], x1_out.at[vectors], sems.at[2 * n]))
        copies.append(pltpu.make_async_copy(
            x2_half.at[:, :, pl.ds(0, half)], x2_out.at[:, vectors], sems.at[2 * n + 1]))
    for copy in copies:
        copy.start()
    views = (fields, {**one, 4: (x1_first, x1)},
             {**two, 4: (x2_first.at[0], x2.at[0]), 5: (x2_first.at[1], x2.at[1])},
             {n: (x3_first.at[n - 4], x3.at[n - 4]) for n in (4, 5, 6, 7)})
    upper = blocks * (blocks + 1) // 2
    acc[pl.ds(0, upper)] = start[pl.ds(0, upper)]
    for moment, layers in LATE.items():
        gram_part(acc, views, moment, layers, blocks, half, width, start if moment in EARLY else None)
    total = jnp.sum(acc[...], axis=1)
    sums = lax.dot_general(
        jnp.ones((8, 128), jnp.float32), total, (((1,), (1,)), ((), ())),
        precision=HIGHEST, preferred_element_type=jnp.float32)
    nu_out[...] = jnp.broadcast_to(sums[:1][None], nu_out.shape)
    for copy in copies:
        copy.wait()


def kernels(blocks, half, width, peers):
    rows = half + 2 * EDGE
    moments = 2 * ITERS + 1
    count = blocks * (blocks + 1) // 2
    vmem = pl.BlockSpec(memory_space=pltpu.VMEM)
    hbm = pl.BlockSpec(memory_space=pltpu.HBM)
    sizes = dict(blocks=blocks, half=half, width=width)
    layer = (blocks, rows, width)
    part_layer = (blocks // 2, rows, width)
    cells = blocks * rows * width

    def out(*shape):
        return jax.ShapeDtypeStruct(shape, jnp.float32)

    def far(*shape):
        return pltpu.HBM(shape, jnp.float32)

    def scales(number):
        return [pltpu.VMEM((rows, width), jnp.float32), pltpu.VMEM((number, rows, width), jnp.float32)]

    def call(kernel, arrays, outs, scratch, mib, ops, **static):
        return pl.pallas_call(
            functools.partial(kernel, **sizes, **static),
            out_shape=outs,
            in_specs=[vmem] * len(arrays),
            out_specs=tuple(vmem if isinstance(o, jax.ShapeDtypeStruct) else hbm for o in outs),
            scratch_shapes=scratch,
            compiler_params=pltpu.CompilerParams(vmem_limit_bytes=mib << 20),
            cost_estimate=pl.CostEstimate(flops=ops * cells, bytes_accessed=16 * cells, transcendentals=0),
        )(*arrays)

    def zero(arrays, layers, add):
        return call(zero_kernel, arrays, (out(count, 8, 128),), [], 4, 20, layers=layers, add=add)[0]

    def first(arrays, part):
        return call(first_kernel, arrays, (out(2, *part_layer), far(2, blocks // 2, half, width)),
                    scales(2) + [pltpu.SemaphoreType.DMA], 8, 20, part=part)

    def early(*arrays):
        outs = (out(2, *layer), out(2, *layer), far(blocks, half, width), far(blocks, half, width),
                out(len(EARLY) * count, 8, 128), far(blocks, half, width))
        return call(early_kernel, arrays, outs, scales(4) + [pltpu.SemaphoreType.DMA((3,))], 12, 200)

    def late(arrays, part):
        mine = ((part_layer), (2, *part_layer), (4, blocks // 2, half, width))
        work = [pltpu.VMEM((3, *part_layer), jnp.float32), pltpu.VMEM((2, *part_layer), jnp.float32)]
        if part == 0:
            return call(late_kernel, arrays, tuple(out(*m) for m in mine), work + scales(8), 12, 100, part=0)
        outs = (far(blocks, half, width), far(2, blocks, half, width), out(peers, 1, moments * count))
        work = [pltpu.VMEM(m, jnp.float32) for m in mine] + work + [
            pltpu.VMEM((moments * count, 8, 128), jnp.float32), *scales(8), pltpu.SemaphoreType.DMA((4,))]
        return call(late_kernel, arrays, outs, work, 18, 200, part=1)

    return zero, first, early, late


def moment_tables(blocks):
    b1, b2 = BETA[1], BETA[2]
    size = 2 * ITERS + 1
    unit = np.eye(size)
    g02 = unit[2] - b1 * unit[0]
    g03 = unit[3] - b2 * unit[1]
    g13 = unit[4] + b1 * g02 - b2 * unit[2]
    table = [[unit[0], unit[1], g02, g03], [unit[1], unit[2], unit[3], g13],
             [g02, unit[3], unit[4], unit[5]], [g03, g13, unit[5], unit[6]]]
    pairs_of = [(m, v, w) for m in range(size) for v in range(blocks) for w in range(v, blocks)]
    rows = np.zeros((2, blocks, len(pairs_of)), np.float32)
    cols = np.zeros((2, len(pairs_of), ITERS + 1, ITERS + 1, blocks), np.float32)
    for n, (m, v, w) in enumerate(pairs_of):
        rows[0, v, n] = 1.0
        rows[1, w, n] = float(v != w)
        for i in range(ITERS + 1):
            for j in range(ITERS + 1):
                cols[0, n, i, j, w] = table[i][j][m]
                cols[1, n, i, j, v] = table[i][j][m]
    return rows, cols.reshape(2, len(pairs_of), -1)


def shift_table(blocks):
    table = np.zeros((ITERS, ITERS + 1))
    for k in range(ITERS):
        table[k, k + 1] = SPREAD
        table[k, k] = CENTER
        if k:
            table[k, k - 1] = SPREAD * BETA[k]
    return np.kron(table, np.eye(blocks)).astype(np.float32)


def contract(left, right, at_left, at_right):
    return lax.dot_general(left, right, (((at_left,), (at_right,)), ((), ())),
                           precision=HIGHEST, preferred_element_type=jnp.float32)


def solve_small(parts, rows, cols, shift, blocks):
    nu = jnp.sum(parts, axis=0)
    wide = sum(contract(rows[n] * nu, cols[n].astype(jnp.float32), 1, 0) for n in range(2))
    total, size = (ITERS + 1) * blocks, ITERS * blocks
    gram = jnp.concatenate([wide[:, total * i:total * i + total] for i in range(ITERS + 1)], axis=0)
    row = lax.broadcasted_iota(jnp.int32, (total, total), 0)
    col = lax.broadcasted_iota(jnp.int32, (total, total), 1)
    eye = jnp.where(row == col, 1.0, 0.0)
    moved = contract(shift, gram, 1, 0)
    factors = jnp.concatenate([gram, eye], axis=1)
    solving = jnp.concatenate([contract(moved, shift, 1, 1), moved[:, :blocks]], axis=1)
    below = lax.broadcasted_iota(jnp.int32, factors.shape, 0)
    here = lax.broadcasted_iota(jnp.int32, solving.shape, 0)
    for j in range(total - 1):
        scale = factors[j:j + 1] / factors[j:j + 1, j:j + 1]
        factors = factors - jnp.where(below > j, factors[:, j:j + 1], 0.0) * scale
        if j < size:
            pivot = solving[j:j + 1] / solving[j:j + 1, j:j + 1]
            solving = jnp.where(here == j, pivot, solving - solving[:, j:j + 1] * pivot)
    pivots = jnp.sum(factors[:, :total] * eye, axis=1, keepdims=True)
    factors = factors / jnp.sqrt(pivots)
    upper = jnp.where(row <= col, factors[:, :total], 0.0)
    inverse = factors[:size, total:total + size]
    hessenberg = contract(inverse, contract(shift, upper, 1, 1), 1, 0)
    row = lax.broadcasted_iota(jnp.int32, hessenberg.shape, 0) // blocks
    col = lax.broadcasted_iota(jnp.int32, hessenberg.shape, 1) // blocks
    return jnp.where(col <= row + 1, hessenberg, 0.0), solving[:, size:]


def blend(buffer, terms, splat, blocks, half, width):
    def tile(step, carry):
        at = pl.multiple_of(step * 8, 8)
        parts = [pl.ds(128 * c, 128) for c in range(width // 128)]
        sums = [[None] * len(parts) for _ in range(blocks)]
        for k, term in enumerate(terms):
            for v in range(blocks):
                values = [term[v, pl.ds(at, 8), lanes] for lanes in parts]
                for w in range(blocks):
                    scale = jnp.broadcast_to(splat[w, pl.ds(k * blocks + v, 1), :], (8, 128))
                    for c, value in enumerate(values):
                        value = scale * value
                        sums[w][c] = value if sums[w][c] is None else sums[w][c] + value
        for w in range(blocks):
            for c, lanes in enumerate(parts):
                buffer[w, pl.ds(at, 8), lanes] = sums[w][c]
        return carry

    lax.fori_loop(0, half // 8, tile, 0)


def place_of(n, half):
    parity = lax.rem(lax.axis_index("gz"), 2)
    layer = (parity, 1 - parity, 1 - parity, parity)[n]
    rows = (parity, parity, 1 - parity, 1 - parity)[n]
    return layer, pl.ds(pl.multiple_of(rows * half, 8), half)


TERMS = (((0, None), (1, None), (2, 0)), ((3, None), (4, None), (2, 1)))


def finish_kernel(parts, rows, cols, shift, *refs, blocks, half, width):
    arrays, (hess_out, splat, out, source, buffer, sems, out_sems) = refs[:5], refs[5:]
    copies = []
    for n, terms in enumerate(TERMS):
        for k, (ref, at) in enumerate(terms):
            ref = arrays[ref] if at is None else arrays[ref].at[at]
            copy = pltpu.make_async_copy(
                ref.at[pl.ds(0, blocks), pl.ds(0, half)], source.at[n, k], sems.at[n, k])
            copy.start()
            copies.append(copy)
    hessenberg, weights = solve_small(parts[...], rows, cols, shift[...], blocks)
    hess_out[...] = hessenberg
    for w in range(blocks):
        splat[w] = jnp.broadcast_to(weights[:, w:w + 1], (ITERS * blocks, 128))
    for copy in copies:
        copy.wait()
    sends = []
    for n in range(len(TERMS)):
        blend(buffer.at[n], [source.at[n, k] for k in range(ITERS)], splat, blocks, half, width)
        layer, at = place_of(n, half)
        sends.append(pltpu.make_async_copy(buffer.at[n], out.at[:, layer, at], out_sems.at[n]))
        sends[-1].start()
    for send in sends:
        send.wait()


def others_kernel(splat, near0, far0, one_first, one_second, near2, far2, _, out, source, buffer, sems, out_sems, *,
                  blocks, half, width):
    loads = []
    for n, (zero, two) in enumerate(((near0, near2), (far0, far2))):
        for k, (term, at) in enumerate((
            (zero.at[pl.ds(0, blocks), pl.ds(0, half)], source.at[n, 0]),
            (one_first.at[n], source.at[n, 1, pl.ds(0, blocks // 2)]),
            (one_second.at[n], source.at[n, 1, pl.ds(blocks // 2, blocks // 2)]),
            (two, source.at[n, 2]),
        )):
            loads.append(pltpu.make_async_copy(term, at, sems.at[n, k]))
            loads[-1].start()
    sends = []
    for n in range(2):
        for load in loads[4 * n:4 * n + 4]:
            load.wait()
        blend(buffer.at[n], [source.at[n, k] for k in range(ITERS)], splat, blocks, half, width)
        layer, at = place_of(2 + n, half)
        sends.append(pltpu.make_async_copy(buffer.at[n], out.at[:, layer, at], out_sems.at[n]))
        sends[-1].start()
    for send in sends:
        send.wait()


def in_hbm(array):
    return pltpu.with_memory_space_constraint(array, pltpu.HBM)


def finish(parts, arrays, blocks, half, width):
    vmem = pl.BlockSpec(memory_space=pltpu.VMEM)
    hbm = pl.BlockSpec(memory_space=pltpu.HBM)
    rows, cols = moment_tables(blocks)
    size = ITERS * blocks
    piece = (blocks, half, width)
    return pl.pallas_call(
        functools.partial(finish_kernel, blocks=blocks, half=half, width=width),
        out_shape=(
            jax.ShapeDtypeStruct((size, size + blocks), jnp.float32),
            jax.ShapeDtypeStruct((blocks, size, 128), jnp.float32),
            jax.ShapeDtypeStruct((blocks, 2, 2 * half, width), jnp.float32),
        ),
        in_specs=[vmem] * 4 + [hbm] * len(arrays),
        out_specs=(vmem, vmem, hbm),
        scratch_shapes=[
            pltpu.VMEM((len(TERMS), ITERS, *piece), jnp.float32),
            pltpu.VMEM((len(TERMS), *piece), jnp.float32),
            pltpu.SemaphoreType.DMA((len(TERMS), ITERS)),
            pltpu.SemaphoreType.DMA((len(TERMS),)),
        ],
        compiler_params=pltpu.CompilerParams(vmem_limit_bytes=16 << 20),
        cost_estimate=pl.CostEstimate(flops=300 * blocks * half * width, bytes_accessed=1 << 23, transcendentals=0),
        name="finish",
    )(parts, rows, cols.astype(jnp.bfloat16), shift_table(blocks), *[in_hbm(array) for array in arrays])


def others(splat, near0, far0, one_first, one_second, near2, far2, result, half, width):
    vmem = pl.BlockSpec(memory_space=pltpu.VMEM)
    hbm = pl.BlockSpec(memory_space=pltpu.HBM)
    blocks = near2.shape[0]
    return pl.pallas_call(
        functools.partial(others_kernel, blocks=blocks, half=half, width=width),
        out_shape=jax.ShapeDtypeStruct(result.shape, result.dtype),
        in_specs=[vmem] + [hbm] * 2 + [pl.BlockSpec(memory_space=pl.ANY)] * 4 + [hbm],
        out_specs=hbm,
        scratch_shapes=[
            pltpu.VMEM((2, ITERS, blocks, half, width), jnp.float32),
            pltpu.VMEM((2, blocks, half, width), jnp.float32),
            pltpu.SemaphoreType.DMA((2, 4)),
            pltpu.SemaphoreType.DMA((2,)),
        ],
        input_output_aliases={7: 0},
        compiler_params=pltpu.CompilerParams(vmem_limit_bytes=8 << 20),
        name="others",
    )(splat, in_hbm(near0), in_hbm(far0), one_first, one_second, near2, far2, result)


def body(right_side, diagonal):
    blocks, _, ny, width = right_side.shape
    half = ny // 2
    peers_z, peers_y = lax.axis_size("gz"), lax.axis_size("gy")
    even = lax.axis_index("gz") % 2 == 0
    field = jnp.concatenate([right_side, diagonal[None]], axis=0)
    above = lax.ppermute(field[:, :, ny - EDGE:], "gy", pairs(peers_y, 1))
    under = lax.ppermute(field[:, :, :EDGE], "gy", pairs(peers_y, -1))
    first = jnp.concatenate([field[:, :, :half + EDGE], above], axis=2)
    second = jnp.concatenate([field[:, :, half:], under, field[:, :, half - EDGE:half]], axis=2)

    swap = swap_pairs(peers_z, 1)
    inward = [(i, j) for i, j in pairs(peers_z, 2) if i % 2 == 0] + [(i, j) for i, j in pairs(peers_z, -2) if i % 2]
    outward = [(j, i) for i, j in inward]
    send_near = jnp.where(even, second[:, 1], first[:, 0])
    send_far = jnp.where(even, second[:, 0], first[:, 1])
    keep_near = jnp.where(even, first[:, 1], second[:, 0])
    keep_far = jnp.where(even, first[:, 0], second[:, 1])
    zero, first_step, early, late = kernels(blocks, half, width, peers_z * peers_y)

    def move(array, links):
        return lax.ppermute(array, "gz", links)

    middle = blocks // 2
    got_near = move(send_near, swap)
    in_one = move(keep_near[:blocks, :half], inward)
    out_one = move(keep_far, outward)
    far_a = move(jnp.concatenate([send_far[:middle], send_far[blocks:]], axis=0), swap)
    far_b = move(send_far[middle:blocks], swap)
    out_two = move(keep_near, outward)
    in_two = move(got_near, inward)
    out_a = move(got_near[:middle, :half], outward)
    out_b = move(got_near[middle:blocks, :half], outward)
    nu_zero = zero((keep_far, keep_near), (4, 5), False)
    mid_a, sent_a = first_step((keep_near, got_near, far_a, far_a, out_one), 0)
    back_a = move(sent_a, swap)
    in_a = move(far_a, inward)
    nu_zero = zero((got_near, nu_zero), (6,), True)
    mid_b, sent_b = first_step((keep_near, got_near, far_a, far_b, out_one), 1)
    back_b = move(sent_b, swap)
    in_b = move(far_b, inward)
    near1, near2, near_sent, far_sent, start, x1_near = early(
        keep_far, keep_near, got_near, far_a, far_b, out_one, out_two, mid_a, mid_b, nu_zero)
    near_back2 = move(near_sent, swap)
    first_half = late((in_one, in_two, in_a, keep_far, keep_near, got_near, far_a, far_b, out_one, out_two,
                       out_a, mid_a, mid_b, near1, near2), 0)
    x1_far, x2, nu = late((in_one, in_two, in_b, keep_far, keep_near, got_near, far_a, far_b, out_one, out_two,
                           out_b, mid_a, mid_b, near1, near2, in_a, *first_half, start), 1)
    parts = lax.all_to_all(nu, ("gz", "gy"), 0, 0)
    far_back2 = move(far_sent, swap)
    hessenberg, splat, result = finish(
        parts, (keep_far, x1_far, x2, keep_near, x1_near), blocks, half, width)
    result = others(splat, send_near, send_far, back_a, back_b, near_back2, far_back2, result, half, width)
    return result, hessenberg


def solution(mesh):
    in_specs = (P(None, "gz", "gy", None), P("gz", "gy", None))
    out_specs = (P(None, "gz", "gy", None), P())

    return jax.shard_map(body, mesh=mesh, in_specs=in_specs, out_specs=out_specs, check_vma=False)
```

time: 127 us -> 122 us (0.961)
  blocking collectives: 0 us -> 19.9 us
  waiting for transfers between devices: 54.4 us -> 36.5 us
  local copies, waits for them, and re-layouts: 9.96 us -> 0.18 us
  starting transfers between devices: 30.5 us -> 34.8 us
  Pallas kernels: 27.7 us -> 26.1 us
    all_to_all x0 -> x1, blocking collectives: none -> 19.9 us  [body(): parts = lax.all_to_all(nu, ('gz', 'gy'), 0, 0)]
    ppermute x11 -> x15, waiting for transfers between devices: 46.4 us -> 33.9 us  [move(): return lax.ppermute(array, 'gz', links)]
    ppermute x11 -> x15, starting transfers between devices: 19.9 us -> 31.1 us  [move(): return lax.ppermute(array, 'gz', links)]
    unnamed x32 -> x24, local copies, waits for them, and re-layouts: 9.25 us -> 0.06 us
    all_to_all x1 -> x0, starting transfers between devices: 6.86 us -> none  [all_parts(): return lax.all_to_all(spread, axes, 0, 0)]
    all_to_all x1 -> x0, waiting for transfers between devices: 5.4 us -> none  [all_parts(): return lax.all_to_all(spread, axes, 0, 0)]
    pallas_call x1, Pallas kernels: 10.3 us -> 6.89 us  [finish(): pl.pallas_call(functools.partial(finish_kernel, blocks=blocks, half=half,...]
    pallas_call x5 -> x8, Pallas kernels: 17.4 us -> 19.2 us  [the longest x7 15.4 us: call(): pl.pallas_call(functools.partial(kernel, **sizes, **static), out_shape=ou...]
  transfers between devices with their start and end apart: 14 -> 17, of which waited for: 6 -> 6; matrix products, arithmetic and copies ran while one was open for 2% -> 1% of each run, Pallas kernels for 20% -> 18%
where the time goes in v6:
time: 122 us
  waiting for transfers between devices  36.5 us (30%)
  starting transfers between devices  34.8 us (29%)
  Pallas kernels  26.1 us (21%)
  blocking collectives  19.9 us (16%)
  other arithmetic  3.3 us (3%)
    ppermute x15, waiting for transfers between devices, move(): return lax.ppermute(array, 'gz', links)  33.9 us
    ppermute x15, starting transfers between devices, move(): return lax.ppermute(array, 'gz', links)  31.1 us
    all_to_all x1, blocking collectives, body(): parts = lax.all_to_all(nu, ('gz', 'gy'), 0, 0)  19.9 us
    pallas_call x7, Pallas kernels, call(): pl.pallas_call(functools.partial(kernel, **sizes, **static), out_shape=ou...  15.4 us
    pallas_call x1, Pallas kernels, finish(): pl.pallas_call(functools.partial(finish_kernel, blocks=blocks, half=half,...  6.89 us
    pallas_call x1, Pallas kernels, others(): pl.pallas_call(functools.partial(others_kernel, blocks=blocks, half=half,...  3.77 us
    ppermute x1, waiting for transfers between devices, body(): under = lax.ppermute(field[:, :, :EDGE], 'gy', pairs(peers_y, -1))  2.65 us
    concatenate x3, other arithmetic, body(): field = jnp.concatenate([right_side, diagonal[None]], axis=0)  2.63 us
  transfers between devices with their start and end apart: 17, of which 6 were waited for; matrix products, arithmetic and copies ran while one was open for 1% of the time, Pallas kernels for 18%

profile of v6, /device:TPU:0, one launch (start us, length us, event | category | flops | bytes accessed | tf_op | source)
XLA Modules:
  0.0 121.8 jit_solution(9754738581065418681)
XLA Ops:
  0.6 1.3 %fusion.5 = (f32[9,2,4,512]{3,2,0,1:T(4,128)S(1)}, f32[9,2,4,512]{3,2,0,1:T(4,128)S(1)}) fusion(f32[1,2,64,512]{3,2,0,1:T(8,128)} %bitcast.15, f32[8,2,64,512]{3,2,1,0:T(8,128)} %param.5), kind=kLoop, calls=%fused_computation.25 | loop fusion | flops 73728 | bytes 2654208 | tf_op jit(solution)/shard_map/concatenate | solution.py:506
  1.9 2.4 %collective-permute-start = (f32[9,2,4,512]{3,2,0,1:T(4,128)S(1)}, f32[9,2,4,512]{3,2,0,1:T(4,128)S(1)}, u32[]{:S(2)}, u32[]{:S(2)}) collective-permute-start(f32[9,2,4,512]{3,2,0,1:T(4,128)S(1)} %get-tuple-element.44), channel_id=1, source_target_pairs={{0,1},{1,2},{2,3},{4,5},{5,6},{6,7},{8,9},{9,10},{10,11},{12,13},{... | collective-permute-start | bytes 442376 | tf_op jit(solution)/shard_map/ppermute | solution.py:507
  4.3 1.3 %collective-permute-start.1 = (f32[9,2,4,512]{3,2,0,1:T(4,128)S(1)}, f32[9,2,4,512]{3,2,0,1:T(4,128)S(1)}, u32[]{:S(2)}, u32[]{:S(2)}) collective-permute-start(f32[9,2,4,512]{3,2,0,1:T(4,128)S(1)} %get-tuple-element.45), channel_id=1, source_target_pairs={{1,0},{2,1},{3,2},{5,4},{6,5},{7,6},{9,8},{10,9},{11,10},{13,12},{... | collective-permute-start | bytes 442376 | tf_op jit(solution)/shard_map/ppermute | solution.py:508
  5.7 1.3 %fusion = f32[9,2,36,512]{3,2,0,1:T(8,128)} fusion(f32[1,2,64,512]{3,2,0,1:T(8,128)S(1)} %bitcast.16, f32[8,2,64,512]{3,2,1,0:T(8,128)S(1)} %copy-done.5), kind=kLoop, calls=%fused_computation.8 | loop fusion | flops 331776 | bytes 3686400 | tf_op jit(solution)/shard_map/concatenate | solution.py:506
  7.0 2.7 %collective-permute-done.1 = f32[9,2,4,512]{3,2,0,1:T(4,128)S(1)} collective-permute-done((f32[9,2,4,512]{3,2,0,1:T(4,128)S(1)}, f32[9,2,4,512]{3,2,0,1:T(4,128)S(1)}, u32[]{:S(2)}, u32[]{:S(2)}) %collective-permute-start.1) | collective-permute-done | bytes 147488 | tf_op jit(solution)/shard_map/ppermute | solution.py:508
  9.9 0.4 select_bitcast_fusion
  10.4 1.6 %collective-permute-start.3 = (f32[9,40,512]{2,1,0:T(8,128)S(1)}, f32[9,40,512]{2,1,0:T(8,128)S(1)}, u32[]{:S(2)}, u32[]{:S(2)}) collective-permute-start(f32[9,40,512]{2,1,0:T(8,128)S(1)} %get-tuple-element.42.near0), channel_id=1, source_target_pairs={{0,4},{4,0},{8,12},{12,8},{16,20},{20,16},{24,28},{28,24},{1,5},{5... | collective-permute-start | bytes 2211848 | tf_op jit(solution)/shard_map/ppermute | solution.py:522
  12.0 1.3 %collective-permute-start.8 = (f32[9,40,512]{2,1,0:T(8,128)S(1)}, f32[9,40,512]{2,1,0:T(8,128)S(1)}, u32[]{:S(2)}, u32[]{:S(2)}) collective-permute-start(f32[9,40,512]{2,1,0:T(8,128)S(1)} %get-tuple-element.40.refs_0_.refs_3_), channel_id=1, source_target_pairs={{8,0},{16,8},{24,16},{4,12},{12,20},{20,28},{9,1},{17,9},{25,17},{... | collective-permute-start | bytes 2211848 | tf_op jit(solution)/shard_map/ppermute | solution.py:522
  13.3 1.3 %collective-permute-start.9 = (f32[9,40,512]{2,1,0:T(8,128)S(1)}, f32[9,40,512]{2,1,0:T(8,128)S(1)}, u32[]{:S(2)}, u32[]{:S(2)}) collective-permute-start(f32[9,40,512]{2,1,0:T(8,128)S(1)} %get-tuple-element.43.refs_0_.refs_1_.refs_4_.refs_3_), channel_id=1, source_target_pairs={{8,0},{16,8},{24,16},{4,12},{12,20},{20,28},{9,1},{17,9},{25,17},{... | collective-permute-start | bytes 2211848 | tf_op jit(solution)/shard_map/ppermute | solution.py:522
  14.7 5.0 %collective-permute-start.7 = (f32[5,40,512]{2,1,0:T(8,128)S(1)}, f32[5,40,512]{2,1,0:T(8,128)S(1)}, u32[]{:S(2)}, u32[]{:S(2)}) collective-permute-start(f32[5,40,512]{2,1,0:T(8,128)S(1)} %pad_maximum_fusion.1), channel_id=1, source_target_pairs={{0,4},{4,0},{8,12},{12,8},{16,20},{20,16},{24,28},{28,24},{1,5},{5... | collective-permute-start | bytes 1228808 | tf_op jit(solution)/shard_map/ppermute | solution.py:522
  19.8 7.3 %collective-permute-done.3.refs_1_.refs_0_.refs_2_.refs_5_ = f32[9,40,512]{2,1,0:T(8,128)S(1)} collective-permute-done((f32[9,40,512]{2,1,0:T(8,128)S(1)}, f32[9,40,512]{2,1,0:T(8,128)S(1)}, u32[]{:S(2)}, u32[]{:S(2)}) %collective-permute-start.3) | collective-permute-done | bytes 737312 | tf_op jit(solution)/shard_map/ppermute | solution.py:522
  27.1 3.5 %collective-permute-start.4 = (f32[9,40,512]{2,1,0:T(8,128)S(1)}, f32[9,40,512]{2,1,0:T(8,128)S(1)}, u32[]{:S(2)}, u32[]{:S(2)}) collective-permute-start(f32[9,40,512]{2,1,0:T(8,128)S(1)} %collective-permute-done.3.refs_1_.refs_0_.refs_2_.refs_5_), channel_id=1, source_target_pairs={{0,8},{8,16},{16,24},{12,4},{20,12},{28,20},{1,9},{9,17},{17,25},{... | collective-permute-start | bytes 2211848 | tf_op jit(solution)/shard_map/ppermute | solution.py:522
  30.7 12.2 %collective-permute-done.5.refs_3_.refs_4_.refs_7_ = f32[4,40,512]{2,1,0:T(8,128)S(1)} collective-permute-done((f32[4,40,512]{2,1,0:T(8,128)S(1)}, f32[4,40,512]{2,1,0:T(8,128)S(1)}, u32[]{:S(2)}, u32[]{:S(2)}) %collective-permute-start.5) | collective-permute-done | bytes 327712 | tf_op jit(solution)/shard_map/ppermute | solution.py:522
  42.9 3.5 %collective-permute-start.2 = (f32[8,32,512]{2,1,0:T(8,128)S(1)}, f32[8,32,512]{2,1,0:T(8,128)S(1)}, u32[]{:S(2)}, u32[]{:S(2)}) collective-permute-start(f32[8,32,512]{2,1,0:T(8,128)S(1)} %slice.87), channel_id=1, source_target_pairs={{0,8},{8,16},{16,24},{12,4},{20,12},{28,20},{1,9},{9,17},{17,25},{... | collective-permute-start | bytes 1572872 | tf_op jit(solution)/shard_map/ppermute | solution.py:522
  46.4 3.5 %collective-permute-start.6 = (f32[4,40,512]{2,1,0:T(8,128)S(1)}, f32[4,40,512]{2,1,0:T(8,128)S(1)}, u32[]{:S(2)}, u32[]{:S(2)}) collective-permute-start(f32[4,40,512]{2,1,0:T(8,128)S(1)} %collective-permute-done.5.refs_3_.refs_4_.refs_7_), channel_id=1, source_target_pairs={{0,8},{8,16},{16,24},{12,4},{20,12},{28,20},{1,9},{9,17},{17,25},{... | collective-permute-start | bytes 983048 | tf_op jit(solution)/shard_map/ppermute | solution.py:522
  49.9 3.5 %collective-permute-start.11 = (f32[5,40,512]{2,1,0:T(8,128)S(1)}, f32[5,40,512]{2,1,0:T(8,128)S(1)}, u32[]{:S(2)}, u32[]{:S(2)}) collective-permute-start(f32[5,40,512]{2,1,0:T(8,128)S(1)} %collective-permute-done.7.refs_2_.refs_3_.refs_6_), channel_id=1, source_target_pairs={{0,8},{8,16},{16,24},{12,4},{20,12},{28,20},{1,9},{9,17},{17,25},{... | collective-permute-start | bytes 1228808 | tf_op jit(solution)/shard_map/ppermute | solution.py:522
  53.5 1.3 %collective-permute-start.12 = (f32[4,32,512]{2,1,0:T(8,128)S(1)}, f32[4,32,512]{2,1,0:T(8,128)S(1)}, u32[]{:S(2)}, u32[]{:S(2)}) collective-permute-start(f32[4,32,512]{2,1,0:T(8,128)S(1)} %get-tuple-element.46), channel_id=1, source_target_pairs={{8,0},{16,8},{24,16},{4,12},{12,20},{20,28},{9,1},{17,9},{25,17},{... | collective-permute-start | bytes 786440 | tf_op jit(solution)/shard_map/ppermute | solution.py:522
  54.8 0.4 shard_map.70.refs_1_
  55.1 1.5 %shard_map.69 = (f32[2,4,40,512]{3,2,1,0:T(8,128)S(1)}, f32[2,4,32,512]{3,2,1,0:T(8,128)}) custom-call(f32[9,40,512]{2,1,0:T(8,128)S(1)} %get-tuple-element.43.refs_0_.refs_1_.refs_4_.refs_3_, f32[9,40,512]{2,1,0:T(8,128)S(1)} %collective-permute-done.3.refs_1_.refs_0_.refs_2_.refs_5_, f32[5,40,512]{2,1,0:T(8,128)S(1)} %collective-permute-done.7.refs_2_.refs_3_.refs_6_, ...), custom_call_target="tpu_custom_call" | custom-call | flops 3276800 | bytes 2621440 | tf_op jit(solution)/shard_map/pallas_call | solution.py:267
  56.6 1.5 %shard_map.68 = (f32[2,4,40,512]{3,2,1,0:T(8,128)S(1)}, f32[2,4,32,512]{3,2,1,0:T(8,128)}) custom-call(f32[9,40,512]{2,1,0:T(8,128)S(1)} %get-tuple-element.43.refs_0_.refs_1_.refs_4_.refs_3_, f32[9,40,512]{2,1,0:T(8,128)S(1)} %collective-permute-done.3.refs_1_.refs_0_.refs_2_.refs_5_, f32[5,40,512]{2,1,0:T(8,128)S(1)} %collective-permute-done.7.refs_2_.refs_3_.refs_6_, ...), custom_call_target="tpu_custom_call" | custom-call | flops 3276800 | bytes 2621440 | tf_op jit(solution)/shard_map/pallas_call | solution.py:267
  58.3 3.9 %shard_map.72 = (f32[2,8,40,512]{3,2,1,0:T(8,128)S(1)}, f32[2,8,40,512]{3,2,1,0:T(8,128)S(1)}, f32[8,32,512]{2,1,0:T(8,128)}, f32[8,32,512]{2,1,0:T(8,128)}, f32...) custom-call(f32[9,40,512]{2,1,0:T(8,128)S(1)} %get-tuple-element.40.refs_0_.refs_3_, ...), custom_call_target="tpu_custom_call" | custom-call | flops 32768000 | bytes 2621440 | tf_op jit(solution)/shard_map/pallas_call | solution.py:267
  62.3 1.5 %collective-permute-done.6.refs_2_ = f32[4,40,512]{2,1,0:T(8,128)S(1)} collective-permute-done((f32[4,40,512]{2,1,0:T(8,128)S(1)}, f32[4,40,512]{2,1,0:T(8,128)S(1)}, u32[]{:S(2)}, u32[]{:S(2)}) %collective-permute-start.6) | collective-permute-done | bytes 327712 | tf_op jit(solution)/shard_map/ppermute | solution.py:522
  63.8 2.6 %collective-permute-start.13 = (f32[2,4,32,512]{3,2,1,0:T(8,128)S(1)}, f32[2,4,32,512]{3,2,1,0:T(8,128)S(1)}, u32[]{:S(2)}, u32[]{:S(2)}) collective-permute-start(f32[2,4,32,512]{3,2,1,0:T(8,128)S(1)} %copy-done.10), channel_id=1, source_target_pairs={{0,4},{4,0},{8,12},{12,8},{16,20},{20,16},{24,28},{28,24},{1,5},{5... | collective-permute-start | bytes 1572872 | tf_op jit(solution)/shard_map/ppermute | solution.py:522
  66.4 6.2 %collective-permute-done.11.refs_2_.refs_15_ = f32[5,40,512]{2,1,0:T(8,128)S(1)} collective-permute-done((f32[5,40,512]{2,1,0:T(8,128)S(1)}, f32[5,40,512]{2,1,0:T(8,128)S(1)}, u32[]{:S(2)}, u32[]{:S(2)}) %collective-permute-start.11) | collective-permute-done | bytes 409632 | tf_op jit(solution)/shard_map/ppermute | solution.py:522
  72.6 2.6 %collective-permute-start.15 = (f32[8,32,512]{2,1,0:T(8,128)}, f32[8,32,512]{2,1,0:T(8,128)S(1)}, u32[]{:S(2)}, u32[]{:S(2)}) collective-permute-start(f32[8,32,512]{2,1,0:T(8,128)} %get-tuple-element.36), channel_id=1, source_target_pairs={{0,4},{4,0},{8,12},{12,8},{16,20},{20,16},{24,28},{28,24},{1,5},{5... | collective-permute-start | bytes 1572872 | tf_op jit(solution)/shard_map/ppermute | solution.py:522
  75.2 1.3 %collective-permute-start.10 = (f32[4,32,512]{2,1,0:T(8,128)S(1)}, f32[4,32,512]{2,1,0:T(8,128)S(1)}, u32[]{:S(2)}, u32[]{:S(2)}) collective-permute-start(f32[4,32,512]{2,1,0:T(8,128)S(1)} %get-tuple-element.47), channel_id=1, source_target_pairs={{8,0},{16,8},{24,16},{4,12},{12,20},{20,28},{9,1},{17,9},{25,17},{... | collective-permute-start | bytes 786440 | tf_op jit(solution)/shard_map/ppermute | solution.py:522
  76.5 2.6 %shard_map.73 = (f32[4,40,512]{2,1,0:T(8,128)S(1)}, f32[2,4,40,512]{3,2,1,0:T(8,128)S(1)}, f32[4,4,32,512]{3,2,1,0:T(8,128)S(1)}) custom-call(f32[8,32,512]{2,1,0:T(8,128)S(1)} %collective-permute-done.2.refs_0_, f32[9,40,512]{2,1,0:T(8,128)S(1)} %collective-permute-done.4.refs_1_, f32[5,40,512]{2,1,0:T(8,128)S(1)} %collective-permute-done.11.refs_2_.refs_15_, ...), custom_call_target="tpu_custom_call" | custom-call | flops 16384000 | bytes 2621440 | tf_op jit(solution)/shard_map/pallas_call | solution.py:267
  79.1 6.6 %collective-permute-done.10.refs_10_ = f32[4,32,512]{2,1,0:T(8,128)S(1)} collective-permute-done((f32[4,32,512]{2,1,0:T(8,128)S(1)}, f32[4,32,512]{2,1,0:T(8,128)S(1)}, u32[]{:S(2)}, u32[]{:S(2)}) %collective-permute-start.10) | collective-permute-done | bytes 262176 | tf_op jit(solution)/shard_map/ppermute | solution.py:522
  85.7 5.5 %shard_map.74 = (f32[8,32,512]{2,1,0:T(8,128)}, f32[2,8,32,512]{3,2,1,0:T(8,128)}, f32[32,1,252]{2,1,0:T(1,128)S(1)}) custom-call(f32[8,32,512]{2,1,0:T(8,128)S(1)} %collective-permute-done.2.refs_0_, f32[9,40,512]{2,1,0:T(8,128)S(1)} %collective-permute-done.4.refs_1_, f32[4,40,512]{2,1,0:T(8,128)S(1)} %collective-permute-done.6.refs_2_, ...), custom_call_target="tpu_custom_call" | custom-call | flops 32768000 | bytes 2621440 | tf_op jit(solution)/shard_map/pallas_call | solution.py:267
  91.2 19.9 %all_to_all.5.parts = f32[32,1,252]{2,1,0:T(1,128)S(1)} all-to-all(f32[32,1,252]{2,1,0:T(1,128)S(1)} %get-tuple-element.29), channel_id=1, replica_groups=mesh['gz'=8,'gy'=4] {'gz','gy'}, dimensions={0} | all-to-all | bytes 64512 | tf_op jit(solution)/shard_map/all_to_all | solution.py:549
  111.1 6.9 %finish.1 = (f32[24,32]{1,0:T(8,128)}, f32[8,24,128]{2,1,0:T(8,128)S(1)}, f32[8,2,64,512]{3,2,1,0:T(8,128)}) custom-call(f32[32,1,252]{2,1,0:T(1,128)S(1)} %all_to_all.5.parts, f32[2,8,252]{2,1,0:T(8,128)S(1)} %copy-done.3, bf16[2,252,128]{2,1,0:T(8,128)(2,1)S(1)} %copy-done.2, f32[24,32]{1,0:T(8,128)S(1)} %copy-done.4, f32[9,40,512]{2,1,0:T(8,128)} %copy-done.1, ...), custom_call_target="tpu_custom_call" | custom-call | flops 39321600 | bytes 8388608 | tf_op jit(solution)/shard_map/finish/pallas_call | solution.py:459
  118.1 3.8 %others.1 = f32[8,2,64,512]{3,2,1,0:T(8,128)} custom-call(f32[8,24,128]{2,1,0:T(8,128)S(1)} %get-tuple-element.33.splat, f32[9,40,512]{2,1,0:T(8,128)} %copy-done.9, f32[9,40,512]{2,1,0:T(8,128)} %bitcast.14, f32[2,4,32,512]{3,2,1,0:T(8,128)S(1)} %collective-permute-done.13.one_first, ...), custom_call_target="tpu_custom_call", output_to_operand_aliasing={{}: (7, {})} | custom-call | tf_op jit(solution)/shard_map/others/pallas_call | solution.py:484
  (46 shorter events, 0.9 us)
Async XLA Ops:
  0.6 5.0 %copy-start.5 = (f32[8,2,64,512]{3,2,1,0:T(8,128)S(1)}, f32[8,2,64,512]{3,2,1,0:T(8,128)}, u32[]{:S(2)}) copy-start(f32[8,2,64,512]{3,2,1,0:T(8,128)} %param.5) | copy-start | bytes 6291460
  0.6 5.0 %copy-start.8 = (f32[2,64,512]{2,1,0:T(8,128)S(1)}, f32[2,64,512]{2,1,0:T(8,128)}, u32[]{:S(2)}) copy-start(f32[2,64,512]{2,1,0:T(8,128)} %param.6) | copy-start | bytes 786436
  1.9 8.0 %collective-permute-start = (f32[9,2,4,512]{3,2,0,1:T(4,128)S(1)}, f32[9,2,4,512]{3,2,0,1:T(4,128)S(1)}, u32[]{:S(2)}, u32[]{:S(2)}) collective-permute-start(f32[9,2,4,512]{3,2,0,1:T(4,128)S(1)} %get-tuple-element.44), channel_id=1, source_target_pairs={{0,1},{1,2},{2,3},{4,5},{5,6},{6,7},{8,9},{9,10},{10,11},{12,13},{... | collective-permute-start | bytes 442376 | tf_op jit(solution)/shard_map/ppermute | solution.py:507
  4.3 5.4 %collective-permute-start.1 = (f32[9,2,4,512]{3,2,0,1:T(4,128)S(1)}, f32[9,2,4,512]{3,2,0,1:T(4,128)S(1)}, u32[]{:S(2)}, u32[]{:S(2)}) collective-permute-start(f32[9,2,4,512]{3,2,0,1:T(4,128)S(1)} %get-tuple-element.45), channel_id=1, source_target_pairs={{1,0},{2,1},{3,2},{5,4},{6,5},{7,6},{9,8},{10,9},{11,10},{13,12},{... | collective-permute-start | bytes 442376 | tf_op jit(solution)/shard_map/ppermute | solution.py:508
  7.0 2.9 %copy-start.7 = (f32[9,2,36,512]{3,2,0,1:T(8,128)S(1)}, f32[9,2,36,512]{3,2,0,1:T(8,128)}, u32[]{:S(2)}) copy-start(f32[9,2,36,512]{3,2,0,1:T(8,128)} %fusion) | copy-start | bytes 3981316
  10.4 20.3 %copy-start.6 = (f32[9,1,40,512]{3,2,0,1:T(8,128)}, f32[9,1,40,512]{3,2,0,1:T(8,128)S(1)}, u32[]{:S(2)}) copy-start(f32[9,1,40,512]{3,2,0,1:T(8,128)S(1)} %get-tuple-element.41) | copy-start | bytes 2211844
  10.4 20.3 %copy-start.9 = (f32[9,40,512]{2,1,0:T(8,128)}, f32[9,40,512]{2,1,0:T(8,128)S(1)}, u32[]{:S(2)}) copy-start(f32[9,40,512]{2,1,0:T(8,128)S(1)} %get-tuple-element.42.near0) | copy-start | bytes 2211844
  10.4 75.3 %copy-start = (f32[9,40,512]{2,1,0:T(8,128)}, f32[9,40,512]{2,1,0:T(8,128)S(1)}, u32[]{:S(2)}) copy-start(f32[9,40,512]{2,1,0:T(8,128)S(1)} %get-tuple-element.43.refs_0_.refs_1_.refs_4_.refs_3_) | copy-start | bytes 2211844
  10.4 75.3 %copy-start.1 = (f32[9,40,512]{2,1,0:T(8,128)}, f32[9,40,512]{2,1,0:T(8,128)S(1)}, u32[]{:S(2)}) copy-start(f32[9,40,512]{2,1,0:T(8,128)S(1)} %get-tuple-element.40.refs_0_.refs_3_) | copy-start | bytes 2211844
  10.4 16.7 %collective-permute-start.3 = (f32[9,40,512]{2,1,0:T(8,128)S(1)}, f32[9,40,512]{2,1,0:T(8,128)S(1)}, u32[]{:S(2)}, u32[]{:S(2)}) collective-permute-start(f32[9,40,512]{2,1,0:T(8,128)S(1)} %get-tuple-element.42.near0), channel_id=1, source_target_pairs={{0,4},{4,0},{8,12},{12,8},{16,20},{20,16},{24,28},{28,24},{1,5},{5... | collective-permute-start | bytes 2211848 | tf_op jit(solution)/shard_map/ppermute | solution.py:522
  12.0 37.9 %collective-permute-start.8 = (f32[9,40,512]{2,1,0:T(8,128)S(1)}, f32[9,40,512]{2,1,0:T(8,128)S(1)}, u32[]{:S(2)}, u32[]{:S(2)}) collective-permute-start(f32[9,40,512]{2,1,0:T(8,128)S(1)} %get-tuple-element.40.refs_0_.refs_3_), channel_id=1, source_target_pairs={{8,0},{16,8},{24,16},{4,12},{12,20},{20,28},{9,1},{17,9},{25,17},{... | collective-permute-start | bytes 2211848 | tf_op jit(solution)/shard_map/ppermute | solution.py:522
  13.3 40.1 %collective-permute-start.9 = (f32[9,40,512]{2,1,0:T(8,128)S(1)}, f32[9,40,512]{2,1,0:T(8,128)S(1)}, u32[]{:S(2)}, u32[]{:S(2)}) collective-permute-start(f32[9,40,512]{2,1,0:T(8,128)S(1)} %get-tuple-element.43.refs_0_.refs_1_.refs_4_.refs_3_), channel_id=1, source_target_pairs={{8,0},{16,8},{24,16},{4,12},{12,20},{20,28},{9,1},{17,9},{25,17},{... | collective-permute-start | bytes 2211848 | tf_op jit(solution)/shard_map/ppermute | solution.py:522
  14.7 31.7 %collective-permute-start.7 = (f32[5,40,512]{2,1,0:T(8,128)S(1)}, f32[5,40,512]{2,1,0:T(8,128)S(1)}, u32[]{:S(2)}, u32[]{:S(2)}) collective-permute-start(f32[5,40,512]{2,1,0:T(8,128)S(1)} %pad_maximum_fusion.1), channel_id=1, source_target_pairs={{0,4},{4,0},{8,12},{12,8},{16,20},{20,16},{24,28},{28,24},{1,5},{5... | collective-permute-start | bytes 1228808 | tf_op jit(solution)/shard_map/ppermute | solution.py:522
  19.7 23.2 %collective-permute-start.5 = (f32[4,40,512]{2,1,0:T(8,128)S(1)}, f32[4,40,512]{2,1,0:T(8,128)S(1)}, u32[]{:S(2)}, u32[]{:S(2)}) collective-permute-start(f32[4,40,512]{2,1,0:T(8,128)S(1)} %get-tuple-element.49), channel_id=1, source_target_pairs={{0,4},{4,0},{8,12},{12,8},{16,20},{20,16},{24,28},{28,24},{1,5},{5... | collective-permute-start | bytes 983048 | tf_op jit(solution)/shard_map/ppermute | solution.py:522
  27.1 48.1 %collective-permute-start.4 = (f32[9,40,512]{2,1,0:T(8,128)S(1)}, f32[9,40,512]{2,1,0:T(8,128)S(1)}, u32[]{:S(2)}, u32[]{:S(2)}) collective-permute-start(f32[9,40,512]{2,1,0:T(8,128)S(1)} %collective-permute-done.3.refs_1_.refs_0_.refs_2_.refs_5_), channel_id=1, source_target_pairs={{0,8},{8,16},{16,24},{12,4},{20,12},{28,20},{1,9},{9,17},{17,25},{... | collective-permute-start | bytes 2211848 | tf_op jit(solution)/shard_map/ppermute | solution.py:522
  42.9 19.3 %collective-permute-start.2 = (f32[8,32,512]{2,1,0:T(8,128)S(1)}, f32[8,32,512]{2,1,0:T(8,128)S(1)}, u32[]{:S(2)}, u32[]{:S(2)}) collective-permute-start(f32[8,32,512]{2,1,0:T(8,128)S(1)} %slice.87), channel_id=1, source_target_pairs={{0,8},{8,16},{16,24},{12,4},{20,12},{28,20},{1,9},{9,17},{17,25},{... | collective-permute-start | bytes 1572872 | tf_op jit(solution)/shard_map/ppermute | solution.py:522
  46.4 17.4 %collective-permute-start.6 = (f32[4,40,512]{2,1,0:T(8,128)S(1)}, f32[4,40,512]{2,1,0:T(8,128)S(1)}, u32[]{:S(2)}, u32[]{:S(2)}) collective-permute-start(f32[4,40,512]{2,1,0:T(8,128)S(1)} %collective-permute-done.5.refs_3_.refs_4_.refs_7_), channel_id=1, source_target_pairs={{0,8},{8,16},{16,24},{12,4},{20,12},{28,20},{1,9},{9,17},{17,25},{... | collective-permute-start | bytes 983048 | tf_op jit(solution)/shard_map/ppermute | solution.py:522
  49.9 22.7 %collective-permute-start.11 = (f32[5,40,512]{2,1,0:T(8,128)S(1)}, f32[5,40,512]{2,1,0:T(8,128)S(1)}, u32[]{:S(2)}, u32[]{:S(2)}) collective-permute-start(f32[5,40,512]{2,1,0:T(8,128)S(1)} %collective-permute-done.7.refs_2_.refs_3_.refs_6_), channel_id=1, source_target_pairs={{0,8},{8,16},{16,24},{12,4},{20,12},{28,20},{1,9},{9,17},{17,25},{... | collective-permute-start | bytes 1228808 | tf_op jit(solution)/shard_map/ppermute | solution.py:522
  53.5 21.7 %collective-permute-start.12 = (f32[4,32,512]{2,1,0:T(8,128)S(1)}, f32[4,32,512]{2,1,0:T(8,128)S(1)}, u32[]{:S(2)}, u32[]{:S(2)}) collective-permute-start(f32[4,32,512]{2,1,0:T(8,128)S(1)} %get-tuple-element.46), channel_id=1, source_target_pairs={{8,0},{16,8},{24,16},{4,12},{12,20},{20,28},{9,1},{17,9},{25,17},{... | collective-permute-start | bytes 786440 | tf_op jit(solution)/shard_map/ppermute | solution.py:522
  58.3 3.9 %copy-start.11 = (f32[2,4,32,512]{3,2,1,0:T(8,128)S(1)}, f32[2,4,32,512]{3,2,1,0:T(8,128)}, u32[]{:S(2)}) copy-start(f32[2,4,32,512]{3,2,1,0:T(8,128)} %get-tuple-element.35) | copy-start | bytes 1572868
  58.3 5.5 %copy-start.10 = (f32[2,4,32,512]{3,2,1,0:T(8,128)S(1)}, f32[2,4,32,512]{3,2,1,0:T(8,128)}, u32[]{:S(2)}) copy-start(f32[2,4,32,512]{3,2,1,0:T(8,128)} %get-tuple-element.34) | copy-start | bytes 1572868
  62.2 55.8 %collective-permute-start.14 = (f32[2,4,32,512]{3,2,1,0:T(8,128)S(1)}, f32[2,4,32,512]{3,2,1,0:T(8,128)S(1)}, u32[]{:S(2)}, u32[]{:S(2)}) collective-permute-start(f32[2,4,32,512]{3,2,1,0:T(8,128)S(1)} %copy-done.11), channel_id=1, source_target_pairs={{0,4},{4,0},{8,12},{12,8},{16,20},{20,16},{24,28},{28,24},{1,5},{5... | collective-permute-start | bytes 1572872 | tf_op jit(solution)/shard_map/ppermute | solution.py:522
  63.8 54.2 %collective-permute-start.13 = (f32[2,4,32,512]{3,2,1,0:T(8,128)S(1)}, f32[2,4,32,512]{3,2,1,0:T(8,128)S(1)}, u32[]{:S(2)}, u32[]{:S(2)}) collective-permute-start(f32[2,4,32,512]{3,2,1,0:T(8,128)S(1)} %copy-done.10), channel_id=1, source_target_pairs={{0,4},{4,0},{8,12},{12,8},{16,20},{20,16},{24,28},{28,24},{1,5},{5... | collective-permute-start | bytes 1572872 | tf_op jit(solution)/shard_map/ppermute | solution.py:522
  72.6 45.4 %collective-permute-start.15 = (f32[8,32,512]{2,1,0:T(8,128)}, f32[8,32,512]{2,1,0:T(8,128)S(1)}, u32[]{:S(2)}, u32[]{:S(2)}) collective-permute-start(f32[8,32,512]{2,1,0:T(8,128)} %get-tuple-element.36), channel_id=1, source_target_pairs={{0,4},{4,0},{8,12},{12,8},{16,20},{20,16},{24,28},{28,24},{1,5},{5... | collective-permute-start | bytes 1572872 | tf_op jit(solution)/shard_map/ppermute | solution.py:522
  75.2 42.9 %collective-permute-start.16 = (f32[8,32,512]{2,1,0:T(8,128)}, f32[8,32,512]{2,1,0:T(8,128)S(1)}, u32[]{:S(2)}, u32[]{:S(2)}) collective-permute-start(f32[8,32,512]{2,1,0:T(8,128)} %get-tuple-element.37), channel_id=1, source_target_pairs={{0,4},{4,0},{8,12},{12,8},{16,20},{20,16},{24,28},{28,24},{1,5},{5... | collective-permute-start | bytes 1572872 | tf_op jit(solution)/shard_map/ppermute | solution.py:522
  75.2 10.4 %collective-permute-start.10 = (f32[4,32,512]{2,1,0:T(8,128)S(1)}, f32[4,32,512]{2,1,0:T(8,128)S(1)}, u32[]{:S(2)}, u32[]{:S(2)}) collective-permute-start(f32[4,32,512]{2,1,0:T(8,128)S(1)} %get-tuple-element.47), channel_id=1, source_target_pairs={{8,0},{16,8},{24,16},{4,12},{12,20},{20,28},{9,1},{17,9},{25,17},{... | collective-permute-start | bytes 786440 | tf_op jit(solution)/shard_map/ppermute | solution.py:522
  85.7 25.5 %copy-start.2 = (bf16[2,252,128]{2,1,0:T(8,128)(2,1)S(1)}, bf16[2,252,128]{2,1,0:T(8,128)(2,1)}, u32[]{:S(2)}) copy-start(bf16[2,252,128]{2,1,0:T(8,128)(2,1)} %constant.27.clone.cols) | copy-start | bytes 387076
  85.7 25.5 %copy-start.3 = (f32[2,8,252]{2,1,0:T(8,128)S(1)}, f32[2,8,252]{2,1,0:T(8,128)}, u32[]{:S(2)}) copy-start(f32[2,8,252]{2,1,0:T(8,128)} %constant.26.clone.rows) | copy-start | bytes 48388
  85.7 25.5 %copy-start.4 = (f32[24,32]{1,0:T(8,128)S(1)}, f32[24,32]{1,0:T(8,128)}, u32[]{:S(2)}) copy-start(f32[24,32]{1,0:T(8,128)} %constant.28.clone.shift) | copy-start | bytes 9220

commit v7 on v6

--- a/solution.py
+++ b/solution.py
@@ -57,11 +57,12 @@
     return view[0][BLK // 2] if isinstance(view, tuple) else view[BLK]
 
 
-def set_scales(scale_ref, diag_ref, fields, slots, half, width):
-    scale_ref[...] = row_masks(half, width) * (1.0 / SPREAD)
+def set_scales(scale_ref, diag_ref, fields, slots, half, width, affine):
+    center, inverse = (CENTER, 1.0 / SPREAD) if affine is None else (affine[0, 0], affine[0, 1])
+    scale_ref[...] = row_masks(half, width) * inverse
     low, high = side_flags()
     for slot, layer in enumerate(slots):
-        value = scale_ref[...] * (diag_of(fields[layer]) + (6.0 - CENTER))
+        value = scale_ref[...] * (diag_of(fields[layer]) + (6.0 - center))
         if layer < 4:
             value = value * low
         if layer > 7:
@@ -120,10 +121,10 @@
 LATE = {1: (4,), 2: (4,), 3: (4, 5), 4: (4, 5), 5: (4, 5, 6, 7), 6: (4, 5, 6, 7)}
 
 
-def first_kernel(*refs, part, blocks, half, width):
+def first_kernel(*refs, affine, part, blocks, half, width):
     near, mid, far_one, far_two, out_one, x1, sent, scale_ref, diag_ref, sem = refs
     fields = {5: near, 6: mid, 7: (far_one, far_two), 8: out_one}
-    set_scales(scale_ref, diag_ref, fields, (6, 7), half, width)
+    set_scales(scale_ref, diag_ref, fields, (6, 7), half, width, affine)
 
     def vector(i):
         for slot, n in enumerate((6, 7)):
@@ -136,17 +137,17 @@
     copy.wait()
 
 
-def zero_kernel(*refs, layers, add, blocks, half, width):
+def zero_kernel(*refs, affine, layers, add, blocks, half, width):
     fields = dict(zip(layers, refs))
     gram_part(refs[-1], (fields,), 0, layers, blocks, half, width, refs[len(layers)] if add else None)
 
 
-def early_kernel(*refs, blocks, half, width):
+def early_kernel(*refs, affine, blocks, half, width):
     (keep_far, keep_near, got_near, far_one, far_two, out_one, out_two, mid_one, mid_two, start,
      x1, x2, near_sent, far_sent, acc, x1_out, scale_ref, diag_ref, sems) = refs
     fields = {4: keep_far, 5: keep_near, 6: got_near, 7: (far_one, far_two), 8: out_one, 9: out_two}
     slots = (5, 6, 7, 8)
-    set_scales(scale_ref, diag_ref, fields, slots, half, width)
+    set_scales(scale_ref, diag_ref, fields, slots, half, width, affine)
     flag = side_flags()[1]
     one = {5: x1.at[0], 6: (mid_one.at[0], mid_two.at[0]), 7: (mid_one.at[1], mid_two.at[1]), 8: x1.at[1]}
 
@@ -174,7 +175,7 @@
         copy.wait()
 
 
-def late_kernel(*refs, part, blocks, half, width):
+def late_kernel(*refs, affine, part, blocks, half, width):
     (in_one, in_two, in_three, keep_far, keep_near, got_near, far_one, far_two, out_one, out_two, out_three,
      mid_one, mid_two, near1, near2) = refs[:15]
     rest = refs[15:]
@@ -189,7 +190,7 @@
     fields = {1: in_one, 2: in_two, 3: third, 4: keep_far, 5: keep_near, 6: got_near, 7: (far_one, far_two),
               8: out_one, 9: out_two, 10: (out_three, out_three)}
     slots = tuple(range(2, 10))
-    set_scales(scale_ref, diag_ref, fields, slots, half, width)
+    set_scales(scale_ref, diag_ref, fields, slots, half, width, affine)
     low, high = side_flags()
     mine = {2: far1.at[0], 3: far1.at[1], 4: x1, 9: far1.at[2]}
     one = {5: near1.at[0], 8: near1.at[1], 6: (mid_one.at[0], mid_two.at[0]), 7: (mid_one.at[1], mid_two.at[1]),
@@ -243,7 +244,11 @@
         copy.wait()
 
 
-def kernels(blocks, half, width, peers):
+def with_affine(kernel, *refs, **static):
+    kernel(*refs[1:], affine=refs[0], **static)
+
+
+def kernels(blocks, half, width, peers, affine):
     rows = half + 2 * EDGE
     moments = 2 * ITERS + 1
     count = blocks * (blocks + 1) // 2
@@ -264,15 +269,19 @@
         return [pltpu.VMEM((rows, width), jnp.float32), pltpu.VMEM((number, rows, width), jnp.float32)]
 
     def call(kernel, arrays, outs, scratch, mib, ops, **static):
+        if affine is None:
+            run, lead = functools.partial(kernel, affine=None, **sizes, **static), ()
+        else:
+            run, lead = functools.partial(with_affine, kernel, **sizes, **static), (affine,)
         return pl.pallas_call(
-            functools.partial(kernel, **sizes, **static),
+            run,
             out_shape=outs,
-            in_specs=[vmem] * len(arrays),
+            in_specs=[pl.BlockSpec(memory_space=pltpu.SMEM)] * len(lead) + [vmem] * len(arrays),
             out_specs=tuple(vmem if isinstance(o, jax.ShapeDtypeStruct) else hbm for o in outs),
             scratch_shapes=scratch,
             compiler_params=pltpu.CompilerParams(vmem_limit_bytes=mib << 20),
             cost_estimate=pl.CostEstimate(flops=ops * cells, bytes_accessed=16 * cells, transcendentals=0),
-        )(*arrays)
+        )(*lead, *arrays)
 
     def zero(arrays, layers, add):
         return call(zero_kernel, arrays, (out(count, 8, 128),), [], 4, 20, layers=layers, add=add)[0]
@@ -309,11 +318,13 @@
     table = [[unit[0], unit[1], g02, g03], [unit[1], unit[2], unit[3], g13],
              [g02, unit[3], unit[4], unit[5]], [g03, g13, unit[5], unit[6]]]
     pairs_of = [(m, v, w) for m in range(size) for v in range(blocks) for w in range(v, blocks)]
-    rows = np.zeros((2, blocks, len(pairs_of)), np.float32)
+    rows = np.zeros((3, blocks, len(pairs_of)), np.float32)
     cols = np.zeros((2, len(pairs_of), ITERS + 1, ITERS + 1, blocks), np.float32)
     for n, (m, v, w) in enumerate(pairs_of):
         rows[0, v, n] = 1.0
         rows[1, w, n] = float(v != w)
+        if v == w and m < 3:
+            rows[2, m, n] = 1.0
         for i in range(ITERS + 1):
             for j in range(ITERS + 1):
                 cols[0, n, i, j, w] = table[i][j][m]
@@ -321,14 +332,14 @@
     return rows, cols.reshape(2, len(pairs_of), -1)
 
 
-def shift_table(blocks):
-    table = np.zeros((ITERS, ITERS + 1))
+def shift_tables(blocks):
+    table = np.zeros((2, ITERS, ITERS + 1))
     for k in range(ITERS):
-        table[k, k + 1] = SPREAD
-        table[k, k] = CENTER
+        table[0, k, k + 1] = 1.0
+        table[1, k, k] = 1.0
         if k:
-            table[k, k - 1] = SPREAD * BETA[k]
-    return np.kron(table, np.eye(blocks)).astype(np.float32)
+            table[0, k, k - 1] = BETA[k]
+    return np.stack([np.kron(t, np.eye(blocks)) for t in table]).astype(np.float32)
 
 
 def contract(left, right, at_left, at_right):
@@ -338,6 +349,11 @@
 
 def solve_small(parts, rows, cols, shift, blocks):
     nu = jnp.sum(parts, axis=0)
+    traces = jnp.sum(rows[2] * nu, axis=1, keepdims=True)
+    mean = traces[1:2] / traces[:1]
+    spread = jnp.sqrt(jnp.maximum(traces[2:3] / traces[:1] - mean * mean, 1e-6))
+    again = jnp.logical_or(spread < 0.35, jnp.abs(mean) > 3.0 * spread)
+    fit = (jnp.max(jnp.where(again, 1, 0)), jnp.max(mean), jnp.max(spread))
     wide = sum(contract(rows[n] * nu, cols[n].astype(jnp.float32), 1, 0) for n in range(2))
     total, size = (ITERS + 1) * blocks, ITERS * blocks
     gram = jnp.concatenate([wide[:, total * i:total * i + total] for i in range(ITERS + 1)], axis=0)
@@ -362,7 +378,7 @@
     hessenberg = contract(inverse, contract(shift, upper, 1, 1), 1, 0)
     row = lax.broadcasted_iota(jnp.int32, hessenberg.shape, 0) // blocks
     col = lax.broadcasted_iota(jnp.int32, hessenberg.shape, 1) // blocks
-    return jnp.where(col <= row + 1, hessenberg, 0.0), solving[:, size:]
+    return jnp.where(col <= row + 1, hessenberg, 0.0), solving[:, size:], fit
 
 
 def blend(buffer, terms, splat, blocks, half, width):
@@ -397,7 +413,7 @@
 
 
 def finish_kernel(parts, rows, cols, shift, *refs, blocks, half, width):
-    arrays, (hess_out, splat, out, source, buffer, sems, out_sems) = refs[:5], refs[5:]
+    arrays, (hess_out, splat, out, again_out, affine_out, source, buffer, sems, out_sems) = refs[:5], refs[5:]
     copies = []
     for n, terms in enumerate(TERMS):
         for k, (ref, at) in enumerate(terms):
@@ -406,7 +422,10 @@
                 ref.at[pl.ds(0, blocks), pl.ds(0, half)], source.at[n, k], sems.at[n, k])
             copy.start()
             copies.append(copy)
-    hessenberg, weights = solve_small(parts[...], rows, cols, shift[...], blocks)
+    hessenberg, weights, (again, mean, spread) = solve_small(parts[...], rows, cols, shift[...], blocks)
+    again_out[0, 0] = again
+    affine_out[0, 0] = mean
+    affine_out[0, 1] = spread
     hess_out[...] = hessenberg
     for w in range(blocks):
         splat[w] = jnp.broadcast_to(weights[:, w:w + 1], (ITERS * blocks, 128))
@@ -450,10 +469,16 @@
     return pltpu.with_memory_space_constraint(array, pltpu.HBM)
 
 
-def finish(parts, arrays, blocks, half, width):
+def finish(parts, arrays, blocks, half, width, affine):
     vmem = pl.BlockSpec(memory_space=pltpu.VMEM)
     hbm = pl.BlockSpec(memory_space=pltpu.HBM)
+    smem = pl.BlockSpec(memory_space=pltpu.SMEM)
     rows, cols = moment_tables(blocks)
+    tables = shift_tables(blocks)
+    if affine is None:
+        shift = (SPREAD * tables[0] + CENTER * tables[1]).astype(np.float32)
+    else:
+        shift = tables[0] / affine[0, 1] + tables[1] * affine[0, 0]
     size = ITERS * blocks
     piece = (blocks, half, width)
     return pl.pallas_call(
@@ -462,9 +487,11 @@
             jax.ShapeDtypeStruct((size, size + blocks), jnp.float32),
             jax.ShapeDtypeStruct((blocks, size, 128), jnp.float32),
             jax.ShapeDtypeStruct((blocks, 2, 2 * half, width), jnp.float32),
+            jax.ShapeDtypeStruct((1, 1), jnp.int32),
+            jax.ShapeDtypeStruct((1, 2), jnp.float32),
         ),
         in_specs=[vmem] * 4 + [hbm] * len(arrays),
-        out_specs=(vmem, vmem, hbm),
+        out_specs=(vmem, vmem, hbm, smem, smem),
         scratch_shapes=[
             pltpu.VMEM((len(TERMS), ITERS, *piece), jnp.float32),
             pltpu.VMEM((len(TERMS), *piece), jnp.float32),
@@ -474,7 +501,7 @@
         compiler_params=pltpu.CompilerParams(vmem_limit_bytes=16 << 20),
         cost_estimate=pl.CostEstimate(flops=300 * blocks * half * width, bytes_accessed=1 << 23, transcendentals=0),
         name="finish",
-    )(parts, rows, cols.astype(jnp.bfloat16), shift_table(blocks), *[in_hbm(array) for array in arrays])
+    )(parts, rows, cols.astype(jnp.bfloat16), shift, *[in_hbm(array) for array in arrays])
 
 
 def others(splat, near0, far0, one_first, one_second, near2, far2, result, half, width):
@@ -498,7 +525,7 @@
     )(splat, in_hbm(near0), in_hbm(far0), one_first, one_second, near2, far2, result)
 
 
-def body(right_side, diagonal):
+def attempt(right_side, diagonal, affine=None):
     blocks, _, ny, width = right_side.shape
     half = ny // 2
     peers_z, peers_y = lax.axis_size("gz"), lax.axis_size("gy")
@@ -516,7 +543,7 @@
     send_far = jnp.where(even, second[:, 0], first[:, 1])
     keep_near = jnp.where(even, first[:, 1], second[:, 0])
     keep_far = jnp.where(even, first[:, 0], second[:, 1])
-    zero, first_step, early, late = kernels(blocks, half, width, peers_z * peers_y)
+    zero, first_step, early, late = kernels(blocks, half, width, peers_z * peers_y, affine)
 
     def move(array, links):
         return lax.ppermute(array, "gz", links)
@@ -548,10 +575,23 @@
                            out_b, mid_a, mid_b, near1, near2, in_a, *first_half, start), 1)
     parts = lax.all_to_all(nu, ("gz", "gy"), 0, 0)
     far_back2 = move(far_sent, swap)
-    hessenberg, splat, result = finish(
-        parts, (keep_far, x1_far, x2, keep_near, x1_near), blocks, half, width)
+    hessenberg, splat, result, again, fit = finish(
+        parts, (keep_far, x1_far, x2, keep_near, x1_near), blocks, half, width, affine)
     result = others(splat, send_near, send_far, back_a, back_b, near_back2, far_back2, result, half, width)
-    return result, hessenberg
+    return result, hessenberg, again, fit
+
+
+def body(right_side, diagonal):
+    result, hessenberg, again, fit = attempt(right_side, diagonal)
+
+    def repeat(right_side, diagonal, fit, result, hessenberg):
+        affine = jnp.stack([CENTER + SPREAD * fit[0, 0], 1.0 / (SPREAD * fit[0, 1])]).reshape(1, 2)
+        return attempt(right_side, diagonal, affine)[:2]
+
+    def accept(right_side, diagonal, fit, result, hessenberg):
+        return result, hessenberg
+
+    return lax.cond(again[0, 0] != 0, repeat, accept, right_side, diagonal, fit, result, hessenberg)
 
 
 def solution(mesh):

time: 122 us -> 126 us (1.033)
  blocking collectives: 19.9 us -> 0 us
  waiting for transfers between devices: 36.5 us -> 48.2 us
  starting transfers between devices: 34.8 us -> 42.6 us
  Pallas kernels: 26.1 us -> 28.1 us
    all_to_all x1 -> x0, blocking collectives: 19.9 us -> none  [body(): parts = lax.all_to_all(nu, ('gz', 'gy'), 0, 0)]
    all_to_all x0 -> x1, waiting for transfers between devices: none -> 13.7 us  [attempt(): parts = lax.all_to_all(nu, ('gz', 'gy'), 0, 0)]
    all_to_all x0 -> x1, starting transfers between devices: none -> 4.07 us  [attempt(): parts = lax.all_to_all(nu, ('gz', 'gy'), 0, 0)]
    ppermute x15, starting transfers between devices: 31.1 us -> 34.2 us  [move(): return lax.ppermute(array, 'gz', links)]
    ppermute x2, waiting for transfers between devices: 2.66 us -> 0.01 us  [the longest x1 0.01 us: attempt(): under = lax.ppermute(field[:, :, :EDGE], 'gy', pairs(peers_y, -1))]
    pallas_call x7, Pallas kernels: 15.4 us -> 16.8 us  [call(): pl.pallas_call(run, out_shape=outs, in_specs=[pl.BlockSpec(memory_space=p...]
  transfers between devices with their start and end apart: 17 -> 18, of which waited for: 6 -> 6; matrix products, arithmetic and copies ran while one was open for 1% -> 1% of each run, Pallas kernels for 18% -> 19%
where the time goes in v7:
time: 126 us
  waiting for transfers between devices  48.2 us (38%)
  starting transfers between devices  42.6 us (34%)
  Pallas kernels  28.1 us (22%)
  other arithmetic  3.25 us (3%)
  between operations  1.86 us (1%)
  local copies, waits for them, and re-layouts  1.31 us (1%)
    ppermute x15, waiting for transfers between devices, move(): return lax.ppermute(array, 'gz', links)  34.5 us
    ppermute x15, starting transfers between devices, move(): return lax.ppermute(array, 'gz', links)  34.2 us
    pallas_call x7, Pallas kernels, call(): pl.pallas_call(run, out_shape=outs, in_specs=[pl.BlockSpec(memory_space=p...  16.8 us
    all_to_all x1, waiting for transfers between devices, attempt(): parts = lax.all_to_all(nu, ('gz', 'gy'), 0, 0)  13.7 us
    pallas_call x1, Pallas kernels, finish(): pl.pallas_call(functools.partial(finish_kernel, blocks=blocks, half=half,...  7.49 us
    all_to_all x1, starting transfers between devices, attempt(): parts = lax.all_to_all(nu, ('gz', 'gy'), 0, 0)  4.07 us
    pallas_call x1, Pallas kernels, others(): pl.pallas_call(functools.partial(others_kernel, blocks=blocks, half=half,...  3.84 us
    ppermute x1, starting transfers between devices, attempt(): above = lax.ppermute(field[:, :, ny - EDGE:], 'gy', pairs(peers_y, 1))  3.04 us
  transfers between devices with their start and end apart: 18, of which 6 were waited for; matrix products, arithmetic and copies ran while one was open for 1% of the time, Pallas kernels for 19%

profile of v7, /device:TPU:0, one launch (start us, length us, event | category | flops | bytes accessed | tf_op | source)
XLA Modules:
  0.0 125.5 jit_solution(12083700534125278616)
XLA Ops:
  0.7 1.3 %fusion.11 = (f32[9,2,4,512]{3,2,0,1:T(4,128)S(1)}, f32[9,2,4,512]{3,2,0,1:T(4,128)S(1)}) fusion(f32[1,2,64,512]{3,2,0,1:T(8,128)} %bitcast.35, f32[8,2,64,512]{3,2,1,0:T(8,128)} %param.11), kind=kLoop, calls=%fused_computation.54 | loop fusion | flops 73728 | bytes 2654208 | tf_op jit(solution)/shard_map/concatenate | solution.py:533
  1.9 1.3 %collective-permute-start.18 = (f32[9,2,4,512]{3,2,0,1:T(4,128)S(1)}, f32[9,2,4,512]{3,2,0,1:T(4,128)S(1)}, u32[]{:S(2)}, u32[]{:S(2)}) collective-permute-start(f32[9,2,4,512]{3,2,0,1:T(4,128)S(1)} %get-tuple-element.122), channel_id=1, source_target_pairs={{1,0},{2,1},{3,2},{5,4},{6,5},{7,6},{9,8},{10,9},{11,10},{13,12},{... | collective-permute-start | bytes 442376 | tf_op jit(solution)/shard_map/ppermute | solution.py:535
  3.2 3.0 %collective-permute-start.17 = (f32[9,2,4,512]{3,2,0,1:T(4,128)S(1)}, f32[9,2,4,512]{3,2,0,1:T(4,128)S(1)}, u32[]{:S(2)}, u32[]{:S(2)}) collective-permute-start(f32[9,2,4,512]{3,2,0,1:T(4,128)S(1)} %get-tuple-element.121), channel_id=1, source_target_pairs={{0,1},{1,2},{2,3},{4,5},{5,6},{6,7},{8,9},{9,10},{10,11},{12,13},{... | collective-permute-start | bytes 442376 | tf_op jit(solution)/shard_map/ppermute | solution.py:534
  6.3 1.3 %fusion.6 = f32[9,2,36,512]{3,2,0,1:T(8,128)} fusion(f32[1,2,64,512]{3,2,0,1:T(8,128)S(1)} %bitcast.36, f32[8,2,64,512]{3,2,1,0:T(8,128)S(1)} %copy-done.5), kind=kLoop, calls=%fused_computation.37 | loop fusion | flops 331776 | bytes 3686400 | tf_op jit(solution)/shard_map/concatenate | solution.py:533
  7.9 1.1 copy-done.10
  9.0 0.4 select_bitcast_fusion.3
  9.5 3.1 %collective-permute-start.20 = (f32[9,40,512]{2,1,0:T(8,128)S(1)}, f32[9,40,512]{2,1,0:T(8,128)S(1)}, u32[]{:S(2)}, u32[]{:S(2)}) collective-permute-start(f32[9,40,512]{2,1,0:T(8,128)S(1)} %get-tuple-element.119.near0), channel_id=1, source_target_pairs={{0,4},{4,0},{8,12},{12,8},{16,20},{20,16},{24,28},{28,24},{1,5},{5... | collective-permute-start | bytes 2211848 | tf_op jit(solution)/shard_map/ppermute | solution.py:549
  12.6 1.3 %collective-permute-start.25 = (f32[9,40,512]{2,1,0:T(8,128)S(1)}, f32[9,40,512]{2,1,0:T(8,128)S(1)}, u32[]{:S(2)}, u32[]{:S(2)}) collective-permute-start(f32[9,40,512]{2,1,0:T(8,128)S(1)} %get-tuple-element.117.refs_0_.refs_3_), channel_id=1, source_target_pairs={{8,0},{16,8},{24,16},{4,12},{12,20},{20,28},{9,1},{17,9},{25,17},{... | collective-permute-start | bytes 2211848 | tf_op jit(solution)/shard_map/ppermute | solution.py:549
  13.9 1.3 %collective-permute-start.26 = (f32[9,40,512]{2,1,0:T(8,128)S(1)}, f32[9,40,512]{2,1,0:T(8,128)S(1)}, u32[]{:S(2)}, u32[]{:S(2)}) collective-permute-start(f32[9,40,512]{2,1,0:T(8,128)S(1)} %get-tuple-element.120.refs_0_.refs_1_.refs_4_.refs_3_), channel_id=1, source_target_pairs={{8,0},{16,8},{24,16},{4,12},{12,20},{20,28},{9,1},{17,9},{25,17},{... | collective-permute-start | bytes 2211848 | tf_op jit(solution)/shard_map/ppermute | solution.py:549
  15.2 5.0 %collective-permute-start.24 = (f32[5,40,512]{2,1,0:T(8,128)S(1)}, f32[5,40,512]{2,1,0:T(8,128)S(1)}, u32[]{:S(2)}, u32[]{:S(2)}) collective-permute-start(f32[5,40,512]{2,1,0:T(8,128)S(1)} %pad_maximum_fusion.3), channel_id=1, source_target_pairs={{0,4},{4,0},{8,12},{12,8},{16,20},{20,16},{24,28},{28,24},{1,5},{5... | collective-permute-start | bytes 1228808 | tf_op jit(solution)/shard_map/ppermute | solution.py:549
  20.3 9.0 %collective-permute-done.20.refs_1_.refs_0_.refs_2_.refs_5_ = f32[9,40,512]{2,1,0:T(8,128)S(1)} collective-permute-done((f32[9,40,512]{2,1,0:T(8,128)S(1)}, f32[9,40,512]{2,1,0:T(8,128)S(1)}, u32[]{:S(2)}, u32[]{:S(2)}) %collective-permute-start.20) | collective-permute-done | bytes 737312 | tf_op jit(solution)/shard_map/ppermute | solution.py:549
  29.3 4.5 %collective-permute-start.21 = (f32[9,40,512]{2,1,0:T(8,128)S(1)}, f32[9,40,512]{2,1,0:T(8,128)S(1)}, u32[]{:S(2)}, u32[]{:S(2)}) collective-permute-start(f32[9,40,512]{2,1,0:T(8,128)S(1)} %collective-permute-done.20.refs_1_.refs_0_.refs_2_.refs_5_), channel_id=1, source_target_pairs={{0,8},{8,16},{16,24},{12,4},{20,12},{28,20},{1,9},{9,17},{17,25},{... | collective-permute-start | bytes 2211848 | tf_op jit(solution)/shard_map/ppermute | solution.py:549
  33.8 11.3 %collective-permute-done.22.refs_3_.refs_4_.refs_7_ = f32[4,40,512]{2,1,0:T(8,128)S(1)} collective-permute-done((f32[4,40,512]{2,1,0:T(8,128)S(1)}, f32[4,40,512]{2,1,0:T(8,128)S(1)}, u32[]{:S(2)}, u32[]{:S(2)}) %collective-permute-start.22) | collective-permute-done | bytes 327712 | tf_op jit(solution)/shard_map/ppermute | solution.py:549
  45.1 4.5 %collective-permute-start.19 = (f32[8,32,512]{2,1,0:T(8,128)S(1)}, f32[8,32,512]{2,1,0:T(8,128)S(1)}, u32[]{:S(2)}, u32[]{:S(2)}) collective-permute-start(f32[8,32,512]{2,1,0:T(8,128)S(1)} %slice.175), channel_id=1, source_target_pairs={{0,8},{8,16},{16,24},{12,4},{20,12},{28,20},{1,9},{9,17},{17,25},{... | collective-permute-start | bytes 1572872 | tf_op jit(solution)/shard_map/ppermute | solution.py:549
  49.6 3.5 %collective-permute-start.23 = (f32[4,40,512]{2,1,0:T(8,128)S(1)}, f32[4,40,512]{2,1,0:T(8,128)S(1)}, u32[]{:S(2)}, u32[]{:S(2)}) collective-permute-start(f32[4,40,512]{2,1,0:T(8,128)S(1)} %collective-permute-done.22.refs_3_.refs_4_.refs_7_), channel_id=1, source_target_pairs={{0,8},{8,16},{16,24},{12,4},{20,12},{28,20},{1,9},{9,17},{17,25},{... | collective-permute-start | bytes 983048 | tf_op jit(solution)/shard_map/ppermute | solution.py:549
  53.0 3.5 %collective-permute-start.28 = (f32[5,40,512]{2,1,0:T(8,128)S(1)}, f32[5,40,512]{2,1,0:T(8,128)S(1)}, u32[]{:S(2)}, u32[]{:S(2)}) collective-permute-start(f32[5,40,512]{2,1,0:T(8,128)S(1)} %collective-permute-done.24.refs_2_.refs_3_.refs_6_), channel_id=1, source_target_pairs={{0,8},{8,16},{16,24},{12,4},{20,12},{28,20},{1,9},{9,17},{17,25},{... | collective-permute-start | bytes 1228808 | tf_op jit(solution)/shard_map/ppermute | solution.py:549
  56.6 1.3 %collective-permute-start.29 = (f32[4,32,512]{2,1,0:T(8,128)S(1)}, f32[4,32,512]{2,1,0:T(8,128)S(1)}, u32[]{:S(2)}, u32[]{:S(2)}) collective-permute-start(f32[4,32,512]{2,1,0:T(8,128)S(1)} %get-tuple-element.123), channel_id=1, source_target_pairs={{8,0},{16,8},{24,16},{4,12},{12,20},{20,28},{9,1},{17,9},{25,17},{... | collective-permute-start | bytes 786440 | tf_op jit(solution)/shard_map/ppermute | solution.py:549
  58.3 1.5 %shard_map.111 = (f32[2,4,40,512]{3,2,1,0:T(8,128)S(1)}, f32[2,4,32,512]{3,2,1,0:T(8,128)}) custom-call(f32[9,40,512]{2,1,0:T(8,128)S(1)} %get-tuple-element.120.refs_0_.refs_1_.refs_4_.refs_3_, f32[9,40,512]{2,1,0:T(8,128)S(1)} %collective-permute-done.20.refs_1_.refs_0_.refs_2_.refs_5_, f32[5,40,512]{2,1,0:T(8,128)S(1)} %collective-permute-done.24.refs_2_.refs_3_.refs_6_, ...), custom_call_target="tpu_custom_call" | custom-call | flops 3276800 | bytes 2621440 | tf_op jit(solution)/shard_map/pallas_call | solution.py:276
  59.7 1.5 %shard_map.110 = (f32[2,4,40,512]{3,2,1,0:T(8,128)S(1)}, f32[2,4,32,512]{3,2,1,0:T(8,128)}) custom-call(f32[9,40,512]{2,1,0:T(8,128)S(1)} %get-tuple-element.120.refs_0_.refs_1_.refs_4_.refs_3_, f32[9,40,512]{2,1,0:T(8,128)S(1)} %collective-permute-done.20.refs_1_.refs_0_.refs_2_.refs_5_, f32[5,40,512]{2,1,0:T(8,128)S(1)} %collective-permute-done.24.refs_2_.refs_3_.refs_6_, ...), custom_call_target="tpu_custom_call" | custom-call | flops 3276800 | bytes 2621440 | tf_op jit(solution)/shard_map/pallas_call | solution.py:276
  61.5 4.0 %shard_map.114 = (f32[2,8,40,512]{3,2,1,0:T(8,128)S(1)}, f32[2,8,40,512]{3,2,1,0:T(8,128)S(1)}, f32[8,32,512]{2,1,0:T(8,128)}, f32[8,32,512]{2,1,0:T(8,128)}, f3...) custom-call(f32[9,40,512]{2,1,0:T(8,128)S(1)} %get-tuple-element.117.refs_0_.refs_3_, ...), custom_call_target="tpu_custom_call" | custom-call | flops 32768000 | bytes 2621440 | tf_op jit(solution)/shard_map/pallas_call | solution.py:276
  65.5 3.3 %collective-permute-done.23.refs_2_ = f32[4,40,512]{2,1,0:T(8,128)S(1)} collective-permute-done((f32[4,40,512]{2,1,0:T(8,128)S(1)}, f32[4,40,512]{2,1,0:T(8,128)S(1)}, u32[]{:S(2)}, u32[]{:S(2)}) %collective-permute-start.23) | collective-permute-done | bytes 327712 | tf_op jit(solution)/shard_map/ppermute | solution.py:549
  68.8 2.4 %collective-permute-start.33 = (f32[8,32,512]{2,1,0:T(8,128)}, f32[8,32,512]{2,1,0:T(8,128)S(1)}, u32[]{:S(2)}, u32[]{:S(2)}) collective-permute-start(f32[8,32,512]{2,1,0:T(8,128)} %get-tuple-element.84), channel_id=1, source_target_pairs={{0,4},{4,0},{8,12},{12,8},{16,20},{20,16},{24,28},{28,24},{1,5},{5... | collective-permute-start | bytes 1572872 | tf_op jit(solution)/shard_map/ppermute | solution.py:549
  71.3 5.8 %collective-permute-done.28.refs_2_.refs_15_ = f32[5,40,512]{2,1,0:T(8,128)S(1)} collective-permute-done((f32[5,40,512]{2,1,0:T(8,128)S(1)}, f32[5,40,512]{2,1,0:T(8,128)S(1)}, u32[]{:S(2)}, u32[]{:S(2)}) %collective-permute-start.28) | collective-permute-done | bytes 409632 | tf_op jit(solution)/shard_map/ppermute | solution.py:549
  77.0 2.4 %collective-permute-start.31 = (f32[2,4,32,512]{3,2,1,0:T(8,128)}, f32[2,4,32,512]{3,2,1,0:T(8,128)S(1)}, u32[]{:S(2)}, u32[]{:S(2)}) collective-permute-start(f32[2,4,32,512]{3,2,1,0:T(8,128)} %get-tuple-element.82), channel_id=1, source_target_pairs={{0,4},{4,0},{8,12},{12,8},{16,20},{20,16},{24,28},{28,24},{1,5},{5... | collective-permute-start | bytes 1572872 | tf_op jit(solution)/shard_map/ppermute | solution.py:549
  79.5 1.3 %collective-permute-start.27 = (f32[4,32,512]{2,1,0:T(8,128)S(1)}, f32[4,32,512]{2,1,0:T(8,128)S(1)}, u32[]{:S(2)}, u32[]{:S(2)}) collective-permute-start(f32[4,32,512]{2,1,0:T(8,128)S(1)} %get-tuple-element.124), channel_id=1, source_target_pairs={{8,0},{16,8},{24,16},{4,12},{12,20},{20,28},{9,1},{17,9},{25,17},{... | collective-permute-start | bytes 786440 | tf_op jit(solution)/shard_map/ppermute | solution.py:549
  80.8 2.9 %shard_map.115 = (f32[4,40,512]{2,1,0:T(8,128)S(1)}, f32[2,4,40,512]{3,2,1,0:T(8,128)S(1)}, f32[4,4,32,512]{3,2,1,0:T(8,128)S(1)}) custom-call(f32[8,32,512]{2,1,0:T(8,128)S(1)} %collective-permute-done.19.refs_0_, f32[9,40,512]{2,1,0:T(8,128)S(1)} %collective-permute-done.21.refs_1_, f32[5,40,512]{2,1,0:T(8,128)S(1)} %collective-permute-done.28.refs_2_.refs_15_, ...), custom_call_target="tpu_custom_call" | custom-call | flops 16384000 | bytes 2621440 | tf_op jit(solution)/shard_map/pallas_call | solution.py:276
  83.7 5.1 %collective-permute-done.27.refs_10_ = f32[4,32,512]{2,1,0:T(8,128)S(1)} collective-permute-done((f32[4,32,512]{2,1,0:T(8,128)S(1)}, f32[4,32,512]{2,1,0:T(8,128)S(1)}, u32[]{:S(2)}, u32[]{:S(2)}) %collective-permute-start.27) | collective-permute-done | bytes 262176 | tf_op jit(solution)/shard_map/ppermute | solution.py:549
  88.9 6.4 %shard_map.116 = (f32[8,32,512]{2,1,0:T(8,128)}, f32[2,8,32,512]{3,2,1,0:T(8,128)}, f32[32,1,252]{2,1,0:T(1,128)}) custom-call(f32[8,32,512]{2,1,0:T(8,128)S(1)} %collective-permute-done.19.refs_0_, f32[9,40,512]{2,1,0:T(8,128)S(1)} %collective-permute-done.21.refs_1_, f32[4,40,512]{2,1,0:T(8,128)S(1)} %collective-permute-done.23.refs_2_, ...), custom_call_target="tpu_custom_call" | custom-call | flops 32768000 | bytes 2621440 | tf_op jit(solution)/shard_map/pallas_call | solution.py:276
  95.3 4.1 %all-to-all-start.1 = ((f32[32,1,252]{2,1,0:T(1,128)}), f32[32,1,252]{2,1,0:T(1,128)S(1)}, u32[]{:S(2)}, u32[]{:S(2)}) async-start(f32[32,1,252]{2,1,0:T(1,128)} %get-tuple-element.75), calls=%async_computation.1 | async-start | bytes 65536 | tf_op jit(solution)/shard_map/all_to_all | solution.py:576
  99.4 13.7 %all-to-all-done.1.parts = f32[32,1,252]{2,1,0:T(1,128)S(1)} async-done(((f32[32,1,252]{2,1,0:T(1,128)}), f32[32,1,252]{2,1,0:T(1,128)S(1)}, u32[]{:S(2)}, u32[]{:S(2)}) %all-to-all-start.1) | async-done | bytes 32288 | tf_op jit(solution)/shard_map/all_to_all | solution.py:576
  113.1 7.5 %finish.3 = (f32[24,32]{1,0:T(8,128)}, f32[8,24,128]{2,1,0:T(8,128)S(1)}, f32[8,2,64,512]{3,2,1,0:T(8,128)}, s32[1,1]{1,0:T(1,128)}, f32[1,2]{1,0:T(1,128)S(1)}) custom-call(f32[32,1,252]{2,1,0:T(1,128)S(1)} %all-to-all-done.1.parts, f32[3,8,252]{2,1,0:T(8,128)S(1)} %copy-done.15, bf16[2,252,128]{2,1,0:T(8,128)(2,1)S(1)} %copy-done.14, ...), custom_call_target="tpu_custom_call" | custom-call | flops 39321600 | bytes 8388608 | tf_op jit(solution)/shard_map/finish/pallas_call | solution.py:484
  121.3 3.8 %others.3 = f32[8,2,64,512]{3,2,1,0:T(8,128)} custom-call(f32[8,24,128]{2,1,0:T(8,128)S(1)} %get-tuple-element.80.splat, f32[9,40,512]{2,1,0:T(8,128)} %copy-done.13, f32[9,40,512]{2,1,0:T(8,128)} %bitcast.44, f32[2,4,32,512]{3,2,1,0:T(8,128)} %collective-permute-done.30.one_first, ...), custom_call_target="tpu_custom_call", output_to_operand_aliasing={{}: (7, {})} | custom-call | tf_op jit(solution)/shard_map/others/pallas_call | solution.py:511
  (46 shorter events, 1.5 us)
Async XLA Ops:
  0.6 5.7 %copy-start.7 = (f32[2,64,512]{2,1,0:T(8,128)S(1)}, f32[2,64,512]{2,1,0:T(8,128)}, u32[]{:S(2)}) copy-start(f32[2,64,512]{2,1,0:T(8,128)} %param.12) | copy-start | bytes 786436
  0.6 5.7 %copy-start.5 = (f32[8,2,64,512]{3,2,1,0:T(8,128)S(1)}, f32[8,2,64,512]{3,2,1,0:T(8,128)}, u32[]{:S(2)}) copy-start(f32[8,2,64,512]{3,2,1,0:T(8,128)} %param.11) | copy-start | bytes 6291460
  1.9 5.7 %collective-permute-start.18 = (f32[9,2,4,512]{3,2,0,1:T(4,128)S(1)}, f32[9,2,4,512]{3,2,0,1:T(4,128)S(1)}, u32[]{:S(2)}, u32[]{:S(2)}) collective-permute-start(f32[9,2,4,512]{3,2,0,1:T(4,128)S(1)} %get-tuple-element.122), channel_id=1, source_target_pairs={{1,0},{2,1},{3,2},{5,4},{6,5},{7,6},{9,8},{10,9},{11,10},{13,12},{... | collective-permute-start | bytes 442376 | tf_op jit(solution)/shard_map/ppermute | solution.py:535
  3.2 4.7 %collective-permute-start.17 = (f32[9,2,4,512]{3,2,0,1:T(4,128)S(1)}, f32[9,2,4,512]{3,2,0,1:T(4,128)S(1)}, u32[]{:S(2)}, u32[]{:S(2)}) collective-permute-start(f32[9,2,4,512]{3,2,0,1:T(4,128)S(1)} %get-tuple-element.121), channel_id=1, source_target_pairs={{0,1},{1,2},{2,3},{4,5},{5,6},{6,7},{8,9},{9,10},{10,11},{12,13},{... | collective-permute-start | bytes 442376 | tf_op jit(solution)/shard_map/ppermute | solution.py:534
  7.7 1.4 %copy-start.10 = (f32[9,2,36,512]{3,2,0,1:T(8,128)S(1)}, f32[9,2,36,512]{3,2,0,1:T(8,128)}, u32[]{:S(2)}) copy-start(f32[9,2,36,512]{3,2,0,1:T(8,128)} %fusion.6) | copy-start | bytes 3981316
  9.4 24.4 %copy-start.9 = (f32[9,1,40,512]{3,2,0,1:T(8,128)}, f32[9,1,40,512]{3,2,0,1:T(8,128)S(1)}, u32[]{:S(2)}) copy-start(f32[9,1,40,512]{3,2,0,1:T(8,128)S(1)} %get-tuple-element.118) | copy-start | bytes 2211844
  9.4 24.4 %copy-start.13 = (f32[9,40,512]{2,1,0:T(8,128)}, f32[9,40,512]{2,1,0:T(8,128)S(1)}, u32[]{:S(2)}) copy-start(f32[9,40,512]{2,1,0:T(8,128)S(1)} %get-tuple-element.119.near0) | copy-start | bytes 2211844
  9.4 79.4 %copy-start = (f32[9,40,512]{2,1,0:T(8,128)}, f32[9,40,512]{2,1,0:T(8,128)S(1)}, u32[]{:S(2)}) copy-start(f32[9,40,512]{2,1,0:T(8,128)S(1)} %get-tuple-element.120.refs_0_.refs_1_.refs_4_.refs_3_) | copy-start | bytes 2211844
  9.5 79.4 %copy-start.2 = (f32[9,40,512]{2,1,0:T(8,128)}, f32[9,40,512]{2,1,0:T(8,128)S(1)}, u32[]{:S(2)}) copy-start(f32[9,40,512]{2,1,0:T(8,128)S(1)} %get-tuple-element.117.refs_0_.refs_3_) | copy-start | bytes 2211844
  9.5 19.8 %collective-permute-start.20 = (f32[9,40,512]{2,1,0:T(8,128)S(1)}, f32[9,40,512]{2,1,0:T(8,128)S(1)}, u32[]{:S(2)}, u32[]{:S(2)}) collective-permute-start(f32[9,40,512]{2,1,0:T(8,128)S(1)} %get-tuple-element.119.near0), channel_id=1, source_target_pairs={{0,4},{4,0},{8,12},{12,8},{16,20},{20,16},{24,28},{28,24},{1,5},{5... | collective-permute-start | bytes 2211848 | tf_op jit(solution)/shard_map/ppermute | solution.py:549
  12.6 40.5 %collective-permute-start.25 = (f32[9,40,512]{2,1,0:T(8,128)S(1)}, f32[9,40,512]{2,1,0:T(8,128)S(1)}, u32[]{:S(2)}, u32[]{:S(2)}) collective-permute-start(f32[9,40,512]{2,1,0:T(8,128)S(1)} %get-tuple-element.117.refs_0_.refs_3_), channel_id=1, source_target_pairs={{8,0},{16,8},{24,16},{4,12},{12,20},{20,28},{9,1},{17,9},{25,17},{... | collective-permute-start | bytes 2211848 | tf_op jit(solution)/shard_map/ppermute | solution.py:549
  13.9 42.7 %collective-permute-start.26 = (f32[9,40,512]{2,1,0:T(8,128)S(1)}, f32[9,40,512]{2,1,0:T(8,128)S(1)}, u32[]{:S(2)}, u32[]{:S(2)}) collective-permute-start(f32[9,40,512]{2,1,0:T(8,128)S(1)} %get-tuple-element.120.refs_0_.refs_1_.refs_4_.refs_3_), channel_id=1, source_target_pairs={{8,0},{16,8},{24,16},{4,12},{12,20},{20,28},{9,1},{17,9},{25,17},{... | collective-permute-start | bytes 2211848 | tf_op jit(solution)/shard_map/ppermute | solution.py:549
  15.2 34.3 %collective-permute-start.24 = (f32[5,40,512]{2,1,0:T(8,128)S(1)}, f32[5,40,512]{2,1,0:T(8,128)S(1)}, u32[]{:S(2)}, u32[]{:S(2)}) collective-permute-start(f32[5,40,512]{2,1,0:T(8,128)S(1)} %pad_maximum_fusion.3), channel_id=1, source_target_pairs={{0,4},{4,0},{8,12},{12,8},{16,20},{20,16},{24,28},{28,24},{1,5},{5... | collective-permute-start | bytes 1228808 | tf_op jit(solution)/shard_map/ppermute | solution.py:549
  20.2 24.8 %collective-permute-start.22 = (f32[4,40,512]{2,1,0:T(8,128)S(1)}, f32[4,40,512]{2,1,0:T(8,128)S(1)}, u32[]{:S(2)}, u32[]{:S(2)}) collective-permute-start(f32[4,40,512]{2,1,0:T(8,128)S(1)} %get-tuple-element.126), channel_id=1, source_target_pairs={{0,4},{4,0},{8,12},{12,8},{16,20},{20,16},{24,28},{28,24},{1,5},{5... | collective-permute-start | bytes 983048 | tf_op jit(solution)/shard_map/ppermute | solution.py:549
  29.3 50.3 %collective-permute-start.21 = (f32[9,40,512]{2,1,0:T(8,128)S(1)}, f32[9,40,512]{2,1,0:T(8,128)S(1)}, u32[]{:S(2)}, u32[]{:S(2)}) collective-permute-start(f32[9,40,512]{2,1,0:T(8,128)S(1)} %collective-permute-done.20.refs_1_.refs_0_.refs_2_.refs_5_), channel_id=1, source_target_pairs={{0,8},{8,16},{16,24},{12,4},{20,12},{28,20},{1,9},{9,17},{17,25},{... | collective-permute-start | bytes 2211848 | tf_op jit(solution)/shard_map/ppermute | solution.py:549
  45.1 20.4 %collective-permute-start.19 = (f32[8,32,512]{2,1,0:T(8,128)S(1)}, f32[8,32,512]{2,1,0:T(8,128)S(1)}, u32[]{:S(2)}, u32[]{:S(2)}) collective-permute-start(f32[8,32,512]{2,1,0:T(8,128)S(1)} %slice.175), channel_id=1, source_target_pairs={{0,8},{8,16},{16,24},{12,4},{20,12},{28,20},{1,9},{9,17},{17,25},{... | collective-permute-start | bytes 1572872 | tf_op jit(solution)/shard_map/ppermute | solution.py:549
  49.6 19.3 %collective-permute-start.23 = (f32[4,40,512]{2,1,0:T(8,128)S(1)}, f32[4,40,512]{2,1,0:T(8,128)S(1)}, u32[]{:S(2)}, u32[]{:S(2)}) collective-permute-start(f32[4,40,512]{2,1,0:T(8,128)S(1)} %collective-permute-done.22.refs_3_.refs_4_.refs_7_), channel_id=1, source_target_pairs={{0,8},{8,16},{16,24},{12,4},{20,12},{28,20},{1,9},{9,17},{17,25},{... | collective-permute-start | bytes 983048 | tf_op jit(solution)/shard_map/ppermute | solution.py:549
  53.0 24.0 %collective-permute-start.28 = (f32[5,40,512]{2,1,0:T(8,128)S(1)}, f32[5,40,512]{2,1,0:T(8,128)S(1)}, u32[]{:S(2)}, u32[]{:S(2)}) collective-permute-start(f32[5,40,512]{2,1,0:T(8,128)S(1)} %collective-permute-done.24.refs_2_.refs_3_.refs_6_), channel_id=1, source_target_pairs={{0,8},{8,16},{16,24},{12,4},{20,12},{28,20},{1,9},{9,17},{17,25},{... | collective-permute-start | bytes 1228808 | tf_op jit(solution)/shard_map/ppermute | solution.py:549
  56.6 22.9 %collective-permute-start.29 = (f32[4,32,512]{2,1,0:T(8,128)S(1)}, f32[4,32,512]{2,1,0:T(8,128)S(1)}, u32[]{:S(2)}, u32[]{:S(2)}) collective-permute-start(f32[4,32,512]{2,1,0:T(8,128)S(1)} %get-tuple-element.123), channel_id=1, source_target_pairs={{8,0},{16,8},{24,16},{4,12},{12,20},{20,28},{9,1},{17,9},{25,17},{... | collective-permute-start | bytes 786440 | tf_op jit(solution)/shard_map/ppermute | solution.py:549
  61.4 18.0 %copy-start.19 = (f32[2,4,32,512]{3,2,1,0:T(8,128)S(1)}, f32[2,4,32,512]{3,2,1,0:T(8,128)}, u32[]{:S(2)}) copy-start(f32[2,4,32,512]{3,2,1,0:T(8,128)} %get-tuple-element.81) | copy-start | bytes 1572868
  65.4 55.8 %collective-permute-start.32 = (f32[8,32,512]{2,1,0:T(8,128)}, f32[8,32,512]{2,1,0:T(8,128)S(1)}, u32[]{:S(2)}, u32[]{:S(2)}) collective-permute-start(f32[8,32,512]{2,1,0:T(8,128)} %get-tuple-element.83), channel_id=1, source_target_pairs={{0,4},{4,0},{8,12},{12,8},{16,20},{20,16},{24,28},{28,24},{1,5},{5... | collective-permute-start | bytes 1572872 | tf_op jit(solution)/shard_map/ppermute | solution.py:549
  68.8 52.4 %collective-permute-start.33 = (f32[8,32,512]{2,1,0:T(8,128)}, f32[8,32,512]{2,1,0:T(8,128)S(1)}, u32[]{:S(2)}, u32[]{:S(2)}) collective-permute-start(f32[8,32,512]{2,1,0:T(8,128)} %get-tuple-element.84), channel_id=1, source_target_pairs={{0,4},{4,0},{8,12},{12,8},{16,20},{20,16},{24,28},{28,24},{1,5},{5... | collective-permute-start | bytes 1572872 | tf_op jit(solution)/shard_map/ppermute | solution.py:549
  77.0 44.2 %collective-permute-start.31 = (f32[2,4,32,512]{3,2,1,0:T(8,128)}, f32[2,4,32,512]{3,2,1,0:T(8,128)S(1)}, u32[]{:S(2)}, u32[]{:S(2)}) collective-permute-start(f32[2,4,32,512]{3,2,1,0:T(8,128)} %get-tuple-element.82), channel_id=1, source_target_pairs={{0,4},{4,0},{8,12},{12,8},{16,20},{20,16},{24,28},{28,24},{1,5},{5... | collective-permute-start | bytes 1572872 | tf_op jit(solution)/shard_map/ppermute | solution.py:549
  79.5 41.8 %collective-permute-start.30 = (f32[2,4,32,512]{3,2,1,0:T(8,128)S(1)}, f32[2,4,32,512]{3,2,1,0:T(8,128)}, u32[]{:S(2)}, u32[]{:S(2)}) collective-permute-start(f32[2,4,32,512]{3,2,1,0:T(8,128)S(1)} %copy-done.19), channel_id=1, source_target_pairs={{0,4},{4,0},{8,12},{12,8},{16,20},{20,16},{24,28},{28,24},{1,5},{5... | collective-permute-start | bytes 1572872 | tf_op jit(solution)/shard_map/ppermute | solution.py:549
  79.5 9.3 %collective-permute-start.27 = (f32[4,32,512]{2,1,0:T(8,128)S(1)}, f32[4,32,512]{2,1,0:T(8,128)S(1)}, u32[]{:S(2)}, u32[]{:S(2)}) collective-permute-start(f32[4,32,512]{2,1,0:T(8,128)S(1)} %get-tuple-element.124), channel_id=1, source_target_pairs={{8,0},{16,8},{24,16},{4,12},{12,20},{20,28},{9,1},{17,9},{25,17},{... | collective-permute-start | bytes 786440 | tf_op jit(solution)/shard_map/ppermute | solution.py:549
  88.9 24.2 %copy-start.4 = (f32[24,32]{1,0:T(8,128)S(1)}, f32[24,32]{1,0:T(8,128)}, u32[]{:S(2)}) copy-start(f32[24,32]{1,0:T(8,128)} %constant.62.clone.shift) | copy-start | bytes 9220
  88.9 24.2 %copy-start.14 = (bf16[2,252,128]{2,1,0:T(8,128)(2,1)S(1)}, bf16[2,252,128]{2,1,0:T(8,128)(2,1)}, u32[]{:S(2)}) copy-start(bf16[2,252,128]{2,1,0:T(8,128)(2,1)} %constant.61.clone.cols) | copy-start | bytes 387076
  88.9 24.2 %copy-start.15 = (f32[3,8,252]{2,1,0:T(8,128)S(1)}, f32[3,8,252]{2,1,0:T(8,128)}, u32[]{:S(2)}) copy-start(f32[3,8,252]{2,1,0:T(8,128)} %constant.60.clone.rows) | copy-start | bytes 72580
  95.3 17.8 %all-to-all-start.1 = ((f32[32,1,252]{2,1,0:T(1,128)}), f32[32,1,252]{2,1,0:T(1,128)S(1)}, u32[]{:S(2)}, u32[]{:S(2)}) async-start(f32[32,1,252]{2,1,0:T(1,128)} %get-tuple-element.75), calls=%async_computation.1 | async-start | bytes 65536 | tf_op jit(solution)/shard_map/all_to_all | solution.py:576

commit v8 on v7

--- a/solution.py
+++ b/solution.py
@@ -409,17 +409,24 @@
     return layer, pl.ds(pl.multiple_of(rows * half, 8), half)
 
 
-TERMS = (((0, None), (1, None), (2, 0)), ((3, None), (4, None), (2, 1)))
+TERMS = (((0, None), (1, None), (2, 0)), ((3, None), (4, None), (2, 1)),
+         ((5, None), (6, 0), (7, 0), (8, None)))
 
 
 def finish_kernel(parts, rows, cols, shift, *refs, blocks, half, width):
-    arrays, (hess_out, splat, out, again_out, affine_out, source, buffer, sems, out_sems) = refs[:5], refs[5:]
+    arrays, (hess_out, splat, out, again_out, affine_out, source, buffer, sems, out_sems) = refs[:9], refs[9:]
     copies = []
+    middle = blocks // 2
     for n, terms in enumerate(TERMS):
         for k, (ref, at) in enumerate(terms):
             ref = arrays[ref] if at is None else arrays[ref].at[at]
-            copy = pltpu.make_async_copy(
-                ref.at[pl.ds(0, blocks), pl.ds(0, half)], source.at[n, k], sems.at[n, k])
+            place = source.at[n, k]
+            if ref.shape[0] == middle:
+                place = source.at[n, 1, pl.ds(0 if k == 1 else middle, middle)]
+            elif k == ITERS:
+                place = source.at[n, ITERS - 1]
+            count = min(blocks, ref.shape[0])
+            copy = pltpu.make_async_copy(ref.at[pl.ds(0, count), pl.ds(0, half)], place, sems.at[n, k])
             copy.start()
             copies.append(copy)
     hessenberg, weights, (again, mean, spread) = solve_small(parts[...], rows, cols, shift[...], blocks)
@@ -441,28 +448,25 @@
         send.wait()
 
 
-def others_kernel(splat, near0, far0, one_first, one_second, near2, far2, _, out, source, buffer, sems, out_sems, *,
+def others_kernel(splat, zero, one_first, one_second, two, _, out, source, buffer, sems, out_sem, *,
                   blocks, half, width):
+    middle = blocks // 2
     loads = []
-    for n, (zero, two) in enumerate(((near0, near2), (far0, far2))):
-        for k, (term, at) in enumerate((
-            (zero.at[pl.ds(0, blocks), pl.ds(0, half)], source.at[n, 0]),
-            (one_first.at[n], source.at[n, 1, pl.ds(0, blocks // 2)]),
-            (one_second.at[n], source.at[n, 1, pl.ds(blocks // 2, blocks // 2)]),
-            (two, source.at[n, 2]),
-        )):
-            loads.append(pltpu.make_async_copy(term, at, sems.at[n, k]))
-            loads[-1].start()
-    sends = []
-    for n in range(2):
-        for load in loads[4 * n:4 * n + 4]:
-            load.wait()
-        blend(buffer.at[n], [source.at[n, k] for k in range(ITERS)], splat, blocks, half, width)
-        layer, at = place_of(2 + n, half)
-        sends.append(pltpu.make_async_copy(buffer.at[n], out.at[:, layer, at], out_sems.at[n]))
-        sends[-1].start()
-    for send in sends:
-        send.wait()
+    for n, (term, at) in enumerate((
+        (zero.at[pl.ds(0, blocks), pl.ds(0, half)], source.at[0]),
+        (one_first.at[1], source.at[1, pl.ds(0, middle)]),
+        (one_second.at[1], source.at[1, pl.ds(middle, middle)]),
+        (two, source.at[2]),
+    )):
+        loads.append(pltpu.make_async_copy(term, at, sems.at[n]))
+        loads[-1].start()
+    for load in loads:
+        load.wait()
+    blend(buffer, [source.at[k] for k in range(ITERS)], splat, blocks, half, width)
+    layer, at = place_of(len(TERMS), half)
+    send = pltpu.make_async_copy(buffer, out.at[:, layer, at], out_sem)
+    send.start()
+    send.wait()
 
 
 def in_hbm(array):
@@ -490,39 +494,39 @@
             jax.ShapeDtypeStruct((1, 1), jnp.int32),
             jax.ShapeDtypeStruct((1, 2), jnp.float32),
         ),
-        in_specs=[vmem] * 4 + [hbm] * len(arrays),
+        in_specs=[vmem] * 4 + [hbm] * 6 + [pl.BlockSpec(memory_space=pl.ANY)] * 3,
         out_specs=(vmem, vmem, hbm, smem, smem),
         scratch_shapes=[
             pltpu.VMEM((len(TERMS), ITERS, *piece), jnp.float32),
             pltpu.VMEM((len(TERMS), *piece), jnp.float32),
-            pltpu.SemaphoreType.DMA((len(TERMS), ITERS)),
+            pltpu.SemaphoreType.DMA((len(TERMS), ITERS + 1)),
             pltpu.SemaphoreType.DMA((len(TERMS),)),
         ],
         compiler_params=pltpu.CompilerParams(vmem_limit_bytes=16 << 20),
         cost_estimate=pl.CostEstimate(flops=300 * blocks * half * width, bytes_accessed=1 << 23, transcendentals=0),
         name="finish",
-    )(parts, rows, cols.astype(jnp.bfloat16), shift, *[in_hbm(array) for array in arrays])
-
-
-def others(splat, near0, far0, one_first, one_second, near2, far2, result, half, width):
+    )(parts, rows, cols.astype(jnp.bfloat16), shift, *[in_hbm(array) for array in arrays[:6]], *arrays[6:])
+
+
+def others(splat, zero, one_first, one_second, two, result, half, width):
     vmem = pl.BlockSpec(memory_space=pltpu.VMEM)
     hbm = pl.BlockSpec(memory_space=pltpu.HBM)
-    blocks = near2.shape[0]
+    blocks = two.shape[0]
     return pl.pallas_call(
         functools.partial(others_kernel, blocks=blocks, half=half, width=width),
         out_shape=jax.ShapeDtypeStruct(result.shape, result.dtype),
-        in_specs=[vmem] + [hbm] * 2 + [pl.BlockSpec(memory_space=pl.ANY)] * 4 + [hbm],
+        in_specs=[vmem, hbm] + [pl.BlockSpec(memory_space=pl.ANY)] * 3 + [hbm],
         out_specs=hbm,
         scratch_shapes=[
-            pltpu.VMEM((2, ITERS, blocks, half, width), jnp.float32),
-            pltpu.VMEM((2, blocks, half, width), jnp.float32),
-            pltpu.SemaphoreType.DMA((2, 4)),
-            pltpu.SemaphoreType.DMA((2,)),
+            pltpu.VMEM((ITERS, blocks, half, width), jnp.float32),
+            pltpu.VMEM((blocks, half, width), jnp.float32),
+            pltpu.SemaphoreType.DMA((4,)),
+            pltpu.SemaphoreType.DMA,
         ],
-        input_output_aliases={7: 0},
+        input_output_aliases={5: 0},
         compiler_params=pltpu.CompilerParams(vmem_limit_bytes=8 << 20),
         name="others",
-    )(splat, in_hbm(near0), in_hbm(far0), one_first, one_second, near2, far2, result)
+    )(splat, in_hbm(zero), one_first, one_second, two, result)
 
 
 def attempt(right_side, diagonal, affine=None):
@@ -576,8 +580,8 @@
     parts = lax.all_to_all(nu, ("gz", "gy"), 0, 0)
     far_back2 = move(far_sent, swap)
     hessenberg, splat, result, again, fit = finish(
-        parts, (keep_far, x1_far, x2, keep_near, x1_near), blocks, half, width, affine)
-    result = others(splat, send_near, send_far, back_a, back_b, near_back2, far_back2, result, half, width)
+        parts, (keep_far, x1_far, x2, keep_near, x1_near, send_near, back_a, back_b, near_back2), blocks, half, width, affine)
+    result = others(splat, send_far, back_a, back_b, far_back2, result, half, width)
     return result, hessenberg, again, fit
 
 

time: 126 us -> 125 us (level)
    all_to_all x1, waiting for transfers between devices: 13.7 us -> 10.1 us  [attempt(): parts = lax.all_to_all(nu, ('gz', 'gy'), 0, 0)]
    ppermute x15, waiting for transfers between devices: 34.5 us -> 38 us  [move(): return lax.ppermute(array, 'gz', links)]
  transfers between devices with their start and end apart: 18 -> 18, of which waited for: 6 -> 7; matrix products, arithmetic and copies ran while one was open for 1% -> 1% of each run, Pallas kernels for 19% -> 20%
where the time goes in v8:
time: 125 us
  waiting for transfers between devices  48.1 us (38%)
  starting transfers between devices  42.6 us (34%)
  Pallas kernels  27.5 us (22%)
  other arithmetic  3.25 us (3%)
  between operations  1.85 us (1%)
  local copies, waits for them, and re-layouts  1.31 us (1%)
    ppermute x15, waiting for transfers between devices, move(): return lax.ppermute(array, 'gz', links)  38 us
    ppermute x15, starting transfers between devices, move(): return lax.ppermute(array, 'gz', links)  34.2 us
    pallas_call x7, Pallas kernels, call(): pl.pallas_call(run, out_shape=outs, in_specs=[pl.BlockSpec(memory_space=p...  16.8 us
    all_to_all x1, waiting for transfers between devices, attempt(): parts = lax.all_to_all(nu, ('gz', 'gy'), 0, 0)  10.1 us
    pallas_call x1, Pallas kernels, finish(): pl.pallas_call(functools.partial(finish_kernel, blocks=blocks, half=half,...  7.95 us
    all_to_all x1, starting transfers between devices, attempt(): parts = lax.all_to_all(nu, ('gz', 'gy'), 0, 0)  4.07 us
    ppermute x1, starting transfers between devices, attempt(): above = lax.ppermute(field[:, :, ny - EDGE:], 'gy', pairs(peers_y, 1))  3.04 us
    pallas_call x1, Pallas kernels, others(): pl.pallas_call(functools.partial(others_kernel, blocks=blocks, half=half,...  2.81 us
  transfers between devices with their start and end apart: 18, of which 7 were waited for; matrix products, arithmetic and copies ran while one was open for 1% of the time, Pallas kernels for 20%

profile of v8, /device:TPU:0, one launch (start us, length us, event | category | flops | bytes accessed | tf_op | source)
XLA Modules:
  0.0 124.8 jit_solution(13373738735809392306)
XLA Ops:
  0.7 1.3 %fusion.11 = (f32[9,2,4,512]{3,2,0,1:T(4,128)S(1)}, f32[9,2,4,512]{3,2,0,1:T(4,128)S(1)}) fusion(f32[1,2,64,512]{3,2,0,1:T(8,128)} %bitcast.35, f32[8,2,64,512]{3,2,1,0:T(8,128)} %param.11), kind=kLoop, calls=%fused_computation.54 | loop fusion | flops 73728 | bytes 2654208 | tf_op jit(solution)/shard_map/concatenate | solution.py:537
  1.9 1.3 %collective-permute-start.18 = (f32[9,2,4,512]{3,2,0,1:T(4,128)S(1)}, f32[9,2,4,512]{3,2,0,1:T(4,128)S(1)}, u32[]{:S(2)}, u32[]{:S(2)}) collective-permute-start(f32[9,2,4,512]{3,2,0,1:T(4,128)S(1)} %get-tuple-element.122), channel_id=1, source_target_pairs={{1,0},{2,1},{3,2},{5,4},{6,5},{7,6},{9,8},{10,9},{11,10},{13,12},{... | collective-permute-start | bytes 442376 | tf_op jit(solution)/shard_map/ppermute | solution.py:539
  3.2 3.0 %collective-permute-start.17 = (f32[9,2,4,512]{3,2,0,1:T(4,128)S(1)}, f32[9,2,4,512]{3,2,0,1:T(4,128)S(1)}, u32[]{:S(2)}, u32[]{:S(2)}) collective-permute-start(f32[9,2,4,512]{3,2,0,1:T(4,128)S(1)} %get-tuple-element.121), channel_id=1, source_target_pairs={{0,1},{1,2},{2,3},{4,5},{5,6},{6,7},{8,9},{9,10},{10,11},{12,13},{... | collective-permute-start | bytes 442376 | tf_op jit(solution)/shard_map/ppermute | solution.py:538
  6.3 1.3 %fusion.6 = f32[9,2,36,512]{3,2,0,1:T(8,128)} fusion(f32[1,2,64,512]{3,2,0,1:T(8,128)S(1)} %bitcast.36, f32[8,2,64,512]{3,2,1,0:T(8,128)S(1)} %copy-done.5), kind=kLoop, calls=%fused_computation.37 | loop fusion | flops 331776 | bytes 3686400 | tf_op jit(solution)/shard_map/concatenate | solution.py:537
  7.9 1.1 copy-done.10
  9.5 3.1 %collective-permute-start.20 = (f32[9,40,512]{2,1,0:T(8,128)S(1)}, f32[9,40,512]{2,1,0:T(8,128)S(1)}, u32[]{:S(2)}, u32[]{:S(2)}) collective-permute-start(f32[9,40,512]{2,1,0:T(8,128)S(1)} %get-tuple-element.119.refs_5_), channel_id=1, source_target_pairs={{0,4},{4,0},{8,12},{12,8},{16,20},{20,16},{24,28},{28,24},{1,5},{5... | collective-permute-start | bytes 2211848 | tf_op jit(solution)/shard_map/ppermute | solution.py:553
  12.6 1.3 %collective-permute-start.25 = (f32[9,40,512]{2,1,0:T(8,128)S(1)}, f32[9,40,512]{2,1,0:T(8,128)S(1)}, u32[]{:S(2)}, u32[]{:S(2)}) collective-permute-start(f32[9,40,512]{2,1,0:T(8,128)S(1)} %get-tuple-element.117.refs_0_.refs_3_), channel_id=1, source_target_pairs={{8,0},{16,8},{24,16},{4,12},{12,20},{20,28},{9,1},{17,9},{25,17},{... | collective-permute-start | bytes 2211848 | tf_op jit(solution)/shard_map/ppermute | solution.py:553
  13.9 1.3 %collective-permute-start.26 = (f32[9,40,512]{2,1,0:T(8,128)S(1)}, f32[9,40,512]{2,1,0:T(8,128)S(1)}, u32[]{:S(2)}, u32[]{:S(2)}) collective-permute-start(f32[9,40,512]{2,1,0:T(8,128)S(1)} %get-tuple-element.120.refs_0_.refs_1_.refs_4_.refs_3_), channel_id=1, source_target_pairs={{8,0},{16,8},{24,16},{4,12},{12,20},{20,28},{9,1},{17,9},{25,17},{... | collective-permute-start | bytes 2211848 | tf_op jit(solution)/shard_map/ppermute | solution.py:553
  15.2 5.0 %collective-permute-start.24 = (f32[5,40,512]{2,1,0:T(8,128)S(1)}, f32[5,40,512]{2,1,0:T(8,128)S(1)}, u32[]{:S(2)}, u32[]{:S(2)}) collective-permute-start(f32[5,40,512]{2,1,0:T(8,128)S(1)} %pad_maximum_fusion.3), channel_id=1, source_target_pairs={{0,4},{4,0},{8,12},{12,8},{16,20},{20,16},{24,28},{28,24},{1,5},{5... | collective-permute-start | bytes 1228808 | tf_op jit(solution)/shard_map/ppermute | solution.py:553
  20.3 9.0 %collective-permute-done.20.refs_1_.refs_0_.refs_2_.refs_5_ = f32[9,40,512]{2,1,0:T(8,128)S(1)} collective-permute-done((f32[9,40,512]{2,1,0:T(8,128)S(1)}, f32[9,40,512]{2,1,0:T(8,128)S(1)}, u32[]{:S(2)}, u32[]{:S(2)}) %collective-permute-start.20) | collective-permute-done | bytes 737312 | tf_op jit(solution)/shard_map/ppermute | solution.py:553
  29.3 4.5 %collective-permute-start.21 = (f32[9,40,512]{2,1,0:T(8,128)S(1)}, f32[9,40,512]{2,1,0:T(8,128)S(1)}, u32[]{:S(2)}, u32[]{:S(2)}) collective-permute-start(f32[9,40,512]{2,1,0:T(8,128)S(1)} %collective-permute-done.20.refs_1_.refs_0_.refs_2_.refs_5_), channel_id=1, source_target_pairs={{0,8},{8,16},{16,24},{12,4},{20,12},{28,20},{1,9},{9,17},{17,25},{... | collective-permute-start | bytes 2211848 | tf_op jit(solution)/shard_map/ppermute | solution.py:553
  33.8 11.3 %collective-permute-done.22.refs_3_.refs_4_.refs_7_ = f32[4,40,512]{2,1,0:T(8,128)S(1)} collective-permute-done((f32[4,40,512]{2,1,0:T(8,128)S(1)}, f32[4,40,512]{2,1,0:T(8,128)S(1)}, u32[]{:S(2)}, u32[]{:S(2)}) %collective-permute-start.22) | collective-permute-done | bytes 327712 | tf_op jit(solution)/shard_map/ppermute | solution.py:553
  45.1 4.5 %collective-permute-start.19 = (f32[8,32,512]{2,1,0:T(8,128)S(1)}, f32[8,32,512]{2,1,0:T(8,128)S(1)}, u32[]{:S(2)}, u32[]{:S(2)}) collective-permute-start(f32[8,32,512]{2,1,0:T(8,128)S(1)} %slice.175), channel_id=1, source_target_pairs={{0,8},{8,16},{16,24},{12,4},{20,12},{28,20},{1,9},{9,17},{17,25},{... | collective-permute-start | bytes 1572872 | tf_op jit(solution)/shard_map/ppermute | solution.py:553
  49.6 3.5 %collective-permute-start.23 = (f32[4,40,512]{2,1,0:T(8,128)S(1)}, f32[4,40,512]{2,1,0:T(8,128)S(1)}, u32[]{:S(2)}, u32[]{:S(2)}) collective-permute-start(f32[4,40,512]{2,1,0:T(8,128)S(1)} %collective-permute-done.22.refs_3_.refs_4_.refs_7_), channel_id=1, source_target_pairs={{0,8},{8,16},{16,24},{12,4},{20,12},{28,20},{1,9},{9,17},{17,25},{... | collective-permute-start | bytes 983048 | tf_op jit(solution)/shard_map/ppermute | solution.py:553
  53.0 3.5 %collective-permute-start.28 = (f32[5,40,512]{2,1,0:T(8,128)S(1)}, f32[5,40,512]{2,1,0:T(8,128)S(1)}, u32[]{:S(2)}, u32[]{:S(2)}) collective-permute-start(f32[5,40,512]{2,1,0:T(8,128)S(1)} %collective-permute-done.24.refs_2_.refs_3_.refs_6_), channel_id=1, source_target_pairs={{0,8},{8,16},{16,24},{12,4},{20,12},{28,20},{1,9},{9,17},{17,25},{... | collective-permute-start | bytes 1228808 | tf_op jit(solution)/shard_map/ppermute | solution.py:553
  56.6 1.3 %collective-permute-start.29 = (f32[4,32,512]{2,1,0:T(8,128)S(1)}, f32[4,32,512]{2,1,0:T(8,128)S(1)}, u32[]{:S(2)}, u32[]{:S(2)}) collective-permute-start(f32[4,32,512]{2,1,0:T(8,128)S(1)} %get-tuple-element.123), channel_id=1, source_target_pairs={{8,0},{16,8},{24,16},{4,12},{12,20},{20,28},{9,1},{17,9},{25,17},{... | collective-permute-start | bytes 786440 | tf_op jit(solution)/shard_map/ppermute | solution.py:553
  58.3 1.5 %shard_map.111 = (f32[2,4,40,512]{3,2,1,0:T(8,128)S(1)}, f32[2,4,32,512]{3,2,1,0:T(8,128)}) custom-call(f32[9,40,512]{2,1,0:T(8,128)S(1)} %get-tuple-element.120.refs_0_.refs_1_.refs_4_.refs_3_, f32[9,40,512]{2,1,0:T(8,128)S(1)} %collective-permute-done.20.refs_1_.refs_0_.refs_2_.refs_5_, f32[5,40,512]{2,1,0:T(8,128)S(1)} %collective-permute-done.24.refs_2_.refs_3_.refs_6_, ...), custom_call_target="tpu_custom_call" | custom-call | flops 3276800 | bytes 2621440 | tf_op jit(solution)/shard_map/pallas_call | solution.py:276
  59.7 1.5 %shard_map.110 = (f32[2,4,40,512]{3,2,1,0:T(8,128)S(1)}, f32[2,4,32,512]{3,2,1,0:T(8,128)}) custom-call(f32[9,40,512]{2,1,0:T(8,128)S(1)} %get-tuple-element.120.refs_0_.refs_1_.refs_4_.refs_3_, f32[9,40,512]{2,1,0:T(8,128)S(1)} %collective-permute-done.20.refs_1_.refs_0_.refs_2_.refs_5_, f32[5,40,512]{2,1,0:T(8,128)S(1)} %collective-permute-done.24.refs_2_.refs_3_.refs_6_, ...), custom_call_target="tpu_custom_call" | custom-call | flops 3276800 | bytes 2621440 | tf_op jit(solution)/shard_map/pallas_call | solution.py:276
  61.4 4.0 %shard_map.114 = (f32[2,8,40,512]{3,2,1,0:T(8,128)S(1)}, f32[2,8,40,512]{3,2,1,0:T(8,128)S(1)}, f32[8,32,512]{2,1,0:T(8,128)}, f32[8,32,512]{2,1,0:T(8,128)}, f3...) custom-call(f32[9,40,512]{2,1,0:T(8,128)S(1)} %get-tuple-element.117.refs_0_.refs_3_, ...), custom_call_target="tpu_custom_call" | custom-call | flops 32768000 | bytes 2621440 | tf_op jit(solution)/shard_map/pallas_call | solution.py:276
  65.5 3.3 %collective-permute-done.23.refs_2_ = f32[4,40,512]{2,1,0:T(8,128)S(1)} collective-permute-done((f32[4,40,512]{2,1,0:T(8,128)S(1)}, f32[4,40,512]{2,1,0:T(8,128)S(1)}, u32[]{:S(2)}, u32[]{:S(2)}) %collective-permute-start.23) | collective-permute-done | bytes 327712 | tf_op jit(solution)/shard_map/ppermute | solution.py:553
  68.8 2.4 %collective-permute-start.31 = (f32[2,4,32,512]{3,2,1,0:T(8,128)}, f32[2,4,32,512]{3,2,1,0:T(8,128)S(1)}, u32[]{:S(2)}, u32[]{:S(2)}) collective-permute-start(f32[2,4,32,512]{3,2,1,0:T(8,128)} %get-tuple-element.80), channel_id=1, source_target_pairs={{0,4},{4,0},{8,12},{12,8},{16,20},{20,16},{24,28},{28,24},{1,5},{5... | collective-permute-start | bytes 1572872 | tf_op jit(solution)/shard_map/ppermute | solution.py:553
  71.3 5.8 %collective-permute-done.28.refs_2_.refs_15_ = f32[5,40,512]{2,1,0:T(8,128)S(1)} collective-permute-done((f32[5,40,512]{2,1,0:T(8,128)S(1)}, f32[5,40,512]{2,1,0:T(8,128)S(1)}, u32[]{:S(2)}, u32[]{:S(2)}) %collective-permute-start.28) | collective-permute-done | bytes 409632 | tf_op jit(solution)/shard_map/ppermute | solution.py:553
  77.0 2.4 %collective-permute-start.30 = (f32[2,4,32,512]{3,2,1,0:T(8,128)S(1)}, f32[2,4,32,512]{3,2,1,0:T(8,128)S(1)}, u32[]{:S(2)}, u32[]{:S(2)}) collective-permute-start(f32[2,4,32,512]{3,2,1,0:T(8,128)S(1)} %copy-done.20), channel_id=1, source_target_pairs={{0,4},{4,0},{8,12},{12,8},{16,20},{20,16},{24,28},{28,24},{1,5},{5... | collective-permute-start | bytes 1572872 | tf_op jit(solution)/shard_map/ppermute | solution.py:553
  79.5 1.3 %collective-permute-start.27 = (f32[4,32,512]{2,1,0:T(8,128)S(1)}, f32[4,32,512]{2,1,0:T(8,128)S(1)}, u32[]{:S(2)}, u32[]{:S(2)}) collective-permute-start(f32[4,32,512]{2,1,0:T(8,128)S(1)} %get-tuple-element.124), channel_id=1, source_target_pairs={{8,0},{16,8},{24,16},{4,12},{12,20},{20,28},{9,1},{17,9},{25,17},{... | collective-permute-start | bytes 786440 | tf_op jit(solution)/shard_map/ppermute | solution.py:553
  80.8 2.9 %shard_map.115 = (f32[4,40,512]{2,1,0:T(8,128)S(1)}, f32[2,4,40,512]{3,2,1,0:T(8,128)S(1)}, f32[4,4,32,512]{3,2,1,0:T(8,128)S(1)}) custom-call(f32[8,32,512]{2,1,0:T(8,128)S(1)} %collective-permute-done.19.refs_0_, f32[9,40,512]{2,1,0:T(8,128)S(1)} %collective-permute-done.21.refs_1_, f32[5,40,512]{2,1,0:T(8,128)S(1)} %collective-permute-done.28.refs_2_.refs_15_, ...), custom_call_target="tpu_custom_call" | custom-call | flops 16384000 | bytes 2621440 | tf_op jit(solution)/shard_map/pallas_call | solution.py:276
  83.7 5.3 %collective-permute-done.27.refs_10_ = f32[4,32,512]{2,1,0:T(8,128)S(1)} collective-permute-done((f32[4,32,512]{2,1,0:T(8,128)S(1)}, f32[4,32,512]{2,1,0:T(8,128)S(1)}, u32[]{:S(2)}, u32[]{:S(2)}) %collective-permute-start.27) | collective-permute-done | bytes 262176 | tf_op jit(solution)/shard_map/ppermute | solution.py:553
  89.0 6.4 %shard_map.116 = (f32[8,32,512]{2,1,0:T(8,128)}, f32[2,8,32,512]{3,2,1,0:T(8,128)}, f32[32,1,252]{2,1,0:T(1,128)}) custom-call(f32[8,32,512]{2,1,0:T(8,128)S(1)} %collective-permute-done.19.refs_0_, f32[9,40,512]{2,1,0:T(8,128)S(1)} %collective-permute-done.21.refs_1_, f32[4,40,512]{2,1,0:T(8,128)S(1)} %collective-permute-done.23.refs_2_, ...), custom_call_target="tpu_custom_call" | custom-call | flops 32768000 | bytes 2621440 | tf_op jit(solution)/shard_map/pallas_call | solution.py:276
  95.4 4.1 %all-to-all-start.1 = ((f32[32,1,252]{2,1,0:T(1,128)}), f32[32,1,252]{2,1,0:T(1,128)S(1)}, u32[]{:S(2)}, u32[]{:S(2)}) async-start(f32[32,1,252]{2,1,0:T(1,128)} %get-tuple-element.75), calls=%async_computation.1 | async-start | bytes 65536 | tf_op jit(solution)/shard_map/all_to_all | solution.py:580
  99.5 3.4 %collective-permute-done.30.refs_6_.one_first = f32[2,4,32,512]{3,2,1,0:T(8,128)S(1)} collective-permute-done((f32[2,4,32,512]{3,2,1,0:T(8,128)S(1)}, f32[2,4,32,512]{3,2,1,0:T(8,128)S(1)}, u32[]{:S(2)}, u32[]{:S(2)}) %collective-permute-start.30) | collective-permute-done | bytes 524320 | tf_op jit(solution)/shard_map/ppermute | solution.py:553
  102.9 10.1 %all-to-all-done.1.parts = f32[32,1,252]{2,1,0:T(1,128)S(1)} async-done(((f32[32,1,252]{2,1,0:T(1,128)}), f32[32,1,252]{2,1,0:T(1,128)S(1)}, u32[]{:S(2)}, u32[]{:S(2)}) %all-to-all-start.1) | async-done | bytes 32288 | tf_op jit(solution)/shard_map/all_to_all | solution.py:580
  113.0 7.9 %finish.3 = (f32[24,32]{1,0:T(8,128)}, f32[8,24,128]{2,1,0:T(8,128)S(1)}, f32[8,2,64,512]{3,2,1,0:T(8,128)}, s32[1,1]{1,0:T(1,128)}, f32[1,2]{1,0:T(1,128)S(1)}) custom-call(f32[32,1,252]{2,1,0:T(1,128)S(1)} %all-to-all-done.1.parts, f32[3,8,252]{2,1,0:T(8,128)S(1)} %copy-done.15, bf16[2,252,128]{2,1,0:T(8,128)(2,1)S(1)} %copy-done.14, ...), custom_call_target="tpu_custom_call" | custom-call | flops 39321600 | bytes 8388608 | tf_op jit(solution)/shard_map/finish/pallas_call | solution.py:488
  121.6 2.8 %others.3 = f32[8,2,64,512]{3,2,1,0:T(8,128)} custom-call(f32[8,24,128]{2,1,0:T(8,128)S(1)} %get-tuple-element.83.splat, f32[9,40,512]{2,1,0:T(8,128)} %bitcast.44, f32[2,4,32,512]{3,2,1,0:T(8,128)S(1)} %collective-permute-done.30.refs_6_.one_first, f32[2,4,32,512]{3,2,1,0:T(8,128)S(1)} %collective-permute-done.31.refs_7_.one_second, ...), custom_call_target="tpu_custom_call", output_to_operand_aliasing={{}: (5, {})} | custom-call | tf_op jit(solution)/shard_map/others/pallas_call | solution.py:515
  (46 shorter events, 1.9 us)
Async XLA Ops:
  0.6 5.7 %copy-start.7 = (f32[2,64,512]{2,1,0:T(8,128)S(1)}, f32[2,64,512]{2,1,0:T(8,128)}, u32[]{:S(2)}) copy-start(f32[2,64,512]{2,1,0:T(8,128)} %param.12) | copy-start | bytes 786436
  0.6 5.7 %copy-start.5 = (f32[8,2,64,512]{3,2,1,0:T(8,128)S(1)}, f32[8,2,64,512]{3,2,1,0:T(8,128)}, u32[]{:S(2)}) copy-start(f32[8,2,64,512]{3,2,1,0:T(8,128)} %param.11) | copy-start | bytes 6291460
  1.9 5.7 %collective-permute-start.18 = (f32[9,2,4,512]{3,2,0,1:T(4,128)S(1)}, f32[9,2,4,512]{3,2,0,1:T(4,128)S(1)}, u32[]{:S(2)}, u32[]{:S(2)}) collective-permute-start(f32[9,2,4,512]{3,2,0,1:T(4,128)S(1)} %get-tuple-element.122), channel_id=1, source_target_pairs={{1,0},{2,1},{3,2},{5,4},{6,5},{7,6},{9,8},{10,9},{11,10},{13,12},{... | collective-permute-start | bytes 442376 | tf_op jit(solution)/shard_map/ppermute | solution.py:539
  3.2 4.7 %collective-permute-start.17 = (f32[9,2,4,512]{3,2,0,1:T(4,128)S(1)}, f32[9,2,4,512]{3,2,0,1:T(4,128)S(1)}, u32[]{:S(2)}, u32[]{:S(2)}) collective-permute-start(f32[9,2,4,512]{3,2,0,1:T(4,128)S(1)} %get-tuple-element.121), channel_id=1, source_target_pairs={{0,1},{1,2},{2,3},{4,5},{5,6},{6,7},{8,9},{9,10},{10,11},{12,13},{... | collective-permute-start | bytes 442376 | tf_op jit(solution)/shard_map/ppermute | solution.py:538
  7.7 1.4 %copy-start.10 = (f32[9,2,36,512]{3,2,0,1:T(8,128)S(1)}, f32[9,2,36,512]{3,2,0,1:T(8,128)}, u32[]{:S(2)}) copy-start(f32[9,2,36,512]{3,2,0,1:T(8,128)} %fusion.6) | copy-start | bytes 3981316
  9.4 24.4 %copy-start.9 = (f32[9,1,40,512]{3,2,0,1:T(8,128)}, f32[9,1,40,512]{3,2,0,1:T(8,128)S(1)}, u32[]{:S(2)}) copy-start(f32[9,1,40,512]{3,2,0,1:T(8,128)S(1)} %get-tuple-element.118) | copy-start | bytes 2211844
  9.4 24.4 %copy-start.13 = (f32[9,40,512]{2,1,0:T(8,128)}, f32[9,40,512]{2,1,0:T(8,128)S(1)}, u32[]{:S(2)}) copy-start(f32[9,40,512]{2,1,0:T(8,128)S(1)} %get-tuple-element.119.refs_5_) | copy-start | bytes 2211844
  9.4 79.5 %copy-start = (f32[9,40,512]{2,1,0:T(8,128)}, f32[9,40,512]{2,1,0:T(8,128)S(1)}, u32[]{:S(2)}) copy-start(f32[9,40,512]{2,1,0:T(8,128)S(1)} %get-tuple-element.120.refs_0_.refs_1_.refs_4_.refs_3_) | copy-start | bytes 2211844
  9.5 79.5 %copy-start.2 = (f32[9,40,512]{2,1,0:T(8,128)}, f32[9,40,512]{2,1,0:T(8,128)S(1)}, u32[]{:S(2)}) copy-start(f32[9,40,512]{2,1,0:T(8,128)S(1)} %get-tuple-element.117.refs_0_.refs_3_) | copy-start | bytes 2211844
  9.5 19.8 %collective-permute-start.20 = (f32[9,40,512]{2,1,0:T(8,128)S(1)}, f32[9,40,512]{2,1,0:T(8,128)S(1)}, u32[]{:S(2)}, u32[]{:S(2)}) collective-permute-start(f32[9,40,512]{2,1,0:T(8,128)S(1)} %get-tuple-element.119.refs_5_), channel_id=1, source_target_pairs={{0,4},{4,0},{8,12},{12,8},{16,20},{20,16},{24,28},{28,24},{1,5},{5... | collective-permute-start | bytes 2211848 | tf_op jit(solution)/shard_map/ppermute | solution.py:553
  12.6 40.5 %collective-permute-start.25 = (f32[9,40,512]{2,1,0:T(8,128)S(1)}, f32[9,40,512]{2,1,0:T(8,128)S(1)}, u32[]{:S(2)}, u32[]{:S(2)}) collective-permute-start(f32[9,40,512]{2,1,0:T(8,128)S(1)} %get-tuple-element.117.refs_0_.refs_3_), channel_id=1, source_target_pairs={{8,0},{16,8},{24,16},{4,12},{12,20},{20,28},{9,1},{17,9},{25,17},{... | collective-permute-start | bytes 2211848 | tf_op jit(solution)/shard_map/ppermute | solution.py:553
  13.9 42.7 %collective-permute-start.26 = (f32[9,40,512]{2,1,0:T(8,128)S(1)}, f32[9,40,512]{2,1,0:T(8,128)S(1)}, u32[]{:S(2)}, u32[]{:S(2)}) collective-permute-start(f32[9,40,512]{2,1,0:T(8,128)S(1)} %get-tuple-element.120.refs_0_.refs_1_.refs_4_.refs_3_), channel_id=1, source_target_pairs={{8,0},{16,8},{24,16},{4,12},{12,20},{20,28},{9,1},{17,9},{25,17},{... | collective-permute-start | bytes 2211848 | tf_op jit(solution)/shard_map/ppermute | solution.py:553
  15.2 34.3 %collective-permute-start.24 = (f32[5,40,512]{2,1,0:T(8,128)S(1)}, f32[5,40,512]{2,1,0:T(8,128)S(1)}, u32[]{:S(2)}, u32[]{:S(2)}) collective-permute-start(f32[5,40,512]{2,1,0:T(8,128)S(1)} %pad_maximum_fusion.3), channel_id=1, source_target_pairs={{0,4},{4,0},{8,12},{12,8},{16,20},{20,16},{24,28},{28,24},{1,5},{5... | collective-permute-start | bytes 1228808 | tf_op jit(solution)/shard_map/ppermute | solution.py:553
  20.2 24.8 %collective-permute-start.22 = (f32[4,40,512]{2,1,0:T(8,128)S(1)}, f32[4,40,512]{2,1,0:T(8,128)S(1)}, u32[]{:S(2)}, u32[]{:S(2)}) collective-permute-start(f32[4,40,512]{2,1,0:T(8,128)S(1)} %get-tuple-element.126), channel_id=1, source_target_pairs={{0,4},{4,0},{8,12},{12,8},{16,20},{20,16},{24,28},{28,24},{1,5},{5... | collective-permute-start | bytes 983048 | tf_op jit(solution)/shard_map/ppermute | solution.py:553
  29.3 50.3 %collective-permute-start.21 = (f32[9,40,512]{2,1,0:T(8,128)S(1)}, f32[9,40,512]{2,1,0:T(8,128)S(1)}, u32[]{:S(2)}, u32[]{:S(2)}) collective-permute-start(f32[9,40,512]{2,1,0:T(8,128)S(1)} %collective-permute-done.20.refs_1_.refs_0_.refs_2_.refs_5_), channel_id=1, source_target_pairs={{0,8},{8,16},{16,24},{12,4},{20,12},{28,20},{1,9},{9,17},{17,25},{... | collective-permute-start | bytes 2211848 | tf_op jit(solution)/shard_map/ppermute | solution.py:553
  45.1 20.3 %collective-permute-start.19 = (f32[8,32,512]{2,1,0:T(8,128)S(1)}, f32[8,32,512]{2,1,0:T(8,128)S(1)}, u32[]{:S(2)}, u32[]{:S(2)}) collective-permute-start(f32[8,32,512]{2,1,0:T(8,128)S(1)} %slice.175), channel_id=1, source_target_pairs={{0,8},{8,16},{16,24},{12,4},{20,12},{28,20},{1,9},{9,17},{17,25},{... | collective-permute-start | bytes 1572872 | tf_op jit(solution)/shard_map/ppermute | solution.py:553
  49.6 19.3 %collective-permute-start.23 = (f32[4,40,512]{2,1,0:T(8,128)S(1)}, f32[4,40,512]{2,1,0:T(8,128)S(1)}, u32[]{:S(2)}, u32[]{:S(2)}) collective-permute-start(f32[4,40,512]{2,1,0:T(8,128)S(1)} %collective-permute-done.22.refs_3_.refs_4_.refs_7_), channel_id=1, source_target_pairs={{0,8},{8,16},{16,24},{12,4},{20,12},{28,20},{1,9},{9,17},{17,25},{... | collective-permute-start | bytes 983048 | tf_op jit(solution)/shard_map/ppermute | solution.py:553
  53.0 24.0 %collective-permute-start.28 = (f32[5,40,512]{2,1,0:T(8,128)S(1)}, f32[5,40,512]{2,1,0:T(8,128)S(1)}, u32[]{:S(2)}, u32[]{:S(2)}) collective-permute-start(f32[5,40,512]{2,1,0:T(8,128)S(1)} %collective-permute-done.24.refs_2_.refs_3_.refs_6_), channel_id=1, source_target_pairs={{0,8},{8,16},{16,24},{12,4},{20,12},{28,20},{1,9},{9,17},{17,25},{... | collective-permute-start | bytes 1228808 | tf_op jit(solution)/shard_map/ppermute | solution.py:553
  56.6 22.9 %collective-permute-start.29 = (f32[4,32,512]{2,1,0:T(8,128)S(1)}, f32[4,32,512]{2,1,0:T(8,128)S(1)}, u32[]{:S(2)}, u32[]{:S(2)}) collective-permute-start(f32[4,32,512]{2,1,0:T(8,128)S(1)} %get-tuple-element.123), channel_id=1, source_target_pairs={{8,0},{16,8},{24,16},{4,12},{12,20},{20,28},{9,1},{17,9},{25,17},{... | collective-permute-start | bytes 786440 | tf_op jit(solution)/shard_map/ppermute | solution.py:553
  61.4 15.6 %copy-start.20 = (f32[2,4,32,512]{3,2,1,0:T(8,128)S(1)}, f32[2,4,32,512]{3,2,1,0:T(8,128)}, u32[]{:S(2)}) copy-start(f32[2,4,32,512]{3,2,1,0:T(8,128)} %get-tuple-element.79) | copy-start | bytes 1572868
  65.4 34.1 %collective-permute-start.32 = (f32[8,32,512]{2,1,0:T(8,128)}, f32[8,32,512]{2,1,0:T(8,128)}, u32[]{:S(2)}, u32[]{:S(2)}) collective-permute-start(f32[8,32,512]{2,1,0:T(8,128)} %get-tuple-element.81), channel_id=1, source_target_pairs={{0,4},{4,0},{8,12},{12,8},{16,20},{20,16},{24,28},{28,24},{1,5},{5... | collective-permute-start | bytes 1572872 | tf_op jit(solution)/shard_map/ppermute | solution.py:553
  68.8 30.7 %collective-permute-start.31 = (f32[2,4,32,512]{3,2,1,0:T(8,128)}, f32[2,4,32,512]{3,2,1,0:T(8,128)S(1)}, u32[]{:S(2)}, u32[]{:S(2)}) collective-permute-start(f32[2,4,32,512]{3,2,1,0:T(8,128)} %get-tuple-element.80), channel_id=1, source_target_pairs={{0,4},{4,0},{8,12},{12,8},{16,20},{20,16},{24,28},{28,24},{1,5},{5... | collective-permute-start | bytes 1572872 | tf_op jit(solution)/shard_map/ppermute | solution.py:553
  77.0 25.9 %collective-permute-start.30 = (f32[2,4,32,512]{3,2,1,0:T(8,128)S(1)}, f32[2,4,32,512]{3,2,1,0:T(8,128)S(1)}, u32[]{:S(2)}, u32[]{:S(2)}) collective-permute-start(f32[2,4,32,512]{3,2,1,0:T(8,128)S(1)} %copy-done.20), channel_id=1, source_target_pairs={{0,4},{4,0},{8,12},{12,8},{16,20},{20,16},{24,28},{28,24},{1,5},{5... | collective-permute-start | bytes 1572872 | tf_op jit(solution)/shard_map/ppermute | solution.py:553
  79.5 42.2 %collective-permute-start.33 = (f32[8,32,512]{2,1,0:T(8,128)}, f32[8,32,512]{2,1,0:T(8,128)S(1)}, u32[]{:S(2)}, u32[]{:S(2)}) collective-permute-start(f32[8,32,512]{2,1,0:T(8,128)} %get-tuple-element.84), channel_id=1, source_target_pairs={{0,4},{4,0},{8,12},{12,8},{16,20},{20,16},{24,28},{28,24},{1,5},{5... | collective-permute-start | bytes 1572872 | tf_op jit(solution)/shard_map/ppermute | solution.py:553
  79.5 9.4 %collective-permute-start.27 = (f32[4,32,512]{2,1,0:T(8,128)S(1)}, f32[4,32,512]{2,1,0:T(8,128)S(1)}, u32[]{:S(2)}, u32[]{:S(2)}) collective-permute-start(f32[4,32,512]{2,1,0:T(8,128)S(1)} %get-tuple-element.124), channel_id=1, source_target_pairs={{8,0},{16,8},{24,16},{4,12},{12,20},{20,28},{9,1},{17,9},{25,17},{... | collective-permute-start | bytes 786440 | tf_op jit(solution)/shard_map/ppermute | solution.py:553
  89.0 24.0 %copy-start.4 = (f32[24,32]{1,0:T(8,128)S(1)}, f32[24,32]{1,0:T(8,128)}, u32[]{:S(2)}) copy-start(f32[24,32]{1,0:T(8,128)} %constant.62.clone.shift) | copy-start | bytes 9220
  89.0 24.0 %copy-start.14 = (bf16[2,252,128]{2,1,0:T(8,128)(2,1)S(1)}, bf16[2,252,128]{2,1,0:T(8,128)(2,1)}, u32[]{:S(2)}) copy-start(bf16[2,252,128]{2,1,0:T(8,128)(2,1)} %constant.61.clone.cols) | copy-start | bytes 387076
  89.0 24.0 %copy-start.15 = (f32[3,8,252]{2,1,0:T(8,128)S(1)}, f32[3,8,252]{2,1,0:T(8,128)}, u32[]{:S(2)}) copy-start(f32[3,8,252]{2,1,0:T(8,128)} %constant.60.clone.rows) | copy-start | bytes 72580
  95.4 17.6 %all-to-all-start.1 = ((f32[32,1,252]{2,1,0:T(1,128)}), f32[32,1,252]{2,1,0:T(1,128)S(1)}, u32[]{:S(2)}, u32[]{:S(2)}) async-start(f32[32,1,252]{2,1,0:T(1,128)} %get-tuple-element.75), calls=%async_computation.1 | async-start | bytes 65536 | tf_op jit(solution)/shard_map/all_to_all | solution.py:580
